TPU v7x, 256 devices: a whole 4x4x8 slice. The times are simulated.
256 devices in a mesh: dp: 32 (over x, z), tensor: 8 (over y, core).
Axes of the slice: x: 4, y: 4, z: 8, core: 2. Of those that a mesh axis runs over, the one named last changes fastest.
Arguments:
- vis_rows: bfloat16 [8, 256, 2, 3200], P(None, 'dp', None, 'tensor'), may hold values from -6 to 6
- ln_gain: float32 [2, 3200], replicated, may hold values from 0.25 to 1.75
- ln_bias: float32 [2, 3200], replicated, may hold values from -3 to 3
- proj_weight: bfloat16 [3200, 2, 8192], P('dp', None, 'tensor'), may hold values from -0.078125 to 0.078125
- text_rows: bfloat16 [32, 384, 8192], P('dp', None, 'tensor'), may hold values from -8 to 8
- attn_gain: float32 [8192], replicated, may hold values from 0.25 to 1.75
- w_query: bfloat16 [8192, 4096], P('dp', 'tensor'), may hold values from -0.088388348 to 0.088388348
- key_value_weight: bfloat16 [8192, 2, 1024], P('dp', None, 'tensor'), may hold values from -0.088388348 to 0.088388348
- tile_counts: int32 [32], replicated, may hold values from 1 to 16, 256 in all
- image_offsets: int32 [32], P('dp'), may hold values from 0 to 256
Outputs:
- attn_context: bfloat16 [32, 384, 4096], P('dp', None, 'tensor')
Inputs may be any that keep to these rules, and one draw needn't show every extreme that they name: tile_counts counts all 256 tiles, and its largest entry is exactly 16.
All inputs are finite; a program needn't handle non-finite values.
Results may differ from a plain program's by a relative error of at most 0.0074.
Values may be sent and summed in bfloat16 or wider, within the bound.
No kernel may reach another device: no remote copies, remote signals or barrier semaphores. Data moves between devices by JAX's collectives and lax.ppermute only.
A program may use at most 128 MiB of HBM per device.

v0:
```python
import jax
import jax.numpy as jnp
from jax import lax
from jax.experimental import pallas as pl
from jax.experimental.pallas import tpu as pltpu
from jax.sharding import Mesh, PartitionSpec as P


HEAD = 128
NX, NZ, NY, NC = 4, 8, 4, 2
SEQ = 384
SPAN = 128
WIDTH = 8192
vision_epsilon = 1e-06
decoder_epsilon = 1e-05
rope_base = 500000.0


def shift(array, axis, by):
    size = lax.axis_size(axis)
    return lax.ppermute(array, axis, [(i, (i + by) % size) for i in range(size)])


def exchange(array, axis):
    return lax.all_to_all(array, axis, 0, 0, tiled=True)


def ring4(array, axis):
    half = array.shape[0] // 2
    below = shift(array, axis, 1)
    above = shift(array, axis, -1)
    far_low = shift(below[:half], axis, 1)
    far_high = shift(above[half:], axis, -1)
    return [(array, 0, 0), (below, -1, 0), (above, 1, 0), (far_low, 2, 0), (far_high, 2, half)]


def ring8(array, axis):
    half = array.shape[0] // 2
    pieces = [(array, 0, 0)]
    below = above = array
    for step in (1, 2, 3):
        below = shift(below, axis, 1)
        above = shift(above, axis, -1)
        pieces += [(below, -step, 0), (above, step, 0)]
    pieces += [(shift(below[:half], axis, 1), 4, 0), (shift(above[half:], axis, -1), 4, half)]
    return pieces


def spread(array, axis):
    size = lax.axis_size(axis)
    return exchange(jnp.broadcast_to(array[None], (size, *array.shape)), axis)


def rope_tables():
    half = HEAD // 2
    exponents = jnp.arange(half, dtype=jnp.float32) * (2.0 / HEAD)
    frequency = rope_base ** (-exponents)
    positions = jnp.arange(SEQ, dtype=jnp.int32).astype(jnp.float32)
    angles = positions[:, None] * frequency[None, :]
    cosine, sine = jnp.cos(angles), jnp.sin(angles)
    return (
        jnp.concatenate([cosine, cosine], axis=1),
        jnp.concatenate([-sine, sine], axis=1),
    )


def decoder(where, text, image, query_w, keyval_w, gain, cosine, sine):
    arrays, plan = [], []
    for pair, name in ((text, "t"), (image, "i")):
        for flip, a in enumerate(pair):
            plan += [(name, len(arrays), n, flip) for n in range(NY)]
            arrays.append(a)
    query_at = len(arrays)
    arrays.append(query_w)
    weights = []
    for a, parts in keyval_w:
        for dx, dz, row, rows, at in parts:
            weights.append((len(arrays), dx, dz, row, rows, at, 512, 256))
        arrays.append(a)
    count = len(arrays)
    n_act, n_w = len(plan), len(weights) + 1

    def kernel(where_ref, *refs):
        srcs = refs[:count]
        gain_ref, cos_ref, sin_ref = refs[count : count + 3]
        out_ref = refs[count + 3]
        a_ref, i_ref, b_ref, q_ref, act_sem, w_sem = refs[count + 4 :]
        x, z, y, c = where_ref[0], where_ref[1], where_ref[2], where_ref[3]
        start, n_rows = where_ref[4], where_ref[5]

        acts = []
        for k, (name, n, yy, flip) in enumerate(plan):
            side = yy if name == "i" else lax.rem(y + (0, 3, 1, 2)[yy], NY)
            t = side * NC + (c if flip == 0 else 1 - c)
            target = (a_ref if name == "t" else i_ref).at[t]
            acts.append(pltpu.make_async_copy(srcs[n].at[yy], target, act_sem.at[k]))
        for copy in acts:
            copy.start()
        loads = [
            pltpu.make_async_copy(srcs[query_at], b_ref.at[:, pl.ds(0, 512)], w_sem.at[len(weights)])
        ]
        for k, (n, dx, dz, row, rows, at, col, cols) in enumerate(weights):
            d = lax.rem(x + (dx + NX), NX) * NZ + lax.rem(z + (dz + NZ), NZ)
            first = pl.multiple_of(d * 256 + row, 64)
            loads.append(
                pltpu.make_async_copy(
                    srcs[n].at[pl.ds(at, rows), :],
                    b_ref.at[pl.ds(first, rows), pl.ds(col, cols)],
                    w_sem.at[k],
                )
            )
        for copy in loads:
            copy.start()
        for copy in acts:
            copy.wait()
        p_at = lax.broadcasted_iota(jnp.int32, (SEQ, SPAN), 0) - start
        j_at = lax.broadcasted_iota(jnp.int32, (SEQ, SPAN), 1)
        pick = jnp.where((p_at == j_at) & (j_at < n_rows), 1.0, 0.0).astype(jnp.bfloat16)
        rows_at = lax.broadcasted_iota(jnp.int32, (SEQ, 1), 0) - start
        is_image = (rows_at >= 0) & (rows_at < n_rows)

        def insert(t, total):
            placed = jnp.dot(pick, i_ref[t], preferred_element_type=jnp.float32)
            value = jnp.where(is_image, placed, a_ref[t].astype(jnp.float32))
            a_ref[t] = value.astype(jnp.bfloat16)
            return total + jnp.sum(value * value, axis=1, keepdims=True)

        total = lax.fori_loop(0, 8, insert, jnp.zeros((SEQ, 1), jnp.float32))
        scale = lax.rsqrt(total * (1.0 / WIDTH) + decoder_epsilon)

        def normalize(t, carry):
            a_ref[t] = (
                a_ref[t].astype(jnp.float32) * scale * gain_ref[pl.ds(t, 1), :]
            ).astype(jnp.bfloat16)
            return carry

        lax.fori_loop(0, 8, normalize, 0)
        for copy in loads:
            copy.wait()
        q_ref[...] = jnp.zeros(q_ref.shape, jnp.float32)

        def project(t, carry):
            q_ref[...] += jnp.dot(
                a_ref[t], b_ref[pl.ds(t * 1024, 1024), :], preferred_element_type=jnp.float32
            )
            return carry

        lax.fori_loop(0, 8, project, 0)
        cos, sin = cos_ref[...], sin_ref[...]

        def rotated(value):
            return (value * cos + pltpu.roll(value, 64, 1) * sin).astype(jnp.bfloat16)

        key = rotated(q_ref[:, 512:640])
        value = q_ref[:, 640:768].astype(jnp.bfloat16)
        causal = lax.broadcasted_iota(jnp.int32, (SEQ, SEQ), 0) >= lax.broadcasted_iota(
            jnp.int32, (SEQ, SEQ), 1
        )
        for h in range(4):
            query = rotated(q_ref[:, h * HEAD : (h + 1) * HEAD])
            scores = lax.dot_general(
                query, key, (((1,), (1,)), ((), ())), preferred_element_type=jnp.float32
            ) * (HEAD ** (-0.5))
            scores = jnp.where(causal, scores, -1e30)
            top = jnp.max(scores, axis=1, keepdims=True)
            e = jnp.exp(scores - top)
            w = (e / jnp.sum(e, axis=1, keepdims=True)).astype(jnp.bfloat16)
            out_ref[:, h * HEAD : (h + 1) * HEAD] = jnp.dot(
                w, value, preferred_element_type=jnp.float32
            ).astype(jnp.bfloat16)

    any_spec = pl.BlockSpec(memory_space=pl.ANY)
    vmem = pl.BlockSpec(memory_space=pltpu.VMEM)
    return pl.pallas_call(
        kernel,
        out_shape=jax.ShapeDtypeStruct((SEQ, 512), jnp.bfloat16),
        in_specs=[pl.BlockSpec(memory_space=pltpu.SMEM)] + [any_spec] * count + [vmem] * 3,
        out_specs=vmem,
        scratch_shapes=[
            pltpu.VMEM((8, SEQ, 1024), jnp.bfloat16),
            pltpu.VMEM((8, SPAN, 1024), jnp.bfloat16),
            pltpu.VMEM((WIDTH, 768), jnp.bfloat16),
            pltpu.VMEM((SEQ, 768), jnp.float32),
            pltpu.SemaphoreType.DMA((n_act,)),
            pltpu.SemaphoreType.DMA((n_w,)),
        ],
        compiler_params=pltpu.CompilerParams(vmem_limit_bytes=48 * 1024 * 1024),
        name="decoder",
    )(where, *arrays, gain, cosine, sine)


def vision(vis_rows, ln_gain, ln_bias, proj_weight, x, z, y, c):
    tokens = vis_rows.shape[0] * vis_rows.shape[1]
    own_w = jnp.swapaxes(proj_weight, 0, 1).reshape(200, 1024)
    below_w = shift(own_w, "x", 1)
    above_w = shift(own_w, "x", -1)
    far_w = shift(own_w, "x", 2)
    part = vis_rows.reshape(tokens, 2, 400).astype(jnp.float32)
    mean = jnp.mean(part, axis=(1, 2))
    dev = jnp.sum(jnp.square(part - mean[:, None, None]), axis=(1, 2))
    stats = jnp.stack([mean, dev])
    other = shift(stats, "c", 1)
    mean2 = (stats[0] + other[0]) * 0.5
    dev2 = stats[1] + other[1] + 400.0 * jnp.square(stats[0] - other[0])
    stats = jnp.stack([mean2, dev2])
    all_stats = jnp.stack([stats, shift(stats, "y", 1), shift(stats, "y", -1), shift(stats, "y", 2)])
    mean = jnp.mean(all_stats[:, 0], axis=0)
    variance = (
        jnp.sum(all_stats[:, 1], axis=0)
        + 1600.0 * jnp.sum(jnp.square(all_stats[:, 0] - mean[None]), axis=0)
    ) * (1.0 / 6400.0)
    t = y * NC + c
    gain = lax.dynamic_slice_in_dim(ln_gain, t * 400, 400, 1)
    bias = lax.dynamic_slice_in_dim(ln_bias, t * 400, 400, 1)
    normed = (
        (part - mean[:, None, None]) * lax.rsqrt(variance + vision_epsilon)[:, None, None] * gain
        + bias
    ).astype(jnp.bfloat16)
    blocks = jnp.moveaxis(normed.reshape(tokens, 2, 4, 100), 2, 0).reshape(4, tokens, 200)
    mask = (jnp.arange(2, dtype=jnp.int32) == c)[:, None, None, None, None]
    outgoing = jnp.where(mask, blocks[None, :, None], jnp.zeros((), jnp.bfloat16))
    outgoing = jnp.broadcast_to(outgoing, (2, 4, 2, tokens, 200)).reshape(16, tokens, 200)
    incoming = exchange(outgoing, ("z", "c")).reshape(8, 2, tokens, 200)
    mine = lax.dynamic_index_in_dim(incoming, z // 4, 1, keepdims=False).reshape(8 * tokens, 200)
    acts = spread(mine, "y")
    partial = None
    for dx, w in ((0, own_w), (-1, below_w), (1, above_w), (2, far_w)):
        a = lax.dynamic_index_in_dim(acts, lax.rem(x + dx + 4, 4), 0, keepdims=False)
        term = jnp.dot(a, w, preferred_element_type=jnp.float32)
        partial = term if partial is None else partial + term
    partial = partial.astype(jnp.bfloat16).reshape(8, tokens, 1024)
    parts = exchange(partial, "z")
    total = jnp.sum(parts.astype(jnp.float32), axis=0)
    return total.astype(jnp.bfloat16).reshape(8, 8, 1024)


def step(
    vis_rows, ln_gain, ln_bias, proj_weight, text_rows, attn_gain, w_query,
    key_value_weight, tile_counts, image_offsets,
):
    x, z = lax.axis_index("x"), lax.axis_index("z")
    y, c = lax.axis_index("y"), lax.axis_index("c")
    dp = x * NZ + z
    tile_ends = jnp.cumsum(tile_counts)
    tile_firsts = tile_ends - tile_counts
    sample_ids = jnp.arange(32, dtype=jnp.int32)
    tiles_here = jnp.arange(8, dtype=jnp.int32) * 32 + dp
    owners = jnp.sum((tile_ends[None, :] <= tiles_here[:, None]).astype(jnp.int32), axis=1)
    is_mine = sample_ids == dp
    my_first = jnp.sum(jnp.where(is_mine, tile_firsts, 0))
    my_count = jnp.sum(jnp.where(is_mine, tile_counts, 0))

    image = vision(vis_rows, ln_gain, ln_bias, proj_weight, x, z, y, c)

    pieces = ring4(text_rows[0], "y")
    own_text = jnp.concatenate([a for a, _, _ in pieces], axis=0).reshape(4, SEQ, 1024)
    text = (own_text, shift(own_text, "c", 1))

    query_w = lax.all_gather(w_query, ("x", "z"), axis=0, tiled=True)

    along_z = ring8(key_value_weight.reshape(256, 256), "z")
    stack = jnp.concatenate([a for a, _, _ in along_z], axis=0)
    offsets, at = [], 0
    for a, dz, row in along_z:
        offsets.append((dz, row, a.shape[0], at))
        at += a.shape[0]
    keyval_w = []
    for a, dx, first in ring4(stack, "x"):
        parts = [
            (dx, dz, row, rows, at - first)
            for dz, row, rows, at in offsets
            if first <= at and at + rows <= first + a.shape[0]
        ]
        keyval_w.append((a, parts))

    slots = jnp.zeros((32, 8, 1024), jnp.bfloat16)
    for r in range(8):
        slots = jnp.where((owners[r] == sample_ids)[:, None, None], image[r][None], slots)
    received = exchange(slots, ("x", "z"))
    sources = (my_first + jnp.arange(16, dtype=jnp.int32)) % 32
    mine = received[sources].reshape(SPAN, 1024)
    own_image = spread(mine, "y")
    image_all = (own_image, shift(own_image, "c", 1))

    where = jnp.stack([x, z, y, c, image_offsets[0], my_count * 8]).astype(jnp.int32)
    cosine, sine = rope_tables()
    out = decoder(
        where, text, image_all, query_w, keyval_w, attn_gain.reshape(8, 1024), cosine, sine
    )
    return out[None]


def solution(mesh):
    fine = Mesh(mesh.devices.reshape(NX, NZ, NY, NC), ("x", "z", "y", "c"))
    dp, tensor = ("x", "z"), ("y", "c")
    in_specs = (
        P(None, dp, None, tensor), P(), P(), P(dp, None, tensor), P(dp, None, tensor), P(),
        P(dp, tensor), P(dp, None, tensor), P(), P(dp),
    )
    return jax.shard_map(
        step, mesh=fine, in_specs=in_specs, out_specs=P(dp, None, tensor), check_vma=False
    )
```

profile of v0, /device:TPU:6, one launch (start us, length us, event | category | flops | bytes accessed | tf_op | source)
XLA Modules:
  0.0 238.6 jit_solution(3001669350291671225)
XLA Ops:
  6.5 0.7 all-gather.2.cloned.1.call-update
  7.3 1.2 convert_reduce_fusion
  8.5 1.3 multiply_reduce_fusion
  10.0 0.8 constant_dynamic-slice_fusion.1
  11.2 1.7 collective-permute-start.6
  12.8 1.7 collective-permute-start.7
  14.5 2.0 collective-permute-start.8
  16.5 1.1 reshape.244
  17.8 1.8 collective-permute-done.8
  20.2 0.9 broadcast_in_dim.164
  21.1 8.6 %all-to-all-start = ((bf16[16,64,200]{2,1,0:T(8,128)(2,1)}), bf16[16,64,200]{2,1,0:T(8,128)(2,1)S(1)}, u32[]{:S(2)}, u32[]{:S(2)}) async-start(bf16[16,64,200]{2,1,0:T(8,128)(2,1)} %bitcast.15), calls=%async_computation | async-start | bytes 1048576 | tf_op jit(solution)/shard_map/all_to_all | solution.py:25
  29.7 18.5 %all-to-all-done = bf16[16,64,200]{2,1,0:T(8,128)(2,1)S(1)} async-done(((bf16[16,64,200]{2,1,0:T(8,128)(2,1)}), bf16[16,64,200]{2,1,0:T(8,128)(2,1)S(1)}, u32[]{:S(2)}, u32[]{:S(2)}) %all-to-all-start) | async-done | bytes 409632 | tf_op jit(solution)/shard_map/all_to_all | solution.py:25
  48.3 1.0 broadcast_in_dim.166
  49.3 5.8 %all-to-all-start.1 = ((bf16[4,512,200]{1,2,0:T(8,128)(2,1)}), bf16[4,512,200]{1,2,0:T(8,128)(2,1)S(1)}, u32[]{:S(2)}, u32[]{:S(2)}) async-start(bf16[4,512,200]{1,2,0:T(8,128)(2,1)} %broadcast_in_dim.166), calls=%async_computation.1 | async-start | bytes 1638400 | tf_op jit(solution)/shard_map/all_to_all | solution.py:25
  55.4 2.0 collective-permute-start.10
  57.4 2.1 collective-permute-start.11
  59.5 8.6 %all-to-all-done.1 = bf16[4,512,200]{1,2,0:T(8,128)(2,1)S(1)} async-done(((bf16[4,512,200]{1,2,0:T(8,128)(2,1)}), bf16[4,512,200]{1,2,0:T(8,128)(2,1)S(1)}, u32[]{:S(2)}, u32[]{:S(2)}) %all-to-all-start.1) | async-done | bytes 819232 | tf_op jit(solution)/shard_map/all_to_all | solution.py:25
  70.1 15.1 %collective-permute-done.11 = bf16[200,1024]{1,0:T(8,128)(2,1)S(1)} collective-permute-done((bf16[200,1024]{1,0:T(8,128)(2,1)S(1)}, bf16[200,1024]{1,0:T(8,128)(2,1)S(1)}, u32[]{:S(2)}, u32[]{:S(2)}) %collective-permute-start.11) | collective-permute-done | bytes 409632 | tf_op jit(solution)/shard_map/ppermute | solution.py:21
  85.3 1.5 add_convert_fusion
  86.7 3.6 %all-to-all-start.2 = ((bf16[8,64,1024]{2,1,0:T(8,128)(2,1)}), bf16[8,64,1024]{2,1,0:T(8,128)(2,1)S(1)}, u32[]{:S(2)}, u32[]{:S(2)}) async-start(bf16[8,64,1024]{2,1,0:T(8,128)(2,1)} %bitcast.23), calls=%async_computation.2 | async-start | bytes 2097152 | tf_op jit(solution)/shard_map/all_to_all | solution.py:25
  90.3 2.0 collective-permute-start.13
  92.3 1.3 collective-permute-start.14
  93.7 2.1 collective-permute-start
  95.8 1.2 collective-permute-start.1
  97.5 0.7 fusion.30
  98.1 1.2 iota_compare_fusion
  99.3 1.3 iota_compare_fusion.2
  100.7 2.1 constant_dynamic-update-slice_fusion.4
  102.8 8.7 %collective-permute-done = bf16[384,1024]{1,0:T(8,128)(2,1)S(1)} collective-permute-done((bf16[384,1024]{1,0:T(8,128)(2,1)}, bf16[384,1024]{1,0:T(8,128)(2,1)S(1)}, u32[]{:S(2)}, u32[]{:S(2)}) %collective-permute-start) | collective-permute-done | bytes 786464 | tf_op jit(solution)/shard_map/ppermute | solution.py:21
  111.5 1.2 collective-permute-start.2
  112.7 1.3 iota_compare_fusion.4
  114.1 1.0 slice.117
  115.1 2.2 collective-permute-start.3
  117.3 1.3 iota_compare_fusion.6
  118.6 1.0 constant_dynamic-update-slice_fusion.3
  119.6 2.1 constant_dynamic-update-slice_fusion.2
  121.6 0.8 constant_dynamic-update-slice_fusion.1
  122.4 0.9 collective-permute-done.3
  123.3 0.8 constant_dynamic-update-slice_fusion
  124.1 5.6 %all-to-all-done.2 = bf16[8,64,1024]{2,1,0:T(8,128)(2,1)S(1)} async-done(((bf16[8,64,1024]{2,1,0:T(8,128)(2,1)}), bf16[8,64,1024]{2,1,0:T(8,128)(2,1)S(1)}, u32[]{:S(2)}, u32[]{:S(2)}) %all-to-all-start.2) | async-done | bytes 1048608 | tf_op jit(solution)/shard_map/all_to_all | solution.py:25
  129.9 1.2 select_select_fusion
  131.1 6.5 %all-to-all-start.3 = ((bf16[32,8,1024]{2,1,0:T(8,128)(2,1)}), bf16[32,8,1024]{2,1,0:T(8,128)(2,1)S(1)}, u32[]{:S(2)}, u32[]{:S(2)}) async-start(bf16[32,8,1024]{2,1,0:T(8,128)(2,1)} %select_select_fusion), calls=%async_computation.3 | async-start | bytes 1048576 | tf_op jit(solution)/shard_map/all_to_all | solution.py:25
  138.2 0.7 fusion.27
  138.9 1.5 collective-permute-start.15
  140.5 1.8 collective-permute-start.16
  142.3 14.9 %collective-permute-done.15 = bf16[256,256]{1,0:T(8,128)(2,1)S(1)} collective-permute-done((bf16[256,256]{1,0:T(8,128)(2,1)S(1)}, bf16[256,256]{1,0:T(8,128)(2,1)S(1)}, u32[]{:S(2)}, u32[]{:S(2)}) %collective-permute-start.15) | collective-permute-done | bytes 131104 | tf_op jit(solution)/shard_map/ppermute | solution.py:21
  157.2 1.1 collective-permute-start.17
  158.3 2.2 collective-permute-start.18
  160.5 2.9 %collective-permute-done.17 = bf16[256,256]{1,0:T(8,128)(2,1)S(1)} collective-permute-done((bf16[256,256]{1,0:T(8,128)(2,1)S(1)}, bf16[256,256]{1,0:T(8,128)(2,1)S(1)}, u32[]{:S(2)}, u32[]{:S(2)}) %collective-permute-start.17) | collective-permute-done | bytes 131104 | tf_op jit(solution)/shard_map/ppermute | solution.py:21
  163.4 3.3 %collective-permute-start.20 = (bf16[128,256]{1,0:T(8,128)(2,1)S(1)}, bf16[128,256]{1,0:T(8,128)(2,1)S(1)}, u32[]{:S(2)}, u32[]{:S(2)}) collective-permute-start(bf16[128,256]{1,0:T(8,128)(2,1)S(1)} %slice.129), channel_id=1, source_target_pairs={{0,56},{8,0},{16,8},{24,16},{32,24},{40,32},{48,40},{56,48},{1,57}... | collective-permute-start | bytes 196616 | tf_op jit(solution)/shard_map/ppermute | solution.py:21
  167.4 1.1 broadcast_in_dim.184
  168.4 4.5 %all-to-all-start.4 = ((bf16[4,128,1024]{2,1,0:T(8,128)(2,1)}), bf16[4,128,1024]{2,1,0:T(8,128)(2,1)S(1)}, u32[]{:S(2)}, u32[]{:S(2)}) async-start(bf16[4,128,1024]{2,1,0:T(8,128)(2,1)} %broadcast_in_dim.184), calls=%async_computation.4 | async-start | bytes 2097152 | tf_op jit(solution)/shard_map/all_to_all | solution.py:25
  173.0 1.3 collective-permute-start.21
  174.3 0.8 collective-permute-start.22
  175.1 10.8 %all-to-all-done.4.refs_2_ = bf16[4,128,1024]{2,1,0:T(8,128)(2,1)S(1)} async-done(((bf16[4,128,1024]{2,1,0:T(8,128)(2,1)}), bf16[4,128,1024]{2,1,0:T(8,128)(2,1)S(1)}, u32[]{:S(2)}, u32[]{:S(2)}) %all-to-all-start.4) | async-done | bytes 1048608 | tf_op jit(solution)/shard_map/all_to_all | solution.py:25
  185.9 9.6 %collective-permute-done.21.refs_6_ = bf16[2048,256]{1,0:T(8,128)(2,1)S(1)} collective-permute-done((bf16[2048,256]{1,0:T(8,128)(2,1)S(1)}, bf16[2048,256]{1,0:T(8,128)(2,1)S(1)}, u32[]{:S(2)}, u32[]{:S(2)}) %collective-permute-start.21) | collective-permute-done | bytes 1048608 | tf_op jit(solution)/shard_map/ppermute | solution.py:21
  195.5 0.8 slice.130
  196.4 2.4 %collective-permute-start.23 = (bf16[1024,256]{1,0:T(8,128)(2,1)}, bf16[1024,256]{1,0:T(8,128)(2,1)}, u32[]{:S(2)}, u32[]{:S(2)}) collective-permute-start(bf16[1024,256]{1,0:T(8,128)(2,1)} %slice.130), channel_id=1, source_target_pairs={{0,64},{64,128},{128,192},{192,0},{1,65},{65,129},{129,193},{193,1... | collective-permute-start | bytes 1572872 | tf_op jit(solution)/shard_map/ppermute | solution.py:21
  198.8 1.9 slice.131
  202.7 0.8 fusion.19
  203.7 3.6 %collective-permute-done.23.refs_8_ = bf16[1024,256]{1,0:T(8,128)(2,1)} collective-permute-done((bf16[1024,256]{1,0:T(8,128)(2,1)}, bf16[1024,256]{1,0:T(8,128)(2,1)}, u32[]{:S(2)}, u32[]{:S(2)}) %collective-permute-start.23) | collective-permute-done | bytes 524320 | tf_op jit(solution)/shard_map/ppermute | solution.py:21
  207.2 5.1 %collective-permute-done.24.refs_9_ = bf16[1024,256]{1,0:T(8,128)(2,1)} collective-permute-done((bf16[1024,256]{1,0:T(8,128)(2,1)}, bf16[1024,256]{1,0:T(8,128)(2,1)}, u32[]{:S(2)}, u32[]{:S(2)}) %collective-permute-start.24) | collective-permute-done | bytes 524320 | tf_op jit(solution)/shard_map/ppermute | solution.py:21
  212.4 0.7 copy-done
  213.2 18.5 %decoder.1 = bf16[384,512]{1,0:T(8,128)(2,1)} custom-call(s32[6]{0:T(128)S(1)} %stack.50.where_ref, bf16[4,384,1024]{2,1,0:T(8,128)(2,1)} %bitcast.6.refs_0_, bf16[4,384,1024]{2,1,0:T(8,128)(2,1)} %collective-permute-done.4.refs_1_, bf16[4,128,1024]{2,1,0:T(8,128)(2,1)S(1)} %all-to-all-done.4.refs_2_, bf16[4,128,1024]{2,1,0:T(8,128)(2,1)} %collective-permute-done.12.refs_3_, ...), custom_call_target="tpu_custom_call" | custom-call | tf_op jit(solution)/shard_map/decoder/pallas_call | solution.py:174
  (87 shorter events, 6.8 us)
Async XLA Ops:
  6.5 205.9 %all-gather.2.cloned.1.call-start = ((), (), s32[]{:S(2)}) async-start(), calls=%async_computation.5 | async-start | bytes 8650752 | tf_op jit(solution)/shard_map/all_gather | solution.py:259
  9.9 1.2 collective-permute-start.5
  11.2 6.6 %collective-permute-start.6 = (f32[2,64]{1,0:T(2,128)S(1)}, f32[2,64]{1,0:T(2,128)S(1)}, u32[]{:S(2)}, u32[]{:S(2)}) collective-permute-start(f32[2,64]{1,0:T(2,128)S(1)} %get-tuple-element.24), channel_id=1, source_target_pairs={{0,2},{2,4},{4,6},{6,0},{1,3},{3,5},{5,7},{7,1},{8,10},{10,12},{12... | collective-permute-start | bytes 1544 | tf_op jit(solution)/shard_map/ppermute | solution.py:21
  12.8 4.9 %collective-permute-start.7 = (f32[2,64]{1,0:T(2,128)S(1)}, f32[2,64]{1,0:T(2,128)S(1)}, u32[]{:S(2)}, u32[]{:S(2)}) collective-permute-start(f32[2,64]{1,0:T(2,128)S(1)} %get-tuple-element.24), channel_id=1, source_target_pairs={{0,6},{2,0},{4,2},{6,4},{1,7},{3,1},{5,3},{7,5},{8,14},{10,8},{12,... | collective-permute-start | bytes 1544 | tf_op jit(solution)/shard_map/ppermute | solution.py:21
  14.5 5.1 %collective-permute-start.8 = (f32[2,64]{1,0:T(2,128)S(1)}, f32[2,64]{1,0:T(2,128)S(1)}, u32[]{:S(2)}, u32[]{:S(2)}) collective-permute-start(f32[2,64]{1,0:T(2,128)S(1)} %get-tuple-element.24), channel_id=1, source_target_pairs={{0,4},{2,6},{4,0},{6,2},{1,5},{3,7},{5,1},{7,3},{8,12},{10,14},{12... | collective-permute-start | bytes 1544 | tf_op jit(solution)/shard_map/ppermute | solution.py:21
  20.0 35.2 %copy-start.2 = (bf16[100,2,1024]{2,1,0:T(2,128)(2,1)S(1)}, bf16[100,2,1024]{2,1,0:T(2,128)(2,1)}, u32[]{:S(2)}) copy-start(bf16[100,2,1024]{2,1,0:T(2,128)(2,1)} %param.13) | copy-start | bytes 1228804
  21.1 27.1 %all-to-all-start = ((bf16[16,64,200]{2,1,0:T(8,128)(2,1)}), bf16[16,64,200]{2,1,0:T(8,128)(2,1)S(1)}, u32[]{:S(2)}, u32[]{:S(2)}) async-start(bf16[16,64,200]{2,1,0:T(8,128)(2,1)} %bitcast.15), calls=%async_computation | async-start | bytes 1048576 | tf_op jit(solution)/shard_map/all_to_all | solution.py:25
  49.3 18.7 %all-to-all-start.1 = ((bf16[4,512,200]{1,2,0:T(8,128)(2,1)}), bf16[4,512,200]{1,2,0:T(8,128)(2,1)S(1)}, u32[]{:S(2)}, u32[]{:S(2)}) async-start(bf16[4,512,200]{1,2,0:T(8,128)(2,1)} %broadcast_in_dim.166), calls=%async_computation.1 | async-start | bytes 1638400 | tf_op jit(solution)/shard_map/all_to_all | solution.py:25
  55.3 13.3 %collective-permute-start.9 = (bf16[200,1024]{1,0:T(8,128)(2,1)S(1)}, bf16[200,1024]{1,0:T(8,128)(2,1)S(1)}, u32[]{:S(2)}, u32[]{:S(2)}) collective-permute-start(bf16[200,1024]{1,0:T(8,128)(2,1)S(1)} %reshape.231), channel_id=1, source_target_pairs={{0,64},{64,128},{128,192},{192,0},{1,65},{65,129},{129,193},{193,1... | collective-permute-start | bytes 1228808 | tf_op jit(solution)/shard_map/ppermute | solution.py:21
  55.4 14.2 %collective-permute-start.10 = (bf16[200,1024]{1,0:T(8,128)(2,1)S(1)}, bf16[200,1024]{1,0:T(8,128)(2,1)S(1)}, u32[]{:S(2)}, u32[]{:S(2)}) collective-permute-start(bf16[200,1024]{1,0:T(8,128)(2,1)S(1)} %reshape.231), channel_id=1, source_target_pairs={{0,192},{64,0},{128,64},{192,128},{1,193},{65,1},{129,65},{193,129... | collective-permute-start | bytes 1228808 | tf_op jit(solution)/shard_map/ppermute | solution.py:21
  57.4 27.8 %collective-permute-start.11 = (bf16[200,1024]{1,0:T(8,128)(2,1)S(1)}, bf16[200,1024]{1,0:T(8,128)(2,1)S(1)}, u32[]{:S(2)}, u32[]{:S(2)}) collective-permute-start(bf16[200,1024]{1,0:T(8,128)(2,1)S(1)} %reshape.231), channel_id=1, source_target_pairs={{0,128},{64,192},{128,0},{192,64},{1,129},{65,193},{129,1},{193,65... | collective-permute-start | bytes 1228808 | tf_op jit(solution)/shard_map/ppermute | solution.py:21
  70.1 20.2 %copy-start.1 = (bf16[256,2,128]{2,1,0:T(2,128)(2,1)S(1)}, bf16[256,2,128]{2,1,0:T(2,128)(2,1)}, u32[]{:S(2)}) copy-start(bf16[256,2,128]{2,1,0:T(2,128)(2,1)} %param.17) | copy-start | bytes 393220
  70.1 26.9 %copy-start.4 = (s32[32]{0:T(128)S(1)}, s32[32]{0:T(128)}, u32[]{:S(2)}) copy-start(s32[32]{0:T(128)} %param.18) | copy-start | bytes 388
  86.7 43.0 %all-to-all-start.2 = ((bf16[8,64,1024]{2,1,0:T(8,128)(2,1)}), bf16[8,64,1024]{2,1,0:T(8,128)(2,1)S(1)}, u32[]{:S(2)}, u32[]{:S(2)}) async-start(bf16[8,64,1024]{2,1,0:T(8,128)(2,1)} %bitcast.23), calls=%async_computation.2 | async-start | bytes 2097152 | tf_op jit(solution)/shard_map/all_to_all | solution.py:25
  90.3 48.6 %collective-permute-start.13 = (bf16[256,256]{1,0:T(8,128)(2,1)S(1)}, bf16[256,256]{1,0:T(8,128)(2,1)S(1)}, u32[]{:S(2)}, u32[]{:S(2)}) collective-permute-start(bf16[256,256]{1,0:T(8,128)(2,1)S(1)} %bitcast.64), channel_id=1, source_target_pairs={{0,8},{8,16},{16,24},{24,32},{32,40},{40,48},{48,56},{56,0},{1,9},... | collective-permute-start | bytes 393224 | tf_op jit(solution)/shard_map/ppermute | solution.py:21
  92.3 48.1 %collective-permute-start.14 = (bf16[256,256]{1,0:T(8,128)(2,1)S(1)}, bf16[256,256]{1,0:T(8,128)(2,1)S(1)}, u32[]{:S(2)}, u32[]{:S(2)}) collective-permute-start(bf16[256,256]{1,0:T(8,128)(2,1)S(1)} %bitcast.65), channel_id=1, source_target_pairs={{0,56},{8,0},{16,8},{24,16},{32,24},{40,32},{48,40},{56,48},{1,57}... | collective-permute-start | bytes 393224 | tf_op jit(solution)/shard_map/ppermute | solution.py:21
  93.7 17.8 %collective-permute-start = (bf16[384,1024]{1,0:T(8,128)(2,1)}, bf16[384,1024]{1,0:T(8,128)(2,1)S(1)}, u32[]{:S(2)}, u32[]{:S(2)}) collective-permute-start(bf16[384,1024]{1,0:T(8,128)(2,1)} %bitcast.5), channel_id=1, source_target_pairs={{0,2},{2,4},{4,6},{6,0},{1,3},{3,5},{5,7},{7,1},{8,10},{10,12},{12... | collective-permute-start | bytes 2359304 | tf_op jit(solution)/shard_map/ppermute | solution.py:21
  95.8 18.2 %collective-permute-start.1 = (bf16[384,1024]{1,0:T(8,128)(2,1)}, bf16[384,1024]{1,0:T(8,128)(2,1)}, u32[]{:S(2)}, u32[]{:S(2)}) collective-permute-start(bf16[384,1024]{1,0:T(8,128)(2,1)} %bitcast.5), channel_id=1, source_target_pairs={{0,6},{2,0},{4,2},{6,4},{1,7},{3,1},{5,3},{7,5},{8,14},{10,8},{12,... | collective-permute-start | bytes 2359304 | tf_op jit(solution)/shard_map/ppermute | solution.py:21
  111.5 10.1 %collective-permute-start.2 = (bf16[192,1024]{1,0:T(8,128)(2,1)S(1)}, bf16[192,1024]{1,0:T(8,128)(2,1)S(1)}, u32[]{:S(2)}, u32[]{:S(2)}) collective-permute-start(bf16[192,1024]{1,0:T(8,128)(2,1)S(1)} %slice.116), channel_id=1, source_target_pairs={{0,2},{2,4},{4,6},{6,0},{1,3},{3,5},{5,7},{7,1},{8,10},{10,12},{12... | collective-permute-start | bytes 1179656 | tf_op jit(solution)/shard_map/ppermute | solution.py:21
  115.1 8.2 %collective-permute-start.3 = (bf16[192,1024]{1,0:T(8,128)(2,1)S(1)}, bf16[192,1024]{1,0:T(8,128)(2,1)S(1)}, u32[]{:S(2)}, u32[]{:S(2)}) collective-permute-start(bf16[192,1024]{1,0:T(8,128)(2,1)S(1)} %slice.117), channel_id=1, source_target_pairs={{0,6},{2,0},{4,2},{6,4},{1,7},{3,1},{5,3},{7,5},{8,14},{10,8},{12,... | collective-permute-start | bytes 1179656 | tf_op jit(solution)/shard_map/ppermute | solution.py:21
  124.1 88.3 %collective-permute-start.4 = (bf16[4,384,1024]{2,1,0:T(8,128)(2,1)}, bf16[4,384,1024]{2,1,0:T(8,128)(2,1)}, u32[]{:S(2)}, u32[]{:S(2)}) collective-permute-start(bf16[4,384,1024]{2,1,0:T(8,128)(2,1)} %bitcast.6.refs_0_), channel_id=1, source_target_pairs={{0,1},{1,0},{2,3},{3,2},{4,5},{5,4},{6,7},{7,6},{8,9},{9,8},{10,11... | collective-permute-start | bytes 9437192 | tf_op jit(solution)/shard_map/ppermute | solution.py:21
  131.1 35.7 %all-to-all-start.3 = ((bf16[32,8,1024]{2,1,0:T(8,128)(2,1)}), bf16[32,8,1024]{2,1,0:T(8,128)(2,1)S(1)}, u32[]{:S(2)}, u32[]{:S(2)}) async-start(bf16[32,8,1024]{2,1,0:T(8,128)(2,1)} %select_select_fusion), calls=%async_computation.3 | async-start | bytes 1048576 | tf_op jit(solution)/shard_map/all_to_all | solution.py:25
  138.9 18.3 %collective-permute-start.15 = (bf16[256,256]{1,0:T(8,128)(2,1)S(1)}, bf16[256,256]{1,0:T(8,128)(2,1)S(1)}, u32[]{:S(2)}, u32[]{:S(2)}) collective-permute-start(bf16[256,256]{1,0:T(8,128)(2,1)S(1)} %collective-permute-done.13), channel_id=1, source_target_pairs={{0,8},{8,16},{16,24},{24,32},{32,40},{40,48},{48,56},{56,0},{1,9},... | collective-permute-start | bytes 393224 | tf_op jit(solution)/shard_map/ppermute | solution.py:21
  140.5 17.8 %collective-permute-start.16 = (bf16[256,256]{1,0:T(8,128)(2,1)S(1)}, bf16[256,256]{1,0:T(8,128)(2,1)S(1)}, u32[]{:S(2)}, u32[]{:S(2)}) collective-permute-start(bf16[256,256]{1,0:T(8,128)(2,1)S(1)} %collective-permute-done.14), channel_id=1, source_target_pairs={{0,56},{8,0},{16,8},{24,16},{32,24},{40,32},{48,40},{56,48},{1,57}... | collective-permute-start | bytes 393224 | tf_op jit(solution)/shard_map/ppermute | solution.py:21
  157.2 6.2 %collective-permute-start.17 = (bf16[256,256]{1,0:T(8,128)(2,1)S(1)}, bf16[256,256]{1,0:T(8,128)(2,1)S(1)}, u32[]{:S(2)}, u32[]{:S(2)}) collective-permute-start(bf16[256,256]{1,0:T(8,128)(2,1)S(1)} %collective-permute-done.15), channel_id=1, source_target_pairs={{0,8},{8,16},{16,24},{24,32},{32,40},{40,48},{48,56},{56,0},{1,9},... | collective-permute-start | bytes 393224 | tf_op jit(solution)/shard_map/ppermute | solution.py:21
  158.3 5.1 %collective-permute-start.18 = (bf16[256,256]{1,0:T(8,128)(2,1)S(1)}, bf16[256,256]{1,0:T(8,128)(2,1)S(1)}, u32[]{:S(2)}, u32[]{:S(2)}) collective-permute-start(bf16[256,256]{1,0:T(8,128)(2,1)S(1)} %collective-permute-done.16), channel_id=1, source_target_pairs={{0,56},{8,0},{16,8},{24,16},{32,24},{40,32},{48,40},{56,48},{1,57}... | collective-permute-start | bytes 393224 | tf_op jit(solution)/shard_map/ppermute | solution.py:21
  163.4 9.5 %collective-permute-start.19 = (bf16[128,256]{1,0:T(8,128)(2,1)S(1)}, bf16[128,256]{1,0:T(8,128)(2,1)S(1)}, u32[]{:S(2)}, u32[]{:S(2)}) collective-permute-start(bf16[128,256]{1,0:T(8,128)(2,1)S(1)} %slice.128), channel_id=1, source_target_pairs={{0,8},{8,16},{16,24},{24,32},{32,40},{40,48},{48,56},{56,0},{1,9},... | collective-permute-start | bytes 196616 | tf_op jit(solution)/shard_map/ppermute | solution.py:21
  163.4 9.5 %collective-permute-start.20 = (bf16[128,256]{1,0:T(8,128)(2,1)S(1)}, bf16[128,256]{1,0:T(8,128)(2,1)S(1)}, u32[]{:S(2)}, u32[]{:S(2)}) collective-permute-start(bf16[128,256]{1,0:T(8,128)(2,1)S(1)} %slice.129), channel_id=1, source_target_pairs={{0,56},{8,0},{16,8},{24,16},{32,24},{40,32},{48,40},{56,48},{1,57}... | collective-permute-start | bytes 196616 | tf_op jit(solution)/shard_map/ppermute | solution.py:21
  166.8 35.2 %copy-start.3 = (f32[8192]{0:T(1024)S(1)}, f32[8192]{0:T(1024)}, u32[]{:S(2)}) copy-start(f32[8192]{0:T(1024)} %param.15) | copy-start | bytes 98308
  168.4 17.5 %all-to-all-start.4 = ((bf16[4,128,1024]{2,1,0:T(8,128)(2,1)}), bf16[4,128,1024]{2,1,0:T(8,128)(2,1)S(1)}, u32[]{:S(2)}, u32[]{:S(2)}) async-start(bf16[4,128,1024]{2,1,0:T(8,128)(2,1)} %broadcast_in_dim.184), calls=%async_computation.4 | async-start | bytes 2097152 | tf_op jit(solution)/shard_map/all_to_all | solution.py:25
  173.0 22.6 %collective-permute-start.21 = (bf16[2048,256]{1,0:T(8,128)(2,1)S(1)}, bf16[2048,256]{1,0:T(8,128)(2,1)S(1)}, u32[]{:S(2)}, u32[]{:S(2)}) collective-permute-start(bf16[2048,256]{1,0:T(8,128)(2,1)S(1)} %constant_dynamic-update-slice_fusion.5.refs_5_), channel_id=1, source_target_pairs={{0,64},{64,128},{128,192},{192,0},{1,65},{65,129},{129,193},{193,1... | collective-permute-start | bytes 3145736 | tf_op jit(solution)/shard_map/ppermute | solution.py:21
  174.3 24.6 %collective-permute-start.22 = (bf16[2048,256]{1,0:T(8,128)(2,1)S(1)}, bf16[2048,256]{1,0:T(8,128)(2,1)}, u32[]{:S(2)}, u32[]{:S(2)}) collective-permute-start(bf16[2048,256]{1,0:T(8,128)(2,1)S(1)} %constant_dynamic-update-slice_fusion.5.refs_5_), channel_id=1, source_target_pairs={{0,192},{64,0},{128,64},{192,128},{1,193},{65,1},{129,65},{193,129... | collective-permute-start | bytes 3145736 | tf_op jit(solution)/shard_map/ppermute | solution.py:21
  185.9 26.5 %collective-permute-start.12 = (bf16[4,128,1024]{2,1,0:T(8,128)(2,1)S(1)}, bf16[4,128,1024]{2,1,0:T(8,128)(2,1)}, u32[]{:S(2)}, u32[]{:S(2)}) collective-permute-start(bf16[4,128,1024]{2,1,0:T(8,128)(2,1)S(1)} %all-to-all-done.4.refs_2_), channel_id=1, source_target_pairs={{0,1},{1,0},{2,3},{3,2},{4,5},{5,4},{6,7},{7,6},{8,9},{9,8},{10,11... | collective-permute-start | bytes 3145736 | tf_op jit(solution)/shard_map/ppermute | solution.py:21
  196.4 10.8 %collective-permute-start.23 = (bf16[1024,256]{1,0:T(8,128)(2,1)}, bf16[1024,256]{1,0:T(8,128)(2,1)}, u32[]{:S(2)}, u32[]{:S(2)}) collective-permute-start(bf16[1024,256]{1,0:T(8,128)(2,1)} %slice.130), channel_id=1, source_target_pairs={{0,64},{64,128},{128,192},{192,0},{1,65},{65,129},{129,193},{193,1... | collective-permute-start | bytes 1572872 | tf_op jit(solution)/shard_map/ppermute | solution.py:21
  200.7 11.7 %collective-permute-start.24 = (bf16[1024,256]{1,0:T(8,128)(2,1)}, bf16[1024,256]{1,0:T(8,128)(2,1)}, u32[]{:S(2)}, u32[]{:S(2)}) collective-permute-start(bf16[1024,256]{1,0:T(8,128)(2,1)} %slice.131), channel_id=1, source_target_pairs={{0,192},{64,0},{128,64},{192,128},{1,193},{65,1},{129,65},{193,129... | collective-permute-start | bytes 1572872 | tf_op jit(solution)/shard_map/ppermute | solution.py:21
  212.4 0.8 copy-start
Sparse Core Ops, SparseCore 0:
  9.9 143.8 all-gather.1
where the time goes:
time: 239 us
  waiting for transfers between devices  108 us (45%)
  starting transfers between devices  62.9 us (26%)
  local copies, waits for them, and re-layouts  19.3 us (8%)
  Pallas kernels  18.5 us (8%)
  between operations  15.1 us (6%)
  other arithmetic  11.9 us (5%)
  matrix products  2.91 us (1%)
    ppermute x25, waiting for transfers between devices, shift(): lax.ppermute(array, axis, [(i, (i + by) % size) for i in range(size)])  63.7 us
    all_to_all x5, waiting for transfers between devices, exchange(): return lax.all_to_all(array, axis, 0, 0, tiled=True)  43.5 us
    ppermute x25, starting transfers between devices, shift(): lax.ppermute(array, axis, [(i, (i + by) % size) for i in range(size)])  34 us
    all_to_all x5, starting transfers between devices, exchange(): return lax.all_to_all(array, axis, 0, 0, tiled=True)  28.9 us
    pallas_call x1, Pallas kernels, decoder(): pl.pallas_call(kernel, out_shape=jax.ShapeDtypeStruct((SEQ, 512), jnp.bfl...  18.5 us
    unnamed x23, local copies, waits for them, and re-layouts  6.81 us
    eq x4, other arithmetic, step(): owners[r] == sample_ids  5.09 us
  transfers between devices with their start and end apart: 31, of which 15 were waited for; matrix products, arithmetic and copies ran while one was open for 14% of the time, Pallas kernels for 0%

commit v1 on v0

v1 whole, which is shorter than its diff:
```python
import jax
import jax.numpy as jnp
from jax import lax
from jax.experimental import pallas as pl
from jax.experimental.pallas import tpu as pltpu
from jax.sharding import Mesh, PartitionSpec as P


HEAD = 128
NX, NZ, NY, NC = 4, 8, 4, 2
SEQ = 384
SPAN = 128
WIDTH = 8192
COLS = 768
WIRE = COLS + 128
vision_epsilon = 1e-06
decoder_epsilon = 1e-05
rope_base = 500000.0


def shift(array, axis, by):
    size = lax.axis_size(axis)
    return lax.ppermute(array, axis, [(i, (i + by) % size) for i in range(size)])


def swap_xy(array):
    pairs = [(i * NY + j, j * NY + i) for i in range(NX) for j in range(NY)]
    return lax.ppermute(array, ("x", "y"), pairs)


def exchange(array, axis):
    return lax.all_to_all(array, axis, 0, 0, tiled=True)


def spread(array, axis):
    size = lax.axis_size(axis)
    return exchange(jnp.broadcast_to(array[None], (size, *array.shape)), axis)


def ring4(array, axis):
    half = array.shape[0] // 2
    below = shift(array, axis, 1)
    above = shift(array, axis, -1)
    far_low = shift(below[:half], axis, 1)
    far_high = shift(above[half:], axis, -1)
    return [(array, 0, 0), (below, -1, 0), (above, 1, 0), (far_low, 2, 0), (far_high, 2, half)]


def rope_tables():
    half = HEAD // 2
    exponents = jnp.arange(half, dtype=jnp.float32) * (2.0 / HEAD)
    frequency = rope_base ** (-exponents)
    positions = jnp.arange(SEQ, dtype=jnp.int32).astype(jnp.float32)
    angles = positions[:, None] * frequency[None, :]
    cosine, sine = jnp.cos(angles), jnp.sin(angles)
    return (
        jnp.concatenate([cosine, cosine], axis=1),
        jnp.concatenate([-sine, sine], axis=1),
    )


def project(where, pieces, weight, gain, rows, relative):
    arrays = [a for a, _ in pieces]
    plan = [(n, *part) for n, (_, parts) in enumerate(pieces) for part in parts]
    count = len(arrays)

    def kernel(where_ref, *refs):
        srcs, b_src, gain_ref, out_ref = refs[:count], refs[count], refs[count + 1], refs[count + 2]
        a_ref, b_ref, a_sem, b_sem = refs[count + 3 :]
        x, y, c = where_ref[0], where_ref[1], where_ref[2]
        loads = [pltpu.make_async_copy(b_src, b_ref, b_sem)]
        for k, (n, at, dy, sample, row, length, flip) in enumerate(plan):
            s = sample if dy is None else lax.rem(y + (dy + NY), NY)
            core = c if flip == 0 else 1 - c
            source = srcs[n] if at is None else srcs[n].at[at]
            target = a_ref.at[s, core, pl.ds(row, length), :]
            loads.append(pltpu.make_async_copy(source, target, a_sem.at[k]))
        for copy in loads:
            copy.start()
        for copy in loads:
            copy.wait()
        lane = lax.broadcasted_iota(jnp.int32, (rows, 128), 1)

        def one(s, carry):
            total = jnp.zeros((rows, 1), jnp.float32)
            acc = jnp.zeros((rows, COLS), jnp.float32)
            for core in range(NC):
                value = a_ref[s, core].astype(jnp.float32)
                total = total + jnp.sum(value * value, axis=1, keepdims=True)
                scaled = (value * gain_ref[core : core + 1, :]).astype(jnp.bfloat16)
                acc = acc + jnp.dot(
                    scaled, b_ref[core * 1024 : (core + 1) * 1024, :],
                    preferred_element_type=jnp.float32,
                )
            high = total.astype(jnp.bfloat16).astype(jnp.float32)
            low = total - high
            slot = lax.rem(s - x + NX, NX) if relative else s
            out_ref[slot, :, :COLS] = acc.astype(jnp.bfloat16)
            out_ref[slot, :, COLS:] = jnp.where(
                lane == 0, high, jnp.where(lane == 1, low, 0.0)
            ).astype(jnp.bfloat16)
            return carry

        lax.fori_loop(0, NX, one, 0)

    any_spec = pl.BlockSpec(memory_space=pl.ANY)
    vmem = pl.BlockSpec(memory_space=pltpu.VMEM)
    return pl.pallas_call(
        kernel,
        out_shape=jax.ShapeDtypeStruct((NX, rows, WIRE), jnp.bfloat16),
        in_specs=[pl.BlockSpec(memory_space=pltpu.SMEM)] + [any_spec] * (count + 1) + [vmem],
        out_specs=vmem,
        scratch_shapes=[
            pltpu.VMEM((NX, NC, rows, 1024), jnp.bfloat16),
            pltpu.VMEM((2048, COLS), jnp.bfloat16),
            pltpu.SemaphoreType.DMA((len(plan),)),
            pltpu.SemaphoreType.DMA,
        ],
        compiler_params=pltpu.CompilerParams(vmem_limit_bytes=40 * 1024 * 1024),
        cost_estimate=pl.CostEstimate(
            flops=2 * NX * rows * 2048 * COLS, bytes_accessed=10000000, transcendentals=0
        ),
    )(where, *arrays, weight, gain)


def attention(where, text_parts, image_parts, tables, image_tables):
    def kernel(where_ref, t0, t1, t2, t3, i_ref, cos_ref, sin_ref, icos_ref, isin_ref, out_ref):
        start, n_rows = where_ref[0], where_ref[1]

        def summed(parts):
            total = parts[0].astype(jnp.float32)
            for p in parts[1:]:
                total = total + p.astype(jnp.float32)
            squares = jnp.sum(total[:, COLS:], axis=1, keepdims=True)
            scale = lax.rsqrt(squares * (1.0 / WIDTH) + decoder_epsilon)
            return total[:, :COLS] * scale

        def heads(total, cos, sin):
            pieces = []
            for h in range(5):
                v = total[:, h * HEAD : (h + 1) * HEAD]
                pieces.append((v * cos + pltpu.roll(v, 64, 1) * sin).astype(jnp.bfloat16))
            pieces.append(total[:, 5 * HEAD :].astype(jnp.bfloat16))
            return pieces

        text = heads(summed([t0[...], t1[...], t2[...], t3[...]]), cos_ref[...], sin_ref[...])
        image = heads(summed([i_ref[n] for n in range(NX)]), icos_ref[...], isin_ref[...])
        p_at = lax.broadcasted_iota(jnp.int32, (SEQ, SPAN), 0) - start
        j_at = lax.broadcasted_iota(jnp.int32, (SEQ, SPAN), 1)
        pick = jnp.where((p_at == j_at) & (j_at < n_rows), 1.0, 0.0).astype(jnp.bfloat16)
        rows_at = lax.broadcasted_iota(jnp.int32, (SEQ, HEAD), 0) - start
        is_image = (rows_at >= 0) & (rows_at < n_rows)

        def merged(h):
            placed = jnp.dot(pick, image[h], preferred_element_type=jnp.float32)
            return jnp.where(is_image, placed, text[h].astype(jnp.float32)).astype(jnp.bfloat16)

        key, value = merged(4), merged(5)
        causal = lax.broadcasted_iota(jnp.int32, (SEQ, SEQ), 0) >= lax.broadcasted_iota(
            jnp.int32, (SEQ, SEQ), 1
        )
        for h in range(4):
            scores = lax.dot_general(
                merged(h), key, (((1,), (1,)), ((), ())), preferred_element_type=jnp.float32
            ) * (HEAD ** (-0.5))
            scores = jnp.where(causal, scores, -1e30)
            top = jnp.max(scores, axis=1, keepdims=True)
            e = jnp.exp(scores - top)
            w = (e / jnp.sum(e, axis=1, keepdims=True)).astype(jnp.bfloat16)
            out_ref[:, h * HEAD : (h + 1) * HEAD] = jnp.dot(
                w, value, preferred_element_type=jnp.float32
            ).astype(jnp.bfloat16)

    vmem = pl.BlockSpec(memory_space=pltpu.VMEM)
    return pl.pallas_call(
        kernel,
        out_shape=jax.ShapeDtypeStruct((SEQ, 512), jnp.bfloat16),
        in_specs=[pl.BlockSpec(memory_space=pltpu.SMEM)] + [vmem] * 9,
        out_specs=vmem,
        compiler_params=pltpu.CompilerParams(vmem_limit_bytes=40 * 1024 * 1024),
        name="attention",
    )(where, *text_parts, image_parts, *tables, *image_tables)


def vision(vis_rows, ln_gain, ln_bias, weight):
    tokens = vis_rows.shape[0] * vis_rows.shape[1]
    whole = spread(vis_rows.reshape(tokens, 2, 400), ("y", "c")).astype(jnp.float32)
    mean = jnp.mean(whole, axis=(0, 2, 3))[None, :, None, None]
    centered = whole - mean
    variance = jnp.mean(centered * centered, axis=(0, 2, 3))[None, :, None, None]
    gain = jnp.swapaxes(ln_gain.reshape(2, 8, 400), 0, 1)[:, None]
    bias = jnp.swapaxes(ln_bias.reshape(2, 8, 400), 0, 1)[:, None]
    normed = (centered * lax.rsqrt(variance + vision_epsilon) * gain + bias).astype(jnp.bfloat16)
    acts = exchange(normed.reshape(4, 2, tokens, 2, 400), "x")
    partial = jnp.einsum(
        "sctmf,cfmo->sto", acts, weight.reshape(2, 400, 2, 1024),
        preferred_element_type=jnp.float32,
    ).astype(jnp.bfloat16)
    parts = exchange(partial, "x")
    return jnp.sum(parts.astype(jnp.float32), axis=0).astype(jnp.bfloat16)


def step(
    vis_rows, ln_gain, ln_bias, proj_weight, text_rows, attn_gain, w_query,
    key_value_weight, tile_counts, image_offsets,
):
    x, z = lax.axis_index("x"), lax.axis_index("z")
    y, c = lax.axis_index("y"), lax.axis_index("c")
    tile_ends = jnp.cumsum(tile_counts)
    tile_firsts = tile_ends - tile_counts
    sample_ids = jnp.arange(32, dtype=jnp.int32)

    def entry(values, index):
        return jnp.sum(jnp.where(sample_ids == index, values, 0))

    proj_all = lax.all_gather(proj_weight, "z", axis=0, tiled=True)
    both = jnp.concatenate([w_query, key_value_weight.reshape(256, 256)], axis=1)
    both_all = lax.all_gather(both, "z", axis=0, tiled=True)

    image = vision(vis_rows, ln_gain, ln_bias, proj_all)

    turned = swap_xy(text_rows[0])
    own = ring4(turned, "y")
    text = []
    for a, dy, row in own:
        other = shift(a, "c", 1)
        text.append((a, [(None, dy, None, row, a.shape[0], 0)]))
        text.append((other, [(None, dy, None, row, a.shape[0], 1)]))

    image = swap_xy(image).reshape(8, 8, 1024)
    place = y * NZ + z
    tiles_here = jnp.arange(8, dtype=jnp.int32) * 32 + place
    owners = jnp.sum((tile_ends[None, :] <= tiles_here[:, None]).astype(jnp.int32), axis=1)
    slots = jnp.zeros((32, 8, 1024), jnp.bfloat16)
    for r in range(8):
        slots = jnp.where((owners[r] == sample_ids)[:, None, None], image[r][None], slots)
    received = exchange(slots, ("y", "z"))
    sources = (entry(tile_firsts, place) + jnp.arange(16, dtype=jnp.int32)) % 32
    mine = received[sources].reshape(SPAN, 1024)
    own_image = spread(mine, "y")
    other_image = shift(own_image, "c", 1)
    image_pieces = [
        (a, [(s, None, s, 0, SPAN, flip) for s in range(NX)])
        for flip, a in enumerate((own_image, other_image))
    ]

    gain = lax.dynamic_slice_in_dim(attn_gain, x * 2048, 2048).reshape(2, 1024)
    where = jnp.stack([x, y, c]).astype(jnp.int32)
    text_out = project(where, text, both_all, gain, SEQ, True)
    text_parts = [
        text_out[0],
        shift(text_out[1], "x", 1),
        shift(text_out[3], "x", -1),
        shift(text_out[2], "x", 2),
    ]
    image_out = project(where, image_pieces, both_all, gain, SPAN, False)
    image_parts = exchange(image_out, "x")

    tables = rope_tables()
    start = image_offsets[0]
    image_tables = [lax.dynamic_slice_in_dim(t, start, SPAN, 0) for t in tables]
    rows = entry(tile_counts, x * NZ + z) * 8
    out = attention(
        jnp.stack([start, rows]).astype(jnp.int32), text_parts, image_parts, tables, image_tables
    )
    return out[None]


def solution(mesh):
    fine = Mesh(mesh.devices.reshape(NX, NZ, NY, NC), ("x", "z", "y", "c"))
    dp, tensor = ("x", "z"), ("y", "c")
    in_specs = (
        P(None, dp, None, tensor), P(), P(), P(dp, None, tensor), P(dp, None, tensor), P(),
        P(dp, tensor), P(dp, None, tensor), P(), P(dp),
    )
    return jax.shard_map(
        step, mesh=fine, in_specs=in_specs, out_specs=P(dp, None, tensor), check_vma=False
    )
```

time: 239 us -> 229 us (0.958)
  the two profiles are of different devices: /device:TPU:6 before, /device:TPU:1 now
where the time goes in v1:
time: 229 us; the launch traced here: 228 us
  waiting for transfers between devices  109 us (48%)
  starting transfers between devices  56.4 us (25%)
  Pallas kernels  18 us (8%)
  between operations  15.1 us (7%)
  local copies, waits for them, and re-layouts  14 us (6%)
  other arithmetic  12.1 us (5%)
  matrix products  4.12 us (2%)
    all_to_all x6, waiting for transfers between devices, exchange(): return lax.all_to_all(array, axis, 0, 0, tiled=True)  63.2 us
    ppermute x13, waiting for transfers between devices, shift(): lax.ppermute(array, axis, [(i, (i + by) % size) for i in range(size)])  36.9 us
    all_to_all x6, starting transfers between devices, exchange(): return lax.all_to_all(array, axis, 0, 0, tiled=True)  32.1 us
    ppermute x13, starting transfers between devices, shift(): lax.ppermute(array, axis, [(i, (i + by) % size) for i in range(size)])  22.9 us
    pallas_call x2, Pallas kernels, project(): pl.pallas_call(kernel, out_shape=jax.ShapeDtypeStruct((NX, rows, WIRE), j...  13.1 us
    all_gather x1, waiting for transfers between devices, step(): proj_all = lax.all_gather(proj_weight, 'z', axis=0, tiled=True)  7.89 us
    unnamed x23, local copies, waits for them, and re-layouts  5.17 us
    eq x4, other arithmetic, step(): owners[r] == sample_ids  4.95 us
  transfers between devices with their start and end apart: 23, of which 11 were waited for; matrix products, arithmetic and copies ran while one was open for 11% of the time, Pallas kernels for 6%

profile of v1, /device:TPU:1, one launch (start us, length us, event | category | flops | bytes accessed | tf_op | source)
XLA Modules:
  0.0 228.4 jit_solution(3031347381176163559)
XLA Ops:
  6.5 0.7 all-gather.5.cloned.1.call-update
  7.3 0.9 copy.41
  8.2 1.1 broadcast_in_dim.131
  9.3 6.8 %all-to-all-start = ((bf16[8,64,2,400]{3,1,2,0:T(8,128)(2,1)}), bf16[8,64,2,400]{3,1,2,0:T(8,128)(2,1)S(1)}, u32[]{:S(2)}, u32[]{:S(2)}) async-start(bf16[8,64,2,400]{3,1,2,0:T(8,128)(2,1)} %broadcast_in_dim.131), calls=%async_computation | async-start | bytes 2097152 | tf_op jit(solution)/shard_map/all_to_all | solution.py:32
  16.1 0.8 pad_maximum_fusion
  17.2 13.9 %all-to-all-done = bf16[8,64,2,400]{3,1,2,0:T(8,128)(2,1)S(1)} async-done(((bf16[8,64,2,400]{3,1,2,0:T(8,128)(2,1)}), bf16[8,64,2,400]{3,1,2,0:T(8,128)(2,1)S(1)}, u32[]{:S(2)}, u32[]{:S(2)}) %all-to-all-start) | async-done | bytes 819232 | tf_op jit(solution)/shard_map/all_to_all | solution.py:32
  31.1 0.3 convert_reduce_fusion
  31.4 0.5 fusion.5
  31.9 1.5 fusion.8
  33.4 3.5 %all-to-all-start.1 = ((bf16[4,2,64,2,400]{4,2,3,1,0:T(8,128)(2,1)}), bf16[4,2,64,2,400]{4,2,3,1,0:T(8,128)(2,1)S(1)}, u32[]{:S(2)}, u32[]{:S(2)}) async-start(bf16[4,2,64,2,400]{4,2,3,1,0:T(8,128)(2,1)} %bitcast.14), calls=%async_computation.1 | async-start | bytes 2097152 | tf_op jit(solution)/shard_map/all_to_all | solution.py:32
  36.9 0.7 collective-permute-start
  37.8 0.1 reduce.1
  37.9 13.1 %all-to-all-done.1 = bf16[4,2,64,2,400]{4,2,3,1,0:T(8,128)(2,1)S(1)} async-done(((bf16[4,2,64,2,400]{4,2,3,1,0:T(8,128)(2,1)}), bf16[4,2,64,2,400]{4,2,3,1,0:T(8,128)(2,1)S(1)}, u32[]{:S(2)}, u32[]{:S(2)}) %all-to-all-start.1) | async-done | bytes 819232 | tf_op jit(solution)/shard_map/all_to_all | solution.py:32
  51.0 7.9 %all-gather.5.cloned.1.call-done = bf16[800,2,1024]{2,1,0:T(2,128)(2,1)} async-done(((bf16[100,2,1024]{2,1,0:T(2,128)(2,1)}), bf16[800,2,1024]{2,1,0:T(2,128)(2,1)}) %all-gather.5.cloned.1.call-update) | async-done | bytes 3276816 | tf_op jit(solution)/shard_map/all_gather | solution.py:216
  58.9 4.1 %fusion.12 = bf16[4,64,1024]{2,1,0:T(8,128)(2,1)} fusion(bf16[4,2,64,2,400]{4,2,3,1,0:T(8,128)(2,1)S(1)} %all-to-all-done.1, bf16[2,400,2,1024,1]{3,2,1,0,4:T(2,128)(2,1)} %bitcast.64), kind=kOutput, calls=%fused_computation.13 | convolution fusion | flops 839122944 | bytes 4620288 | tf_op jit(solution)/shard_map/sctmf,cfmo->sto/dot_general | solution.py:195
  63.0 4.0 %all-to-all-start.2 = ((bf16[4,64,1024]{2,1,0:T(8,128)(2,1)}), bf16[4,64,1024]{2,1,0:T(8,128)(2,1)S(1)}, u32[]{:S(2)}, u32[]{:S(2)}) async-start(bf16[4,64,1024]{2,1,0:T(8,128)(2,1)} %fusion.12), calls=%async_computation.2 | async-start | bytes 1048576 | tf_op jit(solution)/shard_map/all_to_all | solution.py:32
  67.0 0.2 convert_reduce_fusion.1
  67.2 0.7 fusion.23
  67.9 1.2 iota_compare_fusion
  69.1 1.2 iota_compare_fusion.2
  70.3 22.6 %all-to-all-done.2 = bf16[4,64,1024]{2,1,0:T(8,128)(2,1)S(1)} async-done(((bf16[4,64,1024]{2,1,0:T(8,128)(2,1)}), bf16[4,64,1024]{2,1,0:T(8,128)(2,1)S(1)}, u32[]{:S(2)}, u32[]{:S(2)}) %all-to-all-start.2) | async-done | bytes 524320 | tf_op jit(solution)/shard_map/all_to_all | solution.py:32
  93.0 0.7 collective-permute-start.13
  93.7 1.1 iota_compare_fusion.4
  94.8 1.4 iota_compare_fusion.6
  96.2 1.2 select_select_fusion
  97.4 10.8 %all-to-all-start.3 = ((bf16[32,8,1024]{2,1,0:T(8,128)(2,1)}), bf16[32,8,1024]{2,1,0:T(8,128)(2,1)S(1)}, u32[]{:S(2)}, u32[]{:S(2)}) async-start(bf16[32,8,1024]{2,1,0:T(8,128)(2,1)} %select_select_fusion), calls=%async_computation.3 | async-start | bytes 1048576 | tf_op jit(solution)/shard_map/all_to_all | solution.py:32
  108.2 1.3 collective-permute-start.2
  109.6 1.4 collective-permute-start.4
  111.0 0.7 fusion.19
  111.7 0.6 fusion.21
  112.3 4.0 %collective-permute-start.1 = (bf16[384,1024]{1,0:T(8,128)(2,1)S(1)}, bf16[384,1024]{1,0:T(8,128)(2,1)S(1)}, u32[]{:S(2)}, u32[]{:S(2)}) collective-permute-start(bf16[384,1024]{1,0:T(8,128)(2,1)S(1)} %collective-permute-done.refs_0_), channel_id=1, source_target_pairs={{0,1},{1,0},{2,3},{3,2},{4,5},{5,4},{6,7},{7,6},{8,9},{9,8},{10,11... | collective-permute-start | bytes 2359304 | tf_op jit(solution)/shard_map/ppermute | solution.py:23
  116.3 3.8 %all-to-all-done.3 = bf16[32,8,1024]{2,1,0:T(8,128)(2,1)S(1)} async-done(((bf16[32,8,1024]{2,1,0:T(8,128)(2,1)}), bf16[32,8,1024]{2,1,0:T(8,128)(2,1)S(1)}, u32[]{:S(2)}, u32[]{:S(2)}) %all-to-all-start.3) | async-done | bytes 524320 | tf_op jit(solution)/shard_map/all_to_all | solution.py:32
  120.1 0.6 gather_fusion
  120.7 1.1 broadcast_in_dim.149
  121.8 3.5 %all-to-all-start.4 = ((bf16[4,128,1024]{2,1,0:T(8,128)(2,1)}), bf16[4,128,1024]{2,1,0:T(8,128)(2,1)S(1)}, u32[]{:S(2)}, u32[]{:S(2)}) async-start(bf16[4,128,1024]{2,1,0:T(8,128)(2,1)} %broadcast_in_dim.149), calls=%async_computation.4 | async-start | bytes 2097152 | tf_op jit(solution)/shard_map/all_to_all | solution.py:32
  125.3 6.7 %collective-permute-done.2.refs_2_ = bf16[384,1024]{1,0:T(8,128)(2,1)} collective-permute-done((bf16[384,1024]{1,0:T(8,128)(2,1)S(1)}, bf16[384,1024]{1,0:T(8,128)(2,1)}, u32[]{:S(2)}, u32[]{:S(2)}) %collective-permute-start.2) | collective-permute-done | bytes 786464 | tf_op jit(solution)/shard_map/ppermute | solution.py:23
  132.0 1.0 slice.98
  133.0 0.2 collective-permute-start.6
  133.3 5.8 %collective-permute-start.3 = (bf16[384,1024]{1,0:T(8,128)(2,1)}, bf16[384,1024]{1,0:T(8,128)(2,1)}, u32[]{:S(2)}, u32[]{:S(2)}) collective-permute-start(bf16[384,1024]{1,0:T(8,128)(2,1)} %collective-permute-done.2.refs_2_), channel_id=1, source_target_pairs={{0,1},{1,0},{2,3},{3,2},{4,5},{5,4},{6,7},{7,6},{8,9},{9,8},{10,11... | collective-permute-start | bytes 2359304 | tf_op jit(solution)/shard_map/ppermute | solution.py:23
  139.0 0.1 collective-permute-start.5
  139.1 1.0 slice.99
  140.2 2.8 %collective-permute-start.8 = (bf16[192,1024]{1,0:T(8,128)(2,1)S(1)}, bf16[192,1024]{1,0:T(8,128)(2,1)}, u32[]{:S(2)}, u32[]{:S(2)}) collective-permute-start(bf16[192,1024]{1,0:T(8,128)(2,1)S(1)} %slice.99), channel_id=1, source_target_pairs={{0,6},{2,0},{4,2},{6,4},{1,7},{3,1},{5,3},{7,5},{8,14},{10,8},{12,... | collective-permute-start | bytes 1179656 | tf_op jit(solution)/shard_map/ppermute | solution.py:23
  143.0 8.6 %collective-permute-done.6.refs_6_ = bf16[192,1024]{1,0:T(8,128)(2,1)S(1)} collective-permute-done((bf16[192,1024]{1,0:T(8,128)(2,1)S(1)}, bf16[192,1024]{1,0:T(8,128)(2,1)S(1)}, u32[]{:S(2)}, u32[]{:S(2)}) %collective-permute-start.6) | collective-permute-done | bytes 393248 | tf_op jit(solution)/shard_map/ppermute | solution.py:23
  151.6 3.1 %collective-permute-start.7 = (bf16[192,1024]{1,0:T(8,128)(2,1)S(1)}, bf16[192,1024]{1,0:T(8,128)(2,1)}, u32[]{:S(2)}, u32[]{:S(2)}) collective-permute-start(bf16[192,1024]{1,0:T(8,128)(2,1)S(1)} %collective-permute-done.6.refs_6_), channel_id=1, source_target_pairs={{0,1},{1,0},{2,3},{3,2},{4,5},{5,4},{6,7},{7,6},{8,9},{9,8},{10,11... | collective-permute-start | bytes 1179656 | tf_op jit(solution)/shard_map/ppermute | solution.py:23
  154.7 1.0 copy-done.3
  155.7 0.5 collective-permute-start.14
  157.5 0.7 dynamic_slice.9
  158.4 1.9 copy-done
  160.3 1.1 copy-done.2
  161.4 1.1 copy-done.4
  162.5 8.8 %shard_map.100 = bf16[4,384,896]{2,1,0:T(8,128)(2,1)S(1)} custom-call(s32[3]{0:T(128)S(1)} %pad_add_fusion.1.where_ref, bf16[384,1024]{1,0:T(8,128)(2,1)S(1)} %copy-done.2, bf16[384,1024]{1,0:T(8,128)(2,1)S(1)} %copy-done.4, bf16[384,1024]{1,0:T(8,128)(2,1)} %collective-permute-done.2.refs_2_, bf16[384,1024]{1,0:T(8,128)(2,1)} %collective-permute-done.3.refs_3_, ...), custom_call_target="tpu_custom_call" | custom-call | flops 4831838208 | bytes 10000000 | tf_op jit(solution)/shard_map/pallas_call | solution.py:108
  171.4 1.3 slice_bitcast_fusion
  172.8 2.6 %collective-permute-start.11 = (bf16[384,896]{1,0:T(8,128)(2,1)}, bf16[384,896]{1,0:T(8,128)(2,1)}, u32[]{:S(2)}, u32[]{:S(2)}) collective-permute-start(bf16[384,896]{1,0:T(8,128)(2,1)} %get-tuple-element.8), channel_id=1, source_target_pairs={{0,192},{64,0},{128,64},{192,128},{1,193},{65,1},{129,65},{193,129... | collective-permute-start | bytes 2064392 | tf_op jit(solution)/shard_map/ppermute | solution.py:23
  175.4 1.0 collective-permute-start.12
  176.4 4.3 %shard_map.101 = bf16[4,128,896]{2,1,0:T(8,128)(2,1)} custom-call(s32[3]{0:T(128)S(1)} %pad_add_fusion.1.where_ref, bf16[4,128,1024]{2,1,0:T(8,128)(2,1)S(1)} %all-to-all-done.4.refs_0_, bf16[4,128,1024]{2,1,0:T(8,128)(2,1)S(1)} %collective-permute-done.14.refs_1_, bf16[2048,768]{1,0:T(8,128)(2,1)S(1)} %copy-done, f32[2,1024]{1,0:T(2,128)S(1)} %reshape.169.refs_11_.refs_3_), custom_call_target="tpu_custom_call" | custom-call | flops 1610612736 | bytes 10000000 | tf_op jit(solution)/shard_map/pallas_call | solution.py:108
  180.7 3.5 %all-to-all-start.5 = ((bf16[4,128,896]{2,1,0:T(8,128)(2,1)}), bf16[4,128,896]{2,1,0:T(8,128)(2,1)S(1)}, u32[]{:S(2)}, u32[]{:S(2)}) async-start(bf16[4,128,896]{2,1,0:T(8,128)(2,1)} %shard_map.101), calls=%async_computation.5 | async-start | bytes 1835008 | tf_op jit(solution)/shard_map/all_to_all | solution.py:32
  184.3 0.8 fusion.17
  185.1 0.1 fusion.15
  185.2 0.2 pad_maximum_fusion.1
  185.4 5.7 %collective-permute-done.10.t1 = bf16[384,896]{1,0:T(8,128)(2,1)S(1)} collective-permute-done((bf16[384,896]{1,0:T(8,128)(2,1)}, bf16[384,896]{1,0:T(8,128)(2,1)S(1)}, u32[]{:S(2)}, u32[]{:S(2)}) %collective-permute-start.10) | collective-permute-done | bytes 688160 | tf_op jit(solution)/shard_map/ppermute | solution.py:23
  191.1 13.2 %collective-permute-done.11.t2 = bf16[384,896]{1,0:T(8,128)(2,1)} collective-permute-done((bf16[384,896]{1,0:T(8,128)(2,1)}, bf16[384,896]{1,0:T(8,128)(2,1)}, u32[]{:S(2)}, u32[]{:S(2)}) %collective-permute-start.11) | collective-permute-done | bytes 688160 | tf_op jit(solution)/shard_map/ppermute | solution.py:23
  204.3 2.7 %collective-permute-done.12.t3 = bf16[384,896]{1,0:T(8,128)(2,1)} collective-permute-done((bf16[384,896]{1,0:T(8,128)(2,1)}, bf16[384,896]{1,0:T(8,128)(2,1)}, u32[]{:S(2)}, u32[]{:S(2)}) %collective-permute-start.12) | collective-permute-done | bytes 688160 | tf_op jit(solution)/shard_map/ppermute | solution.py:23
  207.0 9.7 %all-to-all-done.5.i_ref = bf16[4,128,896]{2,1,0:T(8,128)(2,1)S(1)} async-done(((bf16[4,128,896]{2,1,0:T(8,128)(2,1)}), bf16[4,128,896]{2,1,0:T(8,128)(2,1)S(1)}, u32[]{:S(2)}, u32[]{:S(2)}) %all-to-all-start.5) | async-done | bytes 917536 | tf_op jit(solution)/shard_map/all_to_all | solution.py:32
  216.7 4.9 %attention.1 = bf16[384,512]{1,0:T(8,128)(2,1)} custom-call(s32[2]{0:T(128)S(1)} %pad_add_fusion.where_ref, bf16[384,896]{1,0:T(8,128)(2,1)S(1)} %get-tuple-element.10.t0, bf16[384,896]{1,0:T(8,128)(2,1)S(1)} %collective-permute-done.10.t1, bf16[384,896]{1,0:T(8,128)(2,1)} %collective-permute-done.11.t2, bf16[384,896]{1,0:T(8,128)(2,1)} %collective-permute-done.12.t3, ...), custom_call_target="tpu_custom_call" | custom-call | tf_op jit(solution)/shard_map/attention/pallas_call | solution.py:175
  (52 shorter events, 0.9 us)
Async XLA Ops:
  6.5 9.6 %copy-start.6 = (bf16[256,2,128]{2,1,0:T(2,128)(2,1)S(1)}, bf16[256,2,128]{2,1,0:T(2,128)(2,1)}, u32[]{:S(2)}) copy-start(bf16[256,2,128]{2,1,0:T(2,128)(2,1)} %param.17) | copy-start | bytes 393220
  6.5 9.6 %copy-start.5 = (bf16[256,512]{1,0:T(8,128)(2,1)S(1)}, bf16[256,512]{1,0:T(8,128)(2,1)}, u32[]{:S(2)}) copy-start(bf16[256,512]{1,0:T(8,128)(2,1)} %param.16) | copy-start | bytes 786436
  6.5 52.4 %all-gather.5.cloned.1.call-start = ((), (), s32[]{:S(2)}) async-start(), calls=%async_computation.7 | async-start | bytes 3686400 | tf_op jit(solution)/shard_map/all_gather | solution.py:216
  8.2 8.8 %copy-start.7 = (f32[2,3200]{1,0:T(2,128)S(1)}, f32[2,3200]{1,0:T(2,128)}, u32[]{:S(2)}) copy-start(f32[2,3200]{1,0:T(2,128)} %param.12) | copy-start | bytes 76804
  9.3 7.7 %copy-start.8 = (f32[2,3200]{1,0:T(2,128)S(1)}, f32[2,3200]{1,0:T(2,128)}, u32[]{:S(2)}) copy-start(f32[2,3200]{1,0:T(2,128)} %param.11) | copy-start | bytes 76804
  9.3 21.8 %all-to-all-start = ((bf16[8,64,2,400]{3,1,2,0:T(8,128)(2,1)}), bf16[8,64,2,400]{3,1,2,0:T(8,128)(2,1)S(1)}, u32[]{:S(2)}, u32[]{:S(2)}) async-start(bf16[8,64,2,400]{3,1,2,0:T(8,128)(2,1)} %broadcast_in_dim.131), calls=%async_computation | async-start | bytes 2097152 | tf_op jit(solution)/shard_map/all_to_all | solution.py:32
  16.1 142.3 %all-gather.3.cloned.1.call-start = ((), (), s32[]{:S(2)}) async-start(), calls=%async_computation.6 | async-start | bytes 3538944 | tf_op jit(solution)/shard_map/all_gather | solution.py:218
  31.8 5.0 %copy-start.10 = (bf16[1,384,1024]{2,1,0:T(8,128)(2,1)S(1)}, bf16[1,384,1024]{2,1,0:T(8,128)(2,1)}, u32[]{:S(2)}) copy-start(bf16[1,384,1024]{2,1,0:T(8,128)(2,1)} %param.14) | copy-start | bytes 2359300
  31.9 5.8 %copy-start.9 = (s32[32]{0:T(128)S(1)}, s32[32]{0:T(128)}, u32[]{:S(2)}) copy-start(s32[32]{0:T(128)} %param.18) | copy-start | bytes 388
  33.4 17.7 %all-to-all-start.1 = ((bf16[4,2,64,2,400]{4,2,3,1,0:T(8,128)(2,1)}), bf16[4,2,64,2,400]{4,2,3,1,0:T(8,128)(2,1)S(1)}, u32[]{:S(2)}, u32[]{:S(2)}) async-start(bf16[4,2,64,2,400]{4,2,3,1,0:T(8,128)(2,1)} %bitcast.14), calls=%async_computation.1 | async-start | bytes 2097152 | tf_op jit(solution)/shard_map/all_to_all | solution.py:32
  36.9 71.3 %collective-permute-start = (bf16[384,1024]{1,0:T(8,128)(2,1)S(1)}, bf16[384,1024]{1,0:T(8,128)(2,1)S(1)}, u32[]{:S(2)}, u32[]{:S(2)}) collective-permute-start(bf16[384,1024]{1,0:T(8,128)(2,1)S(1)} %bitcast.65), channel_id=1, source_target_pairs={{0,0},{2,64},{4,128},{6,192},{64,2},{66,66},{68,130},{70,194},{128... | collective-permute-start | bytes 2359304 | tf_op jit(solution)/shard_map/ppermute | solution.py:28
  63.0 29.9 %all-to-all-start.2 = ((bf16[4,64,1024]{2,1,0:T(8,128)(2,1)}), bf16[4,64,1024]{2,1,0:T(8,128)(2,1)S(1)}, u32[]{:S(2)}, u32[]{:S(2)}) async-start(bf16[4,64,1024]{2,1,0:T(8,128)(2,1)} %fusion.12), calls=%async_computation.2 | async-start | bytes 1048576 | tf_op jit(solution)/shard_map/all_to_all | solution.py:32
  93.0 3.2 %collective-permute-start.13 = (bf16[64,1024]{1,0:T(8,128)(2,1)S(1)}, bf16[64,1024]{1,0:T(8,128)(2,1)S(1)}, u32[]{:S(2)}, u32[]{:S(2)}) collective-permute-start(bf16[64,1024]{1,0:T(8,128)(2,1)S(1)} %reduce_sum.61), channel_id=1, source_target_pairs={{0,0},{2,64},{4,128},{6,192},{64,2},{66,66},{68,130},{70,194},{128... | collective-permute-start | bytes 393224 | tf_op jit(solution)/shard_map/ppermute | solution.py:28
  97.4 22.7 %all-to-all-start.3 = ((bf16[32,8,1024]{2,1,0:T(8,128)(2,1)}), bf16[32,8,1024]{2,1,0:T(8,128)(2,1)S(1)}, u32[]{:S(2)}, u32[]{:S(2)}) async-start(bf16[32,8,1024]{2,1,0:T(8,128)(2,1)} %select_select_fusion), calls=%async_computation.3 | async-start | bytes 1048576 | tf_op jit(solution)/shard_map/all_to_all | solution.py:32
  108.2 24.8 %copy-start.1 = (bf16[384,1024]{1,0:T(8,128)(2,1)}, bf16[384,1024]{1,0:T(8,128)(2,1)S(1)}, u32[]{:S(2)}) copy-start(bf16[384,1024]{1,0:T(8,128)(2,1)S(1)} %collective-permute-done.refs_0_) | copy-start | bytes 2359300
  108.2 23.8 %collective-permute-start.2 = (bf16[384,1024]{1,0:T(8,128)(2,1)S(1)}, bf16[384,1024]{1,0:T(8,128)(2,1)}, u32[]{:S(2)}, u32[]{:S(2)}) collective-permute-start(bf16[384,1024]{1,0:T(8,128)(2,1)S(1)} %collective-permute-done.refs_0_), channel_id=1, source_target_pairs={{0,2},{2,4},{4,6},{6,0},{1,3},{3,5},{5,7},{7,1},{8,10},{10,12},{12... | collective-permute-start | bytes 2359304 | tf_op jit(solution)/shard_map/ppermute | solution.py:23
  109.6 29.5 %collective-permute-start.4 = (bf16[384,1024]{1,0:T(8,128)(2,1)S(1)}, bf16[384,1024]{1,0:T(8,128)(2,1)}, u32[]{:S(2)}, u32[]{:S(2)}) collective-permute-start(bf16[384,1024]{1,0:T(8,128)(2,1)S(1)} %collective-permute-done.refs_0_), channel_id=1, source_target_pairs={{0,6},{2,0},{4,2},{6,4},{1,7},{3,1},{5,3},{7,5},{8,14},{10,8},{12,... | collective-permute-start | bytes 2359304 | tf_op jit(solution)/shard_map/ppermute | solution.py:23
  112.3 42.4 %collective-permute-start.1 = (bf16[384,1024]{1,0:T(8,128)(2,1)S(1)}, bf16[384,1024]{1,0:T(8,128)(2,1)S(1)}, u32[]{:S(2)}, u32[]{:S(2)}) collective-permute-start(bf16[384,1024]{1,0:T(8,128)(2,1)S(1)} %collective-permute-done.refs_0_), channel_id=1, source_target_pairs={{0,1},{1,0},{2,3},{3,2},{4,5},{5,4},{6,7},{7,6},{8,9},{9,8},{10,11... | collective-permute-start | bytes 2359304 | tf_op jit(solution)/shard_map/ppermute | solution.py:23
  121.8 33.9 %all-to-all-start.4 = ((bf16[4,128,1024]{2,1,0:T(8,128)(2,1)}), bf16[4,128,1024]{2,1,0:T(8,128)(2,1)S(1)}, u32[]{:S(2)}, u32[]{:S(2)}) async-start(bf16[4,128,1024]{2,1,0:T(8,128)(2,1)} %broadcast_in_dim.149), calls=%async_computation.4 | async-start | bytes 2097152 | tf_op jit(solution)/shard_map/all_to_all | solution.py:32
  133.0 18.5 %collective-permute-start.6 = (bf16[192,1024]{1,0:T(8,128)(2,1)S(1)}, bf16[192,1024]{1,0:T(8,128)(2,1)S(1)}, u32[]{:S(2)}, u32[]{:S(2)}) collective-permute-start(bf16[192,1024]{1,0:T(8,128)(2,1)S(1)} %slice.98), channel_id=1, source_target_pairs={{0,2},{2,4},{4,6},{6,0},{1,3},{3,5},{5,7},{7,1},{8,10},{10,12},{12... | collective-permute-start | bytes 1179656 | tf_op jit(solution)/shard_map/ppermute | solution.py:23
  133.3 25.1 %collective-permute-start.3 = (bf16[384,1024]{1,0:T(8,128)(2,1)}, bf16[384,1024]{1,0:T(8,128)(2,1)}, u32[]{:S(2)}, u32[]{:S(2)}) collective-permute-start(bf16[384,1024]{1,0:T(8,128)(2,1)} %collective-permute-done.2.refs_2_), channel_id=1, source_target_pairs={{0,1},{1,0},{2,3},{3,2},{4,5},{5,4},{6,7},{7,6},{8,9},{9,8},{10,11... | collective-permute-start | bytes 2359304 | tf_op jit(solution)/shard_map/ppermute | solution.py:23
  139.0 19.3 %collective-permute-start.5 = (bf16[384,1024]{1,0:T(8,128)(2,1)}, bf16[384,1024]{1,0:T(8,128)(2,1)}, u32[]{:S(2)}, u32[]{:S(2)}) collective-permute-start(bf16[384,1024]{1,0:T(8,128)(2,1)} %collective-permute-done.4.refs_4_), channel_id=1, source_target_pairs={{0,1},{1,0},{2,3},{3,2},{4,5},{5,4},{6,7},{7,6},{8,9},{9,8},{10,11... | collective-permute-start | bytes 2359304 | tf_op jit(solution)/shard_map/ppermute | solution.py:23
  140.2 14.5 %collective-permute-start.8 = (bf16[192,1024]{1,0:T(8,128)(2,1)S(1)}, bf16[192,1024]{1,0:T(8,128)(2,1)}, u32[]{:S(2)}, u32[]{:S(2)}) collective-permute-start(bf16[192,1024]{1,0:T(8,128)(2,1)S(1)} %slice.99), channel_id=1, source_target_pairs={{0,6},{2,0},{4,2},{6,4},{1,7},{3,1},{5,3},{7,5},{8,14},{10,8},{12,... | collective-permute-start | bytes 1179656 | tf_op jit(solution)/shard_map/ppermute | solution.py:23
  151.6 6.8 %collective-permute-start.7 = (bf16[192,1024]{1,0:T(8,128)(2,1)S(1)}, bf16[192,1024]{1,0:T(8,128)(2,1)}, u32[]{:S(2)}, u32[]{:S(2)}) collective-permute-start(bf16[192,1024]{1,0:T(8,128)(2,1)S(1)} %collective-permute-done.6.refs_6_), channel_id=1, source_target_pairs={{0,1},{1,0},{2,3},{3,2},{4,5},{5,4},{6,7},{7,6},{8,9},{9,8},{10,11... | collective-permute-start | bytes 1179656 | tf_op jit(solution)/shard_map/ppermute | solution.py:23
  154.7 3.7 %collective-permute-start.9 = (bf16[192,1024]{1,0:T(8,128)(2,1)}, bf16[192,1024]{1,0:T(8,128)(2,1)}, u32[]{:S(2)}, u32[]{:S(2)}) collective-permute-start(bf16[192,1024]{1,0:T(8,128)(2,1)} %collective-permute-done.8.refs_8_), channel_id=1, source_target_pairs={{0,1},{1,0},{2,3},{3,2},{4,5},{5,4},{6,7},{7,6},{8,9},{9,8},{10,11... | collective-permute-start | bytes 1179656 | tf_op jit(solution)/shard_map/ppermute | solution.py:23
  154.7 1.0 copy-start.3
  155.7 20.7 %collective-permute-start.14 = (bf16[4,128,1024]{2,1,0:T(8,128)(2,1)S(1)}, bf16[4,128,1024]{2,1,0:T(8,128)(2,1)S(1)}, u32[]{:S(2)}, u32[]{:S(2)}) collective-permute-start(bf16[4,128,1024]{2,1,0:T(8,128)(2,1)S(1)} %all-to-all-done.4.refs_0_), channel_id=1, source_target_pairs={{0,1},{1,0},{2,3},{3,2},{4,5},{5,4},{6,7},{7,6},{8,9},{9,8},{10,11... | collective-permute-start | bytes 3145736 | tf_op jit(solution)/shard_map/ppermute | solution.py:23
  158.4 1.9 copy-start
  160.3 1.1 copy-start.2
  161.4 1.1 copy-start.4
  172.7 18.4 %collective-permute-start.10 = (bf16[384,896]{1,0:T(8,128)(2,1)}, bf16[384,896]{1,0:T(8,128)(2,1)S(1)}, u32[]{:S(2)}, u32[]{:S(2)}) collective-permute-start(bf16[384,896]{1,0:T(8,128)(2,1)} %get-tuple-element.9), channel_id=1, source_target_pairs={{0,64},{64,128},{128,192},{192,0},{1,65},{65,129},{129,193},{193,1... | collective-permute-start | bytes 2064392 | tf_op jit(solution)/shard_map/ppermute | solution.py:23
  172.8 31.5 %collective-permute-start.11 = (bf16[384,896]{1,0:T(8,128)(2,1)}, bf16[384,896]{1,0:T(8,128)(2,1)}, u32[]{:S(2)}, u32[]{:S(2)}) collective-permute-start(bf16[384,896]{1,0:T(8,128)(2,1)} %get-tuple-element.8), channel_id=1, source_target_pairs={{0,192},{64,0},{128,64},{192,128},{1,193},{65,1},{129,65},{193,129... | collective-permute-start | bytes 2064392 | tf_op jit(solution)/shard_map/ppermute | solution.py:23
  175.4 31.6 %collective-permute-start.12 = (bf16[384,896]{1,0:T(8,128)(2,1)}, bf16[384,896]{1,0:T(8,128)(2,1)}, u32[]{:S(2)}, u32[]{:S(2)}) collective-permute-start(bf16[384,896]{1,0:T(8,128)(2,1)} %get-tuple-element.7), channel_id=1, source_target_pairs={{0,128},{64,192},{128,0},{192,64},{1,129},{65,193},{129,1},{193,65... | collective-permute-start | bytes 2064392 | tf_op jit(solution)/shard_map/ppermute | solution.py:23
  180.7 36.0 %all-to-all-start.5 = ((bf16[4,128,896]{2,1,0:T(8,128)(2,1)}), bf16[4,128,896]{2,1,0:T(8,128)(2,1)S(1)}, u32[]{:S(2)}, u32[]{:S(2)}) async-start(bf16[4,128,896]{2,1,0:T(8,128)(2,1)} %shard_map.101), calls=%async_computation.5 | async-start | bytes 1835008 | tf_op jit(solution)/shard_map/all_to_all | solution.py:32
Sparse Core Ops, SparseCore 0:
  9.1 49.7 all-gather.4
  60.7 43.1 all-gather.2

commit v2 on v1

--- a/solution.py
+++ b/solution.py
@@ -23,8 +23,8 @@
     return lax.ppermute(array, axis, [(i, (i + by) % size) for i in range(size)])
 
 
-def swap_xy(array):
-    pairs = [(i * NY + j, j * NY + i) for i in range(NX) for j in range(NY)]
+def swap_xy(array, flip=0):
+    pairs = [(i * NY + j, j * NY + (i ^ flip)) for i in range(NX) for j in range(NY)]
     return lax.ppermute(array, ("x", "y"), pairs)
 
 
@@ -59,31 +59,79 @@
     )
 
 
-def project(where, pieces, weight, gain, rows, relative):
+def load_all(where_ref, plan, srcs, b_src, a_ref, b_ref, a_sem, b_sem):
+    y, c = where_ref[1], where_ref[2]
+    loads = [pltpu.make_async_copy(b_src, b_ref, b_sem)]
+    for k, (n, at, dy, sample, row, length, flip) in enumerate(plan):
+        s = sample if dy is None else lax.rem(y + (dy + NY), NY)
+        core = c if flip == 0 else 1 - c
+        source = srcs[n] if at is None else srcs[n].at[at]
+        target = a_ref.at[s, core, pl.ds(row, length), :]
+        loads.append(pltpu.make_async_copy(source, target, a_sem.at[k]))
+    for copy in loads:
+        copy.start()
+    for copy in loads:
+        copy.wait()
+
+
+def project_text(where, pieces, weight):
     arrays = [a for a, _ in pieces]
     plan = [(n, *part) for n, (_, parts) in enumerate(pieces) for part in parts]
     count = len(arrays)
+    half = SEQ // 2
 
     def kernel(where_ref, *refs):
-        srcs, b_src, gain_ref, out_ref = refs[:count], refs[count], refs[count + 1], refs[count + 2]
-        a_ref, b_ref, a_sem, b_sem = refs[count + 3 :]
-        x, y, c = where_ref[0], where_ref[1], where_ref[2]
-        loads = [pltpu.make_async_copy(b_src, b_ref, b_sem)]
-        for k, (n, at, dy, sample, row, length, flip) in enumerate(plan):
-            s = sample if dy is None else lax.rem(y + (dy + NY), NY)
-            core = c if flip == 0 else 1 - c
-            source = srcs[n] if at is None else srcs[n].at[at]
-            target = a_ref.at[s, core, pl.ds(row, length), :]
-            loads.append(pltpu.make_async_copy(source, target, a_sem.at[k]))
-        for copy in loads:
-            copy.start()
-        for copy in loads:
-            copy.wait()
-        lane = lax.broadcasted_iota(jnp.int32, (rows, 128), 1)
-
-        def one(s, carry):
-            total = jnp.zeros((rows, 1), jnp.float32)
-            acc = jnp.zeros((rows, COLS), jnp.float32)
+        own_ref, up_ref, down_ref, a_ref, b_ref, a_sem, b_sem = refs[count + 1 :]
+        load_all(where_ref, plan, refs[:count], refs[count], a_ref, b_ref, a_sem, b_sem)
+        x = where_ref[0]
+        for n in range(NX):
+            s = lax.rem(x + n, NX)
+            acc = jnp.dot(a_ref[s, 0], b_ref[:1024, :], preferred_element_type=jnp.float32)
+            acc = acc + jnp.dot(a_ref[s, 1], b_ref[1024:, :], preferred_element_type=jnp.float32)
+            acc = acc.astype(jnp.bfloat16)
+            if n == 0:
+                own_ref[...] = acc
+            elif n == 1:
+                up_ref[:SEQ, :] = acc
+            elif n == 2:
+                up_ref[SEQ:, :] = acc[:half]
+                down_ref[:half, :] = acc[half:]
+            else:
+                down_ref[half:, :] = acc
+
+    any_spec = pl.BlockSpec(memory_space=pl.ANY)
+    vmem = pl.BlockSpec(memory_space=pltpu.VMEM)
+    return pl.pallas_call(
+        kernel,
+        out_shape=[
+            jax.ShapeDtypeStruct((n, COLS), jnp.bfloat16) for n in (SEQ, SEQ + half, SEQ + half)
+        ],
+        in_specs=[pl.BlockSpec(memory_space=pltpu.SMEM)] + [any_spec] * (count + 1),
+        out_specs=[vmem] * 3,
+        scratch_shapes=[
+            pltpu.VMEM((NX, NC, SEQ, 1024), jnp.bfloat16),
+            pltpu.VMEM((2048, COLS), jnp.bfloat16),
+            pltpu.SemaphoreType.DMA((len(plan),)),
+            pltpu.SemaphoreType.DMA,
+        ],
+        compiler_params=pltpu.CompilerParams(vmem_limit_bytes=40 * 1024 * 1024),
+        name="project_text",
+    )(where, *arrays, weight)
+
+
+def project_image(where, pieces, weight, gain):
+    arrays = [a for a, _ in pieces]
+    plan = [(n, *part) for n, (_, parts) in enumerate(pieces) for part in parts]
+    count = len(arrays)
+
+    def kernel(where_ref, *refs):
+        gain_ref, out_ref, a_ref, b_ref, a_sem, b_sem = refs[count + 1 :]
+        load_all(where_ref, plan, refs[:count], refs[count], a_ref, b_ref, a_sem, b_sem)
+        lane = lax.broadcasted_iota(jnp.int32, (SPAN, 128), 1)
+
+        for s in range(NX):
+            total = jnp.zeros((SPAN, 1), jnp.float32)
+            acc = jnp.zeros((SPAN, COLS), jnp.float32)
             for core in range(NC):
                 value = a_ref[s, core].astype(jnp.float32)
                 total = total + jnp.sum(value * value, axis=1, keepdims=True)
@@ -94,46 +142,47 @@
                 )
             high = total.astype(jnp.bfloat16).astype(jnp.float32)
             low = total - high
-            slot = lax.rem(s - x + NX, NX) if relative else s
-            out_ref[slot, :, :COLS] = acc.astype(jnp.bfloat16)
-            out_ref[slot, :, COLS:] = jnp.where(
+            out_ref[s, :, :COLS] = acc.astype(jnp.bfloat16)
+            out_ref[s, :, COLS:] = jnp.where(
                 lane == 0, high, jnp.where(lane == 1, low, 0.0)
             ).astype(jnp.bfloat16)
-            return carry
-
-        lax.fori_loop(0, NX, one, 0)
 
     any_spec = pl.BlockSpec(memory_space=pl.ANY)
     vmem = pl.BlockSpec(memory_space=pltpu.VMEM)
     return pl.pallas_call(
         kernel,
-        out_shape=jax.ShapeDtypeStruct((NX, rows, WIRE), jnp.bfloat16),
+        out_shape=jax.ShapeDtypeStruct((NX, SPAN, WIRE), jnp.bfloat16),
         in_specs=[pl.BlockSpec(memory_space=pltpu.SMEM)] + [any_spec] * (count + 1) + [vmem],
         out_specs=vmem,
         scratch_shapes=[
-            pltpu.VMEM((NX, NC, rows, 1024), jnp.bfloat16),
+            pltpu.VMEM((NX, NC, SPAN, 1024), jnp.bfloat16),
             pltpu.VMEM((2048, COLS), jnp.bfloat16),
             pltpu.SemaphoreType.DMA((len(plan),)),
             pltpu.SemaphoreType.DMA,
         ],
         compiler_params=pltpu.CompilerParams(vmem_limit_bytes=40 * 1024 * 1024),
-        cost_estimate=pl.CostEstimate(
-            flops=2 * NX * rows * 2048 * COLS, bytes_accessed=10000000, transcendentals=0
-        ),
+        name="project_image",
     )(where, *arrays, weight, gain)
 
 
 def attention(where, text_parts, image_parts, tables, image_tables):
-    def kernel(where_ref, t0, t1, t2, t3, i_ref, cos_ref, sin_ref, icos_ref, isin_ref, out_ref):
+    half = SEQ // 2
+
+    def kernel(
+        where_ref, own, up, down, low, high, i_ref, cos_ref, sin_ref, icos_ref, isin_ref, out_ref
+    ):
         start, n_rows = where_ref[0], where_ref[1]
 
-        def summed(parts):
-            total = parts[0].astype(jnp.float32)
-            for p in parts[1:]:
-                total = total + p.astype(jnp.float32)
-            squares = jnp.sum(total[:, COLS:], axis=1, keepdims=True)
-            scale = lax.rsqrt(squares * (1.0 / WIDTH) + decoder_epsilon)
-            return total[:, :COLS] * scale
+        def wide(array):
+            return array.astype(jnp.float32)
+
+        text_sum = wide(own[...]) + wide(up[:SEQ]) + wide(down[half:])
+        text_sum = jnp.concatenate(
+            [text_sum[:half] + wide(low[...]), text_sum[half:] + wide(high[...])], axis=0
+        )
+        image_sum = wide(i_ref[0]) + wide(i_ref[1]) + wide(i_ref[2]) + wide(i_ref[3])
+        squares = jnp.sum(image_sum[:, COLS:], axis=1, keepdims=True)
+        image_sum = image_sum[:, :COLS] * lax.rsqrt(squares * (1.0 / WIDTH) + decoder_epsilon)
 
         def heads(total, cos, sin):
             pieces = []
@@ -143,8 +192,8 @@
             pieces.append(total[:, 5 * HEAD :].astype(jnp.bfloat16))
             return pieces
 
-        text = heads(summed([t0[...], t1[...], t2[...], t3[...]]), cos_ref[...], sin_ref[...])
-        image = heads(summed([i_ref[n] for n in range(NX)]), icos_ref[...], isin_ref[...])
+        text = heads(text_sum, cos_ref[...], sin_ref[...])
+        image = heads(image_sum, icos_ref[...], isin_ref[...])
         p_at = lax.broadcasted_iota(jnp.int32, (SEQ, SPAN), 0) - start
         j_at = lax.broadcasted_iota(jnp.int32, (SEQ, SPAN), 1)
         pick = jnp.where((p_at == j_at) & (j_at < n_rows), 1.0, 0.0).astype(jnp.bfloat16)
@@ -175,29 +224,42 @@
     return pl.pallas_call(
         kernel,
         out_shape=jax.ShapeDtypeStruct((SEQ, 512), jnp.bfloat16),
-        in_specs=[pl.BlockSpec(memory_space=pltpu.SMEM)] + [vmem] * 9,
+        in_specs=[pl.BlockSpec(memory_space=pltpu.SMEM)] + [vmem] * 10,
         out_specs=vmem,
         compiler_params=pltpu.CompilerParams(vmem_limit_bytes=40 * 1024 * 1024),
         name="attention",
     )(where, *text_parts, image_parts, *tables, *image_tables)
 
 
-def vision(vis_rows, ln_gain, ln_bias, weight):
+def vision(vis_rows, squares, ln_gain, ln_bias, weight):
     tokens = vis_rows.shape[0] * vis_rows.shape[1]
-    whole = spread(vis_rows.reshape(tokens, 2, 400), ("y", "c")).astype(jnp.float32)
-    mean = jnp.mean(whole, axis=(0, 2, 3))[None, :, None, None]
+    parts, rest = [], squares
+    for _ in range(3):
+        parts.append(lax.reduce_precision(rest, 8, 7))
+        rest = rest - parts[-1]
+    rows = jnp.pad(jnp.stack(parts), ((0, 13), (0, 400 - SEQ))).astype(jnp.bfloat16)
+    by_part = jnp.moveaxis(vis_rows, 2, 0).reshape(2 * tokens, 400)
+    sent = jnp.concatenate([by_part, rows], axis=0)
+    arrived = spread(sent, ("y", "c")).astype(jnp.float32)
+    text_squares = jnp.sum(arrived[:, 2 * tokens : 2 * tokens + 3, :SEQ], axis=(0, 1))
+    whole = arrived[:, : 2 * tokens].reshape(8, 2, tokens, 400)
+    mean = jnp.mean(whole, axis=(0, 1, 3))[None, None, :, None]
     centered = whole - mean
-    variance = jnp.mean(centered * centered, axis=(0, 2, 3))[None, :, None, None]
-    gain = jnp.swapaxes(ln_gain.reshape(2, 8, 400), 0, 1)[:, None]
-    bias = jnp.swapaxes(ln_bias.reshape(2, 8, 400), 0, 1)[:, None]
+    variance = jnp.mean(centered * centered, axis=(0, 1, 3))[None, None, :, None]
+    gain = jnp.swapaxes(ln_gain.reshape(2, 8, 400), 0, 1)[:, :, None]
+    bias = jnp.swapaxes(ln_bias.reshape(2, 8, 400), 0, 1)[:, :, None]
     normed = (centered * lax.rsqrt(variance + vision_epsilon) * gain + bias).astype(jnp.bfloat16)
-    acts = exchange(normed.reshape(4, 2, tokens, 2, 400), "x")
+    acts = exchange(normed.reshape(4, 2, 2, tokens, 400), "x")
     partial = jnp.einsum(
-        "sctmf,cfmo->sto", acts, weight.reshape(2, 400, 2, 1024),
+        "scmtf,cfmo->sto", acts, weight.reshape(2, 400, 2, 1024),
         preferred_element_type=jnp.float32,
     ).astype(jnp.bfloat16)
-    parts = exchange(partial, "x")
-    return jnp.sum(parts.astype(jnp.float32), axis=0).astype(jnp.bfloat16)
+    total = None
+    for k in range(NX):
+        part = lax.dynamic_index_in_dim(partial, lax.axis_index("x") ^ k, 0, keepdims=False)
+        part = swap_xy(part, k).astype(jnp.float32)
+        total = part if total is None else total + part
+    return total.astype(jnp.bfloat16), text_squares
 
 
 def step(
@@ -217,9 +279,15 @@
     both = jnp.concatenate([w_query, key_value_weight.reshape(256, 256)], axis=1)
     both_all = lax.all_gather(both, "z", axis=0, tiled=True)
 
-    image = vision(vis_rows, ln_gain, ln_bias, proj_all)
-
-    turned = swap_xy(text_rows[0])
+    sequence = text_rows[0]
+    wide = sequence.astype(jnp.float32)
+    squares = jnp.sum(wide * wide, axis=1)
+    image, squares = vision(vis_rows, squares, ln_gain, ln_bias, proj_all)
+    scale = lax.rsqrt(squares * (1.0 / WIDTH) + decoder_epsilon)[:, None]
+    own_gain = lax.dynamic_slice_in_dim(attn_gain, (y * NC + c) * 1024, 1024)
+    normed = (wide * scale * own_gain[None]).astype(jnp.bfloat16)
+
+    turned = swap_xy(normed)
     own = ring4(turned, "y")
     text = []
     for a, dy, row in own:
@@ -227,7 +295,7 @@
         text.append((a, [(None, dy, None, row, a.shape[0], 0)]))
         text.append((other, [(None, dy, None, row, a.shape[0], 1)]))
 
-    image = swap_xy(image).reshape(8, 8, 1024)
+    image = image.reshape(8, 8, 1024)
     place = y * NZ + z
     tiles_here = jnp.arange(8, dtype=jnp.int32) * 32 + place
     owners = jnp.sum((tile_ends[None, :] <= tiles_here[:, None]).astype(jnp.int32), axis=1)
@@ -246,14 +314,13 @@
 
     gain = lax.dynamic_slice_in_dim(attn_gain, x * 2048, 2048).reshape(2, 1024)
     where = jnp.stack([x, y, c]).astype(jnp.int32)
-    text_out = project(where, text, both_all, gain, SEQ, True)
-    text_parts = [
-        text_out[0],
-        shift(text_out[1], "x", 1),
-        shift(text_out[3], "x", -1),
-        shift(text_out[2], "x", 2),
-    ]
-    image_out = project(where, image_pieces, both_all, gain, SPAN, False)
+    own_sum, up, down = project_text(where, text, both_all)
+    up = shift(up, "x", 1)
+    down = shift(down, "x", -1)
+    low = shift(up[SEQ:], "x", 1)
+    high = shift(down[: SEQ // 2], "x", -1)
+    text_parts = [own_sum, up, down, low, high]
+    image_out = project_image(where, image_pieces, both_all, gain)
     image_parts = exchange(image_out, "x")
 
     tables = rope_tables()

time: 229 us -> 257 us (1.12)
  local copies, waits for them, and re-layouts: 14 us -> 28.4 us
  starting transfers between devices: 56.4 us -> 63 us
  other arithmetic: 12.1 us -> 17.6 us
    ppermute x2 -> x5, waiting for transfers between devices: 0.01 us -> 50.4 us  [swap_xy(): return lax.ppermute(array, ('x', 'y'), pairs)]
    all_to_all x6 -> x5, waiting for transfers between devices: 63.2 us -> 32.2 us  [exchange(): return lax.all_to_all(array, axis, 0, 0, tiled=True)]
    ppermute x13 -> x14, waiting for transfers between devices: 36.9 us -> 26.8 us  [shift(): lax.ppermute(array, axis, [(i, (i + by) % size) for i in range(size)])]
    unnamed x23 -> x61, local copies, waits for them, and re-layouts: 5.17 us -> 13.2 us
    all_gather x1, waiting for transfers between devices: 7.89 us -> 0.01 us  [step(): proj_all = lax.all_gather(proj_weight, 'z', axis=0, tiled=True)]
    ppermute x2 -> x5, starting transfers between devices: 1.38 us -> 8.65 us  [swap_xy(): return lax.ppermute(array, ('x', 'y'), pairs)]
    reduce_sum x3 -> x6, other arithmetic: 0.81 us -> 4.91 us  [the longest x2 2.22 us: vision(): jnp.mean(centered * centered, axis=(0, 1, 3))[None, None, :, None]]
    all_to_all x6 -> x5, starting transfers between devices: 32.1 us -> 29.6 us  [exchange(): return lax.all_to_all(array, axis, 0, 0, tiled=True)]
  transfers between devices with their start and end apart: 23 -> 26, of which waited for: 11 -> 11; matrix products, arithmetic and copies ran while one was open for 11% -> 14% of each run, Pallas kernels for 6% -> 5%
where the time goes in v2:
time: 257 us; the launch traced here: 255 us
  waiting for transfers between devices  110 us (43%)
  starting transfers between devices  63 us (25%)
  local copies, waits for them, and re-layouts  28.4 us (11%)
  Pallas kernels  17.7 us (7%)
  other arithmetic  17.6 us (7%)
  between operations  15.1 us (6%)
  matrix products  3.38 us (1%)
    ppermute x5, waiting for transfers between devices, swap_xy(): return lax.ppermute(array, ('x', 'y'), pairs)  50.4 us
    all_to_all x5, waiting for transfers between devices, exchange(): return lax.all_to_all(array, axis, 0, 0, tiled=True)  32.2 us
    all_to_all x5, starting transfers between devices, exchange(): return lax.all_to_all(array, axis, 0, 0, tiled=True)  29.6 us
    ppermute x14, waiting for transfers between devices, shift(): lax.ppermute(array, axis, [(i, (i + by) % size) for i in range(size)])  26.8 us
    ppermute x14, starting transfers between devices, shift(): lax.ppermute(array, axis, [(i, (i + by) % size) for i in range(size)])  24.8 us
    unnamed x61, local copies, waits for them, and re-layouts  13.2 us
    ppermute x5, starting transfers between devices, swap_xy(): return lax.ppermute(array, ('x', 'y'), pairs)  8.65 us
    pallas_call x1, Pallas kernels, project_text(): pl.pallas_call(kernel, out_shape=[jax.ShapeDtypeStruct((n, COLS), jnp.bfl...  8.6 us
  transfers between devices with their start and end apart: 26, of which 11 were waited for; matrix products, arithmetic and copies ran while one was open for 14% of the time, Pallas kernels for 5%

profile of v2, /device:TPU:1, one launch (start us, length us, event | category | flops | bytes accessed | tf_op | source)
XLA Modules:
  0.0 255.3 jit_solution(9784704908290494049)
XLA Ops:
  7.3 0.9 copy.40
  8.2 1.4 fusion.3
  9.6 1.2 broadcast_in_dim.130
  10.9 6.8 %all-to-all-start = ((bf16[8,144,400]{2,1,0:T(8,128)(2,1)}), bf16[8,144,400]{2,1,0:T(8,128)(2,1)S(1)}, u32[]{:S(2)}, u32[]{:S(2)}) async-start(bf16[8,144,400]{2,1,0:T(8,128)(2,1)} %broadcast_in_dim.130), calls=%async_computation | async-start | bytes 2359296 | tf_op jit(solution)/shard_map/all_to_all | solution.py:32
  17.7 0.8 pad_maximum_fusion
  21.2 1.2 iota_compare_fusion.2
  22.4 11.7 %all-to-all-done = bf16[8,144,400]{2,1,0:T(8,128)(2,1)S(1)} async-done(((bf16[8,144,400]{2,1,0:T(8,128)(2,1)}), bf16[8,144,400]{2,1,0:T(8,128)(2,1)S(1)}, u32[]{:S(2)}, u32[]{:S(2)}) %all-to-all-start) | async-done | bytes 921632 | tf_op jit(solution)/shard_map/all_to_all | solution.py:32
  37.6 1.3 sub.50
  38.9 1.6 multiply_reduce_fusion
  40.6 0.8 reduce_sum.88
  42.7 1.5 add_convert_fusion
  44.2 3.5 %all-to-all-start.1 = ((bf16[4,2,2,64,400]{4,3,2,1,0:T(8,128)(2,1)}), bf16[4,2,2,64,400]{4,3,2,1,0:T(8,128)(2,1)S(1)}, u32[]{:S(2)}, u32[]{:S(2)}) async-start(bf16[4,2,2,64,400]{4,3,2,1,0:T(8,128)(2,1)} %add_convert_fusion), calls=%async_computation.1 | async-start | bytes 2097152 | tf_op jit(solution)/shard_map/all_to_all | solution.py:32
  47.7 1.2 iota_compare_fusion.4
  49.0 1.2 iota_compare_fusion.6
  50.2 1.3 iota_compare_fusion.8
  51.6 10.2 %all-to-all-done.1 = bf16[4,2,2,64,400]{4,3,2,1,0:T(8,128)(2,1)S(1)} async-done(((bf16[4,2,2,64,400]{4,3,2,1,0:T(8,128)(2,1)}), bf16[4,2,2,64,400]{4,3,2,1,0:T(8,128)(2,1)S(1)}, u32[]{:S(2)}, u32[]{:S(2)}) %all-to-all-start.1) | async-done | bytes 819232 | tf_op jit(solution)/shard_map/all_to_all | solution.py:32
  61.9 3.4 %fusion.9 = bf16[4,64,1024]{2,1,0:T(8,128)(2,1)S(1)} fusion(bf16[4,2,2,64,400]{4,3,2,1,0:T(8,128)(2,1)S(1)} %all-to-all-done.1, bf16[2,400,2,1024,1]{3,2,1,0,4:T(2,128)(2,1)} %bitcast.74), kind=kOutput, calls=%fused_computation.12 | convolution fusion | flops 839122944 | bytes 4620288 | tf_op jit(solution)/shard_map/scmtf,cfmo->sto/dot_general | solution.py:253
  66.0 2.8 %collective-permute-start.15 = (bf16[64,1024]{1,0:T(8,128)(2,1)S(1)}, bf16[64,1024]{1,0:T(8,128)(2,1)S(1)}, u32[]{:S(2)}, u32[]{:S(2)}) collective-permute-start(bf16[64,1024]{1,0:T(8,128)(2,1)S(1)} %get-tuple-element.16), channel_id=1, source_target_pairs={{0,2},{2,66},{4,130},{6,194},{64,0},{66,64},{68,128},{70,192},{128... | collective-permute-start | bytes 393224 | tf_op jit(solution)/shard_map/ppermute | solution.py:28
  68.8 2.4 collective-permute-start.16
  71.2 2.1 collective-permute-start.17
  74.2 2.6 %collective-permute-done.15 = bf16[64,1024]{1,0:T(8,128)(2,1)S(1)} collective-permute-done((bf16[64,1024]{1,0:T(8,128)(2,1)S(1)}, bf16[64,1024]{1,0:T(8,128)(2,1)S(1)}, u32[]{:S(2)}, u32[]{:S(2)}) %collective-permute-start.15) | collective-permute-done | bytes 131104 | tf_op jit(solution)/shard_map/ppermute | solution.py:28
  76.8 47.8 %collective-permute-done.16 = bf16[64,1024]{1,0:T(8,128)(2,1)S(1)} collective-permute-done((bf16[64,1024]{1,0:T(8,128)(2,1)S(1)}, bf16[64,1024]{1,0:T(8,128)(2,1)S(1)}, u32[]{:S(2)}, u32[]{:S(2)}) %collective-permute-start.16) | collective-permute-done | bytes 131104 | tf_op jit(solution)/shard_map/ppermute | solution.py:28
  124.8 1.2 select_select_fusion
  126.0 11.5 %all-to-all-start.2 = ((bf16[32,8,1024]{2,1,0:T(8,128)(2,1)}), bf16[32,8,1024]{2,1,0:T(8,128)(2,1)}, u32[]{:S(2)}, u32[]{:S(2)}) async-start(bf16[32,8,1024]{2,1,0:T(8,128)(2,1)} %select_select_fusion), calls=%async_computation.2 | async-start | bytes 1048576 | tf_op jit(solution)/shard_map/all_to_all | solution.py:32
  137.5 1.2 collective-permute-start.2
  138.8 1.8 collective-permute-start.4
  141.9 1.8 collective-permute-start.1
  143.7 7.7 %all-to-all-done.2 = bf16[32,8,1024]{2,1,0:T(8,128)(2,1)} async-done(((bf16[32,8,1024]{2,1,0:T(8,128)(2,1)}), bf16[32,8,1024]{2,1,0:T(8,128)(2,1)}, u32[]{:S(2)}, u32[]{:S(2)}) %all-to-all-start.2) | async-done | bytes 524320 | tf_op jit(solution)/shard_map/all_to_all | solution.py:32
  151.4 1.6 gather_fusion
  153.1 1.1 broadcast_in_dim.149
  154.2 4.2 %all-to-all-start.3 = ((bf16[4,128,1024]{2,1,0:T(8,128)(2,1)}), bf16[4,128,1024]{2,1,0:T(8,128)(2,1)}, u32[]{:S(2)}, u32[]{:S(2)}) async-start(bf16[4,128,1024]{2,1,0:T(8,128)(2,1)} %broadcast_in_dim.149), calls=%async_computation.3 | async-start | bytes 2097152 | tf_op jit(solution)/shard_map/all_to_all | solution.py:32
  158.4 4.1 %collective-permute-done.2.refs_2_ = bf16[384,1024]{1,0:T(8,128)(2,1)S(1)} collective-permute-done((bf16[384,1024]{1,0:T(8,128)(2,1)S(1)}, bf16[384,1024]{1,0:T(8,128)(2,1)S(1)}, u32[]{:S(2)}, u32[]{:S(2)}) %collective-permute-start.2) | collective-permute-done | bytes 786464 | tf_op jit(solution)/shard_map/ppermute | solution.py:23
  162.5 0.8 slice.99
  163.4 0.8 slice.100
  164.2 2.7 %collective-permute-start.8 = (bf16[192,1024]{1,0:T(8,128)(2,1)}, bf16[192,1024]{1,0:T(8,128)(2,1)}, u32[]{:S(2)}, u32[]{:S(2)}) collective-permute-start(bf16[192,1024]{1,0:T(8,128)(2,1)} %slice.100), channel_id=1, source_target_pairs={{0,6},{2,0},{4,2},{6,4},{1,7},{3,1},{5,3},{7,5},{8,14},{10,8},{12,... | collective-permute-start | bytes 1179656 | tf_op jit(solution)/shard_map/ppermute | solution.py:23
  166.9 4.0 %collective-permute-start.3 = (bf16[384,1024]{1,0:T(8,128)(2,1)S(1)}, bf16[384,1024]{1,0:T(8,128)(2,1)}, u32[]{:S(2)}, u32[]{:S(2)}) collective-permute-start(bf16[384,1024]{1,0:T(8,128)(2,1)S(1)} %collective-permute-done.2.refs_2_), channel_id=1, source_target_pairs={{0,1},{1,0},{2,3},{3,2},{4,5},{5,4},{6,7},{7,6},{8,9},{9,8},{10,11... | collective-permute-start | bytes 2359304 | tf_op jit(solution)/shard_map/ppermute | solution.py:23
  170.9 0.9 copy-done.9
  171.7 2.5 all-to-all-done.3.refs_0_
  174.3 4.8 %collective-permute-start.18 = (bf16[4,128,1024]{2,1,0:T(8,128)(2,1)}, bf16[4,128,1024]{2,1,0:T(8,128)(2,1)}, u32[]{:S(2)}, u32[]{:S(2)}) collective-permute-start(bf16[4,128,1024]{2,1,0:T(8,128)(2,1)} %all-to-all-done.3.refs_0_), channel_id=1, source_target_pairs={{0,1},{1,0},{2,3},{3,2},{4,5},{5,4},{6,7},{7,6},{8,9},{9,8},{10,11... | collective-permute-start | bytes 3145736 | tf_op jit(solution)/shard_map/ppermute | solution.py:23
  179.1 2.4 collective-permute-done.6.refs_6_
  181.5 2.7 %collective-permute-start.7 = (bf16[192,1024]{1,0:T(8,128)(2,1)S(1)}, bf16[192,1024]{1,0:T(8,128)(2,1)S(1)}, u32[]{:S(2)}, u32[]{:S(2)}) collective-permute-start(bf16[192,1024]{1,0:T(8,128)(2,1)S(1)} %collective-permute-done.6.refs_6_), channel_id=1, source_target_pairs={{0,1},{1,0},{2,3},{3,2},{4,5},{5,4},{6,7},{7,6},{8,9},{9,8},{10,11... | collective-permute-start | bytes 1179656 | tf_op jit(solution)/shard_map/ppermute | solution.py:23
  184.3 1.3 collective-permute-done.7.refs_7_
  186.4 0.8 copy-done.15
  187.2 1.9 copy-done
  189.1 1.1 copy-done.4
  190.2 1.1 copy-done.6
  191.3 1.1 copy-done.8
  192.5 1.1 copy-done.10
  193.6 1.0 copy-done.14
  194.6 1.0 copy-done.16
  195.6 8.6 %project_text.1 = (bf16[384,768]{1,0:T(8,128)(2,1)S(1)}, bf16[576,768]{1,0:T(8,128)(2,1)}, bf16[576,768]{1,0:T(8,128)(2,1)}) custom-call(s32[3]{0:T(128)S(1)} %pad_add_fusion.1.where_ref, bf16[384,1024]{1,0:T(8,128)(2,1)S(1)} %copy-done.8, bf16[384,1024]{1,0:T(8,128)(2,1)S(1)} %copy-done.10, bf16[384,1024]{1,0:T(8,128)(2,1)S(1)} %copy-done.4, ...), custom_call_target="tpu_custom_call" | custom-call | tf_op jit(solution)/shard_map/project_text/pallas_call | solution.py:104
  204.2 0.9 copy-done.11
  205.1 0.9 collective-permute-start.10
  206.0 1.8 collective-permute-start.11
  209.7 4.2 %project_image.1 = bf16[4,128,896]{2,1,0:T(8,128)(2,1)S(1)} custom-call(s32[3]{0:T(128)S(1)} %pad_add_fusion.1.where_ref, bf16[4,128,1024]{2,1,0:T(8,128)(2,1)} %all-to-all-done.3.refs_0_, bf16[4,128,1024]{2,1,0:T(8,128)(2,1)} %collective-permute-done.18.refs_1_, bf16[2048,768]{1,0:T(8,128)(2,1)S(1)} %copy-done.1, f32[2,1024]{1,0:T(2,128)S(1)} %reshape.223.refs_3_), custom_call_target="tpu_custom_call" | custom-call | tf_op jit(solution)/shard_map/project_image/pallas_call | solution.py:152
  214.0 0.9 copy-done.2
  214.9 3.5 %all-to-all-start.4 = ((bf16[4,128,896]{2,1,0:T(8,128)(2,1)}), bf16[4,128,896]{2,1,0:T(8,128)(2,1)S(1)}, u32[]{:S(2)}, u32[]{:S(2)}) async-start(bf16[4,128,896]{2,1,0:T(8,128)(2,1)} %copy-done.2), calls=%async_computation.4 | async-start | bytes 1835008 | tf_op jit(solution)/shard_map/all_to_all | solution.py:32
  218.4 0.8 fusion.14
  219.2 8.3 %collective-permute-done.10.up = bf16[576,768]{1,0:T(8,128)(2,1)} collective-permute-done((bf16[576,768]{1,0:T(8,128)(2,1)}, bf16[576,768]{1,0:T(8,128)(2,1)}, u32[]{:S(2)}, u32[]{:S(2)}) %collective-permute-start.10) | collective-permute-done | bytes 884768 | tf_op jit(solution)/shard_map/ppermute | solution.py:23
  227.5 1.0 slice.101
  228.5 1.0 slice.102
  229.5 3.0 %collective-permute-start.13 = (bf16[192,768]{1,0:T(8,128)(2,1)S(1)}, bf16[192,768]{1,0:T(8,128)(2,1)S(1)}, u32[]{:S(2)}, u32[]{:S(2)}) collective-permute-start(bf16[192,768]{1,0:T(8,128)(2,1)S(1)} %slice.102), channel_id=1, source_target_pairs={{0,192},{64,0},{128,64},{192,128},{1,193},{65,1},{129,65},{193,129... | collective-permute-start | bytes 884744 | tf_op jit(solution)/shard_map/ppermute | solution.py:23
  232.8 10.7 %collective-permute-done.12.low = bf16[192,768]{1,0:T(8,128)(2,1)S(1)} collective-permute-done((bf16[192,768]{1,0:T(8,128)(2,1)S(1)}, bf16[192,768]{1,0:T(8,128)(2,1)S(1)}, u32[]{:S(2)}, u32[]{:S(2)}) %collective-permute-start.12) | collective-permute-done | bytes 294944 | tf_op jit(solution)/shard_map/ppermute | solution.py:23
  243.5 4.9 %attention.1 = bf16[384,512]{1,0:T(8,128)(2,1)} custom-call(s32[2]{0:T(128)S(1)} %pad_add_fusion.where_ref, bf16[384,768]{1,0:T(8,128)(2,1)S(1)} %copy-done.12, bf16[576,768]{1,0:T(8,128)(2,1)} %collective-permute-done.10.up, bf16[576,768]{1,0:T(8,128)(2,1)} %collective-permute-done.11.down, bf16[192,768]{1,0:T(8,128)(2,1)S(1)} %collective-permute-done.12.low, ...), custom_call_target="tpu_custom_call" | custom-call | tf_op jit(solution)/shard_map/attention/pallas_call | solution.py:224
  (116 shorter events, 13.5 us)
Async XLA Ops:
  6.5 55.3 %all-gather.5.cloned.1.call-start = ((), (), s32[]{:S(2)}) async-start(), calls=%async_computation.6 | async-start | bytes 3686400 | tf_op jit(solution)/shard_map/all_gather | solution.py:278
  9.5 8.1 %copy-start.21 = (bf16[256,2,128]{2,1,0:T(2,128)(2,1)S(1)}, bf16[256,2,128]{2,1,0:T(2,128)(2,1)}, u32[]{:S(2)}) copy-start(bf16[256,2,128]{2,1,0:T(2,128)(2,1)} %param.17) | copy-start | bytes 393220
  9.6 8.1 %copy-start.18 = (bf16[256,512]{1,0:T(8,128)(2,1)S(1)}, bf16[256,512]{1,0:T(8,128)(2,1)}, u32[]{:S(2)}) copy-start(bf16[256,512]{1,0:T(8,128)(2,1)} %param.16) | copy-start | bytes 786436
  10.8 7.6 %copy-start.22 = (f32[2,3200]{1,0:T(2,128)S(1)}, f32[2,3200]{1,0:T(2,128)}, u32[]{:S(2)}) copy-start(f32[2,3200]{1,0:T(2,128)} %param.11) | copy-start | bytes 76804
  10.9 8.4 %copy-start.23 = (f32[2,3200]{1,0:T(2,128)S(1)}, f32[2,3200]{1,0:T(2,128)}, u32[]{:S(2)}) copy-start(f32[2,3200]{1,0:T(2,128)} %param.12) | copy-start | bytes 76804
  10.9 9.1 %copy-start.24 = (s32[32]{0:T(128)S(1)}, s32[32]{0:T(128)}, u32[]{:S(2)}) copy-start(s32[32]{0:T(128)} %param.18) | copy-start | bytes 388
  10.9 23.2 %all-to-all-start = ((bf16[8,144,400]{2,1,0:T(8,128)(2,1)}), bf16[8,144,400]{2,1,0:T(8,128)(2,1)S(1)}, u32[]{:S(2)}, u32[]{:S(2)}) async-start(bf16[8,144,400]{2,1,0:T(8,128)(2,1)} %broadcast_in_dim.130), calls=%async_computation | async-start | bytes 2359296 | tf_op jit(solution)/shard_map/all_to_all | solution.py:32
  17.7 169.5 %all-gather.3.cloned.1.call-start = ((), (), s32[]{:S(2)}) async-start(), calls=%async_computation.5 | async-start | bytes 3538944 | tf_op jit(solution)/shard_map/all_gather | solution.py:280
  20.2 0.9 copy-start.25
  37.0 1.9 copy-start.27
  41.9 0.7 copy-start.29
  41.9 0.8 copy-start.19
  41.9 0.8 copy-start.20
  41.9 0.8 copy-start.28
  44.2 17.6 %all-to-all-start.1 = ((bf16[4,2,2,64,400]{4,3,2,1,0:T(8,128)(2,1)}), bf16[4,2,2,64,400]{4,3,2,1,0:T(8,128)(2,1)S(1)}, u32[]{:S(2)}, u32[]{:S(2)}) async-start(bf16[4,2,2,64,400]{4,3,2,1,0:T(8,128)(2,1)} %add_convert_fusion), calls=%async_computation.1 | async-start | bytes 2097152 | tf_op jit(solution)/shard_map/all_to_all | solution.py:32
  61.9 11.4 %copy-start.17 = (bf16[1,384,1024]{2,1,0:T(8,128)(2,1)S(1)}, bf16[1,384,1024]{2,1,0:T(8,128)(2,1)}, u32[]{:S(2)}) copy-start(bf16[1,384,1024]{2,1,0:T(8,128)(2,1)} %param.14) | copy-start | bytes 2359300
  61.9 11.4 %dynamic-slice-start = ((f32[8192]{0:T(1024)}, s32[]{:T(128)}), f32[1024]{0:T(1024)S(1)}, s32[]{:S(2)}) async-start(f32[8192]{0:T(1024)} %param.15, s32[]{:T(128)} %select_n.80), calls=%async_computation.7 | async-start | bytes 8704 | tf_op jit(solution)/shard_map/dynamic_slice | solution.py:287
  65.3 8.9 %collective-permute-start.14 = (bf16[64,1024]{1,0:T(8,128)(2,1)S(1)}, bf16[64,1024]{1,0:T(8,128)(2,1)S(1)}, u32[]{:S(2)}, u32[]{:S(2)}) collective-permute-start(bf16[64,1024]{1,0:T(8,128)(2,1)S(1)} %get-tuple-element.13), channel_id=1, source_target_pairs={{0,0},{2,64},{4,128},{6,192},{64,2},{66,66},{68,130},{70,194},{128... | collective-permute-start | bytes 393224 | tf_op jit(solution)/shard_map/ppermute | solution.py:28
  66.0 10.9 %collective-permute-start.15 = (bf16[64,1024]{1,0:T(8,128)(2,1)S(1)}, bf16[64,1024]{1,0:T(8,128)(2,1)S(1)}, u32[]{:S(2)}, u32[]{:S(2)}) collective-permute-start(bf16[64,1024]{1,0:T(8,128)(2,1)S(1)} %get-tuple-element.16), channel_id=1, source_target_pairs={{0,2},{2,66},{4,130},{6,194},{64,0},{66,64},{68,128},{70,192},{128... | collective-permute-start | bytes 393224 | tf_op jit(solution)/shard_map/ppermute | solution.py:28
  68.8 55.9 %collective-permute-start.16 = (bf16[64,1024]{1,0:T(8,128)(2,1)S(1)}, bf16[64,1024]{1,0:T(8,128)(2,1)S(1)}, u32[]{:S(2)}, u32[]{:S(2)}) collective-permute-start(bf16[64,1024]{1,0:T(8,128)(2,1)S(1)} %get-tuple-element.15), channel_id=1, source_target_pairs={{0,4},{2,68},{4,132},{6,196},{64,6},{66,70},{68,134},{70,198},{128... | collective-permute-start | bytes 393224 | tf_op jit(solution)/shard_map/ppermute | solution.py:28
  71.2 69.4 %copy-start.26 = (s32[32]{0:T(128)S(1)}, s32[32]{0:T(128)}, u32[]{:S(2)}) copy-start(s32[32]{0:T(128)} %copy-done.25) | copy-start | bytes 388
  71.2 53.5 %collective-permute-start.17 = (bf16[64,1024]{1,0:T(8,128)(2,1)S(1)}, bf16[64,1024]{1,0:T(8,128)(2,1)S(1)}, u32[]{:S(2)}, u32[]{:S(2)}) collective-permute-start(bf16[64,1024]{1,0:T(8,128)(2,1)S(1)} %get-tuple-element.14), channel_id=1, source_target_pairs={{0,6},{2,70},{4,134},{6,198},{64,4},{66,68},{68,132},{70,196},{128... | collective-permute-start | bytes 393224 | tf_op jit(solution)/shard_map/ppermute | solution.py:28
  73.5 64.0 %collective-permute-start = (bf16[384,1024]{1,0:T(8,128)(2,1)S(1)}, bf16[384,1024]{1,0:T(8,128)(2,1)S(1)}, u32[]{:S(2)}, u32[]{:S(2)}) collective-permute-start(bf16[384,1024]{1,0:T(8,128)(2,1)S(1)} %fusion.5), channel_id=1, source_target_pairs={{0,0},{2,64},{4,128},{6,192},{64,2},{66,66},{68,130},{70,194},{128... | collective-permute-start | bytes 2359304 | tf_op jit(solution)/shard_map/ppermute | solution.py:28
  126.0 25.5 %all-to-all-start.2 = ((bf16[32,8,1024]{2,1,0:T(8,128)(2,1)}), bf16[32,8,1024]{2,1,0:T(8,128)(2,1)}, u32[]{:S(2)}, u32[]{:S(2)}) async-start(bf16[32,8,1024]{2,1,0:T(8,128)(2,1)} %select_select_fusion), calls=%async_computation.2 | async-start | bytes 1048576 | tf_op jit(solution)/shard_map/all_to_all | solution.py:32
  137.5 25.8 %copy-start.7 = (bf16[384,1024]{1,0:T(8,128)(2,1)}, bf16[384,1024]{1,0:T(8,128)(2,1)S(1)}, u32[]{:S(2)}) copy-start(bf16[384,1024]{1,0:T(8,128)(2,1)S(1)} %collective-permute-done.refs_0_) | copy-start | bytes 2359300
  137.5 25.0 %collective-permute-start.2 = (bf16[384,1024]{1,0:T(8,128)(2,1)S(1)}, bf16[384,1024]{1,0:T(8,128)(2,1)S(1)}, u32[]{:S(2)}, u32[]{:S(2)}) collective-permute-start(bf16[384,1024]{1,0:T(8,128)(2,1)S(1)} %collective-permute-done.refs_0_), channel_id=1, source_target_pairs={{0,2},{2,4},{4,6},{6,0},{1,3},{3,5},{5,7},{7,1},{8,10},{10,12},{12... | collective-permute-start | bytes 2359304 | tf_op jit(solution)/shard_map/ppermute | solution.py:23
  138.8 24.6 %collective-permute-start.4 = (bf16[384,1024]{1,0:T(8,128)(2,1)S(1)}, bf16[384,1024]{1,0:T(8,128)(2,1)S(1)}, u32[]{:S(2)}, u32[]{:S(2)}) collective-permute-start(bf16[384,1024]{1,0:T(8,128)(2,1)S(1)} %collective-permute-done.refs_0_), channel_id=1, source_target_pairs={{0,6},{2,0},{4,2},{6,4},{1,7},{3,1},{5,3},{7,5},{8,14},{10,8},{12,... | collective-permute-start | bytes 2359304 | tf_op jit(solution)/shard_map/ppermute | solution.py:23
  141.9 29.0 %collective-permute-start.1 = (bf16[384,1024]{1,0:T(8,128)(2,1)S(1)}, bf16[384,1024]{1,0:T(8,128)(2,1)S(1)}, u32[]{:S(2)}, u32[]{:S(2)}) collective-permute-start(bf16[384,1024]{1,0:T(8,128)(2,1)S(1)} %collective-permute-done.refs_0_), channel_id=1, source_target_pairs={{0,1},{1,0},{2,3},{3,2},{4,5},{5,4},{6,7},{7,6},{8,9},{9,8},{10,11... | collective-permute-start | bytes 2359304 | tf_op jit(solution)/shard_map/ppermute | solution.py:23
  154.2 20.1 %all-to-all-start.3 = ((bf16[4,128,1024]{2,1,0:T(8,128)(2,1)}), bf16[4,128,1024]{2,1,0:T(8,128)(2,1)}, u32[]{:S(2)}, u32[]{:S(2)}) async-start(bf16[4,128,1024]{2,1,0:T(8,128)(2,1)} %broadcast_in_dim.149), calls=%async_computation.3 | async-start | bytes 2097152 | tf_op jit(solution)/shard_map/all_to_all | solution.py:32
  162.5 24.6 %copy-start.3 = (bf16[384,1024]{1,0:T(8,128)(2,1)}, bf16[384,1024]{1,0:T(8,128)(2,1)S(1)}, u32[]{:S(2)}) copy-start(bf16[384,1024]{1,0:T(8,128)(2,1)S(1)} %collective-permute-done.2.refs_2_) | copy-start | bytes 2359300
  163.4 18.2 %collective-permute-start.6 = (bf16[192,1024]{1,0:T(8,128)(2,1)}, bf16[192,1024]{1,0:T(8,128)(2,1)S(1)}, u32[]{:S(2)}, u32[]{:S(2)}) collective-permute-start(bf16[192,1024]{1,0:T(8,128)(2,1)} %slice.99), channel_id=1, source_target_pairs={{0,2},{2,4},{4,6},{6,0},{1,3},{3,5},{5,7},{7,1},{8,10},{10,12},{12... | collective-permute-start | bytes 1179656 | tf_op jit(solution)/shard_map/ppermute | solution.py:23
  163.4 23.8 %copy-start.5 = (bf16[384,1024]{1,0:T(8,128)(2,1)}, bf16[384,1024]{1,0:T(8,128)(2,1)S(1)}, u32[]{:S(2)}) copy-start(bf16[384,1024]{1,0:T(8,128)(2,1)S(1)} %collective-permute-done.4.refs_4_) | copy-start | bytes 2359300
  164.2 20.1 %collective-permute-start.8 = (bf16[192,1024]{1,0:T(8,128)(2,1)}, bf16[192,1024]{1,0:T(8,128)(2,1)}, u32[]{:S(2)}, u32[]{:S(2)}) collective-permute-start(bf16[192,1024]{1,0:T(8,128)(2,1)} %slice.100), channel_id=1, source_target_pairs={{0,6},{2,0},{4,2},{6,4},{1,7},{3,1},{5,3},{7,5},{8,14},{10,8},{12,... | collective-permute-start | bytes 1179656 | tf_op jit(solution)/shard_map/ppermute | solution.py:23
  166.9 20.3 %collective-permute-start.3 = (bf16[384,1024]{1,0:T(8,128)(2,1)S(1)}, bf16[384,1024]{1,0:T(8,128)(2,1)}, u32[]{:S(2)}, u32[]{:S(2)}) collective-permute-start(bf16[384,1024]{1,0:T(8,128)(2,1)S(1)} %collective-permute-done.2.refs_2_), channel_id=1, source_target_pairs={{0,1},{1,0},{2,3},{3,2},{4,5},{5,4},{6,7},{7,6},{8,9},{9,8},{10,11... | collective-permute-start | bytes 2359304 | tf_op jit(solution)/shard_map/ppermute | solution.py:23
  170.8 16.3 %collective-permute-start.5 = (bf16[384,1024]{1,0:T(8,128)(2,1)S(1)}, bf16[384,1024]{1,0:T(8,128)(2,1)}, u32[]{:S(2)}, u32[]{:S(2)}) collective-permute-start(bf16[384,1024]{1,0:T(8,128)(2,1)S(1)} %collective-permute-done.4.refs_4_), channel_id=1, source_target_pairs={{0,1},{1,0},{2,3},{3,2},{4,5},{5,4},{6,7},{7,6},{8,9},{9,8},{10,11... | collective-permute-start | bytes 2359304 | tf_op jit(solution)/shard_map/ppermute | solution.py:23
  170.9 0.9 copy-start.9
  174.3 35.4 %collective-permute-start.18 = (bf16[4,128,1024]{2,1,0:T(8,128)(2,1)}, bf16[4,128,1024]{2,1,0:T(8,128)(2,1)}, u32[]{:S(2)}, u32[]{:S(2)}) collective-permute-start(bf16[4,128,1024]{2,1,0:T(8,128)(2,1)} %all-to-all-done.3.refs_0_), channel_id=1, source_target_pairs={{0,1},{1,0},{2,3},{3,2},{4,5},{5,4},{6,7},{7,6},{8,9},{9,8},{10,11... | collective-permute-start | bytes 3145736 | tf_op jit(solution)/shard_map/ppermute | solution.py:23
  181.5 4.1 %collective-permute-start.7 = (bf16[192,1024]{1,0:T(8,128)(2,1)S(1)}, bf16[192,1024]{1,0:T(8,128)(2,1)S(1)}, u32[]{:S(2)}, u32[]{:S(2)}) collective-permute-start(bf16[192,1024]{1,0:T(8,128)(2,1)S(1)} %collective-permute-done.6.refs_6_), channel_id=1, source_target_pairs={{0,1},{1,0},{2,3},{3,2},{4,5},{5,4},{6,7},{7,6},{8,9},{9,8},{10,11... | collective-permute-start | bytes 1179656 | tf_op jit(solution)/shard_map/ppermute | solution.py:23
  184.3 2.1 collective-permute-start.9
  185.6 0.7 copy-start.13
  186.4 0.8 copy-start.15
  187.2 1.9 copy-start
  189.1 1.1 copy-start.4
  190.2 1.1 copy-start.6
  191.3 1.1 copy-start.8
  192.5 1.1 copy-start.10
  193.6 1.0 copy-start.14
  194.6 1.0 copy-start.16
  195.6 14.1 %copy-start.1 = (bf16[2048,768]{1,0:T(8,128)(2,1)S(1)}, bf16[2048,768]{1,0:T(8,128)(2,1)}, u32[]{:S(2)}) copy-start(bf16[2048,768]{1,0:T(8,128)(2,1)} %all-gather.3.cloned.1.call-done.refs_10_.refs_2_) | copy-start | bytes 9437188
  204.2 0.9 copy-start.11
  205.1 22.4 %collective-permute-start.10 = (bf16[576,768]{1,0:T(8,128)(2,1)}, bf16[576,768]{1,0:T(8,128)(2,1)}, u32[]{:S(2)}, u32[]{:S(2)}) collective-permute-start(bf16[576,768]{1,0:T(8,128)(2,1)} %get-tuple-element.9), channel_id=1, source_target_pairs={{0,64},{64,128},{128,192},{192,0},{1,65},{65,129},{129,193},{193,1... | collective-permute-start | bytes 2654216 | tf_op jit(solution)/shard_map/ppermute | solution.py:23
  206.0 22.6 %collective-permute-start.11 = (bf16[576,768]{1,0:T(8,128)(2,1)}, bf16[576,768]{1,0:T(8,128)(2,1)}, u32[]{:S(2)}, u32[]{:S(2)}) collective-permute-start(bf16[576,768]{1,0:T(8,128)(2,1)} %get-tuple-element.10), channel_id=1, source_target_pairs={{0,192},{64,0},{128,64},{192,128},{1,193},{65,1},{129,65},{193,129... | collective-permute-start | bytes 2654216 | tf_op jit(solution)/shard_map/ppermute | solution.py:23
  213.9 0.9 copy-start.2
  214.9 28.6 %all-to-all-start.4 = ((bf16[4,128,896]{2,1,0:T(8,128)(2,1)}), bf16[4,128,896]{2,1,0:T(8,128)(2,1)S(1)}, u32[]{:S(2)}, u32[]{:S(2)}) async-start(bf16[4,128,896]{2,1,0:T(8,128)(2,1)} %copy-done.2), calls=%async_computation.4 | async-start | bytes 1835008 | tf_op jit(solution)/shard_map/all_to_all | solution.py:32
  218.4 25.1 %copy-start.12 = (bf16[384,768]{1,0:T(8,128)(2,1)S(1)}, bf16[384,768]{1,0:T(8,128)(2,1)}, u32[]{:S(2)}) copy-start(bf16[384,768]{1,0:T(8,128)(2,1)} %copy-done.11) | copy-start | bytes 1769476
  228.4 15.1 %collective-permute-start.12 = (bf16[192,768]{1,0:T(8,128)(2,1)S(1)}, bf16[192,768]{1,0:T(8,128)(2,1)S(1)}, u32[]{:S(2)}, u32[]{:S(2)}) collective-permute-start(bf16[192,768]{1,0:T(8,128)(2,1)S(1)} %slice.101), channel_id=1, source_target_pairs={{0,64},{64,128},{128,192},{192,0},{1,65},{65,129},{129,193},{193,1... | collective-permute-start | bytes 884744 | tf_op jit(solution)/shard_map/ppermute | solution.py:23
  229.5 14.0 %collective-permute-start.13 = (bf16[192,768]{1,0:T(8,128)(2,1)S(1)}, bf16[192,768]{1,0:T(8,128)(2,1)S(1)}, u32[]{:S(2)}, u32[]{:S(2)}) collective-permute-start(bf16[192,768]{1,0:T(8,128)(2,1)S(1)} %slice.102), channel_id=1, source_target_pairs={{0,192},{64,0},{128,64},{192,128},{1,193},{65,1},{129,65},{193,129... | collective-permute-start | bytes 884744 | tf_op jit(solution)/shard_map/ppermute | solution.py:23
Sparse Core Ops, SparseCore 0:
  9.1 49.7 all-gather.4
  60.7 43.1 all-gather.2

commit v3 on v2

--- a/solution.py
+++ b/solution.py
@@ -24,8 +24,12 @@
 
 
 def swap_xy(array, flip=0):
-    pairs = [(i * NY + j, j * NY + (i ^ flip)) for i in range(NX) for j in range(NY)]
+    pairs = [(i * NY + j, (j ^ flip) * NY + i) for i in range(NX) for j in range(NY)]
     return lax.ppermute(array, ("x", "y"), pairs)
+
+
+def flip_x(array, flip):
+    return lax.ppermute(array, "x", [(i, i ^ flip) for i in range(NX)])
 
 
 def exchange(array, axis):
@@ -60,10 +64,10 @@
 
 
 def load_all(where_ref, plan, srcs, b_src, a_ref, b_ref, a_sem, b_sem):
-    y, c = where_ref[1], where_ref[2]
+    x, c = where_ref[0], where_ref[2]
     loads = [pltpu.make_async_copy(b_src, b_ref, b_sem)]
-    for k, (n, at, dy, sample, row, length, flip) in enumerate(plan):
-        s = sample if dy is None else lax.rem(y + (dy + NY), NY)
+    for k, (n, at, dx, sample, row, length, flip) in enumerate(plan):
+        s = sample if dx is None else lax.rem(x + (dx + NX), NX)
         core = c if flip == 0 else 1 - c
         source = srcs[n] if at is None else srcs[n].at[at]
         target = a_ref.at[s, core, pl.ds(row, length), :]
@@ -74,40 +78,38 @@
         copy.wait()
 
 
-def project_text(where, pieces, weight):
+def project_text(where, pieces, weight, scale, gain):
     arrays = [a for a, _ in pieces]
     plan = [(n, *part) for n, (_, parts) in enumerate(pieces) for part in parts]
     count = len(arrays)
-    half = SEQ // 2
 
     def kernel(where_ref, *refs):
-        own_ref, up_ref, down_ref, a_ref, b_ref, a_sem, b_sem = refs[count + 1 :]
+        scale_ref, gain_ref = refs[count + 1 : count + 3]
+        outs = refs[count + 3 : count + 7]
+        a_ref, b_ref, a_sem, b_sem = refs[count + 7 :]
         load_all(where_ref, plan, refs[:count], refs[count], a_ref, b_ref, a_sem, b_sem)
-        x = where_ref[0]
+        y = where_ref[1]
         for n in range(NX):
-            s = lax.rem(x + n, NX)
-            acc = jnp.dot(a_ref[s, 0], b_ref[:1024, :], preferred_element_type=jnp.float32)
-            acc = acc + jnp.dot(a_ref[s, 1], b_ref[1024:, :], preferred_element_type=jnp.float32)
-            acc = acc.astype(jnp.bfloat16)
-            if n == 0:
-                own_ref[...] = acc
-            elif n == 1:
-                up_ref[:SEQ, :] = acc
-            elif n == 2:
-                up_ref[SEQ:, :] = acc[:half]
-                down_ref[:half, :] = acc[half:]
-            else:
-                down_ref[half:, :] = acc
+            s = y ^ n
+            acc = None
+            for core in range(NC):
+                normed = (
+                    a_ref[s, core].astype(jnp.float32) * scale_ref[s] * gain_ref[core : core + 1, :]
+                ).astype(jnp.bfloat16)
+                term = jnp.dot(
+                    normed, b_ref[core * 1024 : (core + 1) * 1024, :],
+                    preferred_element_type=jnp.float32,
+                )
+                acc = term if acc is None else acc + term
+            outs[n][...] = acc.astype(jnp.bfloat16)
 
     any_spec = pl.BlockSpec(memory_space=pl.ANY)
     vmem = pl.BlockSpec(memory_space=pltpu.VMEM)
     return pl.pallas_call(
         kernel,
-        out_shape=[
-            jax.ShapeDtypeStruct((n, COLS), jnp.bfloat16) for n in (SEQ, SEQ + half, SEQ + half)
-        ],
-        in_specs=[pl.BlockSpec(memory_space=pltpu.SMEM)] + [any_spec] * (count + 1),
-        out_specs=[vmem] * 3,
+        out_shape=[jax.ShapeDtypeStruct((SEQ, COLS), jnp.bfloat16)] * NX,
+        in_specs=[pl.BlockSpec(memory_space=pltpu.SMEM)] + [any_spec] * (count + 1) + [vmem] * 2,
+        out_specs=[vmem] * NX,
         scratch_shapes=[
             pltpu.VMEM((NX, NC, SEQ, 1024), jnp.bfloat16),
             pltpu.VMEM((2048, COLS), jnp.bfloat16),
@@ -116,7 +118,7 @@
         ],
         compiler_params=pltpu.CompilerParams(vmem_limit_bytes=40 * 1024 * 1024),
         name="project_text",
-    )(where, *arrays, weight)
+    )(where, *arrays, weight, scale, gain)
 
 
 def project_image(where, pieces, weight, gain):
@@ -125,11 +127,15 @@
     count = len(arrays)
 
     def kernel(where_ref, *refs):
-        gain_ref, out_ref, a_ref, b_ref, a_sem, b_sem = refs[count + 1 :]
+        gain_ref = refs[count + 1]
+        outs = refs[count + 2 : count + 6]
+        a_ref, b_ref, a_sem, b_sem = refs[count + 6 :]
         load_all(where_ref, plan, refs[:count], refs[count], a_ref, b_ref, a_sem, b_sem)
+        y = where_ref[1]
         lane = lax.broadcasted_iota(jnp.int32, (SPAN, 128), 1)
 
-        for s in range(NX):
+        for n in range(NX):
+            s = y ^ n
             total = jnp.zeros((SPAN, 1), jnp.float32)
             acc = jnp.zeros((SPAN, COLS), jnp.float32)
             for core in range(NC):
@@ -142,8 +148,8 @@
                 )
             high = total.astype(jnp.bfloat16).astype(jnp.float32)
             low = total - high
-            out_ref[s, :, :COLS] = acc.astype(jnp.bfloat16)
-            out_ref[s, :, COLS:] = jnp.where(
+            outs[n][:, :COLS] = acc.astype(jnp.bfloat16)
+            outs[n][:, COLS:] = jnp.where(
                 lane == 0, high, jnp.where(lane == 1, low, 0.0)
             ).astype(jnp.bfloat16)
 
@@ -151,9 +157,9 @@
     vmem = pl.BlockSpec(memory_space=pltpu.VMEM)
     return pl.pallas_call(
         kernel,
-        out_shape=jax.ShapeDtypeStruct((NX, SPAN, WIRE), jnp.bfloat16),
+        out_shape=[jax.ShapeDtypeStruct((SPAN, WIRE), jnp.bfloat16)] * NX,
         in_specs=[pl.BlockSpec(memory_space=pltpu.SMEM)] + [any_spec] * (count + 1) + [vmem],
-        out_specs=vmem,
+        out_specs=[vmem] * NX,
         scratch_shapes=[
             pltpu.VMEM((NX, NC, SPAN, 1024), jnp.bfloat16),
             pltpu.VMEM((2048, COLS), jnp.bfloat16),
@@ -166,21 +172,18 @@
 
 
 def attention(where, text_parts, image_parts, tables, image_tables):
-    half = SEQ // 2
-
-    def kernel(
-        where_ref, own, up, down, low, high, i_ref, cos_ref, sin_ref, icos_ref, isin_ref, out_ref
-    ):
+    def kernel(where_ref, *refs):
+        text_refs, image_refs = refs[:NX], refs[NX : 2 * NX]
+        cos_ref, sin_ref, icos_ref, isin_ref, out_ref = refs[2 * NX :]
         start, n_rows = where_ref[0], where_ref[1]
 
-        def wide(array):
-            return array.astype(jnp.float32)
-
-        text_sum = wide(own[...]) + wide(up[:SEQ]) + wide(down[half:])
-        text_sum = jnp.concatenate(
-            [text_sum[:half] + wide(low[...]), text_sum[half:] + wide(high[...])], axis=0
-        )
-        image_sum = wide(i_ref[0]) + wide(i_ref[1]) + wide(i_ref[2]) + wide(i_ref[3])
+        def summed(parts):
+            total = parts[0][...].astype(jnp.float32)
+            for p in parts[1:]:
+                total = total + p[...].astype(jnp.float32)
+            return total
+
+        text_sum, image_sum = summed(text_refs), summed(image_refs)
         squares = jnp.sum(image_sum[:, COLS:], axis=1, keepdims=True)
         image_sum = image_sum[:, :COLS] * lax.rsqrt(squares * (1.0 / WIDTH) + decoder_epsilon)
 
@@ -224,20 +227,24 @@
     return pl.pallas_call(
         kernel,
         out_shape=jax.ShapeDtypeStruct((SEQ, 512), jnp.bfloat16),
-        in_specs=[pl.BlockSpec(memory_space=pltpu.SMEM)] + [vmem] * 10,
+        in_specs=[pl.BlockSpec(memory_space=pltpu.SMEM)] + [vmem] * (2 * NX + 4),
         out_specs=vmem,
         compiler_params=pltpu.CompilerParams(vmem_limit_bytes=40 * 1024 * 1024),
         name="attention",
-    )(where, *text_parts, image_parts, *tables, *image_tables)
-
-
-def vision(vis_rows, squares, ln_gain, ln_bias, weight):
-    tokens = vis_rows.shape[0] * vis_rows.shape[1]
-    parts, rest = [], squares
+    )(where, *text_parts, *image_parts, *tables, *image_tables)
+
+
+def as_rows(values):
+    parts, rest = [], values
     for _ in range(3):
         parts.append(lax.reduce_precision(rest, 8, 7))
         rest = rest - parts[-1]
-    rows = jnp.pad(jnp.stack(parts), ((0, 13), (0, 400 - SEQ))).astype(jnp.bfloat16)
+    return jnp.pad(jnp.stack(parts), ((0, 13), (0, 400 - SEQ))).astype(jnp.bfloat16)
+
+
+def vision(vis_rows, squares, ln_gain, ln_bias, weight):
+    tokens = vis_rows.shape[0] * vis_rows.shape[1]
+    rows = as_rows(squares)
     by_part = jnp.moveaxis(vis_rows, 2, 0).reshape(2 * tokens, 400)
     sent = jnp.concatenate([by_part, rows], axis=0)
     arrived = spread(sent, ("y", "c")).astype(jnp.float32)
@@ -249,7 +256,14 @@
     gain = jnp.swapaxes(ln_gain.reshape(2, 8, 400), 0, 1)[:, :, None]
     bias = jnp.swapaxes(ln_bias.reshape(2, 8, 400), 0, 1)[:, :, None]
     normed = (centered * lax.rsqrt(variance + vision_epsilon) * gain + bias).astype(jnp.bfloat16)
-    acts = exchange(normed.reshape(4, 2, 2, tokens, 400), "x")
+    scale = lax.rsqrt(text_squares * (1.0 / WIDTH) + decoder_epsilon)
+    rows = as_rows(scale)
+    sent = jnp.concatenate(
+        [normed.reshape(4, 4 * tokens, 400), jnp.broadcast_to(rows[None], (4, *rows.shape))], axis=1
+    )
+    acts = exchange(sent, "x")
+    scales = jnp.sum(acts[:, 4 * tokens : 4 * tokens + 3, :SEQ].astype(jnp.float32), axis=1)
+    acts = acts[:, : 4 * tokens].reshape(4, 2, 2, tokens, 400)
     partial = jnp.einsum(
         "scmtf,cfmo->sto", acts, weight.reshape(2, 400, 2, 1024),
         preferred_element_type=jnp.float32,
@@ -257,9 +271,9 @@
     total = None
     for k in range(NX):
         part = lax.dynamic_index_in_dim(partial, lax.axis_index("x") ^ k, 0, keepdims=False)
-        part = swap_xy(part, k).astype(jnp.float32)
+        part = (part if k == 0 else flip_x(part, k)).astype(jnp.float32)
         total = part if total is None else total + part
-    return total.astype(jnp.bfloat16), text_squares
+    return total.astype(jnp.bfloat16), scales[:, :, None]
 
 
 def step(
@@ -277,56 +291,46 @@
 
     proj_all = lax.all_gather(proj_weight, "z", axis=0, tiled=True)
     both = jnp.concatenate([w_query, key_value_weight.reshape(256, 256)], axis=1)
-    both_all = lax.all_gather(both, "z", axis=0, tiled=True)
+    both_all = lax.all_gather(swap_xy(both), "z", axis=0, tiled=True)
 
     sequence = text_rows[0]
     wide = sequence.astype(jnp.float32)
     squares = jnp.sum(wide * wide, axis=1)
-    image, squares = vision(vis_rows, squares, ln_gain, ln_bias, proj_all)
-    scale = lax.rsqrt(squares * (1.0 / WIDTH) + decoder_epsilon)[:, None]
-    own_gain = lax.dynamic_slice_in_dim(attn_gain, (y * NC + c) * 1024, 1024)
-    normed = (wide * scale * own_gain[None]).astype(jnp.bfloat16)
-
-    turned = swap_xy(normed)
-    own = ring4(turned, "y")
+    image, scales = vision(vis_rows, squares, ln_gain, ln_bias, proj_all)
     text = []
-    for a, dy, row in own:
+    for a, dx, row in ring4(sequence, "x"):
         other = shift(a, "c", 1)
-        text.append((a, [(None, dy, None, row, a.shape[0], 0)]))
-        text.append((other, [(None, dy, None, row, a.shape[0], 1)]))
+        text.append((a, [(None, dx, None, row, a.shape[0], 0)]))
+        text.append((other, [(None, dx, None, row, a.shape[0], 1)]))
 
     image = image.reshape(8, 8, 1024)
-    place = y * NZ + z
+    place = x * NZ + z
     tiles_here = jnp.arange(8, dtype=jnp.int32) * 32 + place
     owners = jnp.sum((tile_ends[None, :] <= tiles_here[:, None]).astype(jnp.int32), axis=1)
     slots = jnp.zeros((32, 8, 1024), jnp.bfloat16)
     for r in range(8):
         slots = jnp.where((owners[r] == sample_ids)[:, None, None], image[r][None], slots)
-    received = exchange(slots, ("y", "z"))
+    received = exchange(slots, ("x", "z"))
     sources = (entry(tile_firsts, place) + jnp.arange(16, dtype=jnp.int32)) % 32
     mine = received[sources].reshape(SPAN, 1024)
-    own_image = spread(mine, "y")
+    own_image = spread(mine, "x")
     other_image = shift(own_image, "c", 1)
     image_pieces = [
         (a, [(s, None, s, 0, SPAN, flip) for s in range(NX)])
         for flip, a in enumerate((own_image, other_image))
     ]
 
-    gain = lax.dynamic_slice_in_dim(attn_gain, x * 2048, 2048).reshape(2, 1024)
+    gain = lax.dynamic_slice_in_dim(attn_gain, y * 2048, 2048).reshape(2, 1024)
     where = jnp.stack([x, y, c]).astype(jnp.int32)
-    own_sum, up, down = project_text(where, text, both_all)
-    up = shift(up, "x", 1)
-    down = shift(down, "x", -1)
-    low = shift(up[SEQ:], "x", 1)
-    high = shift(down[: SEQ // 2], "x", -1)
-    text_parts = [own_sum, up, down, low, high]
-    image_out = project_image(where, image_pieces, both_all, gain)
-    image_parts = exchange(image_out, "x")
+    text_parts = project_text(where, text, both_all, scales, gain)
+    text_parts = [swap_xy(p, n) for n, p in enumerate(text_parts)]
+    image_parts = project_image(where, image_pieces, both_all, gain)
+    image_parts = [swap_xy(p, n) for n, p in enumerate(image_parts)]
 
     tables = rope_tables()
     start = image_offsets[0]
     image_tables = [lax.dynamic_slice_in_dim(t, start, SPAN, 0) for t in tables]
-    rows = entry(tile_counts, x * NZ + z) * 8
+    rows = entry(tile_counts, place) * 8
     out = attention(
         jnp.stack([start, rows]).astype(jnp.int32), text_parts, image_parts, tables, image_tables
     )

time: 257 us -> 251 us (0.977)
  the two profiles are of different devices: /device:TPU:1 before, /device:TPU:60 now
where the time goes in v3:
time: 251 us; the launch traced here: 249 us
  waiting for transfers between devices  110 us (44%)
  starting transfers between devices  61.5 us (25%)
  local copies, waits for them, and re-layouts  25.7 us (10%)
  Pallas kernels  17.9 us (7%)
  other arithmetic  15.9 us (6%)
  between operations  15.1 us (6%)
  matrix products  3.31 us (1%)
    ppermute x9, waiting for transfers between devices, swap_xy(): return lax.ppermute(array, ('x', 'y'), pairs)  58.8 us
    all_to_all x4, waiting for transfers between devices, exchange(): return lax.all_to_all(array, axis, 0, 0, tiled=True)  40.2 us
    all_to_all x4, starting transfers between devices, exchange(): return lax.all_to_all(array, axis, 0, 0, tiled=True)  29.8 us
    ppermute x9, starting transfers between devices, swap_xy(): return lax.ppermute(array, ('x', 'y'), pairs)  23.4 us
    unnamed x49, local copies, waits for them, and re-layouts  13.1 us
    pallas_call x1, Pallas kernels, project_text(): pl.pallas_call(kernel, out_shape=[jax.ShapeDtypeStruct((SEQ, COLS), jnp.b...  8.54 us
    ppermute x10, waiting for transfers between devices, shift(): lax.ppermute(array, axis, [(i, (i + by) % size) for i in range(size)])  6.3 us
    eq x4, other arithmetic, step(): owners[r] == sample_ids  5.17 us
  transfers between devices with their start and end apart: 28, of which 16 were waited for; matrix products, arithmetic and copies ran while one was open for 13% of the time, Pallas kernels for 5%

profile of v3, /device:TPU:60, one launch (start us, length us, event | category | flops | bytes accessed | tf_op | source)
XLA Modules:
  0.0 249.0 jit_solution(15182090333803387880)
XLA Ops:
  6.5 0.7 all-gather.5.cloned.1.call-update
  7.3 0.9 copy.36
  8.2 1.4 multiply_reduce_fusion.1
  9.6 1.1 broadcast_in_dim.137
  10.8 4.8 %all-to-all-start = ((bf16[8,144,400]{2,1,0:T(8,128)(2,1)}), bf16[8,144,400]{2,1,0:T(8,128)(2,1)S(1)}, u32[]{:S(2)}, u32[]{:S(2)}) async-start(bf16[8,144,400]{2,1,0:T(8,128)(2,1)} %broadcast_in_dim.137), calls=%async_computation | async-start | bytes 2359296 | tf_op jit(solution)/shard_map/all_to_all | solution.py:36
  15.7 3.4 %collective-permute-start.9 = (bf16[256,768]{1,0:T(8,128)(2,1)S(1)}, bf16[256,768]{1,0:T(8,128)(2,1)S(1)}, u32[]{:S(2)}, u32[]{:S(2)}) collective-permute-start(bf16[256,768]{1,0:T(8,128)(2,1)S(1)} %pad_maximum_fusion.1), channel_id=1, source_target_pairs={{0,0},{2,64},{4,128},{6,192},{64,2},{66,66},{68,130},{70,194},{128... | collective-permute-start | bytes 1179656 | tf_op jit(solution)/shard_map/ppermute | solution.py:28
  20.5 17.6 %collective-permute-done.9 = bf16[256,768]{1,0:T(8,128)(2,1)S(1)} collective-permute-done((bf16[256,768]{1,0:T(8,128)(2,1)S(1)}, bf16[256,768]{1,0:T(8,128)(2,1)S(1)}, u32[]{:S(2)}, u32[]{:S(2)}) %collective-permute-start.9) | collective-permute-done | bytes 393248 | tf_op jit(solution)/shard_map/ppermute | solution.py:28
  38.1 0.7 copy-done.16
  38.9 4.5 %all-to-all-done = bf16[8,144,400]{2,1,0:T(8,128)(2,1)S(1)} async-done(((bf16[8,144,400]{2,1,0:T(8,128)(2,1)}), bf16[8,144,400]{2,1,0:T(8,128)(2,1)S(1)}, u32[]{:S(2)}, u32[]{:S(2)}) %all-to-all-start) | async-done | bytes 921632 | tf_op jit(solution)/shard_map/all_to_all | solution.py:36
  46.5 1.2 pad_maximum_fusion
  47.7 7.6 %all-to-all-start.1 = ((bf16[4,272,400]{2,1,0:T(8,128)(2,1)}), bf16[4,272,400]{2,1,0:T(8,128)(2,1)S(1)}, u32[]{:S(2)}, u32[]{:S(2)}) async-start(bf16[4,272,400]{2,1,0:T(8,128)(2,1)} %pad_maximum_fusion), calls=%async_computation.1 | async-start | bytes 2228224 | tf_op jit(solution)/shard_map/all_to_all | solution.py:36
  56.5 1.3 iota_compare_fusion.2
  57.8 1.3 iota_compare_fusion.4
  59.1 9.5 %all-to-all-done.1 = bf16[4,272,400]{2,1,0:T(8,128)(2,1)S(1)} async-done(((bf16[4,272,400]{2,1,0:T(8,128)(2,1)}), bf16[4,272,400]{2,1,0:T(8,128)(2,1)S(1)}, u32[]{:S(2)}, u32[]{:S(2)}) %all-to-all-start.1) | async-done | bytes 870432 | tf_op jit(solution)/shard_map/all_to_all | solution.py:36
  68.7 0.9 copy-done.15
  69.6 3.3 %fusion.10 = bf16[4,64,1024]{2,1,0:T(8,128)(2,1)S(1)} fusion(bf16[4,2,2,64,400]{4,3,2,1,0:T(8,128)(2,1)S(1)} %bitcast.82, bf16[2,400,2,1024,1]{3,2,1,0,4:T(2,128)(2,1)} %bitcast.91), kind=kOutput, calls=%fused_computation.12 | convolution fusion | flops 839122944 | bytes 4620288 | tf_op jit(solution)/shard_map/scmtf,cfmo->sto/dot_general | solution.py:267
  73.0 2.2 collective-permute-start.14
  75.1 0.7 collective-permute-start.15
  75.8 0.9 collective-permute-start.16
  76.7 1.3 iota_compare_fusion.6
  78.0 1.3 iota_compare_fusion.8
  79.4 2.3 collective-permute-done.15
  81.7 1.2 collective-permute-done.16
  83.0 1.2 select_select_fusion
  84.2 11.2 %all-to-all-start.2 = ((bf16[32,8,1024]{2,1,0:T(8,128)(2,1)}), bf16[32,8,1024]{2,1,0:T(8,128)(2,1)}, u32[]{:S(2)}, u32[]{:S(2)}) async-start(bf16[32,8,1024]{2,1,0:T(8,128)(2,1)} %select_select_fusion), calls=%async_computation.2 | async-start | bytes 1048576 | tf_op jit(solution)/shard_map/all_to_all | solution.py:36
  95.4 1.3 collective-permute-start.1
  96.7 0.8 collective-permute-start.3
  98.8 16.7 %all-to-all-done.2 = bf16[32,8,1024]{2,1,0:T(8,128)(2,1)} async-done(((bf16[32,8,1024]{2,1,0:T(8,128)(2,1)}), bf16[32,8,1024]{2,1,0:T(8,128)(2,1)}, u32[]{:S(2)}, u32[]{:S(2)}) %all-to-all-start.2) | async-done | bytes 524320 | tf_op jit(solution)/shard_map/all_to_all | solution.py:36
  115.6 1.6 gather_fusion
  117.2 1.1 broadcast_in_dim.158
  118.3 6.2 %all-to-all-start.3 = ((bf16[4,128,1024]{2,1,0:T(8,128)(2,1)}), bf16[4,128,1024]{2,1,0:T(8,128)(2,1)}, u32[]{:S(2)}, u32[]{:S(2)}) async-start(bf16[4,128,1024]{2,1,0:T(8,128)(2,1)} %broadcast_in_dim.158), calls=%async_computation.3 | async-start | bytes 2097152 | tf_op jit(solution)/shard_map/all_to_all | solution.py:36
  124.4 0.8 slice.98
  125.3 1.2 collective-permute-start.5
  126.4 0.8 slice.99
  127.3 0.9 collective-permute-start.7
  128.6 9.4 %all-to-all-done.3.refs_0_ = bf16[4,128,1024]{2,1,0:T(8,128)(2,1)} async-done(((bf16[4,128,1024]{2,1,0:T(8,128)(2,1)}), bf16[4,128,1024]{2,1,0:T(8,128)(2,1)}, u32[]{:S(2)}, u32[]{:S(2)}) %all-to-all-start.3) | async-done | bytes 1048608 | tf_op jit(solution)/shard_map/all_to_all | solution.py:36
  138.1 5.6 %collective-permute-done.5.refs_6_ = bf16[192,1024]{1,0:T(8,128)(2,1)S(1)} collective-permute-done((bf16[192,1024]{1,0:T(8,128)(2,1)}, bf16[192,1024]{1,0:T(8,128)(2,1)S(1)}, u32[]{:S(2)}, u32[]{:S(2)}) %collective-permute-start.5) | collective-permute-done | bytes 393248 | tf_op jit(solution)/shard_map/ppermute | solution.py:23
  143.7 0.7 collective-permute-done.7.refs_8_
  144.4 0.7 dynamic_slice.22
  145.2 1.4 convert_reduce_fusion
  146.5 1.9 copy.39.refs_11_
  148.4 0.7 copy-done.11
  149.1 0.7 copy-done.13
  149.9 1.9 copy-done
  151.8 1.1 copy-done.3
  153.0 1.1 copy-done.4
  154.1 1.1 copy-done.6
  155.2 1.1 copy-done.8
  156.4 1.1 copy-done.10
  157.5 1.0 copy-done.12
  158.5 1.0 copy-done.14
  159.5 8.5 %project_text.1 = (bf16[384,768]{1,0:T(8,128)(2,1)}, bf16[384,768]{1,0:T(8,128)(2,1)}, bf16[384,768]{1,0:T(8,128)(2,1)}, bf16[384,768]{1,0:T(8,128)(2,1)}) custom-call(s32[3]{0:T(128)S(1)} %pad_add_fusion.1.where_ref, bf16[384,1024]{1,0:T(8,128)(2,1)S(1)} %bitcast.77, bf16[384,1024]{1,0:T(8,128)(2,1)S(1)} %copy-done.10, bf16[384,1024]{1,0:T(8,128)(2,1)S(1)} %copy-done.6, ...), custom_call_target="tpu_custom_call" | custom-call | tf_op jit(solution)/shard_map/project_text/pallas_call | solution.py:108
  168.0 3.8 %collective-permute-start.10 = (bf16[384,768]{1,0:T(8,128)(2,1)}, bf16[384,768]{1,0:T(8,128)(2,1)}, u32[]{:S(2)}, u32[]{:S(2)}) collective-permute-start(bf16[384,768]{1,0:T(8,128)(2,1)} %get-tuple-element.13), channel_id=1, source_target_pairs={{0,0},{2,64},{4,128},{6,192},{64,2},{66,66},{68,130},{70,194},{128... | collective-permute-start | bytes 1769480 | tf_op jit(solution)/shard_map/ppermute | solution.py:28
  171.8 3.4 %collective-permute-start.11 = (bf16[384,768]{1,0:T(8,128)(2,1)}, bf16[384,768]{1,0:T(8,128)(2,1)}, u32[]{:S(2)}, u32[]{:S(2)}) collective-permute-start(bf16[384,768]{1,0:T(8,128)(2,1)} %get-tuple-element.14), channel_id=1, source_target_pairs={{0,64},{2,0},{4,192},{6,128},{64,66},{66,2},{68,194},{70,130},{128... | collective-permute-start | bytes 1769480 | tf_op jit(solution)/shard_map/ppermute | solution.py:28
  175.2 1.0 collective-permute-start.12
  176.2 1.9 collective-permute-start.13
  179.9 1.4 fusion.18
  181.5 4.2 %project_image.1 = (bf16[128,896]{1,0:T(8,128)(2,1)S(1)}, bf16[128,896]{1,0:T(8,128)(2,1)S(1)}, bf16[128,896]{1,0:T(8,128)(2,1)S(1)}, bf16[128,896]{1,0:T(8,128)(2,1)S(1)}) custom-call(s32[3]{0:T(128)S(1)} %pad_add_fusion.1.where_ref, bf16[4,128,1024]{2,1,0:T(8,128)(2,1)} %all-to-all-done.3.refs_0_, bf16[4,128,1024]{2,1,0:T(8,128)(2,1)} %collective-permute-done.17.refs_1_, ...), custom_call_target="tpu_custom_call" | custom-call | tf_op jit(solution)/shard_map/project_image/pallas_call | solution.py:158
  185.7 4.6 %collective-permute-start.18 = (bf16[128,896]{1,0:T(8,128)(2,1)S(1)}, bf16[128,896]{1,0:T(8,128)(2,1)S(1)}, u32[]{:S(2)}, u32[]{:S(2)}) collective-permute-start(bf16[128,896]{1,0:T(8,128)(2,1)S(1)} %get-tuple-element.17), channel_id=1, source_target_pairs={{0,0},{2,64},{4,128},{6,192},{64,2},{66,66},{68,130},{70,194},{128... | collective-permute-start | bytes 688136 | tf_op jit(solution)/shard_map/ppermute | solution.py:28
  190.3 9.7 %collective-permute-done.10.refs_0_ = bf16[384,768]{1,0:T(8,128)(2,1)} collective-permute-done((bf16[384,768]{1,0:T(8,128)(2,1)}, bf16[384,768]{1,0:T(8,128)(2,1)}, u32[]{:S(2)}, u32[]{:S(2)}) %collective-permute-start.10) | collective-permute-done | bytes 589856 | tf_op jit(solution)/shard_map/ppermute | solution.py:28
  200.5 5.2 %collective-permute-start.20 = (bf16[128,896]{1,0:T(8,128)(2,1)S(1)}, bf16[128,896]{1,0:T(8,128)(2,1)S(1)}, u32[]{:S(2)}, u32[]{:S(2)}) collective-permute-start(bf16[128,896]{1,0:T(8,128)(2,1)S(1)} %get-tuple-element.19), channel_id=1, source_target_pairs={{0,128},{2,192},{4,0},{6,64},{64,130},{66,194},{68,2},{70,66},{128... | collective-permute-start | bytes 688136 | tf_op jit(solution)/shard_map/ppermute | solution.py:28
  205.8 18.8 %collective-permute-done.12.refs_2_ = bf16[384,768]{1,0:T(8,128)(2,1)} collective-permute-done((bf16[384,768]{1,0:T(8,128)(2,1)}, bf16[384,768]{1,0:T(8,128)(2,1)}, u32[]{:S(2)}, u32[]{:S(2)}) %collective-permute-start.12) | collective-permute-done | bytes 589856 | tf_op jit(solution)/shard_map/ppermute | solution.py:28
  225.1 11.6 %collective-permute-done.20.refs_6_ = bf16[128,896]{1,0:T(8,128)(2,1)S(1)} collective-permute-done((bf16[128,896]{1,0:T(8,128)(2,1)S(1)}, bf16[128,896]{1,0:T(8,128)(2,1)S(1)}, u32[]{:S(2)}, u32[]{:S(2)}) %collective-permute-start.20) | collective-permute-done | bytes 229408 | tf_op jit(solution)/shard_map/ppermute | solution.py:28
  237.0 5.1 %attention.1 = bf16[384,512]{1,0:T(8,128)(2,1)} custom-call(s32[2]{0:T(128)S(1)} %pad_add_fusion.where_ref, bf16[384,768]{1,0:T(8,128)(2,1)} %collective-permute-done.10.refs_0_, bf16[384,768]{1,0:T(8,128)(2,1)} %collective-permute-done.11.refs_1_, bf16[384,768]{1,0:T(8,128)(2,1)} %collective-permute-done.12.refs_2_, ...), custom_call_target="tpu_custom_call" | custom-call | tf_op jit(solution)/shard_map/attention/pallas_call | solution.py:227
  (116 shorter events, 10.2 us)
Async XLA Ops:
  6.5 62.2 %all-gather.5.cloned.1.call-start = ((), (), s32[]{:S(2)}) async-start(), calls=%async_computation.5 | async-start | bytes 3686400 | tf_op jit(solution)/shard_map/all_gather | solution.py:292
  9.5 6.0 %copy-start.20 = (bf16[256,2,128]{2,1,0:T(2,128)(2,1)S(1)}, bf16[256,2,128]{2,1,0:T(2,128)(2,1)}, u32[]{:S(2)}) copy-start(bf16[256,2,128]{2,1,0:T(2,128)(2,1)} %param.17) | copy-start | bytes 393220
  9.6 6.0 %copy-start.17 = (bf16[256,512]{1,0:T(8,128)(2,1)S(1)}, bf16[256,512]{1,0:T(8,128)(2,1)}, u32[]{:S(2)}) copy-start(bf16[256,512]{1,0:T(8,128)(2,1)} %param.16) | copy-start | bytes 786436
  9.6 9.4 %copy-start.21 = (f32[2,3200]{1,0:T(2,128)S(1)}, f32[2,3200]{1,0:T(2,128)}, u32[]{:S(2)}) copy-start(f32[2,3200]{1,0:T(2,128)} %param.12) | copy-start | bytes 76804
  10.8 9.1 %copy-start.22 = (f32[2,3200]{1,0:T(2,128)S(1)}, f32[2,3200]{1,0:T(2,128)}, u32[]{:S(2)}) copy-start(f32[2,3200]{1,0:T(2,128)} %param.11) | copy-start | bytes 76804
  10.8 32.6 %all-to-all-start = ((bf16[8,144,400]{2,1,0:T(8,128)(2,1)}), bf16[8,144,400]{2,1,0:T(8,128)(2,1)S(1)}, u32[]{:S(2)}, u32[]{:S(2)}) async-start(bf16[8,144,400]{2,1,0:T(8,128)(2,1)} %broadcast_in_dim.137), calls=%async_computation | async-start | bytes 2359296 | tf_op jit(solution)/shard_map/all_to_all | solution.py:36
  15.6 134.4 %all-gather.3.cloned.1.call-start = ((), (), s32[]{:S(2)}) async-start(), calls=%async_computation.4 | async-start | bytes 3538944 | tf_op jit(solution)/shard_map/all_gather | solution.py:294
  15.7 22.5 %collective-permute-start.9 = (bf16[256,768]{1,0:T(8,128)(2,1)S(1)}, bf16[256,768]{1,0:T(8,128)(2,1)S(1)}, u32[]{:S(2)}, u32[]{:S(2)}) collective-permute-start(bf16[256,768]{1,0:T(8,128)(2,1)S(1)} %pad_maximum_fusion.1), channel_id=1, source_target_pairs={{0,0},{2,64},{4,128},{6,192},{64,2},{66,66},{68,130},{70,194},{128... | collective-permute-start | bytes 1179656 | tf_op jit(solution)/shard_map/ppermute | solution.py:28
  38.1 0.7 copy-start.16
  44.8 0.8 copy-start.18
  45.1 0.8 copy-start.19
  46.5 8.8 %copy-start.23 = (s32[32]{0:T(128)S(1)}, s32[32]{0:T(128)}, u32[]{:S(2)}) copy-start(s32[32]{0:T(128)} %param.18) | copy-start | bytes 388
  47.7 20.9 %all-to-all-start.1 = ((bf16[4,272,400]{2,1,0:T(8,128)(2,1)}), bf16[4,272,400]{2,1,0:T(8,128)(2,1)S(1)}, u32[]{:S(2)}, u32[]{:S(2)}) async-start(bf16[4,272,400]{2,1,0:T(8,128)(2,1)} %pad_maximum_fusion), calls=%async_computation.1 | async-start | bytes 2228224 | tf_op jit(solution)/shard_map/all_to_all | solution.py:36
  68.6 1.0 copy-start.15
  72.9 22.5 %copy-start.2 = (bf16[1,384,1024]{2,1,0:T(8,128)(2,1)S(1)}, bf16[1,384,1024]{2,1,0:T(8,128)(2,1)}, u32[]{:S(2)}) copy-start(bf16[1,384,1024]{2,1,0:T(8,128)(2,1)} %param.14) | copy-start | bytes 2359300
  73.0 6.4 %collective-permute-start.14 = (bf16[64,1024]{1,0:T(8,128)(2,1)S(1)}, bf16[64,1024]{1,0:T(8,128)(2,1)S(1)}, u32[]{:S(2)}, u32[]{:S(2)}) collective-permute-start(bf16[64,1024]{1,0:T(8,128)(2,1)S(1)} %get-tuple-element.23), channel_id=1, source_target_pairs={{0,64},{64,0},{128,192},{192,128},{1,65},{65,1},{129,193},{193,129... | collective-permute-start | bytes 393224 | tf_op jit(solution)/shard_map/ppermute | solution.py:32
  75.1 6.5 %collective-permute-start.15 = (bf16[64,1024]{1,0:T(8,128)(2,1)S(1)}, bf16[64,1024]{1,0:T(8,128)(2,1)S(1)}, u32[]{:S(2)}, u32[]{:S(2)}) collective-permute-start(bf16[64,1024]{1,0:T(8,128)(2,1)S(1)} %get-tuple-element.25), channel_id=1, source_target_pairs={{0,128},{64,192},{128,0},{192,64},{1,129},{65,193},{129,1},{193,65... | collective-permute-start | bytes 393224 | tf_op jit(solution)/shard_map/ppermute | solution.py:32
  75.8 7.0 %collective-permute-start.16 = (bf16[64,1024]{1,0:T(8,128)(2,1)S(1)}, bf16[64,1024]{1,0:T(8,128)(2,1)S(1)}, u32[]{:S(2)}, u32[]{:S(2)}) collective-permute-start(bf16[64,1024]{1,0:T(8,128)(2,1)S(1)} %get-tuple-element.24), channel_id=1, source_target_pairs={{0,192},{64,128},{128,64},{192,0},{1,193},{65,129},{129,65},{193,1... | collective-permute-start | bytes 393224 | tf_op jit(solution)/shard_map/ppermute | solution.py:32
  84.2 31.4 %all-to-all-start.2 = ((bf16[32,8,1024]{2,1,0:T(8,128)(2,1)}), bf16[32,8,1024]{2,1,0:T(8,128)(2,1)}, u32[]{:S(2)}, u32[]{:S(2)}) async-start(bf16[32,8,1024]{2,1,0:T(8,128)(2,1)} %select_select_fusion), calls=%async_computation.2 | async-start | bytes 1048576 | tf_op jit(solution)/shard_map/all_to_all | solution.py:36
  95.4 29.0 %collective-permute-start.1 = (bf16[384,1024]{1,0:T(8,128)(2,1)S(1)}, bf16[384,1024]{1,0:T(8,128)(2,1)S(1)}, u32[]{:S(2)}, u32[]{:S(2)}) collective-permute-start(bf16[384,1024]{1,0:T(8,128)(2,1)S(1)} %bitcast.74), channel_id=1, source_target_pairs={{0,64},{64,128},{128,192},{192,0},{1,65},{65,129},{129,193},{193,1... | collective-permute-start | bytes 2359304 | tf_op jit(solution)/shard_map/ppermute | solution.py:23
  96.7 29.7 %collective-permute-start.3 = (bf16[384,1024]{1,0:T(8,128)(2,1)S(1)}, bf16[384,1024]{1,0:T(8,128)(2,1)S(1)}, u32[]{:S(2)}, u32[]{:S(2)}) collective-permute-start(bf16[384,1024]{1,0:T(8,128)(2,1)S(1)} %bitcast.75), channel_id=1, source_target_pairs={{0,192},{64,0},{128,64},{192,128},{1,193},{65,1},{129,65},{193,129... | collective-permute-start | bytes 2359304 | tf_op jit(solution)/shard_map/ppermute | solution.py:23
  97.5 31.1 %collective-permute-start = (bf16[384,1024]{1,0:T(8,128)(2,1)S(1)}, bf16[384,1024]{1,0:T(8,128)(2,1)S(1)}, u32[]{:S(2)}, u32[]{:S(2)}) collective-permute-start(bf16[384,1024]{1,0:T(8,128)(2,1)S(1)} %bitcast.76), channel_id=1, source_target_pairs={{0,1},{1,0},{2,3},{3,2},{4,5},{5,4},{6,7},{7,6},{8,9},{9,8},{10,11... | collective-permute-start | bytes 2359304 | tf_op jit(solution)/shard_map/ppermute | solution.py:23
  118.3 19.8 %all-to-all-start.3 = ((bf16[4,128,1024]{2,1,0:T(8,128)(2,1)}), bf16[4,128,1024]{2,1,0:T(8,128)(2,1)}, u32[]{:S(2)}, u32[]{:S(2)}) async-start(bf16[4,128,1024]{2,1,0:T(8,128)(2,1)} %broadcast_in_dim.158), calls=%async_computation.3 | async-start | bytes 2097152 | tf_op jit(solution)/shard_map/all_to_all | solution.py:36
  124.4 25.4 %copy-start.5 = (bf16[384,1024]{1,0:T(8,128)(2,1)}, bf16[384,1024]{1,0:T(8,128)(2,1)S(1)}, u32[]{:S(2)}) copy-start(bf16[384,1024]{1,0:T(8,128)(2,1)S(1)} %collective-permute-done.1.refs_2_) | copy-start | bytes 2359300
  125.3 18.4 %collective-permute-start.5 = (bf16[192,1024]{1,0:T(8,128)(2,1)}, bf16[192,1024]{1,0:T(8,128)(2,1)S(1)}, u32[]{:S(2)}, u32[]{:S(2)}) collective-permute-start(bf16[192,1024]{1,0:T(8,128)(2,1)} %slice.98), channel_id=1, source_target_pairs={{0,64},{64,128},{128,192},{192,0},{1,65},{65,129},{129,193},{193,1... | collective-permute-start | bytes 1179656 | tf_op jit(solution)/shard_map/ppermute | solution.py:23
  126.4 23.4 %copy-start.7 = (bf16[384,1024]{1,0:T(8,128)(2,1)}, bf16[384,1024]{1,0:T(8,128)(2,1)S(1)}, u32[]{:S(2)}) copy-start(bf16[384,1024]{1,0:T(8,128)(2,1)S(1)} %collective-permute-done.3.refs_4_) | copy-start | bytes 2359300
  127.3 17.1 %collective-permute-start.7 = (bf16[192,1024]{1,0:T(8,128)(2,1)}, bf16[192,1024]{1,0:T(8,128)(2,1)}, u32[]{:S(2)}, u32[]{:S(2)}) collective-permute-start(bf16[192,1024]{1,0:T(8,128)(2,1)} %slice.99), channel_id=1, source_target_pairs={{0,192},{64,0},{128,64},{192,128},{1,193},{65,1},{129,65},{193,129... | collective-permute-start | bytes 1179656 | tf_op jit(solution)/shard_map/ppermute | solution.py:23
  128.1 21.7 %collective-permute-start.2 = (bf16[384,1024]{1,0:T(8,128)(2,1)S(1)}, bf16[384,1024]{1,0:T(8,128)(2,1)}, u32[]{:S(2)}, u32[]{:S(2)}) collective-permute-start(bf16[384,1024]{1,0:T(8,128)(2,1)S(1)} %collective-permute-done.1.refs_2_), channel_id=1, source_target_pairs={{0,1},{1,0},{2,3},{3,2},{4,5},{5,4},{6,7},{7,6},{8,9},{9,8},{10,11... | collective-permute-start | bytes 2359304 | tf_op jit(solution)/shard_map/ppermute | solution.py:23
  128.1 21.7 %collective-permute-start.4 = (bf16[384,1024]{1,0:T(8,128)(2,1)S(1)}, bf16[384,1024]{1,0:T(8,128)(2,1)}, u32[]{:S(2)}, u32[]{:S(2)}) collective-permute-start(bf16[384,1024]{1,0:T(8,128)(2,1)S(1)} %collective-permute-done.3.refs_4_), channel_id=1, source_target_pairs={{0,1},{1,0},{2,3},{3,2},{4,5},{5,4},{6,7},{7,6},{8,9},{9,8},{10,11... | collective-permute-start | bytes 2359304 | tf_op jit(solution)/shard_map/ppermute | solution.py:23
  128.6 21.3 %copy-start.9 = (bf16[384,1024]{1,0:T(8,128)(2,1)}, bf16[384,1024]{1,0:T(8,128)(2,1)S(1)}, u32[]{:S(2)}) copy-start(bf16[384,1024]{1,0:T(8,128)(2,1)S(1)} %collective-permute-done.refs_1_) | copy-start | bytes 2359300
  138.1 43.4 %collective-permute-start.17 = (bf16[4,128,1024]{2,1,0:T(8,128)(2,1)}, bf16[4,128,1024]{2,1,0:T(8,128)(2,1)}, u32[]{:S(2)}, u32[]{:S(2)}) collective-permute-start(bf16[4,128,1024]{2,1,0:T(8,128)(2,1)} %all-to-all-done.3.refs_0_), channel_id=1, source_target_pairs={{0,1},{1,0},{2,3},{3,2},{4,5},{5,4},{6,7},{7,6},{8,9},{9,8},{10,11... | collective-permute-start | bytes 3145736 | tf_op jit(solution)/shard_map/ppermute | solution.py:23
  143.7 4.7 %collective-permute-start.6 = (bf16[192,1024]{1,0:T(8,128)(2,1)S(1)}, bf16[192,1024]{1,0:T(8,128)(2,1)S(1)}, u32[]{:S(2)}, u32[]{:S(2)}) collective-permute-start(bf16[192,1024]{1,0:T(8,128)(2,1)S(1)} %collective-permute-done.5.refs_6_), channel_id=1, source_target_pairs={{0,1},{1,0},{2,3},{3,2},{4,5},{5,4},{6,7},{7,6},{8,9},{9,8},{10,11... | collective-permute-start | bytes 1179656 | tf_op jit(solution)/shard_map/ppermute | solution.py:23
  144.4 4.8 %collective-permute-start.8 = (bf16[192,1024]{1,0:T(8,128)(2,1)}, bf16[192,1024]{1,0:T(8,128)(2,1)S(1)}, u32[]{:S(2)}, u32[]{:S(2)}) collective-permute-start(bf16[192,1024]{1,0:T(8,128)(2,1)} %collective-permute-done.7.refs_8_), channel_id=1, source_target_pairs={{0,1},{1,0},{2,3},{3,2},{4,5},{5,4},{6,7},{7,6},{8,9},{9,8},{10,11... | collective-permute-start | bytes 1179656 | tf_op jit(solution)/shard_map/ppermute | solution.py:23
  148.4 0.7 copy-start.11
  149.1 0.7 copy-start.13
  149.9 1.9 copy-start
  151.8 1.1 copy-start.3
  153.0 1.1 copy-start.4
  154.1 1.1 copy-start.6
  155.2 1.1 copy-start.8
  156.4 1.1 copy-start.10
  157.5 1.0 copy-start.12
  158.5 1.0 copy-start.14
  159.5 22.0 %copy-start.1 = (bf16[2048,768]{1,0:T(8,128)(2,1)S(1)}, bf16[2048,768]{1,0:T(8,128)(2,1)}, u32[]{:S(2)}) copy-start(bf16[2048,768]{1,0:T(8,128)(2,1)} %all-gather.3.cloned.1.call-done.refs_10_.refs_2_) | copy-start | bytes 9437188
  168.0 31.9 %collective-permute-start.10 = (bf16[384,768]{1,0:T(8,128)(2,1)}, bf16[384,768]{1,0:T(8,128)(2,1)}, u32[]{:S(2)}, u32[]{:S(2)}) collective-permute-start(bf16[384,768]{1,0:T(8,128)(2,1)} %get-tuple-element.13), channel_id=1, source_target_pairs={{0,0},{2,64},{4,128},{6,192},{64,2},{66,66},{68,130},{70,194},{128... | collective-permute-start | bytes 1769480 | tf_op jit(solution)/shard_map/ppermute | solution.py:28
  171.8 28.7 %collective-permute-start.11 = (bf16[384,768]{1,0:T(8,128)(2,1)}, bf16[384,768]{1,0:T(8,128)(2,1)}, u32[]{:S(2)}, u32[]{:S(2)}) collective-permute-start(bf16[384,768]{1,0:T(8,128)(2,1)} %get-tuple-element.14), channel_id=1, source_target_pairs={{0,64},{2,0},{4,192},{6,128},{64,66},{66,2},{68,194},{70,130},{128... | collective-permute-start | bytes 1769480 | tf_op jit(solution)/shard_map/ppermute | solution.py:28
  175.2 49.4 %collective-permute-start.12 = (bf16[384,768]{1,0:T(8,128)(2,1)}, bf16[384,768]{1,0:T(8,128)(2,1)}, u32[]{:S(2)}, u32[]{:S(2)}) collective-permute-start(bf16[384,768]{1,0:T(8,128)(2,1)} %get-tuple-element.15), channel_id=1, source_target_pairs={{0,128},{2,192},{4,0},{6,64},{64,130},{66,194},{68,2},{70,66},{128... | collective-permute-start | bytes 1769480 | tf_op jit(solution)/shard_map/ppermute | solution.py:28
  176.2 48.6 %collective-permute-start.13 = (bf16[384,768]{1,0:T(8,128)(2,1)}, bf16[384,768]{1,0:T(8,128)(2,1)}, u32[]{:S(2)}, u32[]{:S(2)}) collective-permute-start(bf16[384,768]{1,0:T(8,128)(2,1)} %get-tuple-element.16), channel_id=1, source_target_pairs={{0,192},{2,128},{4,64},{6,0},{64,194},{66,130},{68,66},{70,2},{128... | collective-permute-start | bytes 1769480 | tf_op jit(solution)/shard_map/ppermute | solution.py:28
  185.7 39.4 %collective-permute-start.18 = (bf16[128,896]{1,0:T(8,128)(2,1)S(1)}, bf16[128,896]{1,0:T(8,128)(2,1)S(1)}, u32[]{:S(2)}, u32[]{:S(2)}) collective-permute-start(bf16[128,896]{1,0:T(8,128)(2,1)S(1)} %get-tuple-element.17), channel_id=1, source_target_pairs={{0,0},{2,64},{4,128},{6,192},{64,2},{66,66},{68,130},{70,194},{128... | collective-permute-start | bytes 688136 | tf_op jit(solution)/shard_map/ppermute | solution.py:28
  199.9 25.2 %collective-permute-start.19 = (bf16[128,896]{1,0:T(8,128)(2,1)S(1)}, bf16[128,896]{1,0:T(8,128)(2,1)S(1)}, u32[]{:S(2)}, u32[]{:S(2)}) collective-permute-start(bf16[128,896]{1,0:T(8,128)(2,1)S(1)} %get-tuple-element.18), channel_id=1, source_target_pairs={{0,64},{2,0},{4,192},{6,128},{64,66},{66,2},{68,194},{70,130},{128... | collective-permute-start | bytes 688136 | tf_op jit(solution)/shard_map/ppermute | solution.py:28
  200.5 36.2 %collective-permute-start.20 = (bf16[128,896]{1,0:T(8,128)(2,1)S(1)}, bf16[128,896]{1,0:T(8,128)(2,1)S(1)}, u32[]{:S(2)}, u32[]{:S(2)}) collective-permute-start(bf16[128,896]{1,0:T(8,128)(2,1)S(1)} %get-tuple-element.19), channel_id=1, source_target_pairs={{0,128},{2,192},{4,0},{6,64},{64,130},{66,194},{68,2},{70,66},{128... | collective-permute-start | bytes 688136 | tf_op jit(solution)/shard_map/ppermute | solution.py:28
  224.6 12.4 %collective-permute-start.21 = (bf16[128,896]{1,0:T(8,128)(2,1)S(1)}, bf16[128,896]{1,0:T(8,128)(2,1)S(1)}, u32[]{:S(2)}, u32[]{:S(2)}) collective-permute-start(bf16[128,896]{1,0:T(8,128)(2,1)S(1)} %get-tuple-element.20), channel_id=1, source_target_pairs={{0,192},{2,128},{4,64},{6,0},{64,194},{66,130},{68,66},{70,2},{128... | collective-permute-start | bytes 688136 | tf_op jit(solution)/shard_map/ppermute | solution.py:28
Sparse Core Ops, SparseCore 0:
  9.1 47.6 all-gather.4
  58.6 53.6 all-gather.2

commit v4 on v3

--- a/solution.py
+++ b/solution.py
@@ -78,37 +78,28 @@
         copy.wait()
 
 
-def project_text(where, pieces, weight, scale, gain):
+def project_text(where, pieces, weight):
     arrays = [a for a, _ in pieces]
     plan = [(n, *part) for n, (_, parts) in enumerate(pieces) for part in parts]
     count = len(arrays)
 
     def kernel(where_ref, *refs):
-        scale_ref, gain_ref = refs[count + 1 : count + 3]
-        outs = refs[count + 3 : count + 7]
-        a_ref, b_ref, a_sem, b_sem = refs[count + 7 :]
+        outs = refs[count + 1 : count + 5]
+        a_ref, b_ref, a_sem, b_sem = refs[count + 5 :]
         load_all(where_ref, plan, refs[:count], refs[count], a_ref, b_ref, a_sem, b_sem)
         y = where_ref[1]
         for n in range(NX):
             s = y ^ n
-            acc = None
-            for core in range(NC):
-                normed = (
-                    a_ref[s, core].astype(jnp.float32) * scale_ref[s] * gain_ref[core : core + 1, :]
-                ).astype(jnp.bfloat16)
-                term = jnp.dot(
-                    normed, b_ref[core * 1024 : (core + 1) * 1024, :],
-                    preferred_element_type=jnp.float32,
-                )
-                acc = term if acc is None else acc + term
+            acc = jnp.dot(a_ref[s, 0], b_ref[:1024, :], preferred_element_type=jnp.float32)
+            acc = acc + jnp.dot(a_ref[s, 1], b_ref[1024:, :], preferred_element_type=jnp.float32)
             outs[n][...] = acc.astype(jnp.bfloat16)
 
-    any_spec = pl.BlockSpec(memory_space=pl.ANY)
+    any_spec = pl.BlockSpec(memory_space=pltpu.HBM)
     vmem = pl.BlockSpec(memory_space=pltpu.VMEM)
     return pl.pallas_call(
         kernel,
         out_shape=[jax.ShapeDtypeStruct((SEQ, COLS), jnp.bfloat16)] * NX,
-        in_specs=[pl.BlockSpec(memory_space=pltpu.SMEM)] + [any_spec] * (count + 1) + [vmem] * 2,
+        in_specs=[pl.BlockSpec(memory_space=pltpu.SMEM)] + [any_spec] * (count + 1),
         out_specs=[vmem] * NX,
         scratch_shapes=[
             pltpu.VMEM((NX, NC, SEQ, 1024), jnp.bfloat16),
@@ -118,7 +109,7 @@
         ],
         compiler_params=pltpu.CompilerParams(vmem_limit_bytes=40 * 1024 * 1024),
         name="project_text",
-    )(where, *arrays, weight, scale, gain)
+    )(where, *arrays, weight)
 
 
 def project_image(where, pieces, weight, gain):
@@ -153,7 +144,7 @@
                 lane == 0, high, jnp.where(lane == 1, low, 0.0)
             ).astype(jnp.bfloat16)
 
-    any_spec = pl.BlockSpec(memory_space=pl.ANY)
+    any_spec = pl.BlockSpec(memory_space=pltpu.HBM)
     vmem = pl.BlockSpec(memory_space=pltpu.VMEM)
     return pl.pallas_call(
         kernel,
@@ -242,28 +233,51 @@
     return jnp.pad(jnp.stack(parts), ((0, 13), (0, 400 - SEQ))).astype(jnp.bfloat16)
 
 
+def layer_norm(arrived, gain, bias):
+    tokens = 64
+
+    def kernel(in_ref, gain_ref, bias_ref, out_ref):
+        def read(t, m):
+            return in_ref[t, m * tokens : (m + 1) * tokens, :].astype(jnp.float32)
+
+        parts = [(t, m) for t in range(8) for m in range(2)]
+        total = jnp.zeros((tokens, 1), jnp.float32)
+        for t, m in parts:
+            total = total + jnp.sum(read(t, m), axis=1, keepdims=True)
+        mean = total * (1.0 / 6400)
+        total = jnp.zeros((tokens, 1), jnp.float32)
+        for t, m in parts:
+            centered = read(t, m) - mean
+            total = total + jnp.sum(centered * centered, axis=1, keepdims=True)
+        scale = lax.rsqrt(total * (1.0 / 6400) + vision_epsilon)
+        for t, m in parts:
+            value = (read(t, m) - mean) * scale * gain_ref[t, m : m + 1, :]
+            out_ref[t, m * tokens : (m + 1) * tokens, :] = (
+                value + bias_ref[t, m : m + 1, :]
+            ).astype(jnp.bfloat16)
+
+    vmem = pl.BlockSpec(memory_space=pltpu.VMEM)
+    return pl.pallas_call(
+        kernel,
+        out_shape=jax.ShapeDtypeStruct((8, 2 * tokens, 400), jnp.bfloat16),
+        in_specs=[vmem] * 3,
+        out_specs=vmem,
+        name="layer_norm",
+    )(arrived, gain, bias)
+
+
 def vision(vis_rows, squares, ln_gain, ln_bias, weight):
     tokens = vis_rows.shape[0] * vis_rows.shape[1]
-    rows = as_rows(squares)
     by_part = jnp.moveaxis(vis_rows, 2, 0).reshape(2 * tokens, 400)
-    sent = jnp.concatenate([by_part, rows], axis=0)
-    arrived = spread(sent, ("y", "c")).astype(jnp.float32)
-    text_squares = jnp.sum(arrived[:, 2 * tokens : 2 * tokens + 3, :SEQ], axis=(0, 1))
-    whole = arrived[:, : 2 * tokens].reshape(8, 2, tokens, 400)
-    mean = jnp.mean(whole, axis=(0, 1, 3))[None, None, :, None]
-    centered = whole - mean
-    variance = jnp.mean(centered * centered, axis=(0, 1, 3))[None, None, :, None]
-    gain = jnp.swapaxes(ln_gain.reshape(2, 8, 400), 0, 1)[:, :, None]
-    bias = jnp.swapaxes(ln_bias.reshape(2, 8, 400), 0, 1)[:, :, None]
-    normed = (centered * lax.rsqrt(variance + vision_epsilon) * gain + bias).astype(jnp.bfloat16)
-    scale = lax.rsqrt(text_squares * (1.0 / WIDTH) + decoder_epsilon)
-    rows = as_rows(scale)
-    sent = jnp.concatenate(
-        [normed.reshape(4, 4 * tokens, 400), jnp.broadcast_to(rows[None], (4, *rows.shape))], axis=1
-    )
-    acts = exchange(sent, "x")
-    scales = jnp.sum(acts[:, 4 * tokens : 4 * tokens + 3, :SEQ].astype(jnp.float32), axis=1)
-    acts = acts[:, : 4 * tokens].reshape(4, 2, 2, tokens, 400)
+    sent = jnp.concatenate([by_part, as_rows(squares)], axis=0)
+    arrived = spread(sent, ("y", "c"))
+    squares = jnp.sum(
+        arrived[:, 2 * tokens : 2 * tokens + 3, :SEQ].astype(jnp.float32), axis=(0, 1)
+    )
+    gain = jnp.swapaxes(ln_gain.reshape(2, 8, 400), 0, 1)
+    bias = jnp.swapaxes(ln_bias.reshape(2, 8, 400), 0, 1)
+    normed = layer_norm(arrived, gain, bias)
+    acts = exchange(normed.reshape(4, 2, 2, tokens, 400), "x")
     partial = jnp.einsum(
         "scmtf,cfmo->sto", acts, weight.reshape(2, 400, 2, 1024),
         preferred_element_type=jnp.float32,
@@ -273,7 +287,7 @@
         part = lax.dynamic_index_in_dim(partial, lax.axis_index("x") ^ k, 0, keepdims=False)
         part = (part if k == 0 else flip_x(part, k)).astype(jnp.float32)
         total = part if total is None else total + part
-    return total.astype(jnp.bfloat16), scales[:, :, None]
+    return total.astype(jnp.bfloat16), squares
 
 
 def step(
@@ -296,9 +310,12 @@
     sequence = text_rows[0]
     wide = sequence.astype(jnp.float32)
     squares = jnp.sum(wide * wide, axis=1)
-    image, scales = vision(vis_rows, squares, ln_gain, ln_bias, proj_all)
+    image, squares = vision(vis_rows, squares, ln_gain, ln_bias, proj_all)
+    scale = lax.rsqrt(squares * (1.0 / WIDTH) + decoder_epsilon)[:, None]
+    own_gain = lax.dynamic_slice_in_dim(attn_gain, (y * NC + c) * 1024, 1024)
+    normed = (wide * scale * own_gain[None]).astype(jnp.bfloat16)
     text = []
-    for a, dx, row in ring4(sequence, "x"):
+    for a, dx, row in ring4(normed, "x"):
         other = shift(a, "c", 1)
         text.append((a, [(None, dx, None, row, a.shape[0], 0)]))
         text.append((other, [(None, dx, None, row, a.shape[0], 1)]))
@@ -322,7 +339,7 @@
 
     gain = lax.dynamic_slice_in_dim(attn_gain, y * 2048, 2048).reshape(2, 1024)
     where = jnp.stack([x, y, c]).astype(jnp.int32)
-    text_parts = project_text(where, text, both_all, scales, gain)
+    text_parts = project_text(where, text, both_all)
     text_parts = [swap_xy(p, n) for n, p in enumerate(text_parts)]
     image_parts = project_image(where, image_pieces, both_all, gain)
     image_parts = [swap_xy(p, n) for n, p in enumerate(image_parts)]

time: 251 us -> 253 us (level)
  the two profiles are of different devices: /device:TPU:60 before, /device:TPU:2 now
where the time goes in v4:
time: 253 us; the launch traced here: 251 us
  waiting for transfers between devices  114 us (45%)
  starting transfers between devices  63.6 us (25%)
  local copies, waits for them, and re-layouts  23 us (9%)
  Pallas kernels  20.4 us (8%)
  between operations  15.1 us (6%)
  other arithmetic  11.4 us (5%)
  matrix products  3.34 us (1%)
    ppermute x9, waiting for transfers between devices, swap_xy(): return lax.ppermute(array, ('x', 'y'), pairs)  57.8 us
    all_to_all x4, waiting for transfers between devices, exchange(): return lax.all_to_all(array, axis, 0, 0, tiled=True)  44 us
    all_to_all x4, starting transfers between devices, exchange(): return lax.all_to_all(array, axis, 0, 0, tiled=True)  31.6 us
    ppermute x9, starting transfers between devices, swap_xy(): return lax.ppermute(array, ('x', 'y'), pairs)  23.6 us
    unnamed x45, local copies, waits for them, and re-layouts  14.4 us
    ppermute x10, waiting for transfers between devices, shift(): lax.ppermute(array, axis, [(i, (i + by) % size) for i in range(size)])  9.26 us
    pallas_call x1, Pallas kernels, project_text(): pl.pallas_call(kernel, out_shape=[jax.ShapeDtypeStruct((SEQ, COLS), jnp.b...  7.75 us
    pallas_call x1, Pallas kernels, attention(): pl.pallas_call(kernel, out_shape=jax.ShapeDtypeStruct((SEQ, 512), jnp.bfl...  5.07 us
  transfers between devices with their start and end apart: 28, of which 17 were waited for; matrix products, arithmetic and copies ran while one was open for 10% of the time, Pallas kernels for 6%

profile of v4, /device:TPU:2, one launch (start us, length us, event | category | flops | bytes accessed | tf_op | source)
XLA Modules:
  0.0 251.4 jit_solution(8143695435535811131)
XLA Ops:
  6.5 0.7 all-gather.5.cloned.1.call-update
  7.3 0.9 copy.57
  8.2 1.0 pad_maximum_fusion
  9.2 3.5 %collective-permute-start.9 = (bf16[256,768]{1,0:T(8,128)(2,1)S(1)}, bf16[256,768]{1,0:T(8,128)(2,1)S(1)}, u32[]{:S(2)}, u32[]{:S(2)}) collective-permute-start(bf16[256,768]{1,0:T(8,128)(2,1)S(1)} %pad_maximum_fusion), channel_id=1, source_target_pairs={{0,0},{2,64},{4,128},{6,192},{64,2},{66,66},{68,130},{70,194},{128... | collective-permute-start | bytes 1179656 | tf_op jit(solution)/shard_map/ppermute | solution.py:28
  12.7 16.2 %collective-permute-done.9 = bf16[256,768]{1,0:T(8,128)(2,1)S(1)} collective-permute-done((bf16[256,768]{1,0:T(8,128)(2,1)S(1)}, bf16[256,768]{1,0:T(8,128)(2,1)S(1)}, u32[]{:S(2)}, u32[]{:S(2)}) %collective-permute-start.9) | collective-permute-done | bytes 393248 | tf_op jit(solution)/shard_map/ppermute | solution.py:28
  28.9 0.7 copy-done.17
  30.0 1.1 broadcast_in_dim.126
  31.2 6.9 %all-to-all-start = ((bf16[8,144,400]{2,1,0:T(8,128)(2,1)}), bf16[8,144,400]{2,1,0:T(8,128)(2,1)S(1)}, u32[]{:S(2)}, u32[]{:S(2)}) async-start(bf16[8,144,400]{2,1,0:T(8,128)(2,1)} %broadcast_in_dim.126), calls=%async_computation | async-start | bytes 2359296 | tf_op jit(solution)/shard_map/all_to_all | solution.py:36
  38.9 16.4 %all-to-all-done.in_ref = bf16[8,144,400]{2,1,0:T(8,128)(2,1)S(1)} async-done(((bf16[8,144,400]{2,1,0:T(8,128)(2,1)}), bf16[8,144,400]{2,1,0:T(8,128)(2,1)S(1)}, u32[]{:S(2)}, u32[]{:S(2)}) %all-to-all-start) | async-done | bytes 921632 | tf_op jit(solution)/shard_map/all_to_all | solution.py:36
  55.4 1.0 copy-done.15
  56.4 3.4 %layer_norm.1 = bf16[8,128,400]{2,1,0:T(8,128)(2,1)} custom-call(bf16[8,144,400]{2,1,0:T(8,128)(2,1)} %copy-done.15, f32[8,2,400]{2,1,0:T(2,128)} %get-tuple-element.49.gain_ref, f32[8,2,400]{2,1,0:T(2,128)} %get-tuple-element.48.bias_ref), custom_call_target="tpu_custom_call" | custom-call | tf_op jit(solution)/shard_map/layer_norm/pallas_call | solution.py:260
  59.8 6.4 %all-to-all-start.1 = ((bf16[4,2,2,64,400]{4,3,2,1,0:T(8,128)(2,1)}), bf16[4,2,2,64,400]{4,3,2,1,0:T(8,128)(2,1)S(1)}, u32[]{:S(2)}, u32[]{:S(2)}) async-start(bf16[4,2,2,64,400]{4,3,2,1,0:T(8,128)(2,1)} %bitcast.64), calls=%async_computation.1 | async-start | bytes 2097152 | tf_op jit(solution)/shard_map/all_to_all | solution.py:36
  67.3 1.3 iota_compare_fusion.2
  68.7 1.2 iota_compare_fusion.4
  69.9 9.9 %all-to-all-done.1 = bf16[4,2,2,64,400]{4,3,2,1,0:T(8,128)(2,1)S(1)} async-done(((bf16[4,2,2,64,400]{4,3,2,1,0:T(8,128)(2,1)}), bf16[4,2,2,64,400]{4,3,2,1,0:T(8,128)(2,1)S(1)}, u32[]{:S(2)}, u32[]{:S(2)}) %all-to-all-start.1) | async-done | bytes 819232 | tf_op jit(solution)/shard_map/all_to_all | solution.py:36
  79.8 3.3 %fusion.9 = bf16[4,64,1024]{2,1,0:T(8,128)(2,1)S(1)} fusion(bf16[4,2,2,64,400]{4,3,2,1,0:T(8,128)(2,1)S(1)} %all-to-all-done.1, bf16[2,400,2,1024,1]{3,2,1,0,4:T(2,128)(2,1)} %bitcast.71), kind=kOutput, calls=%fused_computation.10 | convolution fusion | flops 839122944 | bytes 4620288 | tf_op jit(solution)/shard_map/scmtf,cfmo->sto/dot_general | solution.py:281
  83.2 1.5 collective-permute-start.14
  84.9 1.9 collective-permute-start.16
  86.8 1.1 iota_compare_fusion.6
  87.9 1.3 iota_compare_fusion.8
  89.2 2.1 collective-permute-done.15
  92.0 1.2 select_select_fusion
  93.2 12.1 %all-to-all-start.2 = ((bf16[32,8,1024]{2,1,0:T(8,128)(2,1)}), bf16[32,8,1024]{2,1,0:T(8,128)(2,1)}, u32[]{:S(2)}, u32[]{:S(2)}) async-start(bf16[32,8,1024]{2,1,0:T(8,128)(2,1)} %select_select_fusion), calls=%async_computation.2 | async-start | bytes 1048576 | tf_op jit(solution)/shard_map/all_to_all | solution.py:36
  106.0 0.8 convert_reduce_fusion
  107.2 1.5 collective-permute-start.1
  109.3 0.7 fusion.30
  110.7 9.2 %all-to-all-done.2 = bf16[32,8,1024]{2,1,0:T(8,128)(2,1)} async-done(((bf16[32,8,1024]{2,1,0:T(8,128)(2,1)}), bf16[32,8,1024]{2,1,0:T(8,128)(2,1)}, u32[]{:S(2)}, u32[]{:S(2)}) %all-to-all-start.2) | async-done | bytes 524320 | tf_op jit(solution)/shard_map/all_to_all | solution.py:36
  120.0 1.6 gather_fusion
  121.6 1.1 broadcast_in_dim.145
  122.7 6.2 %all-to-all-start.3 = ((bf16[4,128,1024]{2,1,0:T(8,128)(2,1)}), bf16[4,128,1024]{2,1,0:T(8,128)(2,1)}, u32[]{:S(2)}, u32[]{:S(2)}) async-start(bf16[4,128,1024]{2,1,0:T(8,128)(2,1)} %broadcast_in_dim.145), calls=%async_computation.3 | async-start | bytes 2097152 | tf_op jit(solution)/shard_map/all_to_all | solution.py:36
  128.9 2.1 collective-permute-done.1.refs_2_
  131.0 0.8 slice.87
  131.8 1.5 collective-permute-start.5
  133.3 0.8 slice.88
  135.3 0.9 copy-done.8
  136.2 8.4 %all-to-all-done.3.refs_0_ = bf16[4,128,1024]{2,1,0:T(8,128)(2,1)} async-done(((bf16[4,128,1024]{2,1,0:T(8,128)(2,1)}), bf16[4,128,1024]{2,1,0:T(8,128)(2,1)}, u32[]{:S(2)}, u32[]{:S(2)}) %all-to-all-start.3) | async-done | bytes 1048608 | tf_op jit(solution)/shard_map/all_to_all | solution.py:36
  144.5 4.6 %collective-permute-done.5.refs_6_ = bf16[192,1024]{1,0:T(8,128)(2,1)S(1)} collective-permute-done((bf16[192,1024]{1,0:T(8,128)(2,1)}, bf16[192,1024]{1,0:T(8,128)(2,1)S(1)}, u32[]{:S(2)}, u32[]{:S(2)}) %collective-permute-start.5) | collective-permute-done | bytes 393248 | tf_op jit(solution)/shard_map/ppermute | solution.py:23
  149.1 1.5 collective-permute-done.7.refs_8_
  150.8 0.7 copy-done.10
  151.6 1.0 collective-permute-done.8.refs_9_
  152.5 0.8 copy-done.12
  153.4 1.9 copy-done
  155.3 1.1 copy-done.3
  156.4 1.1 copy-done.5
  157.5 1.1 copy-done.7
  158.7 1.1 copy-done.9
  159.8 1.0 copy-done.11
  160.8 1.0 copy-done.13
  161.8 7.7 %project_text.1 = (bf16[384,768]{1,0:T(8,128)(2,1)}, bf16[384,768]{1,0:T(8,128)(2,1)}, bf16[384,768]{1,0:T(8,128)(2,1)}, bf16[384,768]{1,0:T(8,128)(2,1)S(1)}) custom-call(s32[3]{0:T(128)S(1)} %pad_add_fusion.1.where_ref, bf16[384,1024]{1,0:T(8,128)(2,1)S(1)} %copy-done.3, bf16[384,1024]{1,0:T(8,128)(2,1)S(1)} %copy-done.9, bf16[384,1024]{1,0:T(8,128)(2,1)S(1)} %copy-done.5, ...), custom_call_target="tpu_custom_call" | custom-call | tf_op jit(solution)/shard_map/project_text/pallas_call | solution.py:99
  169.5 0.8 copy-done.14
  170.3 3.6 %collective-permute-start.10 = (bf16[384,768]{1,0:T(8,128)(2,1)}, bf16[384,768]{1,0:T(8,128)(2,1)}, u32[]{:S(2)}, u32[]{:S(2)}) collective-permute-start(bf16[384,768]{1,0:T(8,128)(2,1)} %get-tuple-element.13), channel_id=1, source_target_pairs={{0,0},{2,64},{4,128},{6,192},{64,2},{66,66},{68,130},{70,194},{128... | collective-permute-start | bytes 1769480 | tf_op jit(solution)/shard_map/ppermute | solution.py:28
  173.9 2.9 %collective-permute-start.11 = (bf16[384,768]{1,0:T(8,128)(2,1)}, bf16[384,768]{1,0:T(8,128)(2,1)}, u32[]{:S(2)}, u32[]{:S(2)}) collective-permute-start(bf16[384,768]{1,0:T(8,128)(2,1)} %get-tuple-element.14), channel_id=1, source_target_pairs={{0,64},{2,0},{4,192},{6,128},{64,66},{66,2},{68,194},{70,130},{128... | collective-permute-start | bytes 1769480 | tf_op jit(solution)/shard_map/ppermute | solution.py:28
  176.9 1.7 collective-permute-start.12
  178.6 0.7 dynamic_slice.30
  179.3 1.3 collective-permute-start.13
  181.9 0.8 fusion.17
  182.8 4.2 %project_image.1 = (bf16[128,896]{1,0:T(8,128)(2,1)S(1)}, bf16[128,896]{1,0:T(8,128)(2,1)S(1)}, bf16[128,896]{1,0:T(8,128)(2,1)S(1)}, bf16[128,896]{1,0:T(8,128)(2,1)S(1)}) custom-call(s32[3]{0:T(128)S(1)} %pad_add_fusion.1.where_ref, bf16[4,128,1024]{2,1,0:T(8,128)(2,1)} %all-to-all-done.3.refs_0_, bf16[4,128,1024]{2,1,0:T(8,128)(2,1)} %collective-permute-done.17.refs_1_, ...), custom_call_target="tpu_custom_call" | custom-call | tf_op jit(solution)/shard_map/project_image/pallas_call | solution.py:149
  187.0 4.0 %collective-permute-start.18 = (bf16[128,896]{1,0:T(8,128)(2,1)S(1)}, bf16[128,896]{1,0:T(8,128)(2,1)S(1)}, u32[]{:S(2)}, u32[]{:S(2)}) collective-permute-start(bf16[128,896]{1,0:T(8,128)(2,1)S(1)} %get-tuple-element.17), channel_id=1, source_target_pairs={{0,0},{2,64},{4,128},{6,192},{64,2},{66,66},{68,130},{70,194},{128... | collective-permute-start | bytes 688136 | tf_op jit(solution)/shard_map/ppermute | solution.py:28
  191.0 10.5 %collective-permute-done.10.refs_0_ = bf16[384,768]{1,0:T(8,128)(2,1)} collective-permute-done((bf16[384,768]{1,0:T(8,128)(2,1)}, bf16[384,768]{1,0:T(8,128)(2,1)}, u32[]{:S(2)}, u32[]{:S(2)}) %collective-permute-start.10) | collective-permute-done | bytes 589856 | tf_op jit(solution)/shard_map/ppermute | solution.py:28
  201.8 6.7 %collective-permute-start.20 = (bf16[128,896]{1,0:T(8,128)(2,1)S(1)}, bf16[128,896]{1,0:T(8,128)(2,1)S(1)}, u32[]{:S(2)}, u32[]{:S(2)}) collective-permute-start(bf16[128,896]{1,0:T(8,128)(2,1)S(1)} %get-tuple-element.19), channel_id=1, source_target_pairs={{0,128},{2,192},{4,0},{6,64},{64,130},{66,194},{68,2},{70,66},{128... | collective-permute-start | bytes 688136 | tf_op jit(solution)/shard_map/ppermute | solution.py:28
  208.5 17.9 %collective-permute-done.12.refs_2_ = bf16[384,768]{1,0:T(8,128)(2,1)} collective-permute-done((bf16[384,768]{1,0:T(8,128)(2,1)}, bf16[384,768]{1,0:T(8,128)(2,1)}, u32[]{:S(2)}, u32[]{:S(2)}) %collective-permute-start.12) | collective-permute-done | bytes 589856 | tf_op jit(solution)/shard_map/ppermute | solution.py:28
  226.7 2.4 collective-permute-done.18.refs_4_
  229.1 10.3 %collective-permute-done.20.refs_6_ = bf16[128,896]{1,0:T(8,128)(2,1)S(1)} collective-permute-done((bf16[128,896]{1,0:T(8,128)(2,1)S(1)}, bf16[128,896]{1,0:T(8,128)(2,1)S(1)}, u32[]{:S(2)}, u32[]{:S(2)}) %collective-permute-start.20) | collective-permute-done | bytes 229408 | tf_op jit(solution)/shard_map/ppermute | solution.py:28
  239.5 5.1 %attention.1 = bf16[384,512]{1,0:T(8,128)(2,1)} custom-call(s32[2]{0:T(128)S(1)} %pad_add_fusion.where_ref, bf16[384,768]{1,0:T(8,128)(2,1)} %collective-permute-done.10.refs_0_, bf16[384,768]{1,0:T(8,128)(2,1)} %collective-permute-done.11.refs_1_, bf16[384,768]{1,0:T(8,128)(2,1)} %collective-permute-done.12.refs_2_, ...), custom_call_target="tpu_custom_call" | custom-call | tf_op jit(solution)/shard_map/attention/pallas_call | solution.py:218
  (88 shorter events, 7.6 us)
Async XLA Ops:
  6.5 23.1 %copy-start.16 = (bf16[1,384,1024]{2,1,0:T(8,128)(2,1)S(1)}, bf16[1,384,1024]{2,1,0:T(8,128)(2,1)}, u32[]{:S(2)}) copy-start(bf16[1,384,1024]{2,1,0:T(8,128)(2,1)} %param.14) | copy-start | bytes 2359300
  6.5 23.4 %copy-start.18 = (bf16[8,8,2,400]{3,2,1,0:T(2,128)(2,1)S(1)}, bf16[8,8,2,400]{3,2,1,0:T(2,128)(2,1)}, u32[]{:S(2)}) copy-start(bf16[8,8,2,400]{3,2,1,0:T(2,128)(2,1)} %param.10) | copy-start | bytes 307204
  6.5 73.3 %all-gather.5.cloned.1.call-start = ((), (), s32[]{:S(2)}) async-start(), calls=%async_computation.5 | async-start | bytes 3686400 | tf_op jit(solution)/shard_map/all_gather | solution.py:306
  7.3 146.1 %all-gather.3.cloned.1.call-start = ((), (), s32[]{:S(2)}) async-start(), calls=%async_computation.4 | async-start | bytes 3538944 | tf_op jit(solution)/shard_map/all_gather | solution.py:308
  9.2 19.7 %collective-permute-start.9 = (bf16[256,768]{1,0:T(8,128)(2,1)S(1)}, bf16[256,768]{1,0:T(8,128)(2,1)S(1)}, u32[]{:S(2)}, u32[]{:S(2)}) collective-permute-start(bf16[256,768]{1,0:T(8,128)(2,1)S(1)} %pad_maximum_fusion), channel_id=1, source_target_pairs={{0,0},{2,64},{4,128},{6,192},{64,2},{66,66},{68,130},{70,194},{128... | collective-permute-start | bytes 1179656 | tf_op jit(solution)/shard_map/ppermute | solution.py:28
  28.9 0.8 copy-start.17
  30.0 8.0 %copy-start.19 = (f32[2,3200]{1,0:T(2,128)S(1)}, f32[2,3200]{1,0:T(2,128)}, u32[]{:S(2)}) copy-start(f32[2,3200]{1,0:T(2,128)} %param.11) | copy-start | bytes 76804
  30.0 8.1 %copy-start.20 = (f32[2,3200]{1,0:T(2,128)S(1)}, f32[2,3200]{1,0:T(2,128)}, u32[]{:S(2)}) copy-start(f32[2,3200]{1,0:T(2,128)} %param.12) | copy-start | bytes 76804
  31.2 24.2 %all-to-all-start = ((bf16[8,144,400]{2,1,0:T(8,128)(2,1)}), bf16[8,144,400]{2,1,0:T(8,128)(2,1)S(1)}, u32[]{:S(2)}, u32[]{:S(2)}) async-start(bf16[8,144,400]{2,1,0:T(8,128)(2,1)} %broadcast_in_dim.126), calls=%async_computation | async-start | bytes 2359296 | tf_op jit(solution)/shard_map/all_to_all | solution.py:36
  55.4 1.0 copy-start.15
  59.8 6.4 %copy-start.21 = (s32[32]{0:T(128)S(1)}, s32[32]{0:T(128)}, u32[]{:S(2)}) copy-start(s32[32]{0:T(128)} %param.18) | copy-start | bytes 388
  59.8 20.0 %all-to-all-start.1 = ((bf16[4,2,2,64,400]{4,3,2,1,0:T(8,128)(2,1)}), bf16[4,2,2,64,400]{4,3,2,1,0:T(8,128)(2,1)S(1)}, u32[]{:S(2)}, u32[]{:S(2)}) async-start(bf16[4,2,2,64,400]{4,3,2,1,0:T(8,128)(2,1)} %bitcast.64), calls=%async_computation.1 | async-start | bytes 2097152 | tf_op jit(solution)/shard_map/all_to_all | solution.py:36
  83.2 6.0 %collective-permute-start.14 = (bf16[64,1024]{1,0:T(8,128)(2,1)S(1)}, bf16[64,1024]{1,0:T(8,128)(2,1)S(1)}, u32[]{:S(2)}, u32[]{:S(2)}) collective-permute-start(bf16[64,1024]{1,0:T(8,128)(2,1)S(1)} %get-tuple-element.23), channel_id=1, source_target_pairs={{0,64},{64,0},{128,192},{192,128},{1,65},{65,1},{129,193},{193,129... | collective-permute-start | bytes 393224 | tf_op jit(solution)/shard_map/ppermute | solution.py:32
  84.8 6.6 %collective-permute-start.15 = (bf16[64,1024]{1,0:T(8,128)(2,1)S(1)}, bf16[64,1024]{1,0:T(8,128)(2,1)S(1)}, u32[]{:S(2)}, u32[]{:S(2)}) collective-permute-start(bf16[64,1024]{1,0:T(8,128)(2,1)S(1)} %get-tuple-element.25), channel_id=1, source_target_pairs={{0,128},{64,192},{128,0},{192,64},{1,129},{65,193},{129,1},{193,65... | collective-permute-start | bytes 393224 | tf_op jit(solution)/shard_map/ppermute | solution.py:32
  84.9 7.1 %collective-permute-start.16 = (bf16[64,1024]{1,0:T(8,128)(2,1)S(1)}, bf16[64,1024]{1,0:T(8,128)(2,1)S(1)}, u32[]{:S(2)}, u32[]{:S(2)}) collective-permute-start(bf16[64,1024]{1,0:T(8,128)(2,1)S(1)} %get-tuple-element.24), channel_id=1, source_target_pairs={{0,192},{64,128},{128,64},{192,0},{1,193},{65,129},{129,65},{193,1... | collective-permute-start | bytes 393224 | tf_op jit(solution)/shard_map/ppermute | solution.py:32
  93.2 26.8 %all-to-all-start.2 = ((bf16[32,8,1024]{2,1,0:T(8,128)(2,1)}), bf16[32,8,1024]{2,1,0:T(8,128)(2,1)}, u32[]{:S(2)}, u32[]{:S(2)}) async-start(bf16[32,8,1024]{2,1,0:T(8,128)(2,1)} %select_select_fusion), calls=%async_computation.2 | async-start | bytes 1048576 | tf_op jit(solution)/shard_map/all_to_all | solution.py:36
  107.1 15.6 %copy-start.2 = (bf16[384,1024]{1,0:T(8,128)(2,1)}, bf16[384,1024]{1,0:T(8,128)(2,1)S(1)}, u32[]{:S(2)}) copy-start(bf16[384,1024]{1,0:T(8,128)(2,1)S(1)} %fusion.5.refs_0_) | copy-start | bytes 2359300
  107.2 23.8 %collective-permute-start.1 = (bf16[384,1024]{1,0:T(8,128)(2,1)S(1)}, bf16[384,1024]{1,0:T(8,128)(2,1)S(1)}, u32[]{:S(2)}, u32[]{:S(2)}) collective-permute-start(bf16[384,1024]{1,0:T(8,128)(2,1)S(1)} %fusion.5.refs_0_), channel_id=1, source_target_pairs={{0,64},{64,128},{128,192},{192,0},{1,65},{65,129},{129,193},{193,1... | collective-permute-start | bytes 2359304 | tf_op jit(solution)/shard_map/ppermute | solution.py:23
  108.7 24.6 %collective-permute-start.3 = (bf16[384,1024]{1,0:T(8,128)(2,1)S(1)}, bf16[384,1024]{1,0:T(8,128)(2,1)S(1)}, u32[]{:S(2)}, u32[]{:S(2)}) collective-permute-start(bf16[384,1024]{1,0:T(8,128)(2,1)S(1)} %fusion.5.refs_0_), channel_id=1, source_target_pairs={{0,192},{64,0},{128,64},{192,128},{1,193},{65,1},{129,65},{193,129... | collective-permute-start | bytes 2359304 | tf_op jit(solution)/shard_map/ppermute | solution.py:23
  110.6 24.6 %collective-permute-start = (bf16[384,1024]{1,0:T(8,128)(2,1)S(1)}, bf16[384,1024]{1,0:T(8,128)(2,1)S(1)}, u32[]{:S(2)}, u32[]{:S(2)}) collective-permute-start(bf16[384,1024]{1,0:T(8,128)(2,1)S(1)} %fusion.5.refs_0_), channel_id=1, source_target_pairs={{0,1},{1,0},{2,3},{3,2},{4,5},{5,4},{6,7},{7,6},{8,9},{9,8},{10,11... | collective-permute-start | bytes 2359304 | tf_op jit(solution)/shard_map/ppermute | solution.py:23
  122.7 21.8 %all-to-all-start.3 = ((bf16[4,128,1024]{2,1,0:T(8,128)(2,1)}), bf16[4,128,1024]{2,1,0:T(8,128)(2,1)}, u32[]{:S(2)}, u32[]{:S(2)}) async-start(bf16[4,128,1024]{2,1,0:T(8,128)(2,1)} %broadcast_in_dim.145), calls=%async_computation.3 | async-start | bytes 2097152 | tf_op jit(solution)/shard_map/all_to_all | solution.py:36
  131.0 22.3 %copy-start.4 = (bf16[384,1024]{1,0:T(8,128)(2,1)}, bf16[384,1024]{1,0:T(8,128)(2,1)S(1)}, u32[]{:S(2)}) copy-start(bf16[384,1024]{1,0:T(8,128)(2,1)S(1)} %collective-permute-done.1.refs_2_) | copy-start | bytes 2359300
  131.8 17.3 %collective-permute-start.5 = (bf16[192,1024]{1,0:T(8,128)(2,1)}, bf16[192,1024]{1,0:T(8,128)(2,1)S(1)}, u32[]{:S(2)}, u32[]{:S(2)}) collective-permute-start(bf16[192,1024]{1,0:T(8,128)(2,1)} %slice.87), channel_id=1, source_target_pairs={{0,64},{64,128},{128,192},{192,0},{1,65},{65,129},{129,193},{193,1... | collective-permute-start | bytes 1179656 | tf_op jit(solution)/shard_map/ppermute | solution.py:23
  133.3 20.0 %copy-start.6 = (bf16[384,1024]{1,0:T(8,128)(2,1)}, bf16[384,1024]{1,0:T(8,128)(2,1)S(1)}, u32[]{:S(2)}) copy-start(bf16[384,1024]{1,0:T(8,128)(2,1)S(1)} %collective-permute-done.3.refs_4_) | copy-start | bytes 2359300
  134.1 16.5 %collective-permute-start.7 = (bf16[192,1024]{1,0:T(8,128)(2,1)}, bf16[192,1024]{1,0:T(8,128)(2,1)}, u32[]{:S(2)}, u32[]{:S(2)}) collective-permute-start(bf16[192,1024]{1,0:T(8,128)(2,1)} %slice.88), channel_id=1, source_target_pairs={{0,192},{64,0},{128,64},{192,128},{1,193},{65,1},{129,65},{193,129... | collective-permute-start | bytes 1179656 | tf_op jit(solution)/shard_map/ppermute | solution.py:23
  134.7 18.6 %collective-permute-start.2 = (bf16[384,1024]{1,0:T(8,128)(2,1)S(1)}, bf16[384,1024]{1,0:T(8,128)(2,1)}, u32[]{:S(2)}, u32[]{:S(2)}) collective-permute-start(bf16[384,1024]{1,0:T(8,128)(2,1)S(1)} %collective-permute-done.1.refs_2_), channel_id=1, source_target_pairs={{0,1},{1,0},{2,3},{3,2},{4,5},{5,4},{6,7},{7,6},{8,9},{9,8},{10,11... | collective-permute-start | bytes 2359304 | tf_op jit(solution)/shard_map/ppermute | solution.py:23
  134.7 18.6 %collective-permute-start.4 = (bf16[384,1024]{1,0:T(8,128)(2,1)S(1)}, bf16[384,1024]{1,0:T(8,128)(2,1)}, u32[]{:S(2)}, u32[]{:S(2)}) collective-permute-start(bf16[384,1024]{1,0:T(8,128)(2,1)S(1)} %collective-permute-done.3.refs_4_), channel_id=1, source_target_pairs={{0,1},{1,0},{2,3},{3,2},{4,5},{5,4},{6,7},{7,6},{8,9},{9,8},{10,11... | collective-permute-start | bytes 2359304 | tf_op jit(solution)/shard_map/ppermute | solution.py:23
  135.3 0.9 copy-start.8
  144.5 38.2 %collective-permute-start.17 = (bf16[4,128,1024]{2,1,0:T(8,128)(2,1)}, bf16[4,128,1024]{2,1,0:T(8,128)(2,1)}, u32[]{:S(2)}, u32[]{:S(2)}) collective-permute-start(bf16[4,128,1024]{2,1,0:T(8,128)(2,1)} %all-to-all-done.3.refs_0_), channel_id=1, source_target_pairs={{0,1},{1,0},{2,3},{3,2},{4,5},{5,4},{6,7},{7,6},{8,9},{9,8},{10,11... | collective-permute-start | bytes 3145736 | tf_op jit(solution)/shard_map/ppermute | solution.py:23
  149.1 1.7 collective-permute-start.6
  150.6 1.9 collective-permute-start.8
  150.8 0.7 copy-start.10
  152.5 0.8 copy-start.12
  153.4 1.9 copy-start
  155.3 1.1 copy-start.3
  156.4 1.1 copy-start.5
  157.5 1.1 copy-start.7
  158.7 1.1 copy-start.9
  159.8 1.0 copy-start.11
  160.8 1.0 copy-start.13
  161.8 21.0 %copy-start.1 = (bf16[2048,768]{1,0:T(8,128)(2,1)S(1)}, bf16[2048,768]{1,0:T(8,128)(2,1)}, u32[]{:S(2)}) copy-start(bf16[2048,768]{1,0:T(8,128)(2,1)} %all-gather.3.cloned.1.call-done.refs_10_.refs_2_) | copy-start | bytes 9437188
  169.5 0.8 copy-start.14
  170.3 31.1 %collective-permute-start.10 = (bf16[384,768]{1,0:T(8,128)(2,1)}, bf16[384,768]{1,0:T(8,128)(2,1)}, u32[]{:S(2)}, u32[]{:S(2)}) collective-permute-start(bf16[384,768]{1,0:T(8,128)(2,1)} %get-tuple-element.13), channel_id=1, source_target_pairs={{0,0},{2,64},{4,128},{6,192},{64,2},{66,66},{68,130},{70,194},{128... | collective-permute-start | bytes 1769480 | tf_op jit(solution)/shard_map/ppermute | solution.py:28
  173.9 27.9 %collective-permute-start.11 = (bf16[384,768]{1,0:T(8,128)(2,1)}, bf16[384,768]{1,0:T(8,128)(2,1)}, u32[]{:S(2)}, u32[]{:S(2)}) collective-permute-start(bf16[384,768]{1,0:T(8,128)(2,1)} %get-tuple-element.14), channel_id=1, source_target_pairs={{0,64},{2,0},{4,192},{6,128},{64,66},{66,2},{68,194},{70,130},{128... | collective-permute-start | bytes 1769480 | tf_op jit(solution)/shard_map/ppermute | solution.py:28
  176.9 49.6 %collective-permute-start.12 = (bf16[384,768]{1,0:T(8,128)(2,1)}, bf16[384,768]{1,0:T(8,128)(2,1)}, u32[]{:S(2)}, u32[]{:S(2)}) collective-permute-start(bf16[384,768]{1,0:T(8,128)(2,1)} %get-tuple-element.15), channel_id=1, source_target_pairs={{0,128},{2,192},{4,0},{6,64},{64,130},{66,194},{68,2},{70,66},{128... | collective-permute-start | bytes 1769480 | tf_op jit(solution)/shard_map/ppermute | solution.py:28
  179.3 47.4 %collective-permute-start.13 = (bf16[384,768]{1,0:T(8,128)(2,1)}, bf16[384,768]{1,0:T(8,128)(2,1)}, u32[]{:S(2)}, u32[]{:S(2)}) collective-permute-start(bf16[384,768]{1,0:T(8,128)(2,1)} %copy-done.14), channel_id=1, source_target_pairs={{0,192},{2,128},{4,64},{6,0},{64,194},{66,130},{68,66},{70,2},{128... | collective-permute-start | bytes 1769480 | tf_op jit(solution)/shard_map/ppermute | solution.py:28
  187.0 42.2 %collective-permute-start.18 = (bf16[128,896]{1,0:T(8,128)(2,1)S(1)}, bf16[128,896]{1,0:T(8,128)(2,1)S(1)}, u32[]{:S(2)}, u32[]{:S(2)}) collective-permute-start(bf16[128,896]{1,0:T(8,128)(2,1)S(1)} %get-tuple-element.17), channel_id=1, source_target_pairs={{0,0},{2,64},{4,128},{6,192},{64,2},{66,66},{68,130},{70,194},{128... | collective-permute-start | bytes 688136 | tf_op jit(solution)/shard_map/ppermute | solution.py:28
  201.5 27.7 %collective-permute-start.19 = (bf16[128,896]{1,0:T(8,128)(2,1)S(1)}, bf16[128,896]{1,0:T(8,128)(2,1)S(1)}, u32[]{:S(2)}, u32[]{:S(2)}) collective-permute-start(bf16[128,896]{1,0:T(8,128)(2,1)S(1)} %get-tuple-element.18), channel_id=1, source_target_pairs={{0,64},{2,0},{4,192},{6,128},{64,66},{66,2},{68,194},{70,130},{128... | collective-permute-start | bytes 688136 | tf_op jit(solution)/shard_map/ppermute | solution.py:28
  201.8 37.6 %collective-permute-start.20 = (bf16[128,896]{1,0:T(8,128)(2,1)S(1)}, bf16[128,896]{1,0:T(8,128)(2,1)S(1)}, u32[]{:S(2)}, u32[]{:S(2)}) collective-permute-start(bf16[128,896]{1,0:T(8,128)(2,1)S(1)} %get-tuple-element.19), channel_id=1, source_target_pairs={{0,128},{2,192},{4,0},{6,64},{64,130},{66,194},{68,2},{70,66},{128... | collective-permute-start | bytes 688136 | tf_op jit(solution)/shard_map/ppermute | solution.py:28
  226.5 13.0 %collective-permute-start.21 = (bf16[128,896]{1,0:T(8,128)(2,1)S(1)}, bf16[128,896]{1,0:T(8,128)(2,1)S(1)}, u32[]{:S(2)}, u32[]{:S(2)}) collective-permute-start(bf16[128,896]{1,0:T(8,128)(2,1)S(1)} %get-tuple-element.20), channel_id=1, source_target_pairs={{0,192},{2,128},{4,64},{6,0},{64,194},{66,130},{68,66},{70,2},{128... | collective-permute-start | bytes 688136 | tf_op jit(solution)/shard_map/ppermute | solution.py:28
Sparse Core Ops, SparseCore 0:
  9.1 49.0 all-gather.4
  60.0 43.5 all-gather.2

commit v5 on v1

v5 whole, which is shorter than its diff:
```python
import jax
import jax.numpy as jnp
from jax import lax
from jax.experimental import pallas as pl
from jax.experimental.pallas import tpu as pltpu
from jax.sharding import Mesh, PartitionSpec as P


HEAD = 128
NX, NZ, NY, NC = 4, 8, 4, 2
SEQ = 384
SPAN = 128
WIDTH = 8192
vision_epsilon = 1e-06
decoder_epsilon = 1e-05
rope_base = 500000.0


def shift(array, axis, by):
    size = lax.axis_size(axis)
    return lax.ppermute(array, axis, [(i, (i + by) % size) for i in range(size)])


def flip_x(array, flip):
    return lax.ppermute(array, "x", [(i, i ^ flip) for i in range(NX)])


def exchange(array, axis):
    return lax.all_to_all(array, axis, 0, 0, tiled=True)


def spread(array, axis):
    size = lax.axis_size(axis)
    return exchange(jnp.broadcast_to(array[None], (size, *array.shape)), axis)


def ring4(array, axis):
    half = array.shape[0] // 2
    below = shift(array, axis, 1)
    above = shift(array, axis, -1)
    far_low = shift(below[:half], axis, 1)
    far_high = shift(above[half:], axis, -1)
    return [(array, 0, 0), (below, -1, 0), (above, 1, 0), (far_low, 2, 0), (far_high, 2, half)]


def ring8(array, axis):
    half = array.shape[0] // 2
    pieces = [(array, 0, 0)]
    below = above = array
    for step in (1, 2, 3):
        below = shift(below, axis, 1)
        above = shift(above, axis, -1)
        pieces += [(below, -step, 0), (above, step, 0)]
    pieces += [(shift(below[:half], axis, 1), 4, 0), (shift(above[half:], axis, -1), 4, half)]
    return pieces


def rope_tables():
    half = HEAD // 2
    exponents = jnp.arange(half, dtype=jnp.float32) * (2.0 / HEAD)
    frequency = rope_base ** (-exponents)
    positions = jnp.arange(SEQ, dtype=jnp.int32).astype(jnp.float32)
    angles = positions[:, None] * frequency[None, :]
    cosine, sine = jnp.cos(angles), jnp.sin(angles)
    return (
        jnp.concatenate([cosine, cosine], axis=1),
        jnp.concatenate([-sine, sine], axis=1),
    )


VMEM = pl.BlockSpec(memory_space=pltpu.VMEM)
SMEM = pl.BlockSpec(memory_space=pltpu.SMEM)
HBM = pl.BlockSpec(memory_space=pltpu.HBM)


def pack(pieces):
    rows = sum(a.shape[0] for a in pieces)

    def kernel(*refs):
        at = 0
        for ref in refs[:-1]:
            refs[-1][at : at + ref.shape[0], :] = ref[...]
            at += ref.shape[0]

    return pl.pallas_call(
        kernel,
        out_shape=jax.ShapeDtypeStruct((rows, pieces[0].shape[1]), pieces[0].dtype),
        in_specs=[VMEM] * len(pieces),
        out_specs=VMEM,
        name="pack",
    )(*pieces)


def rotated(value, cos, sin):
    return (value * cos + pltpu.roll(value, 64, 1) * sin).astype(jnp.bfloat16)


def prepare(where, text, image, keyval, gain, cosine, sine):
    arrays = [a for a, _, _, _ in text] + list(image) + [a for a, _ in keyval]
    n_text, count = len(text), len(arrays)
    plan = [
        (n_text + 2 + n, *part) for n, (_, parts) in enumerate(keyval) for part in parts
    ]

    def kernel(where_ref, *refs):
        gain_ref, cos_ref, sin_ref = refs[count : count + 3]
        a_ref, key_ref, value_ref = refs[count + 3 : count + 6]
        b_ref, sem = refs[count + 6 :]
        x, z, y, c = where_ref[0], where_ref[1], where_ref[2], where_ref[3]
        start, n_rows = where_ref[4], where_ref[5]
        loads = []
        for k, (n, dx, dz, row, rows, at) in enumerate(plan):
            d = lax.rem(x + (dx + NX), NX) * NZ + lax.rem(z + (dz + NZ), NZ)
            first = pl.multiple_of(d * 256 + row, 128)
            loads.append(
                pltpu.make_async_copy(
                    refs[n].at[pl.ds(at, rows), :], b_ref.at[pl.ds(first, rows), :], sem.at[k]
                )
            )
        for copy in loads:
            copy.start()

        total = {}
        for n, (_, dy, first, flip) in enumerate(text):
            rows = refs[n].shape[0]
            side = lax.rem(y + (dy + NY), NY)
            t = side * NC + (c if flip == 0 else 1 - c)
            p_at = lax.broadcasted_iota(jnp.int32, (rows, SPAN), 0) + first - start
            j_at = lax.broadcasted_iota(jnp.int32, (rows, SPAN), 1)
            pick = jnp.where((p_at == j_at) & (j_at < n_rows), 1.0, 0.0).astype(jnp.bfloat16)
            rows_at = lax.broadcasted_iota(jnp.int32, (rows, 1), 0) + first - start
            is_image = (rows_at >= 0) & (rows_at < n_rows)
            placed = jnp.dot(
                pick, refs[n_text + flip][side], preferred_element_type=jnp.float32
            )
            value = jnp.where(is_image, placed, refs[n][...].astype(jnp.float32))
            a_ref[t, first : first + rows, :] = value.astype(jnp.bfloat16)
            squares = jnp.sum(value * value, axis=1, keepdims=True)
            if rows < SEQ:
                zero = jnp.zeros((SEQ - rows, 1), jnp.float32)
                squares = jnp.concatenate([squares, zero] if first == 0 else [zero, squares], axis=0)
            total = squares if n == 0 else total + squares
        scale = lax.rsqrt(total * (1.0 / WIDTH) + decoder_epsilon)
        for copy in loads:
            copy.wait()
        acc = jnp.zeros((SEQ, 256), jnp.float32)
        for t in range(8):
            normed = (
                a_ref[t].astype(jnp.float32) * scale * gain_ref[t : t + 1, :]
            ).astype(jnp.bfloat16)
            a_ref[t] = normed
            acc = acc + jnp.dot(
                normed, b_ref[t * 1024 : (t + 1) * 1024, :], preferred_element_type=jnp.float32
            )
        key_ref[...] = rotated(acc[:, :HEAD], cos_ref[...], sin_ref[...])
        value_ref[...] = acc[:, HEAD:].astype(jnp.bfloat16)

    return pl.pallas_call(
        kernel,
        out_shape=[
            jax.ShapeDtypeStruct((8, SEQ, 1024), jnp.bfloat16),
            jax.ShapeDtypeStruct((SEQ, HEAD), jnp.bfloat16),
            jax.ShapeDtypeStruct((SEQ, HEAD), jnp.bfloat16),
        ],
        in_specs=[SMEM] + [VMEM] * (n_text + 2) + [HBM] * len(keyval) + [VMEM] * 3,
        out_specs=[VMEM] * 3,
        scratch_shapes=[
            pltpu.VMEM((WIDTH, 256), jnp.bfloat16),
            pltpu.SemaphoreType.DMA((len(plan),)),
        ],
        compiler_params=pltpu.CompilerParams(vmem_limit_bytes=48 * 1024 * 1024),
        name="prepare",
    )(where, *arrays, gain, cosine, sine)


def attention(sequence, query_w, key, value, cosine, sine):
    def kernel(a_ref, w_hbm, key_ref, value_ref, cos_ref, sin_ref, out_ref, w_ref, sem):
        loads = [
            pltpu.make_async_copy(
                w_hbm.at[pl.ds(t * 1024, 1024), :], w_ref.at[pl.ds(t * 1024, 1024), :], sem.at[t]
            )
            for t in range(8)
        ]
        for copy in loads:
            copy.start()
        acc = jnp.zeros((SEQ, 512), jnp.float32)
        for t in range(8):
            loads[t].wait()
            acc = acc + jnp.dot(
                a_ref[t], w_ref[t * 1024 : (t + 1) * 1024, :], preferred_element_type=jnp.float32
            )
        cos, sin = cos_ref[...], sin_ref[...]
        causal = lax.broadcasted_iota(jnp.int32, (SEQ, SEQ), 0) >= lax.broadcasted_iota(
            jnp.int32, (SEQ, SEQ), 1
        )
        for h in range(4):
            query = rotated(acc[:, h * HEAD : (h + 1) * HEAD], cos, sin)
            scores = lax.dot_general(
                query, key_ref[...], (((1,), (1,)), ((), ())), preferred_element_type=jnp.float32
            ) * (HEAD ** (-0.5))
            scores = jnp.where(causal, scores, -1e30)
            top = jnp.max(scores, axis=1, keepdims=True)
            e = jnp.exp(scores - top)
            w = (e / jnp.sum(e, axis=1, keepdims=True)).astype(jnp.bfloat16)
            out_ref[:, h * HEAD : (h + 1) * HEAD] = jnp.dot(
                w, value_ref[...], preferred_element_type=jnp.float32
            ).astype(jnp.bfloat16)

    return pl.pallas_call(
        kernel,
        out_shape=jax.ShapeDtypeStruct((SEQ, 512), jnp.bfloat16),
        in_specs=[VMEM, HBM] + [VMEM] * 4,
        out_specs=VMEM,
        scratch_shapes=[
            pltpu.VMEM((WIDTH, 512), jnp.bfloat16),
            pltpu.SemaphoreType.DMA((8,)),
        ],
        compiler_params=pltpu.CompilerParams(vmem_limit_bytes=48 * 1024 * 1024),
        name="attention",
    )(sequence, query_w, key, value, cosine, sine)


def vision(vis_rows, ln_gain, ln_bias, weight):
    tokens = vis_rows.shape[0] * vis_rows.shape[1]
    whole = spread(vis_rows.reshape(tokens, 2, 400), ("y", "c")).astype(jnp.float32)
    mean = jnp.mean(whole, axis=(0, 2, 3))[None, :, None, None]
    centered = whole - mean
    variance = jnp.mean(centered * centered, axis=(0, 2, 3))[None, :, None, None]
    gain = jnp.swapaxes(ln_gain.reshape(2, 8, 400), 0, 1)[:, None]
    bias = jnp.swapaxes(ln_bias.reshape(2, 8, 400), 0, 1)[:, None]
    normed = (centered * lax.rsqrt(variance + vision_epsilon) * gain + bias).astype(jnp.bfloat16)
    acts = exchange(normed.reshape(4, 2, tokens, 2, 400), "x")
    partial = jnp.einsum(
        "sctmf,cfmo->sto", acts, weight.reshape(2, 400, 2, 1024),
        preferred_element_type=jnp.float32,
    ).astype(jnp.bfloat16)
    total = None
    for k in range(NX):
        part = lax.dynamic_index_in_dim(partial, lax.axis_index("x") ^ k, 0, keepdims=False)
        part = (part if k == 0 else flip_x(part, k)).astype(jnp.float32)
        total = part if total is None else total + part
    return total.astype(jnp.bfloat16)


def step(
    vis_rows, ln_gain, ln_bias, proj_weight, text_rows, attn_gain, w_query,
    key_value_weight, tile_counts, image_offsets,
):
    x, z = lax.axis_index("x"), lax.axis_index("z")
    y, c = lax.axis_index("y"), lax.axis_index("c")
    tile_ends = jnp.cumsum(tile_counts)
    tile_firsts = tile_ends - tile_counts
    sample_ids = jnp.arange(32, dtype=jnp.int32)

    def entry(values, index):
        return jnp.sum(jnp.where(sample_ids == index, values, 0))

    proj_all = lax.all_gather(proj_weight, "z", axis=0, tiled=True)
    query_w = lax.all_gather(w_query, ("x", "z"), axis=0, tiled=True)

    image = vision(vis_rows, ln_gain, ln_bias, proj_all).reshape(8, 8, 1024)

    along_z = ring8(key_value_weight.reshape(256, 256), "z")
    offsets, at = [], 0
    for a, dz, row in along_z:
        offsets.append((dz, row, a.shape[0], at))
        at += a.shape[0]
    keyval = []
    for a, dx, first in ring4(pack([a for a, _, _ in along_z]), "x"):
        parts = [
            (dx, dz, row, rows, at - first)
            for dz, row, rows, at in offsets
            if first <= at and at + rows <= first + a.shape[0]
        ]
        keyval.append((a, parts))

    text = []
    for a, dy, row in ring4(text_rows[0], "y"):
        text.append((a, dy, row, 0))
        text.append((shift(a, "c", 1), dy, row, 1))

    place = x * NZ + z
    tiles_here = jnp.arange(8, dtype=jnp.int32) * 32 + place
    owners = jnp.sum((tile_ends[None, :] <= tiles_here[:, None]).astype(jnp.int32), axis=1)
    slots = jnp.zeros((32, 8, 1024), jnp.bfloat16)
    for r in range(8):
        slots = jnp.where((owners[r] == sample_ids)[:, None, None], image[r][None], slots)
    received = exchange(slots, ("x", "z"))
    sources = (entry(tile_firsts, place) + jnp.arange(16, dtype=jnp.int32)) % 32
    mine = received[sources].reshape(SPAN, 1024)
    own_image = spread(mine, "y")
    other_image = shift(own_image, "c", 1)

    rows = entry(tile_counts, place) * 8
    where = jnp.stack([x, z, y, c, image_offsets[0], rows]).astype(jnp.int32)
    cosine, sine = rope_tables()
    sequence, key, value = prepare(
        where, text, (own_image, other_image), keyval, attn_gain.reshape(8, 1024), cosine, sine
    )
    return attention(sequence, query_w, key, value, cosine, sine)[None]


def solution(mesh):
    fine = Mesh(mesh.devices.reshape(NX, NZ, NY, NC), ("x", "z", "y", "c"))
    dp, tensor = ("x", "z"), ("y", "c")
    in_specs = (
        P(None, dp, None, tensor), P(), P(), P(dp, None, tensor), P(dp, None, tensor), P(),
        P(dp, tensor), P(dp, None, tensor), P(), P(dp),
    )
    return jax.shard_map(
        step, mesh=fine, in_specs=in_specs, out_specs=P(dp, None, tensor), check_vma=False
    )
```

time: 229 us -> 230 us (level)
  waiting for transfers between devices: 109 us -> 95.8 us
  Pallas kernels: 18 us -> 25.5 us
  starting transfers between devices: 56.4 us -> 63 us
    all_to_all x6 -> x4, waiting for transfers between devices: 63.2 us -> 33.4 us  [exchange(): return lax.all_to_all(array, axis, 0, 0, tiled=True)]
    ppermute x13 -> x22, starting transfers between devices: 22.9 us -> 37.4 us  [shift(): lax.ppermute(array, axis, [(i, (i + by) % size) for i in range(size)])]
    ppermute x13 -> x22, waiting for transfers between devices: 36.9 us -> 51.1 us  [shift(): lax.ppermute(array, axis, [(i, (i + by) % size) for i in range(size)])]
    all_to_all x6 -> x4, starting transfers between devices: 32.1 us -> 21.9 us  [exchange(): return lax.all_to_all(array, axis, 0, 0, tiled=True)]
    pallas_call x1, Pallas kernels: 4.91 us -> 10.7 us  [attention(): pl.pallas_call(kernel, out_shape=jax.ShapeDtypeStruct((SEQ, 512), jnp.bfl...]
    ppermute x2 -> x3, waiting for transfers between devices: 0.01 us -> 2.65 us  [flip_x(): return lax.ppermute(array, 'x', [(i, i ^ flip) for i in range(NX)])]
    unnamed x23 -> x39, local copies, waits for them, and re-layouts: 5.17 us -> 4.59 us
  transfers between devices with their start and end apart: 23 -> 31, of which waited for: 11 -> 12; matrix products, arithmetic and copies ran while one was open for 11% -> 11% of each run, Pallas kernels for 6% -> 6%
where the time goes in v5:
time: 230 us; the launch traced here: 228 us
  waiting for transfers between devices  95.8 us (42%)
  starting transfers between devices  63 us (27%)
  Pallas kernels  25.5 us (11%)
  between operations  15.1 us (7%)
  local copies, waits for them, and re-layouts  14.3 us (6%)
  other arithmetic  10.9 us (5%)
  matrix products  3.31 us (1%)
    ppermute x22, waiting for transfers between devices, shift(): lax.ppermute(array, axis, [(i, (i + by) % size) for i in range(size)])  51.1 us
    ppermute x22, starting transfers between devices, shift(): lax.ppermute(array, axis, [(i, (i + by) % size) for i in range(size)])  37.4 us
    all_to_all x4, waiting for transfers between devices, exchange(): return lax.all_to_all(array, axis, 0, 0, tiled=True)  33.4 us
    all_to_all x4, starting transfers between devices, exchange(): return lax.all_to_all(array, axis, 0, 0, tiled=True)  21.9 us
    pallas_call x1, Pallas kernels, prepare(): pl.pallas_call(kernel, out_shape=[jax.ShapeDtypeStruct((8, SEQ, 1024), jn...  12.4 us
    pallas_call x1, Pallas kernels, attention(): pl.pallas_call(kernel, out_shape=jax.ShapeDtypeStruct((SEQ, 512), jnp.bfl...  10.7 us
    all_gather x1, waiting for transfers between devices, step(): proj_all = lax.all_gather(proj_weight, 'z', axis=0, tiled=True)  7.25 us
    eq x4, other arithmetic, step(): owners[r] == sample_ids  4.74 us
  transfers between devices with their start and end apart: 31, of which 12 were waited for; matrix products, arithmetic and copies ran while one was open for 11% of the time, Pallas kernels for 6%

profile of v5, /device:TPU:1, one launch (start us, length us, event | category | flops | bytes accessed | tf_op | source)
XLA Modules:
  0.0 227.9 jit_solution(8625251926845676800)
XLA Ops:
  6.5 0.7 all-gather.3.cloned.1.call-update
  7.3 0.7 all-gather.5.cloned.1.call-update
  8.0 0.9 copy.41
  8.9 1.1 broadcast_in_dim.131
  10.1 6.7 %all-to-all-start = ((bf16[8,64,2,400]{3,1,2,0:T(8,128)(2,1)}), bf16[8,64,2,400]{3,1,2,0:T(8,128)(2,1)S(1)}, u32[]{:S(2)}, u32[]{:S(2)}) async-start(bf16[8,64,2,400]{3,1,2,0:T(8,128)(2,1)} %broadcast_in_dim.131), calls=%async_computation | async-start | bytes 2097152 | tf_op jit(solution)/shard_map/all_to_all | solution.py:29
  17.0 14.7 %all-to-all-done = bf16[8,64,2,400]{3,1,2,0:T(8,128)(2,1)S(1)} async-done(((bf16[8,64,2,400]{3,1,2,0:T(8,128)(2,1)}), bf16[8,64,2,400]{3,1,2,0:T(8,128)(2,1)S(1)}, u32[]{:S(2)}, u32[]{:S(2)}) %all-to-all-start) | async-done | bytes 819232 | tf_op jit(solution)/shard_map/all_to_all | solution.py:29
  31.7 0.3 convert_reduce_fusion
  32.0 0.5 fusion.5
  32.5 1.5 fusion.8
  34.0 3.5 %all-to-all-start.1 = ((bf16[4,2,64,2,400]{4,2,3,1,0:T(8,128)(2,1)}), bf16[4,2,64,2,400]{4,2,3,1,0:T(8,128)(2,1)S(1)}, u32[]{:S(2)}, u32[]{:S(2)}) async-start(bf16[4,2,64,2,400]{4,2,3,1,0:T(8,128)(2,1)} %bitcast.11), calls=%async_computation.1 | async-start | bytes 2097152 | tf_op jit(solution)/shard_map/all_to_all | solution.py:29
  37.9 0.2 convert_reduce_fusion.1
  38.1 0.6 fusion.24
  38.7 1.1 iota_compare_fusion
  39.8 1.1 iota_compare_fusion.2
  41.0 10.7 %all-to-all-done.1 = bf16[4,2,64,2,400]{4,2,3,1,0:T(8,128)(2,1)S(1)} async-done(((bf16[4,2,64,2,400]{4,2,3,1,0:T(8,128)(2,1)}), bf16[4,2,64,2,400]{4,2,3,1,0:T(8,128)(2,1)S(1)}, u32[]{:S(2)}, u32[]{:S(2)}) %all-to-all-start.1) | async-done | bytes 819232 | tf_op jit(solution)/shard_map/all_to_all | solution.py:29
  51.7 7.3 %all-gather.3.cloned.1.call-done = bf16[800,2,1024]{2,1,0:T(2,128)(2,1)} async-done(((bf16[100,2,1024]{2,1,0:T(2,128)(2,1)}), bf16[800,2,1024]{2,1,0:T(2,128)(2,1)}) %all-gather.3.cloned.1.call-update) | async-done | bytes 3276816 | tf_op jit(solution)/shard_map/all_gather | solution.py:258
  58.9 3.3 %fusion.12 = bf16[4,64,1024]{2,1,0:T(8,128)(2,1)S(1)} fusion(bf16[4,2,64,2,400]{4,2,3,1,0:T(8,128)(2,1)S(1)} %all-to-all-done.1, bf16[2,400,2,1024,1]{3,2,1,0,4:T(2,128)(2,1)} %bitcast.68), kind=kOutput, calls=%fused_computation.13 | convolution fusion | flops 839122944 | bytes 4620288 | tf_op jit(solution)/shard_map/sctmf,cfmo->sto/dot_general | solution.py:233
  62.3 2.8 %collective-permute-start.10 = (bf16[64,1024]{1,0:T(8,128)(2,1)S(1)}, bf16[64,1024]{1,0:T(8,128)(2,1)S(1)}, u32[]{:S(2)}, u32[]{:S(2)}) collective-permute-start(bf16[64,1024]{1,0:T(8,128)(2,1)S(1)} %get-tuple-element.15), channel_id=1, source_target_pairs={{0,128},{64,192},{128,0},{192,64},{1,129},{65,193},{129,1},{193,65... | collective-permute-start | bytes 393224 | tf_op jit(solution)/shard_map/ppermute | solution.py:25
  65.1 0.9 collective-permute-start.11
  66.0 1.2 iota_compare_fusion.4
  67.2 1.3 iota_compare_fusion.6
  68.5 2.6 %collective-permute-done.11 = bf16[64,1024]{1,0:T(8,128)(2,1)S(1)} collective-permute-done((bf16[64,1024]{1,0:T(8,128)(2,1)S(1)}, bf16[64,1024]{1,0:T(8,128)(2,1)S(1)}, u32[]{:S(2)}, u32[]{:S(2)}) %collective-permute-start.11) | collective-permute-done | bytes 131104 | tf_op jit(solution)/shard_map/ppermute | solution.py:25
  71.2 1.2 select_select_fusion
  72.4 7.5 %all-to-all-start.2 = ((bf16[32,8,1024]{2,1,0:T(8,128)(2,1)}), bf16[32,8,1024]{2,1,0:T(8,128)(2,1)S(1)}, u32[]{:S(2)}, u32[]{:S(2)}) async-start(bf16[32,8,1024]{2,1,0:T(8,128)(2,1)} %select_select_fusion), calls=%async_computation.2 | async-start | bytes 1048576 | tf_op jit(solution)/shard_map/all_to_all | solution.py:29
  80.0 1.3 collective-permute-start.13
  81.3 1.4 collective-permute-start.14
  82.7 20.4 %collective-permute-done.13.refs_1_ = bf16[256,256]{1,0:T(8,128)(2,1)S(1)} collective-permute-done((bf16[256,256]{1,0:T(8,128)(2,1)S(1)}, bf16[256,256]{1,0:T(8,128)(2,1)S(1)}, u32[]{:S(2)}, u32[]{:S(2)}) %collective-permute-start.13) | collective-permute-done | bytes 131104 | tf_op jit(solution)/shard_map/ppermute | solution.py:21
  103.1 2.7 %collective-permute-start.16 = (bf16[256,256]{1,0:T(8,128)(2,1)S(1)}, bf16[256,256]{1,0:T(8,128)(2,1)S(1)}, u32[]{:S(2)}, u32[]{:S(2)}) collective-permute-start(bf16[256,256]{1,0:T(8,128)(2,1)S(1)} %collective-permute-done.14.refs_2_), channel_id=1, source_target_pairs={{0,56},{8,0},{16,8},{24,16},{32,24},{40,32},{48,40},{56,48},{1,57}... | collective-permute-start | bytes 393224 | tf_op jit(solution)/shard_map/ppermute | solution.py:21
  105.8 1.2 collective-permute-start.1
  107.0 1.5 collective-permute-start.3
  108.5 2.7 %collective-permute-start = (bf16[384,1024]{1,0:T(8,128)(2,1)S(1)}, bf16[384,1024]{1,0:T(8,128)(2,1)S(1)}, u32[]{:S(2)}, u32[]{:S(2)}) collective-permute-start(bf16[384,1024]{1,0:T(8,128)(2,1)S(1)} %bitcast.59), channel_id=1, source_target_pairs={{0,1},{1,0},{2,3},{3,2},{4,5},{5,4},{6,7},{7,6},{8,9},{9,8},{10,11... | collective-permute-start | bytes 2359304 | tf_op jit(solution)/shard_map/ppermute | solution.py:21
  111.1 2.7 %collective-permute-start.18 = (bf16[256,256]{1,0:T(8,128)(2,1)S(1)}, bf16[256,256]{1,0:T(8,128)(2,1)S(1)}, u32[]{:S(2)}, u32[]{:S(2)}) collective-permute-start(bf16[256,256]{1,0:T(8,128)(2,1)S(1)} %collective-permute-done.16.refs_4_), channel_id=1, source_target_pairs={{0,56},{8,0},{16,8},{24,16},{32,24},{40,32},{48,40},{56,48},{1,57}... | collective-permute-start | bytes 393224 | tf_op jit(solution)/shard_map/ppermute | solution.py:21
  113.8 0.7 fusion.20
  114.5 0.6 fusion.22
  115.1 2.2 collective-permute-done.17.refs_5_
  117.5 2.7 %collective-permute-start.20 = (bf16[128,256]{1,0:T(8,128)(2,1)S(1)}, bf16[128,256]{1,0:T(8,128)(2,1)}, u32[]{:S(2)}, u32[]{:S(2)}) collective-permute-start(bf16[128,256]{1,0:T(8,128)(2,1)S(1)} %slice.109), channel_id=1, source_target_pairs={{0,56},{8,0},{16,8},{24,16},{32,24},{40,32},{48,40},{56,48},{1,57}... | collective-permute-start | bytes 196616 | tf_op jit(solution)/shard_map/ppermute | solution.py:21
  120.2 3.6 %collective-permute-done.19.refs_7_ = bf16[128,256]{1,0:T(8,128)(2,1)} collective-permute-done((bf16[128,256]{1,0:T(8,128)(2,1)S(1)}, bf16[128,256]{1,0:T(8,128)(2,1)}, u32[]{:S(2)}, u32[]{:S(2)}) %collective-permute-start.19) | collective-permute-done | bytes 65568 | tf_op jit(solution)/shard_map/ppermute | solution.py:21
  123.8 2.4 %pack.1.refs_12_ = bf16[2048,256]{1,0:T(8,128)(2,1)} custom-call(bf16[256,256]{1,0:T(8,128)(2,1)} %bitcast.64, bf16[256,256]{1,0:T(8,128)(2,1)} %copy-done.10, bf16[256,256]{1,0:T(8,128)(2,1)} %copy-done.11, bf16[256,256]{1,0:T(8,128)(2,1)} %copy-done.12, bf16[256,256]{1,0:T(8,128)(2,1)} %copy-done.13, bf16[256,256]{1,0:T(8,128)(2,1)} %copy-done.8, ...), custom_call_target="tpu_custom_call" | custom-call | tf_op jit(solution)/shard_map/pack/pallas_call | solution.py:85
  126.1 0.6 collective-permute-start.21
  126.8 2.0 collective-permute-start.22
  128.8 0.6 gather_fusion
  129.4 1.1 broadcast_in_dim.149
  130.5 4.2 %all-to-all-start.3 = ((bf16[4,128,1024]{2,1,0:T(8,128)(2,1)}), bf16[4,128,1024]{2,1,0:T(8,128)(2,1)}, u32[]{:S(2)}, u32[]{:S(2)}) async-start(bf16[4,128,1024]{2,1,0:T(8,128)(2,1)} %broadcast_in_dim.149), calls=%async_computation.3 | async-start | bytes 2097152 | tf_op jit(solution)/shard_map/all_to_all | solution.py:29
  134.8 1.5 collective-permute-start.5
  136.3 1.0 slice.99
  137.3 1.3 collective-permute-start.7
  138.7 7.9 %all-to-all-done.3.refs_10_ = bf16[4,128,1024]{2,1,0:T(8,128)(2,1)} async-done(((bf16[4,128,1024]{2,1,0:T(8,128)(2,1)}), bf16[4,128,1024]{2,1,0:T(8,128)(2,1)}, u32[]{:S(2)}, u32[]{:S(2)}) %all-to-all-start.3) | async-done | bytes 1048608 | tf_op jit(solution)/shard_map/all_to_all | solution.py:29
  146.6 7.8 %collective-permute-start.12 = (bf16[4,128,1024]{2,1,0:T(8,128)(2,1)}, bf16[4,128,1024]{2,1,0:T(8,128)(2,1)}, u32[]{:S(2)}, u32[]{:S(2)}) collective-permute-start(bf16[4,128,1024]{2,1,0:T(8,128)(2,1)} %all-to-all-done.3.refs_10_), channel_id=1, source_target_pairs={{0,1},{1,0},{2,3},{3,2},{4,5},{5,4},{6,7},{7,6},{8,9},{9,8},{10,11... | collective-permute-start | bytes 3145736 | tf_op jit(solution)/shard_map/ppermute | solution.py:21
  154.4 1.0 collective-permute-done.5.refs_6_
  155.4 3.5 %collective-permute-start.6 = (bf16[192,1024]{1,0:T(8,128)(2,1)S(1)}, bf16[192,1024]{1,0:T(8,128)(2,1)S(1)}, u32[]{:S(2)}, u32[]{:S(2)}) collective-permute-start(bf16[192,1024]{1,0:T(8,128)(2,1)S(1)} %collective-permute-done.5.refs_6_), channel_id=1, source_target_pairs={{0,1},{1,0},{2,3},{3,2},{4,5},{5,4},{6,7},{7,6},{8,9},{9,8},{10,11... | collective-permute-start | bytes 1179656 | tf_op jit(solution)/shard_map/ppermute | solution.py:21
  159.0 15.4 %collective-permute-done.21.refs_13_ = bf16[2048,256]{1,0:T(8,128)(2,1)} collective-permute-done((bf16[2048,256]{1,0:T(8,128)(2,1)}, bf16[2048,256]{1,0:T(8,128)(2,1)}, u32[]{:S(2)}, u32[]{:S(2)}) %collective-permute-start.21) | collective-permute-done | bytes 1048608 | tf_op jit(solution)/shard_map/ppermute | solution.py:21
  174.4 1.6 collective-permute-start.2
  176.0 1.9 slice.110
  177.9 1.9 slice.111
  179.8 0.7 copy-done.3
  180.5 0.8 copy-done.5
  181.3 2.7 %collective-permute-start.24 = (bf16[1024,256]{1,0:T(8,128)(2,1)}, bf16[1024,256]{1,0:T(8,128)(2,1)}, u32[]{:S(2)}, u32[]{:S(2)}) collective-permute-start(bf16[1024,256]{1,0:T(8,128)(2,1)} %slice.111), channel_id=1, source_target_pairs={{0,192},{64,0},{128,64},{192,128},{1,193},{65,1},{129,65},{193,129... | collective-permute-start | bytes 1572872 | tf_op jit(solution)/shard_map/ppermute | solution.py:21
  185.3 0.8 fusion.18
  186.3 8.6 %collective-permute-done.23.refs_15_ = bf16[1024,256]{1,0:T(8,128)(2,1)S(1)} collective-permute-done((bf16[1024,256]{1,0:T(8,128)(2,1)}, bf16[1024,256]{1,0:T(8,128)(2,1)S(1)}, u32[]{:S(2)}, u32[]{:S(2)}) %collective-permute-start.23) | collective-permute-done | bytes 524320 | tf_op jit(solution)/shard_map/ppermute | solution.py:21
  194.9 1.0 copy-done.2
  195.9 1.0 copy-done.4
  196.9 1.0 copy-done.6
  197.9 12.4 %prepare.1 = (bf16[8,384,1024]{2,1,0:T(8,128)(2,1)}, bf16[384,128]{1,0:T(8,128)(2,1)S(1)}, bf16[384,128]{1,0:T(8,128)(2,1)S(1)}) custom-call(s32[6]{0:T(128)S(1)} %stack.23.where_ref, bf16[384,1024]{1,0:T(8,128)(2,1)S(1)} %bitcast.60, bf16[384,1024]{1,0:T(8,128)(2,1)S(1)} %collective-permute-done.refs_1_, ...), custom_call_target="tpu_custom_call" | custom-call | tf_op jit(solution)/shard_map/prepare/pallas_call | solution.py:158
  210.3 10.7 %attention.1 = bf16[384,512]{1,0:T(8,128)(2,1)} custom-call(bf16[8,384,1024]{2,1,0:T(8,128)(2,1)} %get-tuple-element.8.a_ref, bf16[8192,512]{1,0:T(8,128)(2,1)} %all-gather.5.cloned.1.call-done.w_hbm, bf16[384,128]{1,0:T(8,128)(2,1)S(1)} %get-tuple-element.9.key_ref, bf16[384,128]{1,0:T(8,128)(2,1)S(1)} %get-tuple-element.10.value_ref, ...), custom_call_target="tpu_custom_call" | custom-call | tf_op jit(solution)/shard_map/attention/pallas_call | solution.py:209
  (84 shorter events, 1.5 us)
Async XLA Ops:
  6.5 10.2 %copy-start.16 = (f32[2,3200]{1,0:T(2,128)S(1)}, f32[2,3200]{1,0:T(2,128)}, u32[]{:S(2)}) copy-start(f32[2,3200]{1,0:T(2,128)} %param.11) | copy-start | bytes 76804
  6.5 10.3 %copy-start.17 = (f32[2,3200]{1,0:T(2,128)S(1)}, f32[2,3200]{1,0:T(2,128)}, u32[]{:S(2)}) copy-start(f32[2,3200]{1,0:T(2,128)} %param.12) | copy-start | bytes 76804
  6.5 52.4 %all-gather.3.cloned.1.call-start = ((), (), s32[]{:S(2)}) async-start(), calls=%async_computation.4 | async-start | bytes 3686400 | tf_op jit(solution)/shard_map/all_gather | solution.py:258
  7.3 203.1 %all-gather.5.cloned.1.call-start = ((), (), s32[]{:S(2)}) async-start(), calls=%async_computation.5 | async-start | bytes 8650752 | tf_op jit(solution)/shard_map/all_gather | solution.py:259
  10.1 21.7 %all-to-all-start = ((bf16[8,64,2,400]{3,1,2,0:T(8,128)(2,1)}), bf16[8,64,2,400]{3,1,2,0:T(8,128)(2,1)S(1)}, u32[]{:S(2)}, u32[]{:S(2)}) async-start(bf16[8,64,2,400]{3,1,2,0:T(8,128)(2,1)} %broadcast_in_dim.131), calls=%async_computation | async-start | bytes 2097152 | tf_op jit(solution)/shard_map/all_to_all | solution.py:29
  32.5 5.1 %copy-start.18 = (s32[32]{0:T(128)S(1)}, s32[32]{0:T(128)}, u32[]{:S(2)}) copy-start(s32[32]{0:T(128)} %param.18) | copy-start | bytes 388
  34.0 17.6 %all-to-all-start.1 = ((bf16[4,2,64,2,400]{4,2,3,1,0:T(8,128)(2,1)}), bf16[4,2,64,2,400]{4,2,3,1,0:T(8,128)(2,1)S(1)}, u32[]{:S(2)}, u32[]{:S(2)}) async-start(bf16[4,2,64,2,400]{4,2,3,1,0:T(8,128)(2,1)} %bitcast.11), calls=%async_computation.1 | async-start | bytes 2097152 | tf_op jit(solution)/shard_map/all_to_all | solution.py:29
  62.2 17.7 %copy-start.14 = (bf16[256,2,128]{2,1,0:T(2,128)(2,1)S(1)}, bf16[256,2,128]{2,1,0:T(2,128)(2,1)}, u32[]{:S(2)}) copy-start(bf16[256,2,128]{2,1,0:T(2,128)(2,1)} %param.17) | copy-start | bytes 393220
  62.3 43.5 %copy-start = (bf16[1,384,1024]{2,1,0:T(8,128)(2,1)S(1)}, bf16[1,384,1024]{2,1,0:T(8,128)(2,1)}, u32[]{:S(2)}) copy-start(bf16[1,384,1024]{2,1,0:T(8,128)(2,1)} %param.14) | copy-start | bytes 2359300
  62.3 6.2 %collective-permute-start.10 = (bf16[64,1024]{1,0:T(8,128)(2,1)S(1)}, bf16[64,1024]{1,0:T(8,128)(2,1)S(1)}, u32[]{:S(2)}, u32[]{:S(2)}) collective-permute-start(bf16[64,1024]{1,0:T(8,128)(2,1)S(1)} %get-tuple-element.15), channel_id=1, source_target_pairs={{0,128},{64,192},{128,0},{192,64},{1,129},{65,193},{129,1},{193,65... | collective-permute-start | bytes 393224 | tf_op jit(solution)/shard_map/ppermute | solution.py:25
  65.1 5.9 %collective-permute-start.11 = (bf16[64,1024]{1,0:T(8,128)(2,1)S(1)}, bf16[64,1024]{1,0:T(8,128)(2,1)S(1)}, u32[]{:S(2)}, u32[]{:S(2)}) collective-permute-start(bf16[64,1024]{1,0:T(8,128)(2,1)S(1)} %get-tuple-element.14), channel_id=1, source_target_pairs={{0,192},{64,128},{128,64},{192,0},{1,193},{65,129},{129,65},{193,1... | collective-permute-start | bytes 393224 | tf_op jit(solution)/shard_map/ppermute | solution.py:25
  66.0 5.1 %collective-permute-start.9 = (bf16[64,1024]{1,0:T(8,128)(2,1)S(1)}, bf16[64,1024]{1,0:T(8,128)(2,1)S(1)}, u32[]{:S(2)}, u32[]{:S(2)}) collective-permute-start(bf16[64,1024]{1,0:T(8,128)(2,1)S(1)} %get-tuple-element.13), channel_id=1, source_target_pairs={{0,64},{64,0},{128,192},{192,128},{1,65},{65,1},{129,193},{193,129... | collective-permute-start | bytes 393224 | tf_op jit(solution)/shard_map/ppermute | solution.py:25
  72.4 56.4 %all-to-all-start.2 = ((bf16[32,8,1024]{2,1,0:T(8,128)(2,1)}), bf16[32,8,1024]{2,1,0:T(8,128)(2,1)S(1)}, u32[]{:S(2)}, u32[]{:S(2)}) async-start(bf16[32,8,1024]{2,1,0:T(8,128)(2,1)} %select_select_fusion), calls=%async_computation.2 | async-start | bytes 1048576 | tf_op jit(solution)/shard_map/all_to_all | solution.py:29
  80.0 43.8 %copy-start.7 = (bf16[32,8,2,128]{3,1,2,0:T(8,128)(2,1)}, bf16[32,8,2,128]{3,1,2,0:T(8,128)(2,1)S(1)}, u32[]{:S(2)}) copy-start(bf16[32,8,2,128]{3,1,2,0:T(8,128)(2,1)S(1)} %copy.65) | copy-start | bytes 393220
  80.0 23.1 %collective-permute-start.13 = (bf16[256,256]{1,0:T(8,128)(2,1)S(1)}, bf16[256,256]{1,0:T(8,128)(2,1)S(1)}, u32[]{:S(2)}, u32[]{:S(2)}) collective-permute-start(bf16[256,256]{1,0:T(8,128)(2,1)S(1)} %bitcast.62), channel_id=1, source_target_pairs={{0,8},{8,16},{16,24},{24,32},{32,40},{40,48},{48,56},{56,0},{1,9},... | collective-permute-start | bytes 393224 | tf_op jit(solution)/shard_map/ppermute | solution.py:21
  81.3 21.8 %collective-permute-start.14 = (bf16[256,256]{1,0:T(8,128)(2,1)S(1)}, bf16[256,256]{1,0:T(8,128)(2,1)S(1)}, u32[]{:S(2)}, u32[]{:S(2)}) collective-permute-start(bf16[256,256]{1,0:T(8,128)(2,1)S(1)} %bitcast.63), channel_id=1, source_target_pairs={{0,56},{8,0},{16,8},{24,16},{32,24},{40,32},{48,40},{56,48},{1,57}... | collective-permute-start | bytes 393224 | tf_op jit(solution)/shard_map/ppermute | solution.py:21
  103.1 20.7 %copy-start.10 = (bf16[256,256]{1,0:T(8,128)(2,1)}, bf16[256,256]{1,0:T(8,128)(2,1)S(1)}, u32[]{:S(2)}) copy-start(bf16[256,256]{1,0:T(8,128)(2,1)S(1)} %collective-permute-done.13.refs_1_) | copy-start | bytes 393220
  103.1 8.0 %collective-permute-start.15 = (bf16[256,256]{1,0:T(8,128)(2,1)S(1)}, bf16[256,256]{1,0:T(8,128)(2,1)S(1)}, u32[]{:S(2)}, u32[]{:S(2)}) collective-permute-start(bf16[256,256]{1,0:T(8,128)(2,1)S(1)} %collective-permute-done.13.refs_1_), channel_id=1, source_target_pairs={{0,8},{8,16},{16,24},{24,32},{32,40},{40,48},{48,56},{56,0},{1,9},... | collective-permute-start | bytes 393224 | tf_op jit(solution)/shard_map/ppermute | solution.py:21
  103.1 20.6 %copy-start.11 = (bf16[256,256]{1,0:T(8,128)(2,1)}, bf16[256,256]{1,0:T(8,128)(2,1)S(1)}, u32[]{:S(2)}) copy-start(bf16[256,256]{1,0:T(8,128)(2,1)S(1)} %collective-permute-done.14.refs_2_) | copy-start | bytes 393220
  103.1 8.0 %collective-permute-start.16 = (bf16[256,256]{1,0:T(8,128)(2,1)S(1)}, bf16[256,256]{1,0:T(8,128)(2,1)S(1)}, u32[]{:S(2)}, u32[]{:S(2)}) collective-permute-start(bf16[256,256]{1,0:T(8,128)(2,1)S(1)} %collective-permute-done.14.refs_2_), channel_id=1, source_target_pairs={{0,56},{8,0},{16,8},{24,16},{32,24},{40,32},{48,40},{56,48},{1,57}... | collective-permute-start | bytes 393224 | tf_op jit(solution)/shard_map/ppermute | solution.py:21
  105.8 29.0 %collective-permute-start.1 = (bf16[384,1024]{1,0:T(8,128)(2,1)S(1)}, bf16[384,1024]{1,0:T(8,128)(2,1)S(1)}, u32[]{:S(2)}, u32[]{:S(2)}) collective-permute-start(bf16[384,1024]{1,0:T(8,128)(2,1)S(1)} %bitcast.57), channel_id=1, source_target_pairs={{0,2},{2,4},{4,6},{6,0},{1,3},{3,5},{5,7},{7,1},{8,10},{10,12},{12... | collective-permute-start | bytes 2359304 | tf_op jit(solution)/shard_map/ppermute | solution.py:21
  107.0 29.3 %collective-permute-start.3 = (bf16[384,1024]{1,0:T(8,128)(2,1)S(1)}, bf16[384,1024]{1,0:T(8,128)(2,1)}, u32[]{:S(2)}, u32[]{:S(2)}) collective-permute-start(bf16[384,1024]{1,0:T(8,128)(2,1)S(1)} %bitcast.58), channel_id=1, source_target_pairs={{0,6},{2,0},{4,2},{6,4},{1,7},{3,1},{5,3},{7,5},{8,14},{10,8},{12,... | collective-permute-start | bytes 2359304 | tf_op jit(solution)/shard_map/ppermute | solution.py:21
  108.5 30.2 %collective-permute-start = (bf16[384,1024]{1,0:T(8,128)(2,1)S(1)}, bf16[384,1024]{1,0:T(8,128)(2,1)S(1)}, u32[]{:S(2)}, u32[]{:S(2)}) collective-permute-start(bf16[384,1024]{1,0:T(8,128)(2,1)S(1)} %bitcast.59), channel_id=1, source_target_pairs={{0,1},{1,0},{2,3},{3,2},{4,5},{5,4},{6,7},{7,6},{8,9},{9,8},{10,11... | collective-permute-start | bytes 2359304 | tf_op jit(solution)/shard_map/ppermute | solution.py:21
  111.1 6.3 %copy-start.12 = (bf16[256,256]{1,0:T(8,128)(2,1)}, bf16[256,256]{1,0:T(8,128)(2,1)S(1)}, u32[]{:S(2)}) copy-start(bf16[256,256]{1,0:T(8,128)(2,1)S(1)} %collective-permute-done.15.refs_3_) | copy-start | bytes 393220
  111.1 6.2 %collective-permute-start.17 = (bf16[256,256]{1,0:T(8,128)(2,1)S(1)}, bf16[256,256]{1,0:T(8,128)(2,1)S(1)}, u32[]{:S(2)}, u32[]{:S(2)}) collective-permute-start(bf16[256,256]{1,0:T(8,128)(2,1)S(1)} %collective-permute-done.15.refs_3_), channel_id=1, source_target_pairs={{0,8},{8,16},{16,24},{24,32},{32,40},{40,48},{48,56},{56,0},{1,9},... | collective-permute-start | bytes 393224 | tf_op jit(solution)/shard_map/ppermute | solution.py:21
  111.1 6.3 %copy-start.13 = (bf16[256,256]{1,0:T(8,128)(2,1)}, bf16[256,256]{1,0:T(8,128)(2,1)S(1)}, u32[]{:S(2)}) copy-start(bf16[256,256]{1,0:T(8,128)(2,1)S(1)} %collective-permute-done.16.refs_4_) | copy-start | bytes 393220
  111.1 6.3 %collective-permute-start.18 = (bf16[256,256]{1,0:T(8,128)(2,1)S(1)}, bf16[256,256]{1,0:T(8,128)(2,1)S(1)}, u32[]{:S(2)}, u32[]{:S(2)}) collective-permute-start(bf16[256,256]{1,0:T(8,128)(2,1)S(1)} %collective-permute-done.16.refs_4_), channel_id=1, source_target_pairs={{0,56},{8,0},{16,8},{24,16},{32,24},{40,32},{48,40},{56,48},{1,57}... | collective-permute-start | bytes 393224 | tf_op jit(solution)/shard_map/ppermute | solution.py:21
  117.3 6.4 %copy-start.8 = (bf16[256,256]{1,0:T(8,128)(2,1)}, bf16[256,256]{1,0:T(8,128)(2,1)S(1)}, u32[]{:S(2)}) copy-start(bf16[256,256]{1,0:T(8,128)(2,1)S(1)} %collective-permute-done.17.refs_5_) | copy-start | bytes 393220
  117.3 6.4 %collective-permute-start.19 = (bf16[128,256]{1,0:T(8,128)(2,1)S(1)}, bf16[128,256]{1,0:T(8,128)(2,1)}, u32[]{:S(2)}, u32[]{:S(2)}) collective-permute-start(bf16[128,256]{1,0:T(8,128)(2,1)S(1)} %slice.108), channel_id=1, source_target_pairs={{0,8},{8,16},{16,24},{24,32},{32,40},{40,48},{48,56},{56,0},{1,9},... | collective-permute-start | bytes 196616 | tf_op jit(solution)/shard_map/ppermute | solution.py:21
  117.4 6.3 %copy-start.9 = (bf16[256,256]{1,0:T(8,128)(2,1)}, bf16[256,256]{1,0:T(8,128)(2,1)S(1)}, u32[]{:S(2)}) copy-start(bf16[256,256]{1,0:T(8,128)(2,1)S(1)} %collective-permute-done.18.refs_6_) | copy-start | bytes 393220
  117.5 6.3 %collective-permute-start.20 = (bf16[128,256]{1,0:T(8,128)(2,1)S(1)}, bf16[128,256]{1,0:T(8,128)(2,1)}, u32[]{:S(2)}, u32[]{:S(2)}) collective-permute-start(bf16[128,256]{1,0:T(8,128)(2,1)S(1)} %slice.109), channel_id=1, source_target_pairs={{0,56},{8,0},{16,8},{24,16},{32,24},{40,32},{48,40},{56,48},{1,57}... | collective-permute-start | bytes 196616 | tf_op jit(solution)/shard_map/ppermute | solution.py:21
  126.1 48.2 %collective-permute-start.21 = (bf16[2048,256]{1,0:T(8,128)(2,1)}, bf16[2048,256]{1,0:T(8,128)(2,1)}, u32[]{:S(2)}, u32[]{:S(2)}) collective-permute-start(bf16[2048,256]{1,0:T(8,128)(2,1)} %pack.1.refs_12_), channel_id=1, source_target_pairs={{0,64},{64,128},{128,192},{192,0},{1,65},{65,129},{129,193},{193,1... | collective-permute-start | bytes 3145736 | tf_op jit(solution)/shard_map/ppermute | solution.py:21
  126.8 49.2 %collective-permute-start.22 = (bf16[2048,256]{1,0:T(8,128)(2,1)}, bf16[2048,256]{1,0:T(8,128)(2,1)}, u32[]{:S(2)}, u32[]{:S(2)}) collective-permute-start(bf16[2048,256]{1,0:T(8,128)(2,1)} %pack.1.refs_12_), channel_id=1, source_target_pairs={{0,192},{64,0},{128,64},{192,128},{1,193},{65,1},{129,65},{193,129... | collective-permute-start | bytes 3145736 | tf_op jit(solution)/shard_map/ppermute | solution.py:21
  130.5 16.1 %all-to-all-start.3 = ((bf16[4,128,1024]{2,1,0:T(8,128)(2,1)}), bf16[4,128,1024]{2,1,0:T(8,128)(2,1)}, u32[]{:S(2)}, u32[]{:S(2)}) async-start(bf16[4,128,1024]{2,1,0:T(8,128)(2,1)} %broadcast_in_dim.149), calls=%async_computation.3 | async-start | bytes 2097152 | tf_op jit(solution)/shard_map/all_to_all | solution.py:29
  134.8 20.6 %collective-permute-start.5 = (bf16[192,1024]{1,0:T(8,128)(2,1)S(1)}, bf16[192,1024]{1,0:T(8,128)(2,1)S(1)}, u32[]{:S(2)}, u32[]{:S(2)}) collective-permute-start(bf16[192,1024]{1,0:T(8,128)(2,1)S(1)} %slice.98), channel_id=1, source_target_pairs={{0,2},{2,4},{4,6},{6,0},{1,3},{3,5},{5,7},{7,1},{8,10},{10,12},{12... | collective-permute-start | bytes 1179656 | tf_op jit(solution)/shard_map/ppermute | solution.py:21
  137.3 21.6 %collective-permute-start.7 = (bf16[192,1024]{1,0:T(8,128)(2,1)S(1)}, bf16[192,1024]{1,0:T(8,128)(2,1)}, u32[]{:S(2)}, u32[]{:S(2)}) collective-permute-start(bf16[192,1024]{1,0:T(8,128)(2,1)S(1)} %slice.99), channel_id=1, source_target_pairs={{0,6},{2,0},{4,2},{6,4},{1,7},{3,1},{5,3},{7,5},{8,14},{10,8},{12,... | collective-permute-start | bytes 1179656 | tf_op jit(solution)/shard_map/ppermute | solution.py:21
  146.6 48.3 %collective-permute-start.12 = (bf16[4,128,1024]{2,1,0:T(8,128)(2,1)}, bf16[4,128,1024]{2,1,0:T(8,128)(2,1)}, u32[]{:S(2)}, u32[]{:S(2)}) collective-permute-start(bf16[4,128,1024]{2,1,0:T(8,128)(2,1)} %all-to-all-done.3.refs_10_), channel_id=1, source_target_pairs={{0,1},{1,0},{2,3},{3,2},{4,5},{5,4},{6,7},{7,6},{8,9},{9,8},{10,11... | collective-permute-start | bytes 3145736 | tf_op jit(solution)/shard_map/ppermute | solution.py:21
  155.4 30.7 %copy-start.1 = (bf16[192,1024]{1,0:T(8,128)(2,1)}, bf16[192,1024]{1,0:T(8,128)(2,1)S(1)}, u32[]{:S(2)}) copy-start(bf16[192,1024]{1,0:T(8,128)(2,1)S(1)} %collective-permute-done.5.refs_6_) | copy-start | bytes 1179652
  155.4 24.3 %collective-permute-start.6 = (bf16[192,1024]{1,0:T(8,128)(2,1)S(1)}, bf16[192,1024]{1,0:T(8,128)(2,1)S(1)}, u32[]{:S(2)}, u32[]{:S(2)}) collective-permute-start(bf16[192,1024]{1,0:T(8,128)(2,1)S(1)} %collective-permute-done.5.refs_6_), channel_id=1, source_target_pairs={{0,1},{1,0},{2,3},{3,2},{4,5},{5,4},{6,7},{7,6},{8,9},{9,8},{10,11... | collective-permute-start | bytes 1179656 | tf_op jit(solution)/shard_map/ppermute | solution.py:21
  158.9 26.3 %copy-start.15 = (f32[8192]{0:T(1024)S(1)}, f32[8192]{0:T(1024)}, u32[]{:S(2)}) copy-start(f32[8192]{0:T(1024)} %param.15) | copy-start | bytes 98308
  158.9 21.6 %collective-permute-start.8 = (bf16[192,1024]{1,0:T(8,128)(2,1)}, bf16[192,1024]{1,0:T(8,128)(2,1)S(1)}, u32[]{:S(2)}, u32[]{:S(2)}) collective-permute-start(bf16[192,1024]{1,0:T(8,128)(2,1)} %collective-permute-done.7.refs_8_), channel_id=1, source_target_pairs={{0,1},{1,0},{2,3},{3,2},{4,5},{5,4},{6,7},{7,6},{8,9},{9,8},{10,11... | collective-permute-start | bytes 1179656 | tf_op jit(solution)/shard_map/ppermute | solution.py:21
  174.4 11.9 %collective-permute-start.2 = (bf16[384,1024]{1,0:T(8,128)(2,1)S(1)}, bf16[384,1024]{1,0:T(8,128)(2,1)}, u32[]{:S(2)}, u32[]{:S(2)}) collective-permute-start(bf16[384,1024]{1,0:T(8,128)(2,1)S(1)} %collective-permute-done.1.refs_2_), channel_id=1, source_target_pairs={{0,1},{1,0},{2,3},{3,2},{4,5},{5,4},{6,7},{7,6},{8,9},{9,8},{10,11... | collective-permute-start | bytes 2359304 | tf_op jit(solution)/shard_map/ppermute | solution.py:21
  176.0 10.3 %collective-permute-start.4 = (bf16[384,1024]{1,0:T(8,128)(2,1)}, bf16[384,1024]{1,0:T(8,128)(2,1)}, u32[]{:S(2)}, u32[]{:S(2)}) collective-permute-start(bf16[384,1024]{1,0:T(8,128)(2,1)} %collective-permute-done.3.refs_4_), channel_id=1, source_target_pairs={{0,1},{1,0},{2,3},{3,2},{4,5},{5,4},{6,7},{7,6},{8,9},{9,8},{10,11... | collective-permute-start | bytes 2359304 | tf_op jit(solution)/shard_map/ppermute | solution.py:21
  179.8 0.7 copy-start.3
  180.5 14.4 %collective-permute-start.23 = (bf16[1024,256]{1,0:T(8,128)(2,1)}, bf16[1024,256]{1,0:T(8,128)(2,1)S(1)}, u32[]{:S(2)}, u32[]{:S(2)}) collective-permute-start(bf16[1024,256]{1,0:T(8,128)(2,1)} %slice.110), channel_id=1, source_target_pairs={{0,64},{64,128},{128,192},{192,0},{1,65},{65,129},{129,193},{193,1... | collective-permute-start | bytes 1572872 | tf_op jit(solution)/shard_map/ppermute | solution.py:21
  180.5 0.8 copy-start.5
  181.3 13.6 %collective-permute-start.24 = (bf16[1024,256]{1,0:T(8,128)(2,1)}, bf16[1024,256]{1,0:T(8,128)(2,1)}, u32[]{:S(2)}, u32[]{:S(2)}) collective-permute-start(bf16[1024,256]{1,0:T(8,128)(2,1)} %slice.111), channel_id=1, source_target_pairs={{0,192},{64,0},{128,64},{192,128},{1,193},{65,1},{129,65},{193,129... | collective-permute-start | bytes 1572872 | tf_op jit(solution)/shard_map/ppermute | solution.py:21
  194.9 1.0 copy-start.2
  195.9 1.0 copy-start.4
  196.9 1.0 copy-start.6
Sparse Core Ops, SparseCore 0:
  9.1 49.7 all-gather.2
  61.5 122.0 all-gather.4

commit v6 on v5

--- a/solution.py
+++ b/solution.py
@@ -95,6 +95,19 @@
     return (value * cos + pltpu.roll(value, 64, 1) * sin).astype(jnp.bfloat16)
 
 
+def one_head(query, key, value):
+    at = lax.broadcasted_iota(jnp.int32, (SEQ, SEQ), 0)
+    causal = at >= lax.broadcasted_iota(jnp.int32, (SEQ, SEQ), 1)
+    scores = lax.dot_general(
+        query, key, (((1,), (1,)), ((), ())), preferred_element_type=jnp.float32
+    ) * (HEAD ** (-0.5))
+    scores = jnp.where(causal, scores, -1e30)
+    top = jnp.max(scores, axis=1, keepdims=True)
+    e = jnp.exp(scores - top)
+    w = (e / jnp.sum(e, axis=1, keepdims=True)).astype(jnp.bfloat16)
+    return jnp.dot(w, value, preferred_element_type=jnp.float32).astype(jnp.bfloat16)
+
+
 def prepare(where, text, image, keyval, gain, cosine, sine):
     arrays = [a for a, _, _, _ in text] + list(image) + [a for a, _ in keyval]
     n_text, count = len(text), len(arrays)
@@ -104,8 +117,8 @@
 
     def kernel(where_ref, *refs):
         gain_ref, cos_ref, sin_ref = refs[count : count + 3]
-        a_ref, key_ref, value_ref = refs[count + 3 : count + 6]
-        b_ref, sem = refs[count + 6 :]
+        a_ref, key_ref, value_ref, last_ref = refs[count + 3 : count + 7]
+        b_ref, sem = refs[count + 7 :]
         x, z, y, c = where_ref[0], where_ref[1], where_ref[2], where_ref[3]
         start, n_rows = where_ref[4], where_ref[5]
         loads = []
@@ -143,7 +156,7 @@
         scale = lax.rsqrt(total * (1.0 / WIDTH) + decoder_epsilon)
         for copy in loads:
             copy.wait()
-        acc = jnp.zeros((SEQ, 256), jnp.float32)
+        acc = jnp.zeros((SEQ, 384), jnp.float32)
         for t in range(8):
             normed = (
                 a_ref[t].astype(jnp.float32) * scale * gain_ref[t : t + 1, :]
@@ -152,20 +165,23 @@
             acc = acc + jnp.dot(
                 normed, b_ref[t * 1024 : (t + 1) * 1024, :], preferred_element_type=jnp.float32
             )
-        key_ref[...] = rotated(acc[:, :HEAD], cos_ref[...], sin_ref[...])
-        value_ref[...] = acc[:, HEAD:].astype(jnp.bfloat16)
+        cos, sin = cos_ref[...], sin_ref[...]
+        key = rotated(acc[:, :HEAD], cos, sin)
+        value = acc[:, HEAD : 2 * HEAD].astype(jnp.bfloat16)
+        key_ref[...] = key
+        value_ref[...] = value
+        last_ref[...] = one_head(rotated(acc[:, 2 * HEAD :], cos, sin), key, value)
 
     return pl.pallas_call(
         kernel,
         out_shape=[
             jax.ShapeDtypeStruct((8, SEQ, 1024), jnp.bfloat16),
-            jax.ShapeDtypeStruct((SEQ, HEAD), jnp.bfloat16),
-            jax.ShapeDtypeStruct((SEQ, HEAD), jnp.bfloat16),
-        ],
+        ]
+        + [jax.ShapeDtypeStruct((SEQ, HEAD), jnp.bfloat16)] * 3,
         in_specs=[SMEM] + [VMEM] * (n_text + 2) + [HBM] * len(keyval) + [VMEM] * 3,
-        out_specs=[VMEM] * 3,
+        out_specs=[VMEM] * 4,
         scratch_shapes=[
-            pltpu.VMEM((WIDTH, 256), jnp.bfloat16),
+            pltpu.VMEM((WIDTH, 384), jnp.bfloat16),
             pltpu.SemaphoreType.DMA((len(plan),)),
         ],
         compiler_params=pltpu.CompilerParams(vmem_limit_bytes=48 * 1024 * 1024),
@@ -173,8 +189,8 @@
     )(where, *arrays, gain, cosine, sine)
 
 
-def attention(sequence, query_w, key, value, cosine, sine):
-    def kernel(a_ref, w_hbm, key_ref, value_ref, cos_ref, sin_ref, out_ref, w_ref, sem):
+def attention(sequence, query_w, key, value, last, cosine, sine):
+    def kernel(a_ref, w_hbm, key_ref, value_ref, last_ref, cos_ref, sin_ref, out_ref, w_ref, sem):
         loads = [
             pltpu.make_async_copy(
                 w_hbm.at[pl.ds(t * 1024, 1024), :], w_ref.at[pl.ds(t * 1024, 1024), :], sem.at[t]
@@ -183,41 +199,30 @@
         ]
         for copy in loads:
             copy.start()
-        acc = jnp.zeros((SEQ, 512), jnp.float32)
+        acc = jnp.zeros((SEQ, 384), jnp.float32)
         for t in range(8):
             loads[t].wait()
             acc = acc + jnp.dot(
                 a_ref[t], w_ref[t * 1024 : (t + 1) * 1024, :], preferred_element_type=jnp.float32
             )
         cos, sin = cos_ref[...], sin_ref[...]
-        causal = lax.broadcasted_iota(jnp.int32, (SEQ, SEQ), 0) >= lax.broadcasted_iota(
-            jnp.int32, (SEQ, SEQ), 1
-        )
-        for h in range(4):
+        for h in range(3):
             query = rotated(acc[:, h * HEAD : (h + 1) * HEAD], cos, sin)
-            scores = lax.dot_general(
-                query, key_ref[...], (((1,), (1,)), ((), ())), preferred_element_type=jnp.float32
-            ) * (HEAD ** (-0.5))
-            scores = jnp.where(causal, scores, -1e30)
-            top = jnp.max(scores, axis=1, keepdims=True)
-            e = jnp.exp(scores - top)
-            w = (e / jnp.sum(e, axis=1, keepdims=True)).astype(jnp.bfloat16)
-            out_ref[:, h * HEAD : (h + 1) * HEAD] = jnp.dot(
-                w, value_ref[...], preferred_element_type=jnp.float32
-            ).astype(jnp.bfloat16)
+            out_ref[:, h * HEAD : (h + 1) * HEAD] = one_head(query, key_ref[...], value_ref[...])
+        out_ref[:, 3 * HEAD :] = last_ref[...]
 
     return pl.pallas_call(
         kernel,
         out_shape=jax.ShapeDtypeStruct((SEQ, 512), jnp.bfloat16),
-        in_specs=[VMEM, HBM] + [VMEM] * 4,
+        in_specs=[VMEM, HBM] + [VMEM] * 5,
         out_specs=VMEM,
         scratch_shapes=[
-            pltpu.VMEM((WIDTH, 512), jnp.bfloat16),
+            pltpu.VMEM((WIDTH, 384), jnp.bfloat16),
             pltpu.SemaphoreType.DMA((8,)),
         ],
         compiler_params=pltpu.CompilerParams(vmem_limit_bytes=48 * 1024 * 1024),
         name="attention",
-    )(sequence, query_w, key, value, cosine, sine)
+    )(sequence, query_w, key, value, last, cosine, sine)
 
 
 def vision(vis_rows, ln_gain, ln_bias, weight):
@@ -256,11 +261,14 @@
         return jnp.sum(jnp.where(sample_ids == index, values, 0))
 
     proj_all = lax.all_gather(proj_weight, "z", axis=0, tiled=True)
-    query_w = lax.all_gather(w_query, ("x", "z"), axis=0, tiled=True)
+    query_w = lax.all_gather(w_query[:, : 3 * HEAD], ("x", "z"), axis=0, tiled=True)
 
     image = vision(vis_rows, ln_gain, ln_bias, proj_all).reshape(8, 8, 1024)
 
-    along_z = ring8(key_value_weight.reshape(256, 256), "z")
+    mixed = jnp.concatenate(
+        [key_value_weight.reshape(256, 256), w_query[:, 3 * HEAD :]], axis=1
+    )
+    along_z = ring8(mixed, "z")
     offsets, at = [], 0
     for a, dz, row in along_z:
         offsets.append((dz, row, a.shape[0], at))
@@ -294,10 +302,10 @@
     rows = entry(tile_counts, place) * 8
     where = jnp.stack([x, z, y, c, image_offsets[0], rows]).astype(jnp.int32)
     cosine, sine = rope_tables()
-    sequence, key, value = prepare(
+    sequence, key, value, last = prepare(
         where, text, (own_image, other_image), keyval, attn_gain.reshape(8, 1024), cosine, sine
     )
-    return attention(sequence, query_w, key, value, cosine, sine)[None]
+    return attention(sequence, query_w, key, value, last, cosine, sine)[None]
 
 
 def solution(mesh):

time: 230 us -> 240 us (1.043)
  local copies, waits for them, and re-layouts: 14.3 us -> 19.9 us
    ppermute x22, waiting for transfers between devices: 51.1 us -> 71.3 us  [shift(): lax.ppermute(array, axis, [(i, (i + by) % size) for i in range(size)])]
    all_to_all x4, waiting for transfers between devices: 33.4 us -> 14.7 us  [exchange(): return lax.all_to_all(array, axis, 0, 0, tiled=True)]
    all_gather x1, waiting for transfers between devices: 7.25 us -> 11.2 us  [step(): proj_all = lax.all_gather(proj_weight, 'z', axis=0, tiled=True)]
    unnamed x39 -> x49, local copies, waits for them, and re-layouts: 4.59 us -> 7.66 us
    ppermute x3, waiting for transfers between devices: 2.65 us -> 0.01 us  [flip_x(): return lax.ppermute(array, 'x', [(i, i ^ flip) for i in range(NX)])]
  transfers between devices with their start and end apart: 31 -> 31, of which waited for: 12 -> 8; matrix products, arithmetic and copies ran while one was open for 11% -> 11% of each run, Pallas kernels for 6% -> 7%
where the time goes in v6:
time: 240 us; the launch traced here: 239 us
  waiting for transfers between devices  97.9 us (41%)
  starting transfers between devices  64.4 us (27%)
  Pallas kernels  27.1 us (11%)
  local copies, waits for them, and re-layouts  19.9 us (8%)
  between operations  15.2 us (6%)
  other arithmetic  11.2 us (5%)
  matrix products  3.31 us (1%)
    ppermute x22, waiting for transfers between devices, shift(): lax.ppermute(array, axis, [(i, (i + by) % size) for i in range(size)])  71.3 us
    ppermute x22, starting transfers between devices, shift(): lax.ppermute(array, axis, [(i, (i + by) % size) for i in range(size)])  38.8 us
    all_to_all x4, starting transfers between devices, exchange(): return lax.all_to_all(array, axis, 0, 0, tiled=True)  22.1 us
    all_to_all x4, waiting for transfers between devices, exchange(): return lax.all_to_all(array, axis, 0, 0, tiled=True)  14.7 us
    pallas_call x1, Pallas kernels, prepare(): pl.pallas_call(kernel, out_shape=[jax.ShapeDtypeStruct((8, SEQ, 1024), jn...  14.3 us
    all_gather x1, waiting for transfers between devices, step(): proj_all = lax.all_gather(proj_weight, 'z', axis=0, tiled=True)  11.2 us
    pallas_call x1, Pallas kernels, attention(): pl.pallas_call(kernel, out_shape=jax.ShapeDtypeStruct((SEQ, 512), jnp.bfl...  10.1 us
    unnamed x49, local copies, waits for them, and re-layouts  7.66 us
  transfers between devices with their start and end apart: 31, of which 8 were waited for; matrix products, arithmetic and copies ran while one was open for 11% of the time, Pallas kernels for 7%

profile of v6, /device:TPU:1, one launch (start us, length us, event | category | flops | bytes accessed | tf_op | source)
XLA Modules:
  0.0 238.9 jit_solution(7470989456621484798)
XLA Ops:
  6.5 0.7 all-gather.3.cloned.1.call-update
  7.3 1.7 slice.103
  9.0 0.9 copy.41
  9.9 1.1 broadcast_in_dim.131
  11.0 6.7 %all-to-all-start = ((bf16[8,64,2,400]{3,1,2,0:T(8,128)(2,1)}), bf16[8,64,2,400]{3,1,2,0:T(8,128)(2,1)S(1)}, u32[]{:S(2)}, u32[]{:S(2)}) async-start(bf16[8,64,2,400]{3,1,2,0:T(8,128)(2,1)} %broadcast_in_dim.131), calls=%async_computation | async-start | bytes 2097152 | tf_op jit(solution)/shard_map/all_to_all | solution.py:29
  18.0 14.7 %all-to-all-done = bf16[8,64,2,400]{3,1,2,0:T(8,128)(2,1)S(1)} async-done(((bf16[8,64,2,400]{3,1,2,0:T(8,128)(2,1)}), bf16[8,64,2,400]{3,1,2,0:T(8,128)(2,1)S(1)}, u32[]{:S(2)}, u32[]{:S(2)}) %all-to-all-start) | async-done | bytes 819232 | tf_op jit(solution)/shard_map/all_to_all | solution.py:29
  33.0 0.5 fusion.5
  33.5 1.5 fusion.8
  34.9 3.5 %all-to-all-start.1 = ((bf16[4,2,64,2,400]{4,2,3,1,0:T(8,128)(2,1)}), bf16[4,2,64,2,400]{4,2,3,1,0:T(8,128)(2,1)S(1)}, u32[]{:S(2)}, u32[]{:S(2)}) async-start(bf16[4,2,64,2,400]{4,2,3,1,0:T(8,128)(2,1)} %bitcast.11), calls=%async_computation.1 | async-start | bytes 2097152 | tf_op jit(solution)/shard_map/all_to_all | solution.py:29
  38.5 1.5 collective-permute-start.13
  39.9 4.0 %collective-permute-start.14 = (bf16[256,384]{1,0:T(8,128)(2,1)S(1)}, bf16[256,384]{1,0:T(8,128)(2,1)S(1)}, u32[]{:S(2)}, u32[]{:S(2)}) collective-permute-start(bf16[256,384]{1,0:T(8,128)(2,1)S(1)} %pad_maximum_fusion.refs_0_), channel_id=1, source_target_pairs={{0,56},{8,0},{16,8},{24,16},{32,24},{40,32},{48,40},{56,48},{1,57}... | collective-permute-start | bytes 589832 | tf_op jit(solution)/shard_map/ppermute | solution.py:21
  44.4 0.7 fusion.24
  45.1 1.3 iota_compare_fusion
  46.4 1.3 iota_compare_fusion.2
  47.7 5.7 %collective-permute-done.13.refs_1_ = bf16[256,384]{1,0:T(8,128)(2,1)S(1)} collective-permute-done((bf16[256,384]{1,0:T(8,128)(2,1)S(1)}, bf16[256,384]{1,0:T(8,128)(2,1)S(1)}, u32[]{:S(2)}, u32[]{:S(2)}) %collective-permute-start.13) | collective-permute-done | bytes 196640 | tf_op jit(solution)/shard_map/ppermute | solution.py:21
  53.4 2.7 %collective-permute-start.16 = (bf16[256,384]{1,0:T(8,128)(2,1)S(1)}, bf16[256,384]{1,0:T(8,128)(2,1)S(1)}, u32[]{:S(2)}, u32[]{:S(2)}) collective-permute-start(bf16[256,384]{1,0:T(8,128)(2,1)S(1)} %collective-permute-done.14.refs_2_), channel_id=1, source_target_pairs={{0,56},{8,0},{16,8},{24,16},{32,24},{40,32},{48,40},{56,48},{1,57}... | collective-permute-start | bytes 589832 | tf_op jit(solution)/shard_map/ppermute | solution.py:21
  56.0 11.2 %all-gather.3.cloned.1.call-done = bf16[800,2,1024]{2,1,0:T(2,128)(2,1)} async-done(((bf16[100,2,1024]{2,1,0:T(2,128)(2,1)}), bf16[800,2,1024]{2,1,0:T(2,128)(2,1)}) %all-gather.3.cloned.1.call-update) | async-done | bytes 3276816 | tf_op jit(solution)/shard_map/all_gather | solution.py:263
  67.2 3.3 %fusion.12 = bf16[4,64,1024]{2,1,0:T(8,128)(2,1)S(1)} fusion(bf16[4,2,64,2,400]{4,2,3,1,0:T(8,128)(2,1)S(1)} %all-to-all-done.1, bf16[2,400,2,1024,1]{3,2,1,0,4:T(2,128)(2,1)} %bitcast.66), kind=kOutput, calls=%fused_computation.13 | convolution fusion | flops 839122944 | bytes 4620288 | tf_op jit(solution)/shard_map/sctmf,cfmo->sto/dot_general | solution.py:238
  70.6 2.6 %collective-permute-start.10 = (bf16[64,1024]{1,0:T(8,128)(2,1)S(1)}, bf16[64,1024]{1,0:T(8,128)(2,1)S(1)}, u32[]{:S(2)}, u32[]{:S(2)}) collective-permute-start(bf16[64,1024]{1,0:T(8,128)(2,1)S(1)} %get-tuple-element.17), channel_id=1, source_target_pairs={{0,128},{64,192},{128,0},{192,64},{1,129},{65,193},{129,1},{193,65... | collective-permute-start | bytes 393224 | tf_op jit(solution)/shard_map/ppermute | solution.py:25
  73.2 0.9 collective-permute-start.11
  74.1 1.3 iota_compare_fusion.4
  75.4 1.2 iota_compare_fusion.6
  76.7 2.6 %collective-permute-start.18 = (bf16[256,384]{1,0:T(8,128)(2,1)S(1)}, bf16[256,384]{1,0:T(8,128)(2,1)S(1)}, u32[]{:S(2)}, u32[]{:S(2)}) collective-permute-start(bf16[256,384]{1,0:T(8,128)(2,1)S(1)} %collective-permute-done.16.refs_4_), channel_id=1, source_target_pairs={{0,56},{8,0},{16,8},{24,16},{32,24},{40,32},{48,40},{56,48},{1,57}... | collective-permute-start | bytes 589832 | tf_op jit(solution)/shard_map/ppermute | solution.py:21
  79.5 1.2 select_select_fusion
  80.7 7.7 %all-to-all-start.2 = ((bf16[32,8,1024]{2,1,0:T(8,128)(2,1)}), bf16[32,8,1024]{2,1,0:T(8,128)(2,1)S(1)}, u32[]{:S(2)}, u32[]{:S(2)}) async-start(bf16[32,8,1024]{2,1,0:T(8,128)(2,1)} %select_select_fusion), calls=%async_computation.2 | async-start | bytes 1048576 | tf_op jit(solution)/shard_map/all_to_all | solution.py:29
  88.4 1.3 collective-permute-start.19
  89.8 1.7 collective-permute-start.20
  91.5 16.9 %collective-permute-done.19.refs_7_ = bf16[128,384]{1,0:T(8,128)(2,1)S(1)} collective-permute-done((bf16[128,384]{1,0:T(8,128)(2,1)S(1)}, bf16[128,384]{1,0:T(8,128)(2,1)S(1)}, u32[]{:S(2)}, u32[]{:S(2)}) %collective-permute-start.19) | collective-permute-done | bytes 98336 | tf_op jit(solution)/shard_map/ppermute | solution.py:21
  108.4 0.6 copy-done.19
  109.0 0.6 copy-done.20
  109.7 2.7 %pack.1.refs_12_ = bf16[2048,384]{1,0:T(8,128)(2,1)} custom-call(bf16[256,384]{1,0:T(8,128)(2,1)} %copy-done.11, bf16[256,384]{1,0:T(8,128)(2,1)} %copy-done.14, bf16[256,384]{1,0:T(8,128)(2,1)} %copy-done.15, bf16[256,384]{1,0:T(8,128)(2,1)} %copy-done.16, bf16[256,384]{1,0:T(8,128)(2,1)} %copy-done.17, bf16[256,384]{1,0:T(8,128)(2,1)} %copy-done.12, ...), custom_call_target="tpu_custom_call" | custom-call | tf_op jit(solution)/shard_map/pack/pallas_call | solution.py:85
  112.4 2.7 %collective-permute-start.22 = (bf16[2048,384]{1,0:T(8,128)(2,1)}, bf16[2048,384]{1,0:T(8,128)(2,1)}, u32[]{:S(2)}, u32[]{:S(2)}) collective-permute-start(bf16[2048,384]{1,0:T(8,128)(2,1)} %pack.1.refs_12_), channel_id=1, source_target_pairs={{0,192},{64,0},{128,64},{192,128},{1,193},{65,1},{129,65},{193,129... | collective-permute-start | bytes 4718600 | tf_op jit(solution)/shard_map/ppermute | solution.py:21
  115.1 1.4 collective-permute-start.1
  116.5 1.3 collective-permute-start.3
  117.8 0.7 fusion.20
  118.4 0.7 fusion.22
  119.1 0.6 gather_fusion
  119.7 1.1 broadcast_in_dim.149
  120.8 4.2 %all-to-all-start.3 = ((bf16[4,128,1024]{2,1,0:T(8,128)(2,1)}), bf16[4,128,1024]{2,1,0:T(8,128)(2,1)}, u32[]{:S(2)}, u32[]{:S(2)}) async-start(bf16[4,128,1024]{2,1,0:T(8,128)(2,1)} %broadcast_in_dim.149), calls=%async_computation.3 | async-start | bytes 2097152 | tf_op jit(solution)/shard_map/all_to_all | solution.py:29
  125.1 3.5 %collective-permute-start = (bf16[384,1024]{1,0:T(8,128)(2,1)S(1)}, bf16[384,1024]{1,0:T(8,128)(2,1)S(1)}, u32[]{:S(2)}, u32[]{:S(2)}) collective-permute-start(bf16[384,1024]{1,0:T(8,128)(2,1)S(1)} %bitcast.59), channel_id=1, source_target_pairs={{0,1},{1,0},{2,3},{3,2},{4,5},{5,4},{6,7},{7,6},{8,9},{9,8},{10,11... | collective-permute-start | bytes 2359304 | tf_op jit(solution)/shard_map/ppermute | solution.py:21
  128.5 4.1 %collective-permute-done.1.refs_2_ = bf16[384,1024]{1,0:T(8,128)(2,1)S(1)} collective-permute-done((bf16[384,1024]{1,0:T(8,128)(2,1)S(1)}, bf16[384,1024]{1,0:T(8,128)(2,1)S(1)}, u32[]{:S(2)}, u32[]{:S(2)}) %collective-permute-start.1) | collective-permute-done | bytes 786464 | tf_op jit(solution)/shard_map/ppermute | solution.py:21
  132.7 0.3 collective-permute-start.5
  133.1 2.5 %collective-permute-start.7 = (bf16[192,1024]{1,0:T(8,128)(2,1)S(1)}, bf16[192,1024]{1,0:T(8,128)(2,1)}, u32[]{:S(2)}, u32[]{:S(2)}) collective-permute-start(bf16[192,1024]{1,0:T(8,128)(2,1)S(1)} %slice.107), channel_id=1, source_target_pairs={{0,6},{2,0},{4,2},{6,4},{1,7},{3,1},{5,3},{7,5},{8,14},{10,8},{12,... | collective-permute-start | bytes 1179656 | tf_op jit(solution)/shard_map/ppermute | solution.py:21
  135.6 16.8 %collective-permute-done.5.refs_6_ = bf16[192,1024]{1,0:T(8,128)(2,1)S(1)} collective-permute-done((bf16[192,1024]{1,0:T(8,128)(2,1)S(1)}, bf16[192,1024]{1,0:T(8,128)(2,1)S(1)}, u32[]{:S(2)}, u32[]{:S(2)}) %collective-permute-start.5) | collective-permute-done | bytes 393248 | tf_op jit(solution)/shard_map/ppermute | solution.py:21
  152.3 3.6 %collective-permute-start.6 = (bf16[192,1024]{1,0:T(8,128)(2,1)S(1)}, bf16[192,1024]{1,0:T(8,128)(2,1)}, u32[]{:S(2)}, u32[]{:S(2)}) collective-permute-start(bf16[192,1024]{1,0:T(8,128)(2,1)S(1)} %collective-permute-done.5.refs_6_), channel_id=1, source_target_pairs={{0,1},{1,0},{2,3},{3,2},{4,5},{5,4},{6,7},{7,6},{8,9},{9,8},{10,11... | collective-permute-start | bytes 1179656 | tf_op jit(solution)/shard_map/ppermute | solution.py:21
  156.2 13.7 %collective-permute-done.21.refs_13_ = bf16[2048,384]{1,0:T(8,128)(2,1)} collective-permute-done((bf16[2048,384]{1,0:T(8,128)(2,1)}, bf16[2048,384]{1,0:T(8,128)(2,1)}, u32[]{:S(2)}, u32[]{:S(2)}) %collective-permute-start.21) | collective-permute-done | bytes 1572896 | tf_op jit(solution)/shard_map/ppermute | solution.py:21
  169.9 6.1 %collective-permute-start.12 = (bf16[4,128,1024]{2,1,0:T(8,128)(2,1)}, bf16[4,128,1024]{2,1,0:T(8,128)(2,1)}, u32[]{:S(2)}, u32[]{:S(2)}) collective-permute-start(bf16[4,128,1024]{2,1,0:T(8,128)(2,1)} %all-to-all-done.3.refs_10_), channel_id=1, source_target_pairs={{0,1},{1,0},{2,3},{3,2},{4,5},{5,4},{6,7},{7,6},{8,9},{9,8},{10,11... | collective-permute-start | bytes 3145736 | tf_op jit(solution)/shard_map/ppermute | solution.py:21
  176.0 2.1 slice.118
  178.1 2.2 slice.119
  180.3 0.5 collective-permute-start.4
  180.8 2.7 %collective-permute-start.24 = (bf16[1024,384]{1,0:T(8,128)(2,1)}, bf16[1024,384]{1,0:T(8,128)(2,1)}, u32[]{:S(2)}, u32[]{:S(2)}) collective-permute-start(bf16[1024,384]{1,0:T(8,128)(2,1)} %slice.119), channel_id=1, source_target_pairs={{0,192},{64,0},{128,64},{192,128},{1,193},{65,1},{129,65},{193,129... | collective-permute-start | bytes 2359304 | tf_op jit(solution)/shard_map/ppermute | solution.py:21
  184.7 1.4 reshape.177.refs_17_
  186.2 0.8 fusion.18
  187.2 14.1 %collective-permute-done.23.refs_15_ = bf16[1024,384]{1,0:T(8,128)(2,1)} collective-permute-done((bf16[1024,384]{1,0:T(8,128)(2,1)}, bf16[1024,384]{1,0:T(8,128)(2,1)}, u32[]{:S(2)}, u32[]{:S(2)}) %collective-permute-start.23) | collective-permute-done | bytes 786464 | tf_op jit(solution)/shard_map/ppermute | solution.py:21
  201.4 1.0 copy-done.2
  202.4 0.8 copy-done.3
  203.1 14.3 %prepare.1 = (bf16[8,384,1024]{2,1,0:T(8,128)(2,1)}, bf16[384,128]{1,0:T(8,128)(2,1)S(1)}, bf16[384,128]{1,0:T(8,128)(2,1)S(1)}, bf16[384,128]{1,0:T(8,128)(2,1)S(1)}) custom-call(s32[6]{0:T(128)S(1)} %stack.23.where_ref, bf16[384,1024]{1,0:T(8,128)(2,1)S(1)} %bitcast.60, bf16[384,1024]{1,0:T(8,128)(2,1)S(1)} %collective-permute-done.refs_1_, ...), custom_call_target="tpu_custom_call" | custom-call | tf_op jit(solution)/shard_map/prepare/pallas_call | solution.py:175
  217.4 0.6 copy-done.4
  218.0 0.6 copy-done.6
  218.7 0.6 copy-done.8
  219.3 0.9 copy-done.5
  220.2 0.9 copy-done.7
  221.1 0.9 copy-done.9
  222.0 10.1 %attention.1 = bf16[384,512]{1,0:T(8,128)(2,1)} custom-call(bf16[8,384,1024]{2,1,0:T(8,128)(2,1)} %get-tuple-element.9.a_ref, bf16[8192,384]{1,0:T(8,128)(2,1)} %all-gather.5.cloned.1.call-done.w_hbm, bf16[384,128]{1,0:T(8,128)(2,1)S(1)} %copy-done.5, bf16[384,128]{1,0:T(8,128)(2,1)S(1)} %copy-done.7, bf16[384,128]{1,0:T(8,128)(2,1)S(1)} %copy-done.9, ...), custom_call_target="tpu_custom_call" | custom-call | tf_op jit(solution)/shard_map/attention/pallas_call | solution.py:214
  (98 shorter events, 2.1 us)
Async XLA Ops:
  6.5 60.7 %all-gather.3.cloned.1.call-start = ((), (), s32[]{:S(2)}) async-start(), calls=%async_computation.4 | async-start | bytes 3686400 | tf_op jit(solution)/shard_map/all_gather | solution.py:263
  7.3 10.4 %copy-start.21 = (f32[2,3200]{1,0:T(2,128)S(1)}, f32[2,3200]{1,0:T(2,128)}, u32[]{:S(2)}) copy-start(f32[2,3200]{1,0:T(2,128)} %param.11) | copy-start | bytes 76804
  7.3 10.5 %copy-start.22 = (f32[2,3200]{1,0:T(2,128)S(1)}, f32[2,3200]{1,0:T(2,128)}, u32[]{:S(2)}) copy-start(f32[2,3200]{1,0:T(2,128)} %param.12) | copy-start | bytes 76804
  7.3 10.6 %copy-start.18 = (bf16[256,2,128]{2,1,0:T(2,128)(2,1)S(1)}, bf16[256,2,128]{2,1,0:T(2,128)(2,1)}, u32[]{:S(2)}) copy-start(bf16[256,2,128]{2,1,0:T(2,128)(2,1)} %param.17) | copy-start | bytes 393220
  7.3 212.0 %all-gather.5.cloned.1.call-start = ((), (), s32[]{:S(2)}) async-start(), calls=%async_computation.5 | async-start | bytes 6488064 | tf_op jit(solution)/shard_map/all_gather | solution.py:264
  11.0 21.7 %all-to-all-start = ((bf16[8,64,2,400]{3,1,2,0:T(8,128)(2,1)}), bf16[8,64,2,400]{3,1,2,0:T(8,128)(2,1)S(1)}, u32[]{:S(2)}, u32[]{:S(2)}) async-start(bf16[8,64,2,400]{3,1,2,0:T(8,128)(2,1)} %broadcast_in_dim.131), calls=%async_computation | async-start | bytes 2097152 | tf_op jit(solution)/shard_map/all_to_all | solution.py:29
  33.4 5.0 %slice-start = ((bf16[256,512]{1,0:T(8,128)(2,1)}), bf16[256,128]{1,0:T(8,128)(2,1)S(1)}, s32[]{:S(2)}) async-start(bf16[256,512]{1,0:T(8,128)(2,1)} %param.16), calls=%async_computation.6 | async-start | bytes 131072 | tf_op jit(solution)/shard_map/slice | solution.py:269
  33.4 10.5 %copy-start.23 = (s32[32]{0:T(128)S(1)}, s32[32]{0:T(128)}, u32[]{:S(2)}) copy-start(s32[32]{0:T(128)} %param.18) | copy-start | bytes 388
  34.9 21.1 %all-to-all-start.1 = ((bf16[4,2,64,2,400]{4,2,3,1,0:T(8,128)(2,1)}), bf16[4,2,64,2,400]{4,2,3,1,0:T(8,128)(2,1)S(1)}, u32[]{:S(2)}, u32[]{:S(2)}) async-start(bf16[4,2,64,2,400]{4,2,3,1,0:T(8,128)(2,1)} %bitcast.11), calls=%async_computation.1 | async-start | bytes 2097152 | tf_op jit(solution)/shard_map/all_to_all | solution.py:29
  38.5 32.1 %copy-start.11 = (bf16[256,384]{1,0:T(8,128)(2,1)}, bf16[256,384]{1,0:T(8,128)(2,1)S(1)}, u32[]{:S(2)}) copy-start(bf16[256,384]{1,0:T(8,128)(2,1)S(1)} %pad_maximum_fusion.refs_0_) | copy-start | bytes 589828
  38.5 14.9 %collective-permute-start.13 = (bf16[256,384]{1,0:T(8,128)(2,1)S(1)}, bf16[256,384]{1,0:T(8,128)(2,1)S(1)}, u32[]{:S(2)}, u32[]{:S(2)}) collective-permute-start(bf16[256,384]{1,0:T(8,128)(2,1)S(1)} %pad_maximum_fusion.refs_0_), channel_id=1, source_target_pairs={{0,8},{8,16},{16,24},{24,32},{32,40},{40,48},{48,56},{56,0},{1,9},... | collective-permute-start | bytes 589832 | tf_op jit(solution)/shard_map/ppermute | solution.py:21
  39.9 13.4 %collective-permute-start.14 = (bf16[256,384]{1,0:T(8,128)(2,1)S(1)}, bf16[256,384]{1,0:T(8,128)(2,1)S(1)}, u32[]{:S(2)}, u32[]{:S(2)}) collective-permute-start(bf16[256,384]{1,0:T(8,128)(2,1)S(1)} %pad_maximum_fusion.refs_0_), channel_id=1, source_target_pairs={{0,56},{8,0},{16,8},{24,16},{32,24},{40,32},{48,40},{56,48},{1,57}... | collective-permute-start | bytes 589832 | tf_op jit(solution)/shard_map/ppermute | solution.py:21
  53.4 17.2 %copy-start.14 = (bf16[256,384]{1,0:T(8,128)(2,1)}, bf16[256,384]{1,0:T(8,128)(2,1)S(1)}, u32[]{:S(2)}) copy-start(bf16[256,384]{1,0:T(8,128)(2,1)S(1)} %collective-permute-done.13.refs_1_) | copy-start | bytes 589828
  53.4 23.2 %collective-permute-start.15 = (bf16[256,384]{1,0:T(8,128)(2,1)S(1)}, bf16[256,384]{1,0:T(8,128)(2,1)S(1)}, u32[]{:S(2)}, u32[]{:S(2)}) collective-permute-start(bf16[256,384]{1,0:T(8,128)(2,1)S(1)} %collective-permute-done.13.refs_1_), channel_id=1, source_target_pairs={{0,8},{8,16},{16,24},{24,32},{32,40},{40,48},{48,56},{56,0},{1,9},... | collective-permute-start | bytes 589832 | tf_op jit(solution)/shard_map/ppermute | solution.py:21
  53.4 17.2 %copy-start.15 = (bf16[256,384]{1,0:T(8,128)(2,1)}, bf16[256,384]{1,0:T(8,128)(2,1)S(1)}, u32[]{:S(2)}) copy-start(bf16[256,384]{1,0:T(8,128)(2,1)S(1)} %collective-permute-done.14.refs_2_) | copy-start | bytes 589828
  53.4 23.3 %collective-permute-start.16 = (bf16[256,384]{1,0:T(8,128)(2,1)S(1)}, bf16[256,384]{1,0:T(8,128)(2,1)S(1)}, u32[]{:S(2)}, u32[]{:S(2)}) collective-permute-start(bf16[256,384]{1,0:T(8,128)(2,1)S(1)} %collective-permute-done.14.refs_2_), channel_id=1, source_target_pairs={{0,56},{8,0},{16,8},{24,16},{32,24},{40,32},{48,40},{56,48},{1,57}... | collective-permute-start | bytes 589832 | tf_op jit(solution)/shard_map/ppermute | solution.py:21
  70.6 8.8 %collective-permute-start.10 = (bf16[64,1024]{1,0:T(8,128)(2,1)S(1)}, bf16[64,1024]{1,0:T(8,128)(2,1)S(1)}, u32[]{:S(2)}, u32[]{:S(2)}) collective-permute-start(bf16[64,1024]{1,0:T(8,128)(2,1)S(1)} %get-tuple-element.17), channel_id=1, source_target_pairs={{0,128},{64,192},{128,0},{192,64},{1,129},{65,193},{129,1},{193,65... | collective-permute-start | bytes 393224 | tf_op jit(solution)/shard_map/ppermute | solution.py:25
  73.2 6.2 %collective-permute-start.11 = (bf16[64,1024]{1,0:T(8,128)(2,1)S(1)}, bf16[64,1024]{1,0:T(8,128)(2,1)S(1)}, u32[]{:S(2)}, u32[]{:S(2)}) collective-permute-start(bf16[64,1024]{1,0:T(8,128)(2,1)S(1)} %get-tuple-element.16), channel_id=1, source_target_pairs={{0,192},{64,128},{128,64},{192,0},{1,193},{65,129},{129,65},{193,1... | collective-permute-start | bytes 393224 | tf_op jit(solution)/shard_map/ppermute | solution.py:25
  74.1 5.3 %collective-permute-start.9 = (bf16[64,1024]{1,0:T(8,128)(2,1)S(1)}, bf16[64,1024]{1,0:T(8,128)(2,1)S(1)}, u32[]{:S(2)}, u32[]{:S(2)}) collective-permute-start(bf16[64,1024]{1,0:T(8,128)(2,1)S(1)} %get-tuple-element.15), channel_id=1, source_target_pairs={{0,64},{64,0},{128,192},{192,128},{1,65},{65,1},{129,193},{193,129... | collective-permute-start | bytes 393224 | tf_op jit(solution)/shard_map/ppermute | solution.py:25
  76.6 31.8 %copy-start.16 = (bf16[256,384]{1,0:T(8,128)(2,1)}, bf16[256,384]{1,0:T(8,128)(2,1)S(1)}, u32[]{:S(2)}) copy-start(bf16[256,384]{1,0:T(8,128)(2,1)S(1)} %collective-permute-done.15.refs_3_) | copy-start | bytes 589828
  76.6 11.8 %collective-permute-start.17 = (bf16[256,384]{1,0:T(8,128)(2,1)S(1)}, bf16[256,384]{1,0:T(8,128)(2,1)S(1)}, u32[]{:S(2)}, u32[]{:S(2)}) collective-permute-start(bf16[256,384]{1,0:T(8,128)(2,1)S(1)} %collective-permute-done.15.refs_3_), channel_id=1, source_target_pairs={{0,8},{8,16},{16,24},{24,32},{32,40},{40,48},{48,56},{56,0},{1,9},... | collective-permute-start | bytes 589832 | tf_op jit(solution)/shard_map/ppermute | solution.py:21
  76.7 31.7 %copy-start.17 = (bf16[256,384]{1,0:T(8,128)(2,1)}, bf16[256,384]{1,0:T(8,128)(2,1)S(1)}, u32[]{:S(2)}) copy-start(bf16[256,384]{1,0:T(8,128)(2,1)S(1)} %collective-permute-done.16.refs_4_) | copy-start | bytes 589828
  76.7 13.0 %collective-permute-start.18 = (bf16[256,384]{1,0:T(8,128)(2,1)S(1)}, bf16[256,384]{1,0:T(8,128)(2,1)S(1)}, u32[]{:S(2)}, u32[]{:S(2)}) collective-permute-start(bf16[256,384]{1,0:T(8,128)(2,1)S(1)} %collective-permute-done.16.refs_4_), channel_id=1, source_target_pairs={{0,56},{8,0},{16,8},{24,16},{32,24},{40,32},{48,40},{56,48},{1,57}... | collective-permute-start | bytes 589832 | tf_op jit(solution)/shard_map/ppermute | solution.py:21
  80.7 34.4 %copy-start = (bf16[1,384,1024]{2,1,0:T(8,128)(2,1)S(1)}, bf16[1,384,1024]{2,1,0:T(8,128)(2,1)}, u32[]{:S(2)}) copy-start(bf16[1,384,1024]{2,1,0:T(8,128)(2,1)} %param.14) | copy-start | bytes 2359300
  80.7 38.4 %all-to-all-start.2 = ((bf16[32,8,1024]{2,1,0:T(8,128)(2,1)}), bf16[32,8,1024]{2,1,0:T(8,128)(2,1)S(1)}, u32[]{:S(2)}, u32[]{:S(2)}) async-start(bf16[32,8,1024]{2,1,0:T(8,128)(2,1)} %select_select_fusion), calls=%async_computation.2 | async-start | bytes 1048576 | tf_op jit(solution)/shard_map/all_to_all | solution.py:29
  88.4 20.0 %copy-start.12 = (bf16[256,384]{1,0:T(8,128)(2,1)}, bf16[256,384]{1,0:T(8,128)(2,1)S(1)}, u32[]{:S(2)}) copy-start(bf16[256,384]{1,0:T(8,128)(2,1)S(1)} %collective-permute-done.17.refs_5_) | copy-start | bytes 589828
  88.4 19.9 %collective-permute-start.19 = (bf16[128,384]{1,0:T(8,128)(2,1)S(1)}, bf16[128,384]{1,0:T(8,128)(2,1)S(1)}, u32[]{:S(2)}, u32[]{:S(2)}) collective-permute-start(bf16[128,384]{1,0:T(8,128)(2,1)S(1)} %slice.116), channel_id=1, source_target_pairs={{0,8},{8,16},{16,24},{24,32},{32,40},{40,48},{48,56},{56,0},{1,9},... | collective-permute-start | bytes 294920 | tf_op jit(solution)/shard_map/ppermute | solution.py:21
  89.7 18.7 %copy-start.13 = (bf16[256,384]{1,0:T(8,128)(2,1)}, bf16[256,384]{1,0:T(8,128)(2,1)S(1)}, u32[]{:S(2)}) copy-start(bf16[256,384]{1,0:T(8,128)(2,1)S(1)} %collective-permute-done.18.refs_6_) | copy-start | bytes 589828
  89.8 18.6 %collective-permute-start.20 = (bf16[128,384]{1,0:T(8,128)(2,1)S(1)}, bf16[128,384]{1,0:T(8,128)(2,1)S(1)}, u32[]{:S(2)}, u32[]{:S(2)}) collective-permute-start(bf16[128,384]{1,0:T(8,128)(2,1)S(1)} %slice.117), channel_id=1, source_target_pairs={{0,56},{8,0},{16,8},{24,16},{32,24},{40,32},{48,40},{56,48},{1,57}... | collective-permute-start | bytes 294920 | tf_op jit(solution)/shard_map/ppermute | solution.py:21
  108.4 0.6 copy-start.19
  109.0 0.6 copy-start.20
  112.4 57.5 %collective-permute-start.21 = (bf16[2048,384]{1,0:T(8,128)(2,1)}, bf16[2048,384]{1,0:T(8,128)(2,1)}, u32[]{:S(2)}, u32[]{:S(2)}) collective-permute-start(bf16[2048,384]{1,0:T(8,128)(2,1)} %pack.1.refs_12_), channel_id=1, source_target_pairs={{0,64},{64,128},{128,192},{192,0},{1,65},{65,129},{129,193},{193,1... | collective-permute-start | bytes 4718600 | tf_op jit(solution)/shard_map/ppermute | solution.py:21
  112.4 65.7 %collective-permute-start.22 = (bf16[2048,384]{1,0:T(8,128)(2,1)}, bf16[2048,384]{1,0:T(8,128)(2,1)}, u32[]{:S(2)}, u32[]{:S(2)}) collective-permute-start(bf16[2048,384]{1,0:T(8,128)(2,1)} %pack.1.refs_12_), channel_id=1, source_target_pairs={{0,192},{64,0},{128,64},{192,128},{1,193},{65,1},{129,65},{193,129... | collective-permute-start | bytes 4718600 | tf_op jit(solution)/shard_map/ppermute | solution.py:21
  115.1 17.6 %collective-permute-start.1 = (bf16[384,1024]{1,0:T(8,128)(2,1)S(1)}, bf16[384,1024]{1,0:T(8,128)(2,1)S(1)}, u32[]{:S(2)}, u32[]{:S(2)}) collective-permute-start(bf16[384,1024]{1,0:T(8,128)(2,1)S(1)} %bitcast.57), channel_id=1, source_target_pairs={{0,2},{2,4},{4,6},{6,0},{1,3},{3,5},{5,7},{7,1},{8,10},{10,12},{12... | collective-permute-start | bytes 2359304 | tf_op jit(solution)/shard_map/ppermute | solution.py:21
  116.5 16.5 %collective-permute-start.3 = (bf16[384,1024]{1,0:T(8,128)(2,1)S(1)}, bf16[384,1024]{1,0:T(8,128)(2,1)S(1)}, u32[]{:S(2)}, u32[]{:S(2)}) collective-permute-start(bf16[384,1024]{1,0:T(8,128)(2,1)S(1)} %bitcast.58), channel_id=1, source_target_pairs={{0,6},{2,0},{4,2},{6,4},{1,7},{3,1},{5,3},{7,5},{8,14},{10,8},{12,... | collective-permute-start | bytes 2359304 | tf_op jit(solution)/shard_map/ppermute | solution.py:21
  120.8 49.1 %all-to-all-start.3 = ((bf16[4,128,1024]{2,1,0:T(8,128)(2,1)}), bf16[4,128,1024]{2,1,0:T(8,128)(2,1)}, u32[]{:S(2)}, u32[]{:S(2)}) async-start(bf16[4,128,1024]{2,1,0:T(8,128)(2,1)} %broadcast_in_dim.149), calls=%async_computation.3 | async-start | bytes 2097152 | tf_op jit(solution)/shard_map/all_to_all | solution.py:29
  125.1 55.2 %collective-permute-start = (bf16[384,1024]{1,0:T(8,128)(2,1)S(1)}, bf16[384,1024]{1,0:T(8,128)(2,1)S(1)}, u32[]{:S(2)}, u32[]{:S(2)}) collective-permute-start(bf16[384,1024]{1,0:T(8,128)(2,1)S(1)} %bitcast.59), channel_id=1, source_target_pairs={{0,1},{1,0},{2,3},{3,2},{4,5},{5,4},{6,7},{7,6},{8,9},{9,8},{10,11... | collective-permute-start | bytes 2359304 | tf_op jit(solution)/shard_map/ppermute | solution.py:21
  132.7 19.6 %collective-permute-start.5 = (bf16[192,1024]{1,0:T(8,128)(2,1)S(1)}, bf16[192,1024]{1,0:T(8,128)(2,1)S(1)}, u32[]{:S(2)}, u32[]{:S(2)}) collective-permute-start(bf16[192,1024]{1,0:T(8,128)(2,1)S(1)} %slice.106), channel_id=1, source_target_pairs={{0,2},{2,4},{4,6},{6,0},{1,3},{3,5},{5,7},{7,1},{8,10},{10,12},{12... | collective-permute-start | bytes 1179656 | tf_op jit(solution)/shard_map/ppermute | solution.py:21
  133.1 45.0 %copy-start.10 = (bf16[384,1024]{1,0:T(8,128)(2,1)}, bf16[384,1024]{1,0:T(8,128)(2,1)S(1)}, u32[]{:S(2)}) copy-start(bf16[384,1024]{1,0:T(8,128)(2,1)S(1)} %collective-permute-done.3.refs_4_) | copy-start | bytes 2359300
  133.1 22.8 %collective-permute-start.7 = (bf16[192,1024]{1,0:T(8,128)(2,1)S(1)}, bf16[192,1024]{1,0:T(8,128)(2,1)}, u32[]{:S(2)}, u32[]{:S(2)}) collective-permute-start(bf16[192,1024]{1,0:T(8,128)(2,1)S(1)} %slice.107), channel_id=1, source_target_pairs={{0,6},{2,0},{4,2},{6,4},{1,7},{3,1},{5,3},{7,5},{8,14},{10,8},{12,... | collective-permute-start | bytes 1179656 | tf_op jit(solution)/shard_map/ppermute | solution.py:21
  152.3 34.7 %copy-start.1 = (bf16[192,1024]{1,0:T(8,128)(2,1)}, bf16[192,1024]{1,0:T(8,128)(2,1)S(1)}, u32[]{:S(2)}) copy-start(bf16[192,1024]{1,0:T(8,128)(2,1)S(1)} %collective-permute-done.5.refs_6_) | copy-start | bytes 1179652
  152.3 28.5 %collective-permute-start.6 = (bf16[192,1024]{1,0:T(8,128)(2,1)S(1)}, bf16[192,1024]{1,0:T(8,128)(2,1)}, u32[]{:S(2)}, u32[]{:S(2)}) collective-permute-start(bf16[192,1024]{1,0:T(8,128)(2,1)S(1)} %collective-permute-done.5.refs_6_), channel_id=1, source_target_pairs={{0,1},{1,0},{2,3},{3,2},{4,5},{5,4},{6,7},{7,6},{8,9},{9,8},{10,11... | collective-permute-start | bytes 1179656 | tf_op jit(solution)/shard_map/ppermute | solution.py:21
  155.9 24.9 %collective-permute-start.8 = (bf16[192,1024]{1,0:T(8,128)(2,1)}, bf16[192,1024]{1,0:T(8,128)(2,1)}, u32[]{:S(2)}, u32[]{:S(2)}) collective-permute-start(bf16[192,1024]{1,0:T(8,128)(2,1)} %collective-permute-done.7.refs_8_), channel_id=1, source_target_pairs={{0,1},{1,0},{2,3},{3,2},{4,5},{5,4},{6,7},{7,6},{8,9},{9,8},{10,11... | collective-permute-start | bytes 1179656 | tf_op jit(solution)/shard_map/ppermute | solution.py:21
  169.9 31.5 %collective-permute-start.12 = (bf16[4,128,1024]{2,1,0:T(8,128)(2,1)}, bf16[4,128,1024]{2,1,0:T(8,128)(2,1)}, u32[]{:S(2)}, u32[]{:S(2)}) collective-permute-start(bf16[4,128,1024]{2,1,0:T(8,128)(2,1)} %all-to-all-done.3.refs_10_), channel_id=1, source_target_pairs={{0,1},{1,0},{2,3},{3,2},{4,5},{5,4},{6,7},{7,6},{8,9},{9,8},{10,11... | collective-permute-start | bytes 3145736 | tf_op jit(solution)/shard_map/ppermute | solution.py:21
  178.1 9.1 %collective-permute-start.2 = (bf16[384,1024]{1,0:T(8,128)(2,1)S(1)}, bf16[384,1024]{1,0:T(8,128)(2,1)S(1)}, u32[]{:S(2)}, u32[]{:S(2)}) collective-permute-start(bf16[384,1024]{1,0:T(8,128)(2,1)S(1)} %collective-permute-done.1.refs_2_), channel_id=1, source_target_pairs={{0,1},{1,0},{2,3},{3,2},{4,5},{5,4},{6,7},{7,6},{8,9},{9,8},{10,11... | collective-permute-start | bytes 2359304 | tf_op jit(solution)/shard_map/ppermute | solution.py:21
  180.3 6.9 %collective-permute-start.4 = (bf16[384,1024]{1,0:T(8,128)(2,1)}, bf16[384,1024]{1,0:T(8,128)(2,1)}, u32[]{:S(2)}, u32[]{:S(2)}) collective-permute-start(bf16[384,1024]{1,0:T(8,128)(2,1)} %copy-done.10), channel_id=1, source_target_pairs={{0,1},{1,0},{2,3},{3,2},{4,5},{5,4},{6,7},{7,6},{8,9},{9,8},{10,11... | collective-permute-start | bytes 2359304 | tf_op jit(solution)/shard_map/ppermute | solution.py:21
  180.8 20.5 %collective-permute-start.23 = (bf16[1024,384]{1,0:T(8,128)(2,1)}, bf16[1024,384]{1,0:T(8,128)(2,1)}, u32[]{:S(2)}, u32[]{:S(2)}) collective-permute-start(bf16[1024,384]{1,0:T(8,128)(2,1)} %slice.118), channel_id=1, source_target_pairs={{0,64},{64,128},{128,192},{192,0},{1,65},{65,129},{129,193},{193,1... | collective-permute-start | bytes 2359304 | tf_op jit(solution)/shard_map/ppermute | solution.py:21
  180.8 20.5 %collective-permute-start.24 = (bf16[1024,384]{1,0:T(8,128)(2,1)}, bf16[1024,384]{1,0:T(8,128)(2,1)}, u32[]{:S(2)}, u32[]{:S(2)}) collective-permute-start(bf16[1024,384]{1,0:T(8,128)(2,1)} %slice.119), channel_id=1, source_target_pairs={{0,192},{64,0},{128,64},{192,128},{1,193},{65,1},{129,65},{193,129... | collective-permute-start | bytes 2359304 | tf_op jit(solution)/shard_map/ppermute | solution.py:21
  201.4 1.0 copy-start.2
  202.4 0.8 copy-start.3
  217.4 0.6 copy-start.4
  218.0 0.6 copy-start.6
  218.7 0.6 copy-start.8
  219.3 0.9 copy-start.5
  220.2 0.9 copy-start.7
  221.1 0.9 copy-start.9
Sparse Core Ops, SparseCore 0:
  9.1 58.0 all-gather.2
  69.8 112.1 all-gather.4

commit v7 on v5

--- a/solution.py
+++ b/solution.py
@@ -190,21 +190,23 @@
                 a_ref[t], w_ref[t * 1024 : (t + 1) * 1024, :], preferred_element_type=jnp.float32
             )
         cos, sin = cos_ref[...], sin_ref[...]
-        causal = lax.broadcasted_iota(jnp.int32, (SEQ, SEQ), 0) >= lax.broadcasted_iota(
-            jnp.int32, (SEQ, SEQ), 1
-        )
         for h in range(4):
             query = rotated(acc[:, h * HEAD : (h + 1) * HEAD], cos, sin)
-            scores = lax.dot_general(
-                query, key_ref[...], (((1,), (1,)), ((), ())), preferred_element_type=jnp.float32
-            ) * (HEAD ** (-0.5))
-            scores = jnp.where(causal, scores, -1e30)
-            top = jnp.max(scores, axis=1, keepdims=True)
-            e = jnp.exp(scores - top)
-            w = (e / jnp.sum(e, axis=1, keepdims=True)).astype(jnp.bfloat16)
-            out_ref[:, h * HEAD : (h + 1) * HEAD] = jnp.dot(
-                w, value_ref[...], preferred_element_type=jnp.float32
-            ).astype(jnp.bfloat16)
+            for first in range(0, SEQ, 128):
+                last = first + 128
+                scores = lax.dot_general(
+                    query[first:last], key_ref[:last, :], (((1,), (1,)), ((), ())),
+                    preferred_element_type=jnp.float32,
+                ) * (HEAD ** (-0.5))
+                row = lax.broadcasted_iota(jnp.int32, (128, last), 0) + first
+                column = lax.broadcasted_iota(jnp.int32, (128, last), 1)
+                scores = jnp.where(row >= column, scores, -1e30)
+                top = jnp.max(scores, axis=1, keepdims=True)
+                e = jnp.exp(scores - top)
+                w = (e / jnp.sum(e, axis=1, keepdims=True)).astype(jnp.bfloat16)
+                out_ref[first:last, h * HEAD : (h + 1) * HEAD] = jnp.dot(
+                    w, value_ref[:last, :], preferred_element_type=jnp.float32
+                ).astype(jnp.bfloat16)
 
     return pl.pallas_call(
         kernel,

time: 230 us -> 232 us (level)
  transfers between devices with their start and end apart: 31 -> 31, of which waited for: 12 -> 12; matrix products, arithmetic and copies ran while one was open for 11% -> 10% of each run, Pallas kernels for 6% -> 6%
where the time goes in v7:
time: 232 us; the launch traced here: 230 us
  waiting for transfers between devices  95.8 us (41%)
  starting transfers between devices  63 us (27%)
  Pallas kernels  27.5 us (12%)
  between operations  15.1 us (7%)
  local copies, waits for them, and re-layouts  14.3 us (6%)
  other arithmetic  10.9 us (5%)
  matrix products  3.31 us (1%)
    ppermute x22, waiting for transfers between devices, shift(): lax.ppermute(array, axis, [(i, (i + by) % size) for i in range(size)])  51.1 us
    ppermute x22, starting transfers between devices, shift(): lax.ppermute(array, axis, [(i, (i + by) % size) for i in range(size)])  37.4 us
    all_to_all x4, waiting for transfers between devices, exchange(): return lax.all_to_all(array, axis, 0, 0, tiled=True)  33.4 us
    all_to_all x4, starting transfers between devices, exchange(): return lax.all_to_all(array, axis, 0, 0, tiled=True)  21.9 us
    pallas_call x1, Pallas kernels, attention(): pl.pallas_call(kernel, out_shape=jax.ShapeDtypeStruct((SEQ, 512), jnp.bfl...  12.7 us
    pallas_call x1, Pallas kernels, prepare(): pl.pallas_call(kernel, out_shape=[jax.ShapeDtypeStruct((8, SEQ, 1024), jn...  12.4 us
    all_gather x1, waiting for transfers between devices, step(): proj_all = lax.all_gather(proj_weight, 'z', axis=0, tiled=True)  7.25 us
    eq x4, other arithmetic, step(): owners[r] == sample_ids  4.74 us
  transfers between devices with their start and end apart: 31, of which 12 were waited for; matrix products, arithmetic and copies ran while one was open for 10% of the time, Pallas kernels for 6%

profile of v7, /device:TPU:1, one launch (start us, length us, event | category | flops | bytes accessed | tf_op | source)
XLA Modules:
  0.0 230.0 jit_solution(7146324973963113997)
XLA Ops:
  6.5 0.7 all-gather.3.cloned.1.call-update
  7.3 0.7 all-gather.5.cloned.1.call-update
  8.0 0.9 copy.41
  8.9 1.1 broadcast_in_dim.131
  10.1 6.7 %all-to-all-start = ((bf16[8,64,2,400]{3,1,2,0:T(8,128)(2,1)}), bf16[8,64,2,400]{3,1,2,0:T(8,128)(2,1)S(1)}, u32[]{:S(2)}, u32[]{:S(2)}) async-start(bf16[8,64,2,400]{3,1,2,0:T(8,128)(2,1)} %broadcast_in_dim.131), calls=%async_computation | async-start | bytes 2097152 | tf_op jit(solution)/shard_map/all_to_all | solution.py:29
  17.0 14.7 %all-to-all-done = bf16[8,64,2,400]{3,1,2,0:T(8,128)(2,1)S(1)} async-done(((bf16[8,64,2,400]{3,1,2,0:T(8,128)(2,1)}), bf16[8,64,2,400]{3,1,2,0:T(8,128)(2,1)S(1)}, u32[]{:S(2)}, u32[]{:S(2)}) %all-to-all-start) | async-done | bytes 819232 | tf_op jit(solution)/shard_map/all_to_all | solution.py:29
  31.7 0.3 convert_reduce_fusion
  32.0 0.5 fusion.5
  32.5 1.5 fusion.8
  34.0 3.5 %all-to-all-start.1 = ((bf16[4,2,64,2,400]{4,2,3,1,0:T(8,128)(2,1)}), bf16[4,2,64,2,400]{4,2,3,1,0:T(8,128)(2,1)S(1)}, u32[]{:S(2)}, u32[]{:S(2)}) async-start(bf16[4,2,64,2,400]{4,2,3,1,0:T(8,128)(2,1)} %bitcast.11), calls=%async_computation.1 | async-start | bytes 2097152 | tf_op jit(solution)/shard_map/all_to_all | solution.py:29
  37.9 0.2 convert_reduce_fusion.1
  38.1 0.6 fusion.24
  38.7 1.1 iota_compare_fusion
  39.8 1.1 iota_compare_fusion.2
  41.0 10.7 %all-to-all-done.1 = bf16[4,2,64,2,400]{4,2,3,1,0:T(8,128)(2,1)S(1)} async-done(((bf16[4,2,64,2,400]{4,2,3,1,0:T(8,128)(2,1)}), bf16[4,2,64,2,400]{4,2,3,1,0:T(8,128)(2,1)S(1)}, u32[]{:S(2)}, u32[]{:S(2)}) %all-to-all-start.1) | async-done | bytes 819232 | tf_op jit(solution)/shard_map/all_to_all | solution.py:29
  51.7 7.3 %all-gather.3.cloned.1.call-done = bf16[800,2,1024]{2,1,0:T(2,128)(2,1)} async-done(((bf16[100,2,1024]{2,1,0:T(2,128)(2,1)}), bf16[800,2,1024]{2,1,0:T(2,128)(2,1)}) %all-gather.3.cloned.1.call-update) | async-done | bytes 3276816 | tf_op jit(solution)/shard_map/all_gather | solution.py:260
  58.9 3.3 %fusion.12 = bf16[4,64,1024]{2,1,0:T(8,128)(2,1)S(1)} fusion(bf16[4,2,64,2,400]{4,2,3,1,0:T(8,128)(2,1)S(1)} %all-to-all-done.1, bf16[2,400,2,1024,1]{3,2,1,0,4:T(2,128)(2,1)} %bitcast.68), kind=kOutput, calls=%fused_computation.13 | convolution fusion | flops 839122944 | bytes 4620288 | tf_op jit(solution)/shard_map/sctmf,cfmo->sto/dot_general | solution.py:235
  62.3 2.8 %collective-permute-start.10 = (bf16[64,1024]{1,0:T(8,128)(2,1)S(1)}, bf16[64,1024]{1,0:T(8,128)(2,1)S(1)}, u32[]{:S(2)}, u32[]{:S(2)}) collective-permute-start(bf16[64,1024]{1,0:T(8,128)(2,1)S(1)} %get-tuple-element.15), channel_id=1, source_target_pairs={{0,128},{64,192},{128,0},{192,64},{1,129},{65,193},{129,1},{193,65... | collective-permute-start | bytes 393224 | tf_op jit(solution)/shard_map/ppermute | solution.py:25
  65.1 0.9 collective-permute-start.11
  66.0 1.2 iota_compare_fusion.4
  67.2 1.3 iota_compare_fusion.6
  68.5 2.6 %collective-permute-done.11 = bf16[64,1024]{1,0:T(8,128)(2,1)S(1)} collective-permute-done((bf16[64,1024]{1,0:T(8,128)(2,1)S(1)}, bf16[64,1024]{1,0:T(8,128)(2,1)S(1)}, u32[]{:S(2)}, u32[]{:S(2)}) %collective-permute-start.11) | collective-permute-done | bytes 131104 | tf_op jit(solution)/shard_map/ppermute | solution.py:25
  71.2 1.2 select_select_fusion
  72.4 7.5 %all-to-all-start.2 = ((bf16[32,8,1024]{2,1,0:T(8,128)(2,1)}), bf16[32,8,1024]{2,1,0:T(8,128)(2,1)S(1)}, u32[]{:S(2)}, u32[]{:S(2)}) async-start(bf16[32,8,1024]{2,1,0:T(8,128)(2,1)} %select_select_fusion), calls=%async_computation.2 | async-start | bytes 1048576 | tf_op jit(solution)/shard_map/all_to_all | solution.py:29
  80.0 1.3 collective-permute-start.13
  81.3 1.4 collective-permute-start.14
  82.7 20.4 %collective-permute-done.13.refs_1_ = bf16[256,256]{1,0:T(8,128)(2,1)S(1)} collective-permute-done((bf16[256,256]{1,0:T(8,128)(2,1)S(1)}, bf16[256,256]{1,0:T(8,128)(2,1)S(1)}, u32[]{:S(2)}, u32[]{:S(2)}) %collective-permute-start.13) | collective-permute-done | bytes 131104 | tf_op jit(solution)/shard_map/ppermute | solution.py:21
  103.1 2.7 %collective-permute-start.16 = (bf16[256,256]{1,0:T(8,128)(2,1)S(1)}, bf16[256,256]{1,0:T(8,128)(2,1)S(1)}, u32[]{:S(2)}, u32[]{:S(2)}) collective-permute-start(bf16[256,256]{1,0:T(8,128)(2,1)S(1)} %collective-permute-done.14.refs_2_), channel_id=1, source_target_pairs={{0,56},{8,0},{16,8},{24,16},{32,24},{40,32},{48,40},{56,48},{1,57}... | collective-permute-start | bytes 393224 | tf_op jit(solution)/shard_map/ppermute | solution.py:21
  105.8 1.2 collective-permute-start.1
  107.0 1.5 collective-permute-start.3
  108.5 2.7 %collective-permute-start = (bf16[384,1024]{1,0:T(8,128)(2,1)S(1)}, bf16[384,1024]{1,0:T(8,128)(2,1)S(1)}, u32[]{:S(2)}, u32[]{:S(2)}) collective-permute-start(bf16[384,1024]{1,0:T(8,128)(2,1)S(1)} %bitcast.59), channel_id=1, source_target_pairs={{0,1},{1,0},{2,3},{3,2},{4,5},{5,4},{6,7},{7,6},{8,9},{9,8},{10,11... | collective-permute-start | bytes 2359304 | tf_op jit(solution)/shard_map/ppermute | solution.py:21
  111.1 2.7 %collective-permute-start.18 = (bf16[256,256]{1,0:T(8,128)(2,1)S(1)}, bf16[256,256]{1,0:T(8,128)(2,1)S(1)}, u32[]{:S(2)}, u32[]{:S(2)}) collective-permute-start(bf16[256,256]{1,0:T(8,128)(2,1)S(1)} %collective-permute-done.16.refs_4_), channel_id=1, source_target_pairs={{0,56},{8,0},{16,8},{24,16},{32,24},{40,32},{48,40},{56,48},{1,57}... | collective-permute-start | bytes 393224 | tf_op jit(solution)/shard_map/ppermute | solution.py:21
  113.8 0.7 fusion.20
  114.5 0.6 fusion.22
  115.1 2.2 collective-permute-done.17.refs_5_
  117.5 2.7 %collective-permute-start.20 = (bf16[128,256]{1,0:T(8,128)(2,1)S(1)}, bf16[128,256]{1,0:T(8,128)(2,1)}, u32[]{:S(2)}, u32[]{:S(2)}) collective-permute-start(bf16[128,256]{1,0:T(8,128)(2,1)S(1)} %slice.109), channel_id=1, source_target_pairs={{0,56},{8,0},{16,8},{24,16},{32,24},{40,32},{48,40},{56,48},{1,57}... | collective-permute-start | bytes 196616 | tf_op jit(solution)/shard_map/ppermute | solution.py:21
  120.2 3.6 %collective-permute-done.19.refs_7_ = bf16[128,256]{1,0:T(8,128)(2,1)} collective-permute-done((bf16[128,256]{1,0:T(8,128)(2,1)S(1)}, bf16[128,256]{1,0:T(8,128)(2,1)}, u32[]{:S(2)}, u32[]{:S(2)}) %collective-permute-start.19) | collective-permute-done | bytes 65568 | tf_op jit(solution)/shard_map/ppermute | solution.py:21
  123.8 2.4 %pack.1.refs_12_ = bf16[2048,256]{1,0:T(8,128)(2,1)} custom-call(bf16[256,256]{1,0:T(8,128)(2,1)} %bitcast.64, bf16[256,256]{1,0:T(8,128)(2,1)} %copy-done.10, bf16[256,256]{1,0:T(8,128)(2,1)} %copy-done.11, bf16[256,256]{1,0:T(8,128)(2,1)} %copy-done.12, bf16[256,256]{1,0:T(8,128)(2,1)} %copy-done.13, bf16[256,256]{1,0:T(8,128)(2,1)} %copy-done.8, ...), custom_call_target="tpu_custom_call" | custom-call | tf_op jit(solution)/shard_map/pack/pallas_call | solution.py:85
  126.1 0.6 collective-permute-start.21
  126.8 2.0 collective-permute-start.22
  128.8 0.6 gather_fusion
  129.4 1.1 broadcast_in_dim.149
  130.5 4.2 %all-to-all-start.3 = ((bf16[4,128,1024]{2,1,0:T(8,128)(2,1)}), bf16[4,128,1024]{2,1,0:T(8,128)(2,1)}, u32[]{:S(2)}, u32[]{:S(2)}) async-start(bf16[4,128,1024]{2,1,0:T(8,128)(2,1)} %broadcast_in_dim.149), calls=%async_computation.3 | async-start | bytes 2097152 | tf_op jit(solution)/shard_map/all_to_all | solution.py:29
  134.8 1.5 collective-permute-start.5
  136.3 1.0 slice.99
  137.3 1.3 collective-permute-start.7
  138.7 7.9 %all-to-all-done.3.refs_10_ = bf16[4,128,1024]{2,1,0:T(8,128)(2,1)} async-done(((bf16[4,128,1024]{2,1,0:T(8,128)(2,1)}), bf16[4,128,1024]{2,1,0:T(8,128)(2,1)}, u32[]{:S(2)}, u32[]{:S(2)}) %all-to-all-start.3) | async-done | bytes 1048608 | tf_op jit(solution)/shard_map/all_to_all | solution.py:29
  146.6 7.8 %collective-permute-start.12 = (bf16[4,128,1024]{2,1,0:T(8,128)(2,1)}, bf16[4,128,1024]{2,1,0:T(8,128)(2,1)}, u32[]{:S(2)}, u32[]{:S(2)}) collective-permute-start(bf16[4,128,1024]{2,1,0:T(8,128)(2,1)} %all-to-all-done.3.refs_10_), channel_id=1, source_target_pairs={{0,1},{1,0},{2,3},{3,2},{4,5},{5,4},{6,7},{7,6},{8,9},{9,8},{10,11... | collective-permute-start | bytes 3145736 | tf_op jit(solution)/shard_map/ppermute | solution.py:21
  154.4 1.0 collective-permute-done.5.refs_6_
  155.4 3.5 %collective-permute-start.6 = (bf16[192,1024]{1,0:T(8,128)(2,1)S(1)}, bf16[192,1024]{1,0:T(8,128)(2,1)S(1)}, u32[]{:S(2)}, u32[]{:S(2)}) collective-permute-start(bf16[192,1024]{1,0:T(8,128)(2,1)S(1)} %collective-permute-done.5.refs_6_), channel_id=1, source_target_pairs={{0,1},{1,0},{2,3},{3,2},{4,5},{5,4},{6,7},{7,6},{8,9},{9,8},{10,11... | collective-permute-start | bytes 1179656 | tf_op jit(solution)/shard_map/ppermute | solution.py:21
  159.0 15.4 %collective-permute-done.21.refs_13_ = bf16[2048,256]{1,0:T(8,128)(2,1)} collective-permute-done((bf16[2048,256]{1,0:T(8,128)(2,1)}, bf16[2048,256]{1,0:T(8,128)(2,1)}, u32[]{:S(2)}, u32[]{:S(2)}) %collective-permute-start.21) | collective-permute-done | bytes 1048608 | tf_op jit(solution)/shard_map/ppermute | solution.py:21
  174.4 1.6 collective-permute-start.2
  176.0 1.9 slice.110
  177.9 1.9 slice.111
  179.8 0.7 copy-done.3
  180.5 0.8 copy-done.5
  181.3 2.7 %collective-permute-start.24 = (bf16[1024,256]{1,0:T(8,128)(2,1)}, bf16[1024,256]{1,0:T(8,128)(2,1)}, u32[]{:S(2)}, u32[]{:S(2)}) collective-permute-start(bf16[1024,256]{1,0:T(8,128)(2,1)} %slice.111), channel_id=1, source_target_pairs={{0,192},{64,0},{128,64},{192,128},{1,193},{65,1},{129,65},{193,129... | collective-permute-start | bytes 1572872 | tf_op jit(solution)/shard_map/ppermute | solution.py:21
  185.3 0.8 fusion.18
  186.3 8.6 %collective-permute-done.23.refs_15_ = bf16[1024,256]{1,0:T(8,128)(2,1)S(1)} collective-permute-done((bf16[1024,256]{1,0:T(8,128)(2,1)}, bf16[1024,256]{1,0:T(8,128)(2,1)S(1)}, u32[]{:S(2)}, u32[]{:S(2)}) %collective-permute-start.23) | collective-permute-done | bytes 524320 | tf_op jit(solution)/shard_map/ppermute | solution.py:21
  194.9 1.0 copy-done.2
  195.9 1.0 copy-done.4
  196.9 1.0 copy-done.6
  197.9 12.4 %prepare.1 = (bf16[8,384,1024]{2,1,0:T(8,128)(2,1)}, bf16[384,128]{1,0:T(8,128)(2,1)S(1)}, bf16[384,128]{1,0:T(8,128)(2,1)S(1)}) custom-call(s32[6]{0:T(128)S(1)} %stack.23.where_ref, bf16[384,1024]{1,0:T(8,128)(2,1)S(1)} %bitcast.60, bf16[384,1024]{1,0:T(8,128)(2,1)S(1)} %collective-permute-done.refs_1_, ...), custom_call_target="tpu_custom_call" | custom-call | tf_op jit(solution)/shard_map/prepare/pallas_call | solution.py:158
  210.3 12.7 %attention.1 = bf16[384,512]{1,0:T(8,128)(2,1)} custom-call(bf16[8,384,1024]{2,1,0:T(8,128)(2,1)} %get-tuple-element.8.a_ref, bf16[8192,512]{1,0:T(8,128)(2,1)} %all-gather.5.cloned.1.call-done.w_hbm, bf16[384,128]{1,0:T(8,128)(2,1)S(1)} %get-tuple-element.9.key_ref, bf16[384,128]{1,0:T(8,128)(2,1)S(1)} %get-tuple-element.10.value_ref, ...), custom_call_target="tpu_custom_call" | custom-call | tf_op jit(solution)/shard_map/attention/pallas_call | solution.py:211
  (84 shorter events, 1.5 us)
Async XLA Ops:
  6.5 10.2 %copy-start.16 = (f32[2,3200]{1,0:T(2,128)S(1)}, f32[2,3200]{1,0:T(2,128)}, u32[]{:S(2)}) copy-start(f32[2,3200]{1,0:T(2,128)} %param.11) | copy-start | bytes 76804
  6.5 10.3 %copy-start.17 = (f32[2,3200]{1,0:T(2,128)S(1)}, f32[2,3200]{1,0:T(2,128)}, u32[]{:S(2)}) copy-start(f32[2,3200]{1,0:T(2,128)} %param.12) | copy-start | bytes 76804
  6.5 52.4 %all-gather.3.cloned.1.call-start = ((), (), s32[]{:S(2)}) async-start(), calls=%async_computation.4 | async-start | bytes 3686400 | tf_op jit(solution)/shard_map/all_gather | solution.py:260
  7.3 203.1 %all-gather.5.cloned.1.call-start = ((), (), s32[]{:S(2)}) async-start(), calls=%async_computation.5 | async-start | bytes 8650752 | tf_op jit(solution)/shard_map/all_gather | solution.py:261
  10.1 21.7 %all-to-all-start = ((bf16[8,64,2,400]{3,1,2,0:T(8,128)(2,1)}), bf16[8,64,2,400]{3,1,2,0:T(8,128)(2,1)S(1)}, u32[]{:S(2)}, u32[]{:S(2)}) async-start(bf16[8,64,2,400]{3,1,2,0:T(8,128)(2,1)} %broadcast_in_dim.131), calls=%async_computation | async-start | bytes 2097152 | tf_op jit(solution)/shard_map/all_to_all | solution.py:29
  32.5 5.1 %copy-start.18 = (s32[32]{0:T(128)S(1)}, s32[32]{0:T(128)}, u32[]{:S(2)}) copy-start(s32[32]{0:T(128)} %param.18) | copy-start | bytes 388
  34.0 17.6 %all-to-all-start.1 = ((bf16[4,2,64,2,400]{4,2,3,1,0:T(8,128)(2,1)}), bf16[4,2,64,2,400]{4,2,3,1,0:T(8,128)(2,1)S(1)}, u32[]{:S(2)}, u32[]{:S(2)}) async-start(bf16[4,2,64,2,400]{4,2,3,1,0:T(8,128)(2,1)} %bitcast.11), calls=%async_computation.1 | async-start | bytes 2097152 | tf_op jit(solution)/shard_map/all_to_all | solution.py:29
  62.2 17.7 %copy-start.14 = (bf16[256,2,128]{2,1,0:T(2,128)(2,1)S(1)}, bf16[256,2,128]{2,1,0:T(2,128)(2,1)}, u32[]{:S(2)}) copy-start(bf16[256,2,128]{2,1,0:T(2,128)(2,1)} %param.17) | copy-start | bytes 393220
  62.3 43.5 %copy-start = (bf16[1,384,1024]{2,1,0:T(8,128)(2,1)S(1)}, bf16[1,384,1024]{2,1,0:T(8,128)(2,1)}, u32[]{:S(2)}) copy-start(bf16[1,384,1024]{2,1,0:T(8,128)(2,1)} %param.14) | copy-start | bytes 2359300
  62.3 6.2 %collective-permute-start.10 = (bf16[64,1024]{1,0:T(8,128)(2,1)S(1)}, bf16[64,1024]{1,0:T(8,128)(2,1)S(1)}, u32[]{:S(2)}, u32[]{:S(2)}) collective-permute-start(bf16[64,1024]{1,0:T(8,128)(2,1)S(1)} %get-tuple-element.15), channel_id=1, source_target_pairs={{0,128},{64,192},{128,0},{192,64},{1,129},{65,193},{129,1},{193,65... | collective-permute-start | bytes 393224 | tf_op jit(solution)/shard_map/ppermute | solution.py:25
  65.1 5.9 %collective-permute-start.11 = (bf16[64,1024]{1,0:T(8,128)(2,1)S(1)}, bf16[64,1024]{1,0:T(8,128)(2,1)S(1)}, u32[]{:S(2)}, u32[]{:S(2)}) collective-permute-start(bf16[64,1024]{1,0:T(8,128)(2,1)S(1)} %get-tuple-element.14), channel_id=1, source_target_pairs={{0,192},{64,128},{128,64},{192,0},{1,193},{65,129},{129,65},{193,1... | collective-permute-start | bytes 393224 | tf_op jit(solution)/shard_map/ppermute | solution.py:25
  66.0 5.1 %collective-permute-start.9 = (bf16[64,1024]{1,0:T(8,128)(2,1)S(1)}, bf16[64,1024]{1,0:T(8,128)(2,1)S(1)}, u32[]{:S(2)}, u32[]{:S(2)}) collective-permute-start(bf16[64,1024]{1,0:T(8,128)(2,1)S(1)} %get-tuple-element.13), channel_id=1, source_target_pairs={{0,64},{64,0},{128,192},{192,128},{1,65},{65,1},{129,193},{193,129... | collective-permute-start | bytes 393224 | tf_op jit(solution)/shard_map/ppermute | solution.py:25
  72.4 56.4 %all-to-all-start.2 = ((bf16[32,8,1024]{2,1,0:T(8,128)(2,1)}), bf16[32,8,1024]{2,1,0:T(8,128)(2,1)S(1)}, u32[]{:S(2)}, u32[]{:S(2)}) async-start(bf16[32,8,1024]{2,1,0:T(8,128)(2,1)} %select_select_fusion), calls=%async_computation.2 | async-start | bytes 1048576 | tf_op jit(solution)/shard_map/all_to_all | solution.py:29
  80.0 43.8 %copy-start.7 = (bf16[32,8,2,128]{3,1,2,0:T(8,128)(2,1)}, bf16[32,8,2,128]{3,1,2,0:T(8,128)(2,1)S(1)}, u32[]{:S(2)}) copy-start(bf16[32,8,2,128]{3,1,2,0:T(8,128)(2,1)S(1)} %copy.65) | copy-start | bytes 393220
  80.0 23.1 %collective-permute-start.13 = (bf16[256,256]{1,0:T(8,128)(2,1)S(1)}, bf16[256,256]{1,0:T(8,128)(2,1)S(1)}, u32[]{:S(2)}, u32[]{:S(2)}) collective-permute-start(bf16[256,256]{1,0:T(8,128)(2,1)S(1)} %bitcast.62), channel_id=1, source_target_pairs={{0,8},{8,16},{16,24},{24,32},{32,40},{40,48},{48,56},{56,0},{1,9},... | collective-permute-start | bytes 393224 | tf_op jit(solution)/shard_map/ppermute | solution.py:21
  81.3 21.8 %collective-permute-start.14 = (bf16[256,256]{1,0:T(8,128)(2,1)S(1)}, bf16[256,256]{1,0:T(8,128)(2,1)S(1)}, u32[]{:S(2)}, u32[]{:S(2)}) collective-permute-start(bf16[256,256]{1,0:T(8,128)(2,1)S(1)} %bitcast.63), channel_id=1, source_target_pairs={{0,56},{8,0},{16,8},{24,16},{32,24},{40,32},{48,40},{56,48},{1,57}... | collective-permute-start | bytes 393224 | tf_op jit(solution)/shard_map/ppermute | solution.py:21
  103.1 20.7 %copy-start.10 = (bf16[256,256]{1,0:T(8,128)(2,1)}, bf16[256,256]{1,0:T(8,128)(2,1)S(1)}, u32[]{:S(2)}) copy-start(bf16[256,256]{1,0:T(8,128)(2,1)S(1)} %collective-permute-done.13.refs_1_) | copy-start | bytes 393220
  103.1 8.0 %collective-permute-start.15 = (bf16[256,256]{1,0:T(8,128)(2,1)S(1)}, bf16[256,256]{1,0:T(8,128)(2,1)S(1)}, u32[]{:S(2)}, u32[]{:S(2)}) collective-permute-start(bf16[256,256]{1,0:T(8,128)(2,1)S(1)} %collective-permute-done.13.refs_1_), channel_id=1, source_target_pairs={{0,8},{8,16},{16,24},{24,32},{32,40},{40,48},{48,56},{56,0},{1,9},... | collective-permute-start | bytes 393224 | tf_op jit(solution)/shard_map/ppermute | solution.py:21
  103.1 20.6 %copy-start.11 = (bf16[256,256]{1,0:T(8,128)(2,1)}, bf16[256,256]{1,0:T(8,128)(2,1)S(1)}, u32[]{:S(2)}) copy-start(bf16[256,256]{1,0:T(8,128)(2,1)S(1)} %collective-permute-done.14.refs_2_) | copy-start | bytes 393220
  103.1 8.0 %collective-permute-start.16 = (bf16[256,256]{1,0:T(8,128)(2,1)S(1)}, bf16[256,256]{1,0:T(8,128)(2,1)S(1)}, u32[]{:S(2)}, u32[]{:S(2)}) collective-permute-start(bf16[256,256]{1,0:T(8,128)(2,1)S(1)} %collective-permute-done.14.refs_2_), channel_id=1, source_target_pairs={{0,56},{8,0},{16,8},{24,16},{32,24},{40,32},{48,40},{56,48},{1,57}... | collective-permute-start | bytes 393224 | tf_op jit(solution)/shard_map/ppermute | solution.py:21
  105.8 29.0 %collective-permute-start.1 = (bf16[384,1024]{1,0:T(8,128)(2,1)S(1)}, bf16[384,1024]{1,0:T(8,128)(2,1)S(1)}, u32[]{:S(2)}, u32[]{:S(2)}) collective-permute-start(bf16[384,1024]{1,0:T(8,128)(2,1)S(1)} %bitcast.57), channel_id=1, source_target_pairs={{0,2},{2,4},{4,6},{6,0},{1,3},{3,5},{5,7},{7,1},{8,10},{10,12},{12... | collective-permute-start | bytes 2359304 | tf_op jit(solution)/shard_map/ppermute | solution.py:21
  107.0 29.3 %collective-permute-start.3 = (bf16[384,1024]{1,0:T(8,128)(2,1)S(1)}, bf16[384,1024]{1,0:T(8,128)(2,1)}, u32[]{:S(2)}, u32[]{:S(2)}) collective-permute-start(bf16[384,1024]{1,0:T(8,128)(2,1)S(1)} %bitcast.58), channel_id=1, source_target_pairs={{0,6},{2,0},{4,2},{6,4},{1,7},{3,1},{5,3},{7,5},{8,14},{10,8},{12,... | collective-permute-start | bytes 2359304 | tf_op jit(solution)/shard_map/ppermute | solution.py:21
  108.5 30.2 %collective-permute-start = (bf16[384,1024]{1,0:T(8,128)(2,1)S(1)}, bf16[384,1024]{1,0:T(8,128)(2,1)S(1)}, u32[]{:S(2)}, u32[]{:S(2)}) collective-permute-start(bf16[384,1024]{1,0:T(8,128)(2,1)S(1)} %bitcast.59), channel_id=1, source_target_pairs={{0,1},{1,0},{2,3},{3,2},{4,5},{5,4},{6,7},{7,6},{8,9},{9,8},{10,11... | collective-permute-start | bytes 2359304 | tf_op jit(solution)/shard_map/ppermute | solution.py:21
  111.1 6.3 %copy-start.12 = (bf16[256,256]{1,0:T(8,128)(2,1)}, bf16[256,256]{1,0:T(8,128)(2,1)S(1)}, u32[]{:S(2)}) copy-start(bf16[256,256]{1,0:T(8,128)(2,1)S(1)} %collective-permute-done.15.refs_3_) | copy-start | bytes 393220
  111.1 6.2 %collective-permute-start.17 = (bf16[256,256]{1,0:T(8,128)(2,1)S(1)}, bf16[256,256]{1,0:T(8,128)(2,1)S(1)}, u32[]{:S(2)}, u32[]{:S(2)}) collective-permute-start(bf16[256,256]{1,0:T(8,128)(2,1)S(1)} %collective-permute-done.15.refs_3_), channel_id=1, source_target_pairs={{0,8},{8,16},{16,24},{24,32},{32,40},{40,48},{48,56},{56,0},{1,9},... | collective-permute-start | bytes 393224 | tf_op jit(solution)/shard_map/ppermute | solution.py:21
  111.1 6.3 %copy-start.13 = (bf16[256,256]{1,0:T(8,128)(2,1)}, bf16[256,256]{1,0:T(8,128)(2,1)S(1)}, u32[]{:S(2)}) copy-start(bf16[256,256]{1,0:T(8,128)(2,1)S(1)} %collective-permute-done.16.refs_4_) | copy-start | bytes 393220
  111.1 6.3 %collective-permute-start.18 = (bf16[256,256]{1,0:T(8,128)(2,1)S(1)}, bf16[256,256]{1,0:T(8,128)(2,1)S(1)}, u32[]{:S(2)}, u32[]{:S(2)}) collective-permute-start(bf16[256,256]{1,0:T(8,128)(2,1)S(1)} %collective-permute-done.16.refs_4_), channel_id=1, source_target_pairs={{0,56},{8,0},{16,8},{24,16},{32,24},{40,32},{48,40},{56,48},{1,57}... | collective-permute-start | bytes 393224 | tf_op jit(solution)/shard_map/ppermute | solution.py:21
  117.3 6.4 %copy-start.8 = (bf16[256,256]{1,0:T(8,128)(2,1)}, bf16[256,256]{1,0:T(8,128)(2,1)S(1)}, u32[]{:S(2)}) copy-start(bf16[256,256]{1,0:T(8,128)(2,1)S(1)} %collective-permute-done.17.refs_5_) | copy-start | bytes 393220
  117.3 6.4 %collective-permute-start.19 = (bf16[128,256]{1,0:T(8,128)(2,1)S(1)}, bf16[128,256]{1,0:T(8,128)(2,1)}, u32[]{:S(2)}, u32[]{:S(2)}) collective-permute-start(bf16[128,256]{1,0:T(8,128)(2,1)S(1)} %slice.108), channel_id=1, source_target_pairs={{0,8},{8,16},{16,24},{24,32},{32,40},{40,48},{48,56},{56,0},{1,9},... | collective-permute-start | bytes 196616 | tf_op jit(solution)/shard_map/ppermute | solution.py:21
  117.4 6.3 %copy-start.9 = (bf16[256,256]{1,0:T(8,128)(2,1)}, bf16[256,256]{1,0:T(8,128)(2,1)S(1)}, u32[]{:S(2)}) copy-start(bf16[256,256]{1,0:T(8,128)(2,1)S(1)} %collective-permute-done.18.refs_6_) | copy-start | bytes 393220
  117.5 6.3 %collective-permute-start.20 = (bf16[128,256]{1,0:T(8,128)(2,1)S(1)}, bf16[128,256]{1,0:T(8,128)(2,1)}, u32[]{:S(2)}, u32[]{:S(2)}) collective-permute-start(bf16[128,256]{1,0:T(8,128)(2,1)S(1)} %slice.109), channel_id=1, source_target_pairs={{0,56},{8,0},{16,8},{24,16},{32,24},{40,32},{48,40},{56,48},{1,57}... | collective-permute-start | bytes 196616 | tf_op jit(solution)/shard_map/ppermute | solution.py:21
  126.1 48.2 %collective-permute-start.21 = (bf16[2048,256]{1,0:T(8,128)(2,1)}, bf16[2048,256]{1,0:T(8,128)(2,1)}, u32[]{:S(2)}, u32[]{:S(2)}) collective-permute-start(bf16[2048,256]{1,0:T(8,128)(2,1)} %pack.1.refs_12_), channel_id=1, source_target_pairs={{0,64},{64,128},{128,192},{192,0},{1,65},{65,129},{129,193},{193,1... | collective-permute-start | bytes 3145736 | tf_op jit(solution)/shard_map/ppermute | solution.py:21
  126.8 49.2 %collective-permute-start.22 = (bf16[2048,256]{1,0:T(8,128)(2,1)}, bf16[2048,256]{1,0:T(8,128)(2,1)}, u32[]{:S(2)}, u32[]{:S(2)}) collective-permute-start(bf16[2048,256]{1,0:T(8,128)(2,1)} %pack.1.refs_12_), channel_id=1, source_target_pairs={{0,192},{64,0},{128,64},{192,128},{1,193},{65,1},{129,65},{193,129... | collective-permute-start | bytes 3145736 | tf_op jit(solution)/shard_map/ppermute | solution.py:21
  130.5 16.1 %all-to-all-start.3 = ((bf16[4,128,1024]{2,1,0:T(8,128)(2,1)}), bf16[4,128,1024]{2,1,0:T(8,128)(2,1)}, u32[]{:S(2)}, u32[]{:S(2)}) async-start(bf16[4,128,1024]{2,1,0:T(8,128)(2,1)} %broadcast_in_dim.149), calls=%async_computation.3 | async-start | bytes 2097152 | tf_op jit(solution)/shard_map/all_to_all | solution.py:29
  134.8 20.6 %collective-permute-start.5 = (bf16[192,1024]{1,0:T(8,128)(2,1)S(1)}, bf16[192,1024]{1,0:T(8,128)(2,1)S(1)}, u32[]{:S(2)}, u32[]{:S(2)}) collective-permute-start(bf16[192,1024]{1,0:T(8,128)(2,1)S(1)} %slice.98), channel_id=1, source_target_pairs={{0,2},{2,4},{4,6},{6,0},{1,3},{3,5},{5,7},{7,1},{8,10},{10,12},{12... | collective-permute-start | bytes 1179656 | tf_op jit(solution)/shard_map/ppermute | solution.py:21
  137.3 21.6 %collective-permute-start.7 = (bf16[192,1024]{1,0:T(8,128)(2,1)S(1)}, bf16[192,1024]{1,0:T(8,128)(2,1)}, u32[]{:S(2)}, u32[]{:S(2)}) collective-permute-start(bf16[192,1024]{1,0:T(8,128)(2,1)S(1)} %slice.99), channel_id=1, source_target_pairs={{0,6},{2,0},{4,2},{6,4},{1,7},{3,1},{5,3},{7,5},{8,14},{10,8},{12,... | collective-permute-start | bytes 1179656 | tf_op jit(solution)/shard_map/ppermute | solution.py:21
  146.6 48.3 %collective-permute-start.12 = (bf16[4,128,1024]{2,1,0:T(8,128)(2,1)}, bf16[4,128,1024]{2,1,0:T(8,128)(2,1)}, u32[]{:S(2)}, u32[]{:S(2)}) collective-permute-start(bf16[4,128,1024]{2,1,0:T(8,128)(2,1)} %all-to-all-done.3.refs_10_), channel_id=1, source_target_pairs={{0,1},{1,0},{2,3},{3,2},{4,5},{5,4},{6,7},{7,6},{8,9},{9,8},{10,11... | collective-permute-start | bytes 3145736 | tf_op jit(solution)/shard_map/ppermute | solution.py:21
  155.4 30.7 %copy-start.1 = (bf16[192,1024]{1,0:T(8,128)(2,1)}, bf16[192,1024]{1,0:T(8,128)(2,1)S(1)}, u32[]{:S(2)}) copy-start(bf16[192,1024]{1,0:T(8,128)(2,1)S(1)} %collective-permute-done.5.refs_6_) | copy-start | bytes 1179652
  155.4 24.3 %collective-permute-start.6 = (bf16[192,1024]{1,0:T(8,128)(2,1)S(1)}, bf16[192,1024]{1,0:T(8,128)(2,1)S(1)}, u32[]{:S(2)}, u32[]{:S(2)}) collective-permute-start(bf16[192,1024]{1,0:T(8,128)(2,1)S(1)} %collective-permute-done.5.refs_6_), channel_id=1, source_target_pairs={{0,1},{1,0},{2,3},{3,2},{4,5},{5,4},{6,7},{7,6},{8,9},{9,8},{10,11... | collective-permute-start | bytes 1179656 | tf_op jit(solution)/shard_map/ppermute | solution.py:21
  158.9 26.3 %copy-start.15 = (f32[8192]{0:T(1024)S(1)}, f32[8192]{0:T(1024)}, u32[]{:S(2)}) copy-start(f32[8192]{0:T(1024)} %param.15) | copy-start | bytes 98308
  158.9 21.6 %collective-permute-start.8 = (bf16[192,1024]{1,0:T(8,128)(2,1)}, bf16[192,1024]{1,0:T(8,128)(2,1)S(1)}, u32[]{:S(2)}, u32[]{:S(2)}) collective-permute-start(bf16[192,1024]{1,0:T(8,128)(2,1)} %collective-permute-done.7.refs_8_), channel_id=1, source_target_pairs={{0,1},{1,0},{2,3},{3,2},{4,5},{5,4},{6,7},{7,6},{8,9},{9,8},{10,11... | collective-permute-start | bytes 1179656 | tf_op jit(solution)/shard_map/ppermute | solution.py:21
  174.4 11.9 %collective-permute-start.2 = (bf16[384,1024]{1,0:T(8,128)(2,1)S(1)}, bf16[384,1024]{1,0:T(8,128)(2,1)}, u32[]{:S(2)}, u32[]{:S(2)}) collective-permute-start(bf16[384,1024]{1,0:T(8,128)(2,1)S(1)} %collective-permute-done.1.refs_2_), channel_id=1, source_target_pairs={{0,1},{1,0},{2,3},{3,2},{4,5},{5,4},{6,7},{7,6},{8,9},{9,8},{10,11... | collective-permute-start | bytes 2359304 | tf_op jit(solution)/shard_map/ppermute | solution.py:21
  176.0 10.3 %collective-permute-start.4 = (bf16[384,1024]{1,0:T(8,128)(2,1)}, bf16[384,1024]{1,0:T(8,128)(2,1)}, u32[]{:S(2)}, u32[]{:S(2)}) collective-permute-start(bf16[384,1024]{1,0:T(8,128)(2,1)} %collective-permute-done.3.refs_4_), channel_id=1, source_target_pairs={{0,1},{1,0},{2,3},{3,2},{4,5},{5,4},{6,7},{7,6},{8,9},{9,8},{10,11... | collective-permute-start | bytes 2359304 | tf_op jit(solution)/shard_map/ppermute | solution.py:21
  179.8 0.7 copy-start.3
  180.5 14.4 %collective-permute-start.23 = (bf16[1024,256]{1,0:T(8,128)(2,1)}, bf16[1024,256]{1,0:T(8,128)(2,1)S(1)}, u32[]{:S(2)}, u32[]{:S(2)}) collective-permute-start(bf16[1024,256]{1,0:T(8,128)(2,1)} %slice.110), channel_id=1, source_target_pairs={{0,64},{64,128},{128,192},{192,0},{1,65},{65,129},{129,193},{193,1... | collective-permute-start | bytes 1572872 | tf_op jit(solution)/shard_map/ppermute | solution.py:21
  180.5 0.8 copy-start.5
  181.3 13.6 %collective-permute-start.24 = (bf16[1024,256]{1,0:T(8,128)(2,1)}, bf16[1024,256]{1,0:T(8,128)(2,1)}, u32[]{:S(2)}, u32[]{:S(2)}) collective-permute-start(bf16[1024,256]{1,0:T(8,128)(2,1)} %slice.111), channel_id=1, source_target_pairs={{0,192},{64,0},{128,64},{192,128},{1,193},{65,1},{129,65},{193,129... | collective-permute-start | bytes 1572872 | tf_op jit(solution)/shard_map/ppermute | solution.py:21
  194.9 1.0 copy-start.2
  195.9 1.0 copy-start.4
  196.9 1.0 copy-start.6
Sparse Core Ops, SparseCore 0:
  9.1 49.7 all-gather.2
  61.5 122.0 all-gather.4

commit v8 on v5

--- a/solution.py
+++ b/solution.py
@@ -174,25 +174,30 @@
 
 
 def attention(sequence, query_w, key, value, cosine, sine):
-    def kernel(a_ref, w_hbm, key_ref, value_ref, cos_ref, sin_ref, out_ref, w_ref, sem):
-        loads = [
-            pltpu.make_async_copy(
-                w_hbm.at[pl.ds(t * 1024, 1024), :], w_ref.at[pl.ds(t * 1024, 1024), :], sem.at[t]
-            )
-            for t in range(8)
-        ]
-        for copy in loads:
-            copy.start()
+    def kernel(
+        a_hbm, w_hbm, key_ref, value_ref, cos_ref, sin_ref, out_ref, a_ref, w_ref, a_sem, w_sem
+    ):
+        loads = []
+        for t in range(8):
+            rows = pl.ds(t * 1024, 1024)
+            loads.append(
+                (
+                    pltpu.make_async_copy(a_hbm.at[t], a_ref.at[t], a_sem.at[t]),
+                    pltpu.make_async_copy(w_hbm.at[rows, :], w_ref.at[rows, :], w_sem.at[t]),
+                )
+            )
+            for copy in loads[-1]:
+                copy.start()
         acc = jnp.zeros((SEQ, 512), jnp.float32)
         for t in range(8):
-            loads[t].wait()
+            for copy in loads[t]:
+                copy.wait()
             acc = acc + jnp.dot(
                 a_ref[t], w_ref[t * 1024 : (t + 1) * 1024, :], preferred_element_type=jnp.float32
             )
         cos, sin = cos_ref[...], sin_ref[...]
-        causal = lax.broadcasted_iota(jnp.int32, (SEQ, SEQ), 0) >= lax.broadcasted_iota(
-            jnp.int32, (SEQ, SEQ), 1
-        )
+        at = lax.broadcasted_iota(jnp.int32, (SEQ, SEQ), 0)
+        causal = at >= lax.broadcasted_iota(jnp.int32, (SEQ, SEQ), 1)
         for h in range(4):
             query = rotated(acc[:, h * HEAD : (h + 1) * HEAD], cos, sin)
             scores = lax.dot_general(
@@ -201,7 +206,7 @@
             scores = jnp.where(causal, scores, -1e30)
             top = jnp.max(scores, axis=1, keepdims=True)
             e = jnp.exp(scores - top)
-            w = (e / jnp.sum(e, axis=1, keepdims=True)).astype(jnp.bfloat16)
+            w = (e * (1.0 / jnp.sum(e, axis=1, keepdims=True))).astype(jnp.bfloat16)
             out_ref[:, h * HEAD : (h + 1) * HEAD] = jnp.dot(
                 w, value_ref[...], preferred_element_type=jnp.float32
             ).astype(jnp.bfloat16)
@@ -209,13 +214,15 @@
     return pl.pallas_call(
         kernel,
         out_shape=jax.ShapeDtypeStruct((SEQ, 512), jnp.bfloat16),
-        in_specs=[VMEM, HBM] + [VMEM] * 4,
+        in_specs=[HBM] * 2 + [VMEM] * 4,
         out_specs=VMEM,
         scratch_shapes=[
+            pltpu.VMEM((8, SEQ, 1024), jnp.bfloat16),
             pltpu.VMEM((WIDTH, 512), jnp.bfloat16),
             pltpu.SemaphoreType.DMA((8,)),
+            pltpu.SemaphoreType.DMA((8,)),
         ],
-        compiler_params=pltpu.CompilerParams(vmem_limit_bytes=48 * 1024 * 1024),
+        compiler_params=pltpu.CompilerParams(vmem_limit_bytes=56 * 1024 * 1024),
         name="attention",
     )(sequence, query_w, key, value, cosine, sine)
 

time: 230 us -> 230 us (level)
    unnamed x39 -> x47, local copies, waits for them, and re-layouts: 4.59 us -> 5.87 us
where the time goes in v8:
time: 230 us; the launch traced here: 228 us
  waiting for transfers between devices  95.5 us (42%)
  starting transfers between devices  63.2 us (27%)
  Pallas kernels  24.3 us (11%)
  local copies, waits for them, and re-layouts  15.6 us (7%)
  between operations  15.1 us (7%)
  other arithmetic  11 us (5%)
  matrix products  3.31 us (1%)
    ppermute x22, waiting for transfers between devices, shift(): lax.ppermute(array, axis, [(i, (i + by) % size) for i in range(size)])  51.1 us
    ppermute x22, starting transfers between devices, shift(): lax.ppermute(array, axis, [(i, (i + by) % size) for i in range(size)])  37.6 us
    all_to_all x4, waiting for transfers between devices, exchange(): return lax.all_to_all(array, axis, 0, 0, tiled=True)  33 us
    all_to_all x4, starting transfers between devices, exchange(): return lax.all_to_all(array, axis, 0, 0, tiled=True)  21.9 us
    pallas_call x1, Pallas kernels, prepare(): pl.pallas_call(kernel, out_shape=[jax.ShapeDtypeStruct((8, SEQ, 1024), jn...  12.4 us
    pallas_call x1, Pallas kernels, attention(): pl.pallas_call(kernel, out_shape=jax.ShapeDtypeStruct((SEQ, 512), jnp.bfl...  9.56 us
    all_gather x1, waiting for transfers between devices, step(): proj_all = lax.all_gather(proj_weight, 'z', axis=0, tiled=True)  7.25 us
    unnamed x47, local copies, waits for them, and re-layouts  5.87 us
  transfers between devices with their start and end apart: 31, of which 12 were waited for; matrix products, arithmetic and copies ran while one was open for 11% of the time, Pallas kernels for 6%

profile of v8, /device:TPU:1, one launch (start us, length us, event | category | flops | bytes accessed | tf_op | source)
XLA Modules:
  0.0 228.0 jit_solution(12014951993316260962)
XLA Ops:
  6.5 0.7 all-gather.3.cloned.1.call-update
  7.3 0.7 all-gather.5.cloned.1.call-update
  8.0 0.9 copy.41
  8.9 1.1 broadcast_in_dim.131
  10.1 6.7 %all-to-all-start = ((bf16[8,64,2,400]{3,1,2,0:T(8,128)(2,1)}), bf16[8,64,2,400]{3,1,2,0:T(8,128)(2,1)S(1)}, u32[]{:S(2)}, u32[]{:S(2)}) async-start(bf16[8,64,2,400]{3,1,2,0:T(8,128)(2,1)} %broadcast_in_dim.131), calls=%async_computation | async-start | bytes 2097152 | tf_op jit(solution)/shard_map/all_to_all | solution.py:29
  17.0 14.7 %all-to-all-done = bf16[8,64,2,400]{3,1,2,0:T(8,128)(2,1)S(1)} async-done(((bf16[8,64,2,400]{3,1,2,0:T(8,128)(2,1)}), bf16[8,64,2,400]{3,1,2,0:T(8,128)(2,1)S(1)}, u32[]{:S(2)}, u32[]{:S(2)}) %all-to-all-start) | async-done | bytes 819232 | tf_op jit(solution)/shard_map/all_to_all | solution.py:29
  32.0 0.5 fusion.5
  32.5 1.5 fusion.8
  34.0 3.5 %all-to-all-start.1 = ((bf16[4,2,64,2,400]{4,2,3,1,0:T(8,128)(2,1)}), bf16[4,2,64,2,400]{4,2,3,1,0:T(8,128)(2,1)S(1)}, u32[]{:S(2)}, u32[]{:S(2)}) async-start(bf16[4,2,64,2,400]{4,2,3,1,0:T(8,128)(2,1)} %bitcast.11), calls=%async_computation.1 | async-start | bytes 2097152 | tf_op jit(solution)/shard_map/all_to_all | solution.py:29
  38.1 0.7 fusion.24
  38.7 1.2 iota_compare_fusion
  39.9 1.3 iota_compare_fusion.2
  41.2 10.4 %all-to-all-done.1 = bf16[4,2,64,2,400]{4,2,3,1,0:T(8,128)(2,1)S(1)} async-done(((bf16[4,2,64,2,400]{4,2,3,1,0:T(8,128)(2,1)}), bf16[4,2,64,2,400]{4,2,3,1,0:T(8,128)(2,1)S(1)}, u32[]{:S(2)}, u32[]{:S(2)}) %all-to-all-start.1) | async-done | bytes 819232 | tf_op jit(solution)/shard_map/all_to_all | solution.py:29
  51.7 7.3 %all-gather.3.cloned.1.call-done = bf16[800,2,1024]{2,1,0:T(2,128)(2,1)} async-done(((bf16[100,2,1024]{2,1,0:T(2,128)(2,1)}), bf16[800,2,1024]{2,1,0:T(2,128)(2,1)}) %all-gather.3.cloned.1.call-update) | async-done | bytes 3276816 | tf_op jit(solution)/shard_map/all_gather | solution.py:265
  58.9 3.3 %fusion.12 = bf16[4,64,1024]{2,1,0:T(8,128)(2,1)S(1)} fusion(bf16[4,2,64,2,400]{4,2,3,1,0:T(8,128)(2,1)S(1)} %all-to-all-done.1, bf16[2,400,2,1024,1]{3,2,1,0,4:T(2,128)(2,1)} %bitcast.68), kind=kOutput, calls=%fused_computation.13 | convolution fusion | flops 839122944 | bytes 4620288 | tf_op jit(solution)/shard_map/sctmf,cfmo->sto/dot_general | solution.py:240
  62.3 2.8 %collective-permute-start.10 = (bf16[64,1024]{1,0:T(8,128)(2,1)S(1)}, bf16[64,1024]{1,0:T(8,128)(2,1)S(1)}, u32[]{:S(2)}, u32[]{:S(2)}) collective-permute-start(bf16[64,1024]{1,0:T(8,128)(2,1)S(1)} %get-tuple-element.15), channel_id=1, source_target_pairs={{0,128},{64,192},{128,0},{192,64},{1,129},{65,193},{129,1},{193,65... | collective-permute-start | bytes 393224 | tf_op jit(solution)/shard_map/ppermute | solution.py:25
  65.1 0.9 collective-permute-start.11
  66.0 1.1 iota_compare_fusion.4
  67.1 1.2 iota_compare_fusion.6
  68.4 2.7 %collective-permute-done.11 = bf16[64,1024]{1,0:T(8,128)(2,1)S(1)} collective-permute-done((bf16[64,1024]{1,0:T(8,128)(2,1)S(1)}, bf16[64,1024]{1,0:T(8,128)(2,1)S(1)}, u32[]{:S(2)}, u32[]{:S(2)}) %collective-permute-start.11) | collective-permute-done | bytes 131104 | tf_op jit(solution)/shard_map/ppermute | solution.py:25
  71.2 1.2 select_select_fusion
  72.4 7.5 %all-to-all-start.2 = ((bf16[32,8,1024]{2,1,0:T(8,128)(2,1)}), bf16[32,8,1024]{2,1,0:T(8,128)(2,1)S(1)}, u32[]{:S(2)}, u32[]{:S(2)}) async-start(bf16[32,8,1024]{2,1,0:T(8,128)(2,1)} %select_select_fusion), calls=%async_computation.2 | async-start | bytes 1048576 | tf_op jit(solution)/shard_map/all_to_all | solution.py:29
  80.0 1.3 collective-permute-start.13
  81.3 1.4 collective-permute-start.14
  82.7 20.4 %collective-permute-done.13.refs_1_ = bf16[256,256]{1,0:T(8,128)(2,1)S(1)} collective-permute-done((bf16[256,256]{1,0:T(8,128)(2,1)S(1)}, bf16[256,256]{1,0:T(8,128)(2,1)S(1)}, u32[]{:S(2)}, u32[]{:S(2)}) %collective-permute-start.13) | collective-permute-done | bytes 131104 | tf_op jit(solution)/shard_map/ppermute | solution.py:21
  103.1 2.7 %collective-permute-start.16 = (bf16[256,256]{1,0:T(8,128)(2,1)S(1)}, bf16[256,256]{1,0:T(8,128)(2,1)S(1)}, u32[]{:S(2)}, u32[]{:S(2)}) collective-permute-start(bf16[256,256]{1,0:T(8,128)(2,1)S(1)} %collective-permute-done.14.refs_2_), channel_id=1, source_target_pairs={{0,56},{8,0},{16,8},{24,16},{32,24},{40,32},{48,40},{56,48},{1,57}... | collective-permute-start | bytes 393224 | tf_op jit(solution)/shard_map/ppermute | solution.py:21
  105.8 1.2 collective-permute-start.1
  107.0 1.5 collective-permute-start.3
  108.5 2.7 %collective-permute-start = (bf16[384,1024]{1,0:T(8,128)(2,1)S(1)}, bf16[384,1024]{1,0:T(8,128)(2,1)S(1)}, u32[]{:S(2)}, u32[]{:S(2)}) collective-permute-start(bf16[384,1024]{1,0:T(8,128)(2,1)S(1)} %bitcast.59), channel_id=1, source_target_pairs={{0,1},{1,0},{2,3},{3,2},{4,5},{5,4},{6,7},{7,6},{8,9},{9,8},{10,11... | collective-permute-start | bytes 2359304 | tf_op jit(solution)/shard_map/ppermute | solution.py:21
  111.2 2.7 %collective-permute-start.18 = (bf16[256,256]{1,0:T(8,128)(2,1)S(1)}, bf16[256,256]{1,0:T(8,128)(2,1)S(1)}, u32[]{:S(2)}, u32[]{:S(2)}) collective-permute-start(bf16[256,256]{1,0:T(8,128)(2,1)S(1)} %collective-permute-done.16.refs_4_), channel_id=1, source_target_pairs={{0,56},{8,0},{16,8},{24,16},{32,24},{40,32},{48,40},{56,48},{1,57}... | collective-permute-start | bytes 393224 | tf_op jit(solution)/shard_map/ppermute | solution.py:21
  113.9 0.6 fusion.20
  114.5 0.6 fusion.22
  115.1 2.2 collective-permute-done.17.refs_5_
  117.5 2.7 %collective-permute-start.20 = (bf16[128,256]{1,0:T(8,128)(2,1)S(1)}, bf16[128,256]{1,0:T(8,128)(2,1)}, u32[]{:S(2)}, u32[]{:S(2)}) collective-permute-start(bf16[128,256]{1,0:T(8,128)(2,1)S(1)} %slice.109), channel_id=1, source_target_pairs={{0,56},{8,0},{16,8},{24,16},{32,24},{40,32},{48,40},{56,48},{1,57}... | collective-permute-start | bytes 196616 | tf_op jit(solution)/shard_map/ppermute | solution.py:21
  120.3 3.6 %collective-permute-done.19.refs_7_ = bf16[128,256]{1,0:T(8,128)(2,1)} collective-permute-done((bf16[128,256]{1,0:T(8,128)(2,1)S(1)}, bf16[128,256]{1,0:T(8,128)(2,1)}, u32[]{:S(2)}, u32[]{:S(2)}) %collective-permute-start.19) | collective-permute-done | bytes 65568 | tf_op jit(solution)/shard_map/ppermute | solution.py:21
  123.9 2.3 %pack.1.refs_12_ = bf16[2048,256]{1,0:T(8,128)(2,1)} custom-call(bf16[256,256]{1,0:T(8,128)(2,1)} %bitcast.64, bf16[256,256]{1,0:T(8,128)(2,1)} %copy-done.14, bf16[256,256]{1,0:T(8,128)(2,1)} %copy-done.15, bf16[256,256]{1,0:T(8,128)(2,1)} %copy-done.16, bf16[256,256]{1,0:T(8,128)(2,1)} %copy-done.17, bf16[256,256]{1,0:T(8,128)(2,1)} %copy-done.12, ...), custom_call_target="tpu_custom_call" | custom-call | tf_op jit(solution)/shard_map/pack/pallas_call | solution.py:85
  126.2 0.5 collective-permute-start.21
  126.8 2.1 collective-permute-start.22
  128.9 0.6 gather_fusion
  129.5 1.1 broadcast_in_dim.149
  130.6 4.2 %all-to-all-start.3 = ((bf16[4,128,1024]{2,1,0:T(8,128)(2,1)}), bf16[4,128,1024]{2,1,0:T(8,128)(2,1)}, u32[]{:S(2)}, u32[]{:S(2)}) async-start(bf16[4,128,1024]{2,1,0:T(8,128)(2,1)} %broadcast_in_dim.149), calls=%async_computation.3 | async-start | bytes 2097152 | tf_op jit(solution)/shard_map/all_to_all | solution.py:29
  134.9 1.5 collective-permute-start.5
  136.3 1.0 slice.99
  137.4 1.3 collective-permute-start.7
  138.7 7.8 %all-to-all-done.3.refs_10_ = bf16[4,128,1024]{2,1,0:T(8,128)(2,1)} async-done(((bf16[4,128,1024]{2,1,0:T(8,128)(2,1)}), bf16[4,128,1024]{2,1,0:T(8,128)(2,1)}, u32[]{:S(2)}, u32[]{:S(2)}) %all-to-all-start.3) | async-done | bytes 1048608 | tf_op jit(solution)/shard_map/all_to_all | solution.py:29
  146.6 8.0 %collective-permute-start.12 = (bf16[4,128,1024]{2,1,0:T(8,128)(2,1)}, bf16[4,128,1024]{2,1,0:T(8,128)(2,1)}, u32[]{:S(2)}, u32[]{:S(2)}) collective-permute-start(bf16[4,128,1024]{2,1,0:T(8,128)(2,1)} %all-to-all-done.3.refs_10_), channel_id=1, source_target_pairs={{0,1},{1,0},{2,3},{3,2},{4,5},{5,4},{6,7},{7,6},{8,9},{9,8},{10,11... | collective-permute-start | bytes 3145736 | tf_op jit(solution)/shard_map/ppermute | solution.py:21
  154.6 0.9 collective-permute-done.5.refs_6_
  155.5 3.5 %collective-permute-start.6 = (bf16[192,1024]{1,0:T(8,128)(2,1)S(1)}, bf16[192,1024]{1,0:T(8,128)(2,1)S(1)}, u32[]{:S(2)}, u32[]{:S(2)}) collective-permute-start(bf16[192,1024]{1,0:T(8,128)(2,1)S(1)} %collective-permute-done.5.refs_6_), channel_id=1, source_target_pairs={{0,1},{1,0},{2,3},{3,2},{4,5},{5,4},{6,7},{7,6},{8,9},{9,8},{10,11... | collective-permute-start | bytes 1179656 | tf_op jit(solution)/shard_map/ppermute | solution.py:21
  159.1 15.3 %collective-permute-done.21.refs_13_ = bf16[2048,256]{1,0:T(8,128)(2,1)} collective-permute-done((bf16[2048,256]{1,0:T(8,128)(2,1)}, bf16[2048,256]{1,0:T(8,128)(2,1)}, u32[]{:S(2)}, u32[]{:S(2)}) %collective-permute-start.21) | collective-permute-done | bytes 1048608 | tf_op jit(solution)/shard_map/ppermute | solution.py:21
  174.4 1.6 collective-permute-start.2
  176.0 1.9 slice.110
  177.9 1.9 slice.111
  179.7 0.8 copy-done.5
  180.5 0.8 copy-done.7
  181.3 2.7 %collective-permute-start.24 = (bf16[1024,256]{1,0:T(8,128)(2,1)}, bf16[1024,256]{1,0:T(8,128)(2,1)}, u32[]{:S(2)}, u32[]{:S(2)}) collective-permute-start(bf16[1024,256]{1,0:T(8,128)(2,1)} %slice.111), channel_id=1, source_target_pairs={{0,192},{64,0},{128,64},{192,128},{1,193},{65,1},{129,65},{193,129... | collective-permute-start | bytes 1572872 | tf_op jit(solution)/shard_map/ppermute | solution.py:21
  185.3 0.8 fusion.18
  186.3 8.6 %collective-permute-done.23.refs_15_ = bf16[1024,256]{1,0:T(8,128)(2,1)S(1)} collective-permute-done((bf16[1024,256]{1,0:T(8,128)(2,1)}, bf16[1024,256]{1,0:T(8,128)(2,1)S(1)}, u32[]{:S(2)}, u32[]{:S(2)}) %collective-permute-start.23) | collective-permute-done | bytes 524320 | tf_op jit(solution)/shard_map/ppermute | solution.py:21
  194.9 1.0 copy-done.4
  195.9 1.0 copy-done.6
  196.9 1.0 copy-done.8
  197.9 12.4 %prepare.1 = (bf16[8,384,1024]{2,1,0:T(8,128)(2,1)}, bf16[384,128]{1,0:T(8,128)(2,1)S(1)}, bf16[384,128]{1,0:T(8,128)(2,1)S(1)}) custom-call(s32[6]{0:T(128)S(1)} %stack.23.where_ref, bf16[384,1024]{1,0:T(8,128)(2,1)S(1)} %bitcast.60, bf16[384,1024]{1,0:T(8,128)(2,1)S(1)} %collective-permute-done.refs_1_, ...), custom_call_target="tpu_custom_call" | custom-call | tf_op jit(solution)/shard_map/prepare/pallas_call | solution.py:158
  210.3 0.6 copy-done.9
  211.0 0.6 copy-done.10
  211.6 9.6 %attention.1 = bf16[384,512]{1,0:T(8,128)(2,1)} custom-call(bf16[8,384,1024]{2,1,0:T(8,128)(2,1)} %get-tuple-element.8.a_hbm, bf16[8192,512]{1,0:T(8,128)(2,1)} %all-gather.5.cloned.1.call-done.w_hbm, bf16[384,128]{1,0:T(8,128)(2,1)} %copy-done.9, bf16[384,128]{1,0:T(8,128)(2,1)} %copy-done.10, f32[384,128]{1,0:T(8,128)} %copy-done, f32[384,128]{1,0:T(8,128)} %copy-done.1), custom_call_target="tpu_custom_call" | custom-call | tf_op jit(solution)/shard_map/attention/pallas_call | solution.py:214
  (92 shorter events, 1.9 us)
Async XLA Ops:
  6.5 10.2 %copy-start.20 = (f32[2,3200]{1,0:T(2,128)S(1)}, f32[2,3200]{1,0:T(2,128)}, u32[]{:S(2)}) copy-start(f32[2,3200]{1,0:T(2,128)} %param.11) | copy-start | bytes 76804
  6.5 10.3 %copy-start.21 = (f32[2,3200]{1,0:T(2,128)S(1)}, f32[2,3200]{1,0:T(2,128)}, u32[]{:S(2)}) copy-start(f32[2,3200]{1,0:T(2,128)} %param.12) | copy-start | bytes 76804
  6.5 52.4 %all-gather.3.cloned.1.call-start = ((), (), s32[]{:S(2)}) async-start(), calls=%async_computation.4 | async-start | bytes 3686400 | tf_op jit(solution)/shard_map/all_gather | solution.py:265
  7.3 204.4 %all-gather.5.cloned.1.call-start = ((), (), s32[]{:S(2)}) async-start(), calls=%async_computation.5 | async-start | bytes 8650752 | tf_op jit(solution)/shard_map/all_gather | solution.py:266
  10.1 21.7 %all-to-all-start = ((bf16[8,64,2,400]{3,1,2,0:T(8,128)(2,1)}), bf16[8,64,2,400]{3,1,2,0:T(8,128)(2,1)S(1)}, u32[]{:S(2)}, u32[]{:S(2)}) async-start(bf16[8,64,2,400]{3,1,2,0:T(8,128)(2,1)} %broadcast_in_dim.131), calls=%async_computation | async-start | bytes 2097152 | tf_op jit(solution)/shard_map/all_to_all | solution.py:29
  32.5 5.1 %copy-start.22 = (s32[32]{0:T(128)S(1)}, s32[32]{0:T(128)}, u32[]{:S(2)}) copy-start(s32[32]{0:T(128)} %param.18) | copy-start | bytes 388
  34.0 17.6 %all-to-all-start.1 = ((bf16[4,2,64,2,400]{4,2,3,1,0:T(8,128)(2,1)}), bf16[4,2,64,2,400]{4,2,3,1,0:T(8,128)(2,1)S(1)}, u32[]{:S(2)}, u32[]{:S(2)}) async-start(bf16[4,2,64,2,400]{4,2,3,1,0:T(8,128)(2,1)} %bitcast.11), calls=%async_computation.1 | async-start | bytes 2097152 | tf_op jit(solution)/shard_map/all_to_all | solution.py:29
  62.2 17.7 %copy-start.18 = (bf16[256,2,128]{2,1,0:T(2,128)(2,1)S(1)}, bf16[256,2,128]{2,1,0:T(2,128)(2,1)}, u32[]{:S(2)}) copy-start(bf16[256,2,128]{2,1,0:T(2,128)(2,1)} %param.17) | copy-start | bytes 393220
  62.3 43.6 %copy-start.2 = (bf16[1,384,1024]{2,1,0:T(8,128)(2,1)S(1)}, bf16[1,384,1024]{2,1,0:T(8,128)(2,1)}, u32[]{:S(2)}) copy-start(bf16[1,384,1024]{2,1,0:T(8,128)(2,1)} %param.14) | copy-start | bytes 2359300
  62.3 6.0 %collective-permute-start.10 = (bf16[64,1024]{1,0:T(8,128)(2,1)S(1)}, bf16[64,1024]{1,0:T(8,128)(2,1)S(1)}, u32[]{:S(2)}, u32[]{:S(2)}) collective-permute-start(bf16[64,1024]{1,0:T(8,128)(2,1)S(1)} %get-tuple-element.15), channel_id=1, source_target_pairs={{0,128},{64,192},{128,0},{192,64},{1,129},{65,193},{129,1},{193,65... | collective-permute-start | bytes 393224 | tf_op jit(solution)/shard_map/ppermute | solution.py:25
  65.1 5.9 %collective-permute-start.11 = (bf16[64,1024]{1,0:T(8,128)(2,1)S(1)}, bf16[64,1024]{1,0:T(8,128)(2,1)S(1)}, u32[]{:S(2)}, u32[]{:S(2)}) collective-permute-start(bf16[64,1024]{1,0:T(8,128)(2,1)S(1)} %get-tuple-element.14), channel_id=1, source_target_pairs={{0,192},{64,128},{128,64},{192,0},{1,193},{65,129},{129,65},{193,1... | collective-permute-start | bytes 393224 | tf_op jit(solution)/shard_map/ppermute | solution.py:25
  66.0 5.1 %collective-permute-start.9 = (bf16[64,1024]{1,0:T(8,128)(2,1)S(1)}, bf16[64,1024]{1,0:T(8,128)(2,1)S(1)}, u32[]{:S(2)}, u32[]{:S(2)}) collective-permute-start(bf16[64,1024]{1,0:T(8,128)(2,1)S(1)} %get-tuple-element.13), channel_id=1, source_target_pairs={{0,64},{64,0},{128,192},{192,128},{1,65},{65,1},{129,193},{193,129... | collective-permute-start | bytes 393224 | tf_op jit(solution)/shard_map/ppermute | solution.py:25
  72.4 56.5 %all-to-all-start.2 = ((bf16[32,8,1024]{2,1,0:T(8,128)(2,1)}), bf16[32,8,1024]{2,1,0:T(8,128)(2,1)S(1)}, u32[]{:S(2)}, u32[]{:S(2)}) async-start(bf16[32,8,1024]{2,1,0:T(8,128)(2,1)} %select_select_fusion), calls=%async_computation.2 | async-start | bytes 1048576 | tf_op jit(solution)/shard_map/all_to_all | solution.py:29
  79.9 43.9 %copy-start.11 = (bf16[32,8,2,128]{3,1,2,0:T(8,128)(2,1)}, bf16[32,8,2,128]{3,1,2,0:T(8,128)(2,1)S(1)}, u32[]{:S(2)}) copy-start(bf16[32,8,2,128]{3,1,2,0:T(8,128)(2,1)S(1)} %copy.65) | copy-start | bytes 393220
  80.0 23.2 %collective-permute-start.13 = (bf16[256,256]{1,0:T(8,128)(2,1)S(1)}, bf16[256,256]{1,0:T(8,128)(2,1)S(1)}, u32[]{:S(2)}, u32[]{:S(2)}) collective-permute-start(bf16[256,256]{1,0:T(8,128)(2,1)S(1)} %bitcast.62), channel_id=1, source_target_pairs={{0,8},{8,16},{16,24},{24,32},{32,40},{40,48},{48,56},{56,0},{1,9},... | collective-permute-start | bytes 393224 | tf_op jit(solution)/shard_map/ppermute | solution.py:21
  81.3 21.9 %collective-permute-start.14 = (bf16[256,256]{1,0:T(8,128)(2,1)S(1)}, bf16[256,256]{1,0:T(8,128)(2,1)S(1)}, u32[]{:S(2)}, u32[]{:S(2)}) collective-permute-start(bf16[256,256]{1,0:T(8,128)(2,1)S(1)} %bitcast.63), channel_id=1, source_target_pairs={{0,56},{8,0},{16,8},{24,16},{32,24},{40,32},{48,40},{56,48},{1,57}... | collective-permute-start | bytes 393224 | tf_op jit(solution)/shard_map/ppermute | solution.py:21
  103.1 20.7 %copy-start.14 = (bf16[256,256]{1,0:T(8,128)(2,1)}, bf16[256,256]{1,0:T(8,128)(2,1)S(1)}, u32[]{:S(2)}) copy-start(bf16[256,256]{1,0:T(8,128)(2,1)S(1)} %collective-permute-done.13.refs_1_) | copy-start | bytes 393220
  103.1 8.1 %collective-permute-start.15 = (bf16[256,256]{1,0:T(8,128)(2,1)S(1)}, bf16[256,256]{1,0:T(8,128)(2,1)S(1)}, u32[]{:S(2)}, u32[]{:S(2)}) collective-permute-start(bf16[256,256]{1,0:T(8,128)(2,1)S(1)} %collective-permute-done.13.refs_1_), channel_id=1, source_target_pairs={{0,8},{8,16},{16,24},{24,32},{32,40},{40,48},{48,56},{56,0},{1,9},... | collective-permute-start | bytes 393224 | tf_op jit(solution)/shard_map/ppermute | solution.py:21
  103.1 20.7 %copy-start.15 = (bf16[256,256]{1,0:T(8,128)(2,1)}, bf16[256,256]{1,0:T(8,128)(2,1)S(1)}, u32[]{:S(2)}) copy-start(bf16[256,256]{1,0:T(8,128)(2,1)S(1)} %collective-permute-done.14.refs_2_) | copy-start | bytes 393220
  103.1 8.1 %collective-permute-start.16 = (bf16[256,256]{1,0:T(8,128)(2,1)S(1)}, bf16[256,256]{1,0:T(8,128)(2,1)S(1)}, u32[]{:S(2)}, u32[]{:S(2)}) collective-permute-start(bf16[256,256]{1,0:T(8,128)(2,1)S(1)} %collective-permute-done.14.refs_2_), channel_id=1, source_target_pairs={{0,56},{8,0},{16,8},{24,16},{32,24},{40,32},{48,40},{56,48},{1,57}... | collective-permute-start | bytes 393224 | tf_op jit(solution)/shard_map/ppermute | solution.py:21
  105.8 29.0 %collective-permute-start.1 = (bf16[384,1024]{1,0:T(8,128)(2,1)S(1)}, bf16[384,1024]{1,0:T(8,128)(2,1)S(1)}, u32[]{:S(2)}, u32[]{:S(2)}) collective-permute-start(bf16[384,1024]{1,0:T(8,128)(2,1)S(1)} %bitcast.57), channel_id=1, source_target_pairs={{0,2},{2,4},{4,6},{6,0},{1,3},{3,5},{5,7},{7,1},{8,10},{10,12},{12... | collective-permute-start | bytes 2359304 | tf_op jit(solution)/shard_map/ppermute | solution.py:21
  107.0 29.3 %collective-permute-start.3 = (bf16[384,1024]{1,0:T(8,128)(2,1)S(1)}, bf16[384,1024]{1,0:T(8,128)(2,1)}, u32[]{:S(2)}, u32[]{:S(2)}) collective-permute-start(bf16[384,1024]{1,0:T(8,128)(2,1)S(1)} %bitcast.58), channel_id=1, source_target_pairs={{0,6},{2,0},{4,2},{6,4},{1,7},{3,1},{5,3},{7,5},{8,14},{10,8},{12,... | collective-permute-start | bytes 2359304 | tf_op jit(solution)/shard_map/ppermute | solution.py:21
  108.5 30.2 %collective-permute-start = (bf16[384,1024]{1,0:T(8,128)(2,1)S(1)}, bf16[384,1024]{1,0:T(8,128)(2,1)S(1)}, u32[]{:S(2)}, u32[]{:S(2)}) collective-permute-start(bf16[384,1024]{1,0:T(8,128)(2,1)S(1)} %bitcast.59), channel_id=1, source_target_pairs={{0,1},{1,0},{2,3},{3,2},{4,5},{5,4},{6,7},{7,6},{8,9},{9,8},{10,11... | collective-permute-start | bytes 2359304 | tf_op jit(solution)/shard_map/ppermute | solution.py:21
  111.2 6.3 %copy-start.16 = (bf16[256,256]{1,0:T(8,128)(2,1)}, bf16[256,256]{1,0:T(8,128)(2,1)S(1)}, u32[]{:S(2)}) copy-start(bf16[256,256]{1,0:T(8,128)(2,1)S(1)} %collective-permute-done.15.refs_3_) | copy-start | bytes 393220
  111.2 6.2 %collective-permute-start.17 = (bf16[256,256]{1,0:T(8,128)(2,1)S(1)}, bf16[256,256]{1,0:T(8,128)(2,1)S(1)}, u32[]{:S(2)}, u32[]{:S(2)}) collective-permute-start(bf16[256,256]{1,0:T(8,128)(2,1)S(1)} %collective-permute-done.15.refs_3_), channel_id=1, source_target_pairs={{0,8},{8,16},{16,24},{24,32},{32,40},{40,48},{48,56},{56,0},{1,9},... | collective-permute-start | bytes 393224 | tf_op jit(solution)/shard_map/ppermute | solution.py:21
  111.2 6.3 %copy-start.17 = (bf16[256,256]{1,0:T(8,128)(2,1)}, bf16[256,256]{1,0:T(8,128)(2,1)S(1)}, u32[]{:S(2)}) copy-start(bf16[256,256]{1,0:T(8,128)(2,1)S(1)} %collective-permute-done.16.refs_4_) | copy-start | bytes 393220
  111.2 6.3 %collective-permute-start.18 = (bf16[256,256]{1,0:T(8,128)(2,1)S(1)}, bf16[256,256]{1,0:T(8,128)(2,1)S(1)}, u32[]{:S(2)}, u32[]{:S(2)}) collective-permute-start(bf16[256,256]{1,0:T(8,128)(2,1)S(1)} %collective-permute-done.16.refs_4_), channel_id=1, source_target_pairs={{0,56},{8,0},{16,8},{24,16},{32,24},{40,32},{48,40},{56,48},{1,57}... | collective-permute-start | bytes 393224 | tf_op jit(solution)/shard_map/ppermute | solution.py:21
  117.4 6.5 %copy-start.12 = (bf16[256,256]{1,0:T(8,128)(2,1)}, bf16[256,256]{1,0:T(8,128)(2,1)S(1)}, u32[]{:S(2)}) copy-start(bf16[256,256]{1,0:T(8,128)(2,1)S(1)} %collective-permute-done.17.refs_5_) | copy-start | bytes 393220
  117.4 6.4 %collective-permute-start.19 = (bf16[128,256]{1,0:T(8,128)(2,1)S(1)}, bf16[128,256]{1,0:T(8,128)(2,1)}, u32[]{:S(2)}, u32[]{:S(2)}) collective-permute-start(bf16[128,256]{1,0:T(8,128)(2,1)S(1)} %slice.108), channel_id=1, source_target_pairs={{0,8},{8,16},{16,24},{24,32},{32,40},{40,48},{48,56},{56,0},{1,9},... | collective-permute-start | bytes 196616 | tf_op jit(solution)/shard_map/ppermute | solution.py:21
  117.5 6.4 %copy-start.13 = (bf16[256,256]{1,0:T(8,128)(2,1)}, bf16[256,256]{1,0:T(8,128)(2,1)S(1)}, u32[]{:S(2)}) copy-start(bf16[256,256]{1,0:T(8,128)(2,1)S(1)} %collective-permute-done.18.refs_6_) | copy-start | bytes 393220
  117.5 6.3 %collective-permute-start.20 = (bf16[128,256]{1,0:T(8,128)(2,1)S(1)}, bf16[128,256]{1,0:T(8,128)(2,1)}, u32[]{:S(2)}, u32[]{:S(2)}) collective-permute-start(bf16[128,256]{1,0:T(8,128)(2,1)S(1)} %slice.109), channel_id=1, source_target_pairs={{0,56},{8,0},{16,8},{24,16},{32,24},{40,32},{48,40},{56,48},{1,57}... | collective-permute-start | bytes 196616 | tf_op jit(solution)/shard_map/ppermute | solution.py:21
  126.2 48.2 %collective-permute-start.21 = (bf16[2048,256]{1,0:T(8,128)(2,1)}, bf16[2048,256]{1,0:T(8,128)(2,1)}, u32[]{:S(2)}, u32[]{:S(2)}) collective-permute-start(bf16[2048,256]{1,0:T(8,128)(2,1)} %pack.1.refs_12_), channel_id=1, source_target_pairs={{0,64},{64,128},{128,192},{192,0},{1,65},{65,129},{129,193},{193,1... | collective-permute-start | bytes 3145736 | tf_op jit(solution)/shard_map/ppermute | solution.py:21
  126.8 49.2 %collective-permute-start.22 = (bf16[2048,256]{1,0:T(8,128)(2,1)}, bf16[2048,256]{1,0:T(8,128)(2,1)}, u32[]{:S(2)}, u32[]{:S(2)}) collective-permute-start(bf16[2048,256]{1,0:T(8,128)(2,1)} %pack.1.refs_12_), channel_id=1, source_target_pairs={{0,192},{64,0},{128,64},{192,128},{1,193},{65,1},{129,65},{193,129... | collective-permute-start | bytes 3145736 | tf_op jit(solution)/shard_map/ppermute | solution.py:21
  130.6 16.0 %all-to-all-start.3 = ((bf16[4,128,1024]{2,1,0:T(8,128)(2,1)}), bf16[4,128,1024]{2,1,0:T(8,128)(2,1)}, u32[]{:S(2)}, u32[]{:S(2)}) async-start(bf16[4,128,1024]{2,1,0:T(8,128)(2,1)} %broadcast_in_dim.149), calls=%async_computation.3 | async-start | bytes 2097152 | tf_op jit(solution)/shard_map/all_to_all | solution.py:29
  134.9 20.6 %collective-permute-start.5 = (bf16[192,1024]{1,0:T(8,128)(2,1)S(1)}, bf16[192,1024]{1,0:T(8,128)(2,1)S(1)}, u32[]{:S(2)}, u32[]{:S(2)}) collective-permute-start(bf16[192,1024]{1,0:T(8,128)(2,1)S(1)} %slice.98), channel_id=1, source_target_pairs={{0,2},{2,4},{4,6},{6,0},{1,3},{3,5},{5,7},{7,1},{8,10},{10,12},{12... | collective-permute-start | bytes 1179656 | tf_op jit(solution)/shard_map/ppermute | solution.py:21
  137.4 21.6 %collective-permute-start.7 = (bf16[192,1024]{1,0:T(8,128)(2,1)S(1)}, bf16[192,1024]{1,0:T(8,128)(2,1)}, u32[]{:S(2)}, u32[]{:S(2)}) collective-permute-start(bf16[192,1024]{1,0:T(8,128)(2,1)S(1)} %slice.99), channel_id=1, source_target_pairs={{0,6},{2,0},{4,2},{6,4},{1,7},{3,1},{5,3},{7,5},{8,14},{10,8},{12,... | collective-permute-start | bytes 1179656 | tf_op jit(solution)/shard_map/ppermute | solution.py:21
  146.6 48.3 %collective-permute-start.12 = (bf16[4,128,1024]{2,1,0:T(8,128)(2,1)}, bf16[4,128,1024]{2,1,0:T(8,128)(2,1)}, u32[]{:S(2)}, u32[]{:S(2)}) collective-permute-start(bf16[4,128,1024]{2,1,0:T(8,128)(2,1)} %all-to-all-done.3.refs_10_), channel_id=1, source_target_pairs={{0,1},{1,0},{2,3},{3,2},{4,5},{5,4},{6,7},{7,6},{8,9},{9,8},{10,11... | collective-permute-start | bytes 3145736 | tf_op jit(solution)/shard_map/ppermute | solution.py:21
  155.5 30.6 %copy-start.3 = (bf16[192,1024]{1,0:T(8,128)(2,1)}, bf16[192,1024]{1,0:T(8,128)(2,1)S(1)}, u32[]{:S(2)}) copy-start(bf16[192,1024]{1,0:T(8,128)(2,1)S(1)} %collective-permute-done.5.refs_6_) | copy-start | bytes 1179652
  155.5 24.3 %collective-permute-start.6 = (bf16[192,1024]{1,0:T(8,128)(2,1)S(1)}, bf16[192,1024]{1,0:T(8,128)(2,1)S(1)}, u32[]{:S(2)}, u32[]{:S(2)}) collective-permute-start(bf16[192,1024]{1,0:T(8,128)(2,1)S(1)} %collective-permute-done.5.refs_6_), channel_id=1, source_target_pairs={{0,1},{1,0},{2,3},{3,2},{4,5},{5,4},{6,7},{7,6},{8,9},{9,8},{10,11... | collective-permute-start | bytes 1179656 | tf_op jit(solution)/shard_map/ppermute | solution.py:21
  159.0 26.2 %copy-start.19 = (f32[8192]{0:T(1024)S(1)}, f32[8192]{0:T(1024)}, u32[]{:S(2)}) copy-start(f32[8192]{0:T(1024)} %param.15) | copy-start | bytes 98308
  159.0 21.5 %collective-permute-start.8 = (bf16[192,1024]{1,0:T(8,128)(2,1)}, bf16[192,1024]{1,0:T(8,128)(2,1)S(1)}, u32[]{:S(2)}, u32[]{:S(2)}) collective-permute-start(bf16[192,1024]{1,0:T(8,128)(2,1)} %collective-permute-done.7.refs_8_), channel_id=1, source_target_pairs={{0,1},{1,0},{2,3},{3,2},{4,5},{5,4},{6,7},{7,6},{8,9},{9,8},{10,11... | collective-permute-start | bytes 1179656 | tf_op jit(solution)/shard_map/ppermute | solution.py:21
  174.4 11.9 %collective-permute-start.2 = (bf16[384,1024]{1,0:T(8,128)(2,1)S(1)}, bf16[384,1024]{1,0:T(8,128)(2,1)}, u32[]{:S(2)}, u32[]{:S(2)}) collective-permute-start(bf16[384,1024]{1,0:T(8,128)(2,1)S(1)} %collective-permute-done.1.refs_2_), channel_id=1, source_target_pairs={{0,1},{1,0},{2,3},{3,2},{4,5},{5,4},{6,7},{7,6},{8,9},{9,8},{10,11... | collective-permute-start | bytes 2359304 | tf_op jit(solution)/shard_map/ppermute | solution.py:21
  176.0 10.3 %collective-permute-start.4 = (bf16[384,1024]{1,0:T(8,128)(2,1)}, bf16[384,1024]{1,0:T(8,128)(2,1)}, u32[]{:S(2)}, u32[]{:S(2)}) collective-permute-start(bf16[384,1024]{1,0:T(8,128)(2,1)} %collective-permute-done.3.refs_4_), channel_id=1, source_target_pairs={{0,1},{1,0},{2,3},{3,2},{4,5},{5,4},{6,7},{7,6},{8,9},{9,8},{10,11... | collective-permute-start | bytes 2359304 | tf_op jit(solution)/shard_map/ppermute | solution.py:21
  179.7 0.8 copy-start.5
  180.5 14.4 %collective-permute-start.23 = (bf16[1024,256]{1,0:T(8,128)(2,1)}, bf16[1024,256]{1,0:T(8,128)(2,1)S(1)}, u32[]{:S(2)}, u32[]{:S(2)}) collective-permute-start(bf16[1024,256]{1,0:T(8,128)(2,1)} %slice.110), channel_id=1, source_target_pairs={{0,64},{64,128},{128,192},{192,0},{1,65},{65,129},{129,193},{193,1... | collective-permute-start | bytes 1572872 | tf_op jit(solution)/shard_map/ppermute | solution.py:21
  180.5 0.8 copy-start.7
  181.3 13.6 %collective-permute-start.24 = (bf16[1024,256]{1,0:T(8,128)(2,1)}, bf16[1024,256]{1,0:T(8,128)(2,1)}, u32[]{:S(2)}, u32[]{:S(2)}) collective-permute-start(bf16[1024,256]{1,0:T(8,128)(2,1)} %slice.111), channel_id=1, source_target_pairs={{0,192},{64,0},{128,64},{192,128},{1,193},{65,1},{129,65},{193,129... | collective-permute-start | bytes 1572872 | tf_op jit(solution)/shard_map/ppermute | solution.py:21
  186.3 24.1 %copy-start = (f32[384,128]{1,0:T(8,128)}, f32[384,128]{1,0:T(8,128)S(1)}, u32[]{:S(2)}) copy-start(f32[384,128]{1,0:T(8,128)S(1)} %get-tuple-element.45.refs_18_.cos_ref) | copy-start | bytes 589828
  186.3 24.1 %copy-start.1 = (f32[384,128]{1,0:T(8,128)}, f32[384,128]{1,0:T(8,128)S(1)}, u32[]{:S(2)}) copy-start(f32[384,128]{1,0:T(8,128)S(1)} %get-tuple-element.46.refs_19_.sin_ref) | copy-start | bytes 589828
  194.9 1.0 copy-start.4
  195.9 1.0 copy-start.6
  196.9 1.0 copy-start.8
  210.3 0.6 copy-start.9
  211.0 0.6 copy-start.10
Sparse Core Ops, SparseCore 0:
  9.1 49.7 all-gather.2
  61.5 121.9 all-gather.4
